TPU v7x, 32 devices: a whole 2x2x4 slice. The times are simulated.
32 devices in a mesh: freq: 2 (over x), base: 4 (over y, core), pix: 4 (over z).
Axes of the slice: x: 2, y: 2, z: 4, core: 2. Of those that a mesh axis runs over, the one named last changes fastest.
Arguments:
- sensing_operator_parts: bfloat16 [2, 4096, 2048], P('freq', 'base', 'pix'), may hold values from -1 to 1
- sampled_correlations: float32 [64, 4096], P('freq', 'base'), may hold values from -40 to 40
- first_sky_estimate: float32 [64, 4, 4, 128], P('freq', 'pix', 'base'), may hold values from -2.5 to 2.5
- patch_order_record: int32 [6, 16], P(None, 'pix'), may hold values from 0 to 15, as said below
Outputs:
- image: float32 [64, 4, 4, 128], P('freq', 'pix', 'base')
Inputs may be any that keep to these rules, and one draw needn't show every extreme that they name: `patch_order_record`: each row holds every tile number once; the tiles of rank under 4 are the same in every row.
All inputs are finite; a program needn't handle non-finite values.
Results may differ from a plain program's by a relative error of at most 0.0014.
Values may be sent and summed in bfloat16 or wider, within the bound.
No kernel may reach another device: no remote copies, remote signals or barrier semaphores. Data moves between devices by JAX's collectives and lax.ppermute only.
A program may use at most 64 MiB of HBM per device.

v0:
```python
import jax
import jax.numpy as jnp
from jax import lax
from jax.sharding import PartitionSpec as P

CH = 64
TILE = 128
ITERS = 6


descent_stride = 0.6
lam_shrink = 0.3
eps_norm = 1e-06


def project_rows(rounded_amount, columns):
    return lax.dot_general(
        rounded_amount, columns, (((1,), (1,)), ((), ())), preferred_element_type=jnp.float32
    )


def residual_of(sampled_correlations, partial_value):
    shares = lax.psum_scatter(partial_value, "pix", scatter_dimension=1, tiled=True)
    width = shares.shape[1]
    own_rows = lax.dynamic_slice_in_dim(
        sampled_correlations, lax.axis_index("pix") * width, width, 1
    )
    return lax.all_gather((own_rows - shares).astype(jnp.bfloat16), "pix", axis=1, tiled=True)


def on_device(sensing_operator_parts, sampled_correlations, first_sky_estimate, patch_order_record):
    sensing_operator = sensing_operator_parts[0]
    chans, m_dev = sampled_correlations.shape
    share_width = first_sky_estimate.shape[3]
    tiles_share = share_width // TILE
    keep_count = tiles_share * lax.axis_size("base") * lax.axis_size("pix") // 4
    base_index = lax.axis_index("base")
    own_share = first_sky_estimate[:, 0, 0, :]
    current = own_share
    for step in range(ITERS):
        rounded_amount = current.astype(jnp.bfloat16)
        partial_value = project_rows(
            lax.all_gather(rounded_amount, "base", axis=1, tiled=True), sensing_operator
        )
        resid = residual_of(sampled_correlations, partial_value)
        gradient_portion = jnp.dot(resid, sensing_operator, preferred_element_type=jnp.float32)
        grad_share = lax.psum_scatter(gradient_portion, "base", scatter_dimension=1, tiled=True)
        moved = current + descent_stride * grad_share
        tiles = moved.reshape(chans, tiles_share, TILE)
        local_sum = jnp.sum(tiles * tiles, axis=(0, 2))
        total = lax.psum(local_sum, "freq")
        ranks = lax.dynamic_slice_in_dim(
            patch_order_record[step], base_index * tiles_share, tiles_share, 0
        )
        rms_tile = jnp.sqrt(total / (CH * TILE) + eps_norm)
        keeping = (ranks < keep_count).astype(jnp.float32)
        factor = keeping * rms_tile / (rms_tile + lam_shrink)
        current = (tiles * factor[None, :, None]).reshape(chans, share_width)
    return current.reshape(chans, 1, 1, share_width)


def solution(mesh):
    in_specs = (
        P("freq", "base", "pix"),
        P("freq", "base"),
        P("freq", "pix", "base", None),
        P(None, "pix"),
    )
    out_specs = P("freq", "pix", "base", None)
    return jax.shard_map(
        on_device, mesh=mesh, in_specs=in_specs, out_specs=out_specs, check_vma=False
    )
```

profile of v0, /device:TPU:0, one launch (start us, length us, event | category | flops | bytes accessed | tf_op | source)
XLA Modules:
  0.0 418.8 jit_solution(5193370528719612826)
XLA Ops:
  7.3 6.1 %all_gather.36 = bf16[32,512]{1,0:T(8,128)(2,1)S(1)} all-gather(bf16[32,128]{1,0:T(8,128)(2,1)S(1)} %convert_element_type.42), channel_id=1, replica_groups=mesh['freq'=2,'base'=4,'pix'=4] {'base'}, dimensions={1}, use_global_device_ids=true | all-gather | bytes 40960 | tf_op jit(solution)/shard_map/all_gather | solution.py:43
  13.5 1.1 fusion.22
  14.6 21.3 %reduce-scatter.13.cloned.1.call-done = f32[32,256]{1,0:T(8,128)} async-done(((f32[32,1024]{1,0:T(8,128)}), f32[32,256]{1,0:T(8,128)}) %reduce-scatter.13.cloned.1.call-update) | async-done | bytes 32784 | tf_op jit(solution)/shard_map/reduce_scatter | solution.py:23
  36.7 13.1 %all_gather.37 = bf16[32,1024]{1,0:T(8,128)(2,1)S(1)} all-gather(bf16[32,256]{1,0:T(8,128)(2,1)S(1)} %subtract_convert_fusion.5), channel_id=1, replica_groups=mesh['freq'=2,'base'=4,'pix'=4] {'pix'}, dimensions={1}, use_global_device_ids=true | all-gather | bytes 81920 | tf_op jit(solution)/shard_map/all_gather | solution.py:28
  49.8 0.9 fusion.20
  52.0 16.6 %reduce-scatter.15.cloned.1.call-done = f32[32,128]{1,0:T(8,128)} async-done(((f32[32,512]{1,0:T(8,128)}), f32[32,128]{1,0:T(8,128)}) %reduce-scatter.15.cloned.1.call-update) | async-done | bytes 16400 | tf_op jit(solution)/shard_map/reduce_scatter | solution.py:47
  68.6 1.4 multiply_reduce_fusion.5
  70.0 5.5 %psum.42 = f32[1]{0:T(128)} all-reduce(f32[1]{0:T(128)} %bitcast.3), channel_id=1, replica_groups=mesh['freq'=2,'base'=4,'pix'=4] {'freq'}, use_global_device_ids=true, to_apply=%region_3.0 | all-reduce | flops 1 | bytes 8 | tf_op jit(solution)/shard_map/psum | solution.py:51
  76.9 5.2 %all_gather.38 = bf16[32,512]{1,0:T(8,128)(2,1)S(1)} all-gather(bf16[32,128]{1,0:T(8,128)(2,1)S(1)} %multiply_convert_fusion.4), channel_id=1, replica_groups=mesh['freq'=2,'base'=4,'pix'=4] {'base'}, dimensions={1}, use_global_device_ids=true | all-gather | bytes 40960 | tf_op jit(solution)/shard_map/all_gather | solution.py:43
  82.1 1.1 fusion.18
  83.2 19.6 %reduce-scatter.17.cloned.1.call-done = f32[32,256]{1,0:T(8,128)} async-done(((f32[32,1024]{1,0:T(8,128)}), f32[32,256]{1,0:T(8,128)}) %reduce-scatter.17.cloned.1.call-update) | async-done | bytes 32784 | tf_op jit(solution)/shard_map/reduce_scatter | solution.py:23
  103.5 13.1 %all_gather.39 = bf16[32,1024]{1,0:T(8,128)(2,1)S(1)} all-gather(bf16[32,256]{1,0:T(8,128)(2,1)S(1)} %subtract_convert_fusion.4), channel_id=1, replica_groups=mesh['freq'=2,'base'=4,'pix'=4] {'pix'}, dimensions={1}, use_global_device_ids=true | all-gather | bytes 81920 | tf_op jit(solution)/shard_map/all_gather | solution.py:28
  116.6 0.9 fusion.16
  118.2 17.3 %reduce-scatter.19.cloned.1.call-done = f32[32,128]{1,0:T(8,128)} async-done(((f32[32,512]{1,0:T(8,128)}), f32[32,128]{1,0:T(8,128)}) %reduce-scatter.19.cloned.1.call-update) | async-done | bytes 16400 | tf_op jit(solution)/shard_map/reduce_scatter | solution.py:47
  135.5 1.4 multiply_reduce_fusion.4
  136.9 5.5 %psum.43 = f32[1]{0:T(128)} all-reduce(f32[1]{0:T(128)} %bitcast.6), channel_id=1, replica_groups=mesh['freq'=2,'base'=4,'pix'=4] {'freq'}, use_global_device_ids=true, to_apply=%region_7.0 | all-reduce | flops 1 | bytes 8 | tf_op jit(solution)/shard_map/psum | solution.py:51
  143.8 5.2 %all_gather.40 = bf16[32,512]{1,0:T(8,128)(2,1)S(1)} all-gather(bf16[32,128]{1,0:T(8,128)(2,1)S(1)} %multiply_convert_fusion.3), channel_id=1, replica_groups=mesh['freq'=2,'base'=4,'pix'=4] {'base'}, dimensions={1}, use_global_device_ids=true | all-gather | bytes 40960 | tf_op jit(solution)/shard_map/all_gather | solution.py:43
  149.0 1.1 fusion.14
  150.1 19.6 %reduce-scatter.21.cloned.1.call-done = f32[32,256]{1,0:T(8,128)} async-done(((f32[32,1024]{1,0:T(8,128)}), f32[32,256]{1,0:T(8,128)}) %reduce-scatter.21.cloned.1.call-update) | async-done | bytes 32784 | tf_op jit(solution)/shard_map/reduce_scatter | solution.py:23
  170.5 13.1 %all_gather.41 = bf16[32,1024]{1,0:T(8,128)(2,1)S(1)} all-gather(bf16[32,256]{1,0:T(8,128)(2,1)S(1)} %subtract_convert_fusion.3), channel_id=1, replica_groups=mesh['freq'=2,'base'=4,'pix'=4] {'pix'}, dimensions={1}, use_global_device_ids=true | all-gather | bytes 81920 | tf_op jit(solution)/shard_map/all_gather | solution.py:28
  183.6 0.9 fusion.12
  185.1 17.3 %reduce-scatter.23.cloned.1.call-done = f32[32,128]{1,0:T(8,128)} async-done(((f32[32,512]{1,0:T(8,128)}), f32[32,128]{1,0:T(8,128)}) %reduce-scatter.23.cloned.1.call-update) | async-done | bytes 16400 | tf_op jit(solution)/shard_map/reduce_scatter | solution.py:47
  202.4 1.4 multiply_reduce_fusion.3
  203.8 5.5 %psum.44 = f32[1]{0:T(128)} all-reduce(f32[1]{0:T(128)} %bitcast.9), channel_id=1, replica_groups=mesh['freq'=2,'base'=4,'pix'=4] {'freq'}, use_global_device_ids=true, to_apply=%region_11.0 | all-reduce | flops 1 | bytes 8 | tf_op jit(solution)/shard_map/psum | solution.py:51
  210.7 5.2 %all_gather.42 = bf16[32,512]{1,0:T(8,128)(2,1)S(1)} all-gather(bf16[32,128]{1,0:T(8,128)(2,1)S(1)} %multiply_convert_fusion.2), channel_id=1, replica_groups=mesh['freq'=2,'base'=4,'pix'=4] {'base'}, dimensions={1}, use_global_device_ids=true | all-gather | bytes 40960 | tf_op jit(solution)/shard_map/all_gather | solution.py:43
  215.9 1.1 fusion.10
  217.0 19.6 %reduce-scatter.25.cloned.1.call-done = f32[32,256]{1,0:T(8,128)} async-done(((f32[32,1024]{1,0:T(8,128)}), f32[32,256]{1,0:T(8,128)}) %reduce-scatter.25.cloned.1.call-update) | async-done | bytes 32784 | tf_op jit(solution)/shard_map/reduce_scatter | solution.py:23
  237.3 13.1 %all_gather.43 = bf16[32,1024]{1,0:T(8,128)(2,1)S(1)} all-gather(bf16[32,256]{1,0:T(8,128)(2,1)S(1)} %subtract_convert_fusion.2), channel_id=1, replica_groups=mesh['freq'=2,'base'=4,'pix'=4] {'pix'}, dimensions={1}, use_global_device_ids=true | all-gather | bytes 81920 | tf_op jit(solution)/shard_map/all_gather | solution.py:28
  250.4 0.9 fusion.8
  252.0 17.3 %reduce-scatter.27.cloned.1.call-done = f32[32,128]{1,0:T(8,128)} async-done(((f32[32,512]{1,0:T(8,128)}), f32[32,128]{1,0:T(8,128)}) %reduce-scatter.27.cloned.1.call-update) | async-done | bytes 16400 | tf_op jit(solution)/shard_map/reduce_scatter | solution.py:47
  269.3 1.4 multiply_reduce_fusion.2
  270.7 5.5 %psum.45 = f32[1]{0:T(128)} all-reduce(f32[1]{0:T(128)} %bitcast.12), channel_id=1, replica_groups=mesh['freq'=2,'base'=4,'pix'=4] {'freq'}, use_global_device_ids=true, to_apply=%region_15.0 | all-reduce | flops 1 | bytes 8 | tf_op jit(solution)/shard_map/psum | solution.py:51
  277.6 5.2 %all_gather.44 = bf16[32,512]{1,0:T(8,128)(2,1)S(1)} all-gather(bf16[32,128]{1,0:T(8,128)(2,1)S(1)} %multiply_convert_fusion.1), channel_id=1, replica_groups=mesh['freq'=2,'base'=4,'pix'=4] {'base'}, dimensions={1}, use_global_device_ids=true | all-gather | bytes 40960 | tf_op jit(solution)/shard_map/all_gather | solution.py:43
  282.8 1.1 fusion.6
  283.9 19.6 %reduce-scatter.29.cloned.1.call-done = f32[32,256]{1,0:T(8,128)} async-done(((f32[32,1024]{1,0:T(8,128)}), f32[32,256]{1,0:T(8,128)}) %reduce-scatter.29.cloned.1.call-update) | async-done | bytes 32784 | tf_op jit(solution)/shard_map/reduce_scatter | solution.py:23
  304.2 13.1 %all_gather.45 = bf16[32,1024]{1,0:T(8,128)(2,1)S(1)} all-gather(bf16[32,256]{1,0:T(8,128)(2,1)S(1)} %subtract_convert_fusion.1), channel_id=1, replica_groups=mesh['freq'=2,'base'=4,'pix'=4] {'pix'}, dimensions={1}, use_global_device_ids=true | all-gather | bytes 81920 | tf_op jit(solution)/shard_map/all_gather | solution.py:28
  317.3 0.9 fusion.4
  318.9 17.3 %reduce-scatter.31.cloned.1.call-done = f32[32,128]{1,0:T(8,128)} async-done(((f32[32,512]{1,0:T(8,128)}), f32[32,128]{1,0:T(8,128)}) %reduce-scatter.31.cloned.1.call-update) | async-done | bytes 16400 | tf_op jit(solution)/shard_map/reduce_scatter | solution.py:47
  336.2 1.4 multiply_reduce_fusion.1
  337.6 5.5 %psum.46 = f32[1]{0:T(128)} all-reduce(f32[1]{0:T(128)} %bitcast.15), channel_id=1, replica_groups=mesh['freq'=2,'base'=4,'pix'=4] {'freq'}, use_global_device_ids=true, to_apply=%region_19.0 | all-reduce | flops 1 | bytes 8 | tf_op jit(solution)/shard_map/psum | solution.py:51
  344.5 5.2 %all_gather.46 = bf16[32,512]{1,0:T(8,128)(2,1)S(1)} all-gather(bf16[32,128]{1,0:T(8,128)(2,1)S(1)} %multiply_convert_fusion), channel_id=1, replica_groups=mesh['freq'=2,'base'=4,'pix'=4] {'base'}, dimensions={1}, use_global_device_ids=true | all-gather | bytes 40960 | tf_op jit(solution)/shard_map/all_gather | solution.py:43
  349.7 1.1 fusion.2
  350.8 19.6 %reduce-scatter.33.cloned.1.call-done = f32[32,256]{1,0:T(8,128)} async-done(((f32[32,1024]{1,0:T(8,128)}), f32[32,256]{1,0:T(8,128)}) %reduce-scatter.33.cloned.1.call-update) | async-done | bytes 32784 | tf_op jit(solution)/shard_map/reduce_scatter | solution.py:23
  371.1 13.1 %all_gather.47 = bf16[32,1024]{1,0:T(8,128)(2,1)S(1)} all-gather(bf16[32,256]{1,0:T(8,128)(2,1)S(1)} %subtract_convert_fusion), channel_id=1, replica_groups=mesh['freq'=2,'base'=4,'pix'=4] {'pix'}, dimensions={1}, use_global_device_ids=true | all-gather | bytes 81920 | tf_op jit(solution)/shard_map/all_gather | solution.py:28
  384.2 0.9 fusion
  385.7 17.4 %reduce-scatter.35.cloned.1.call-done = f32[32,128]{1,0:T(8,128)} async-done(((f32[32,512]{1,0:T(8,128)}), f32[32,128]{1,0:T(8,128)}) %reduce-scatter.35.cloned.1.call-update) | async-done | bytes 16400 | tf_op jit(solution)/shard_map/reduce_scatter | solution.py:47
  403.1 1.4 multiply_reduce_fusion
  404.5 5.5 %psum.47 = f32[1]{0:T(128)} all-reduce(f32[1]{0:T(128)} %bitcast.18), channel_id=1, replica_groups=mesh['freq'=2,'base'=4,'pix'=4] {'freq'}, use_global_device_ids=true, to_apply=%region_23.0 | all-reduce | flops 1 | bytes 8 | tf_op jit(solution)/shard_map/psum | solution.py:51
  (56 shorter events, 10.6 us)
Async XLA Ops:
  6.5 7.0 %copy-start = (bf16[1,1024,512]{2,1,0:T(8,128)(2,1)S(1)}, bf16[1,1024,512]{2,1,0:T(8,128)(2,1)}, u32[]{:S(2)}) copy-start(bf16[1,1024,512]{2,1,0:T(8,128)(2,1)} %param.4) | copy-start | bytes 3145732
  6.5 29.4 %reduce-scatter.13.cloned.1.call-start = ((), (), s32[]{:S(2)}) async-start(), calls=%async_computation.12 | async-start | bytes 163840 | tf_op jit(solution)/shard_map/reduce_scatter | solution.py:23
  14.5 21.4 %copy-start.1 = (f32[32,1024]{1,0:T(8,128)S(1)}, f32[32,1024]{1,0:T(8,128)}, u32[]{:S(2)}) copy-start(f32[32,1024]{1,0:T(8,128)} %param.5) | copy-start | bytes 393220
  14.6 54.1 %reduce-scatter.15.cloned.1.call-start = ((), (), s32[]{:S(2)}) async-start(), calls=%async_computation.13 | async-start | bytes 81920 | tf_op jit(solution)/shard_map/reduce_scatter | solution.py:47
  50.7 0.7 copy-start.4
  50.7 17.9 %copy-start.2 = (f32[32,1,1,128]{3,2,1,0:T(1,128)S(1)}, f32[32,1,1,128]{3,2,1,0:T(1,128)}, u32[]{:S(2)}) copy-start(f32[32,1,1,128]{3,2,1,0:T(1,128)} %param.6) | copy-start | bytes 49156
  50.8 52.0 %reduce-scatter.17.cloned.1.call-start = ((), (), s32[]{:S(2)}) async-start(), calls=%async_computation.14 | async-start | bytes 163840 | tf_op jit(solution)/shard_map/reduce_scatter | solution.py:23
  70.0 6.8 %copy-start.3 = (f32[32,128]{1,0:T(8,128)S(1)}, f32[32,128]{1,0:T(8,128)}, u32[]{:S(2)}) copy-start(f32[32,128]{1,0:T(8,128)} %reduce-scatter.15.cloned.1.call-done) | copy-start | bytes 49156
  83.2 52.3 %reduce-scatter.19.cloned.1.call-start = ((), (), s32[]{:S(2)}) async-start(), calls=%async_computation.15 | async-start | bytes 81920 | tf_op jit(solution)/shard_map/reduce_scatter | solution.py:47
  117.6 52.1 %reduce-scatter.21.cloned.1.call-start = ((), (), s32[]{:S(2)}) async-start(), calls=%async_computation.16 | async-start | bytes 163840 | tf_op jit(solution)/shard_map/reduce_scatter | solution.py:23
  150.1 52.3 %reduce-scatter.23.cloned.1.call-start = ((), (), s32[]{:S(2)}) async-start(), calls=%async_computation.17 | async-start | bytes 81920 | tf_op jit(solution)/shard_map/reduce_scatter | solution.py:47
  184.5 52.1 %reduce-scatter.25.cloned.1.call-start = ((), (), s32[]{:S(2)}) async-start(), calls=%async_computation.18 | async-start | bytes 163840 | tf_op jit(solution)/shard_map/reduce_scatter | solution.py:23
  217.0 52.3 %reduce-scatter.27.cloned.1.call-start = ((), (), s32[]{:S(2)}) async-start(), calls=%async_computation.19 | async-start | bytes 81920 | tf_op jit(solution)/shard_map/reduce_scatter | solution.py:47
  251.4 52.1 %reduce-scatter.29.cloned.1.call-start = ((), (), s32[]{:S(2)}) async-start(), calls=%async_computation.20 | async-start | bytes 163840 | tf_op jit(solution)/shard_map/reduce_scatter | solution.py:23
  283.9 52.3 %reduce-scatter.31.cloned.1.call-start = ((), (), s32[]{:S(2)}) async-start(), calls=%async_computation.21 | async-start | bytes 81920 | tf_op jit(solution)/shard_map/reduce_scatter | solution.py:47
  318.3 52.1 %reduce-scatter.33.cloned.1.call-start = ((), (), s32[]{:S(2)}) async-start(), calls=%async_computation.22 | async-start | bytes 163840 | tf_op jit(solution)/shard_map/reduce_scatter | solution.py:23
  350.7 52.3 %reduce-scatter.35.cloned.1.call-start = ((), (), s32[]{:S(2)}) async-start(), calls=%async_computation.23 | async-start | bytes 81920 | tf_op jit(solution)/shard_map/reduce_scatter | solution.py:47
  404.5 6.8 %copy-start.5 = (f32[32,128]{1,0:T(8,128)S(1)}, f32[32,128]{1,0:T(8,128)}, u32[]{:S(2)}) copy-start(f32[32,128]{1,0:T(8,128)} %reduce-scatter.35.cloned.1.call-done) | copy-start | bytes 49156
Sparse Core Ops, SparseCore 0:
  14.7 21.1 reduce-scatter.12
  50.9 17.7 reduce-scatter.14
  83.3 19.4 reduce-scatter.16
  117.7 17.7 reduce-scatter.18
  150.2 19.4 reduce-scatter.20
  184.6 17.7 reduce-scatter.22
  217.1 19.4 reduce-scatter.24
  251.5 17.7 reduce-scatter.26
  284.0 19.4 reduce-scatter.28
  318.4 17.7 reduce-scatter.30
  350.9 19.4 reduce-scatter.32
  385.3 17.7 reduce-scatter.34
where the time goes:
time: 420 us; the launch traced here: 419 us
  waiting for transfers between devices  223 us (53%)
  blocking collectives  144 us (34%)
  between operations  21.7 us (5%)
  other arithmetic  17.7 us (4%)
  matrix products  11.8 us (3%)
    reduce_scatter x6, waiting for transfers between devices, residual_of(): lax.psum_scatter(partial_value, 'pix', scatter_dimension=1, tiled=True)  119 us
    reduce_scatter x6, waiting for transfers between devices, on_device(): lax.psum_scatter(gradient_portion, 'base', scatter_dimension=1, tiled=True)  103 us
    all_gather x6, blocking collectives, residual_of(): lax.all_gather((own_rows - shares).astype(jnp.bfloat16), 'pix', axis=1, t...  78.7 us
    psum x6, blocking collectives, on_device(): total = lax.psum(local_sum, 'freq')  33.2 us
    all_gather x6, blocking collectives, on_device(): lax.all_gather(rounded_amount, 'base', axis=1, tiled=True)  32 us
    reduce_sum x6, other arithmetic, on_device(): local_sum = jnp.sum(tiles * tiles, axis=(0, 2))  8.45 us
  transfers between devices with their start and end apart: 12, of which 12 were waited for; matrix products, arithmetic and copies ran while one was open for 1% of the time, Pallas kernels for 0%

commit v1 on v0

--- a/solution.py
+++ b/solution.py
@@ -1,6 +1,10 @@
+import functools
+
 import jax
 import jax.numpy as jnp
 from jax import lax
+from jax.experimental import pallas as pl
+from jax.experimental.pallas import tpu as pltpu
 from jax.sharding import PartitionSpec as P
 
 CH = 64
@@ -11,6 +15,9 @@
 descent_stride = 0.6
 lam_shrink = 0.3
 eps_norm = 1e-06
+
+GRAM_LIMIT = 1 << 20
+PAD = 16
 
 
 def project_rows(rounded_amount, columns):
@@ -28,7 +35,7 @@
     return lax.all_gather((own_rows - shares).astype(jnp.bfloat16), "pix", axis=1, tiled=True)
 
 
-def on_device(sensing_operator_parts, sampled_correlations, first_sky_estimate, patch_order_record):
+def streaming(sensing_operator_parts, sampled_correlations, first_sky_estimate, patch_order_record):
     sensing_operator = sensing_operator_parts[0]
     chans, m_dev = sampled_correlations.shape
     share_width = first_sky_estimate.shape[3]
@@ -59,6 +66,300 @@
     return current.reshape(chans, 1, 1, share_width)
 
 
+def swap(value, axis, offset):
+    size = lax.axis_size(axis)
+    return lax.ppermute(value, axis, [(i, i ^ offset) for i in range(size)])
+
+
+def call(body, out_shape, args, scratch=(), smem=(), name=None):
+    specs = [
+        pl.BlockSpec(memory_space=pltpu.SMEM if i in smem else pltpu.VMEM) for i in range(len(args))
+    ]
+    out_specs = jax.tree.map(lambda _: pl.BlockSpec(memory_space=pltpu.VMEM), out_shape)
+    return pl.pallas_call(
+        body,
+        out_shape=out_shape,
+        in_specs=specs,
+        out_specs=out_specs,
+        scratch_shapes=list(scratch),
+        name=name,
+    )(*args)
+
+
+def split(value):
+    high = value.astype(jnp.bfloat16)
+    return high, (value - high.astype(jnp.float32)).astype(jnp.bfloat16)
+
+
+def pack_body(slots, where_ref, ranks_ref, a_ref, *outs):
+    pix = where_ref[0]
+    tiles = a_ref.shape[1] // TILE
+    quarter = outs[0].shape[0]
+    for d, out in enumerate(outs):
+        rows = pl.ds(pl.multiple_of((pix ^ d) * quarter, quarter), quarter)
+        for r in range(slots):
+            tile = jnp.int32(0)
+            owned = jnp.int32(0)
+            for j in range(tiles):
+                hit = ranks_ref[0, j] == r
+                tile = jnp.where(hit, j, tile)
+                owned = jnp.where(hit, 1, owned)
+            block = a_ref[rows, pl.ds(pl.multiple_of(tile * TILE, TILE), TILE)]
+            out[:, r * TILE : (r + 1) * TILE] = jnp.where(owned == 1, block, jnp.zeros_like(block))
+
+
+def first_body(where_ref, a_ref, *refs):
+    pix, base = where_ref[0], where_ref[1]
+    n_base = a_ref.shape[1] // TILE
+    shares, rest = refs[:n_base], refs[n_base:]
+    outs, x_ref = rest[:-1], rest[-1]
+    quarter = outs[0].shape[1]
+    for d, share in enumerate(shares):
+        x_ref[:, pl.ds(pl.multiple_of((base ^ d) * TILE, TILE), TILE)] = share[...]
+    for d, out in enumerate(outs):
+        rows = pl.ds(pl.multiple_of((pix ^ d) * quarter, quarter), quarter)
+        out[...] = lax.dot_general(
+            x_ref[...], a_ref[rows, :], (((1,), (1,)), ((), ())), preferred_element_type=jnp.float32
+        )
+
+
+def in_order(values, index):
+    bit = 1
+    while bit < len(values):
+        odd = (index & bit) != 0
+        values = [jnp.where(odd, values[d ^ bit], values[d]) for d in range(len(values))]
+        bit *= 2
+    return values
+
+
+def pairs(slots):
+    return [(r, s) for r in range(slots) for s in range(r, slots)]
+
+
+def gram_body(slots, n_pix, where_ref, ranks_ref, y_ref, x0_ref, *refs):
+    pix, base = where_ref[0], where_ref[1]
+    parts, preds = refs[:n_pix], refs[n_pix : 2 * n_pix]
+    *outs, all_ref = refs[2 * n_pix :]
+    n_base = len(outs)
+    chans, quarter = preds[0].shape
+    a = parts[0][...]
+    for part in parts[1:]:
+        a = a + part[...]
+    pred = preds[0][...]
+    for piece in preds[1:]:
+        pred = pred + piece[...]
+    y = y_ref[:, pl.ds(pl.multiple_of(pix * quarter, quarter), quarter)]
+    resid = (y - pred).astype(jnp.bfloat16)
+    y_hi, y_lo = split(y)
+    left = jnp.concatenate([y_hi, y_lo, resid], axis=0)
+    sides = jnp.dot(left, a, preferred_element_type=jnp.float32)
+    data = sides[:chans] + sides[chans : 2 * chans]
+    moved = descent_stride * sides[2 * chans :]
+    rank = ranks_ref[0, base]
+    gram = lax.dot_general(a, a, (((0,), (0,)), ((), ())), preferred_element_type=jnp.float32)
+    rows = lax.broadcasted_iota(jnp.int32, (TILE, TILE), 0)
+    cols = lax.broadcasted_iota(jnp.int32, (TILE, TILE), 1)
+    here = rows == cols
+    n_pairs = len(pairs(slots))
+    g_rows = n_pairs * TILE // n_base
+    per = slots // n_base
+    side_rows = 4 * chans + PAD
+    half = min(TILE, g_rows & -g_rows)
+    diags = {}
+    for i, (r, s) in enumerate(pairs(slots)):
+        block = gram[r * TILE : (r + 1) * TILE, s * TILE : (s + 1) * TILE]
+        if r == s:
+            diags[r] = jnp.sum(jnp.where(here, block, 0.0), axis=0, keepdims=True)
+            block = jnp.where(here, 0.0, block)
+        block = block.astype(jnp.bfloat16)
+        for q in range(TILE // half):
+            at = i * TILE + q * half
+            all_ref[at // g_rows, at % g_rows : at % g_rows + half, :] = block[q * half : (q + 1) * half]
+    for r in range(slots):
+        lanes = slice(r * TILE, (r + 1) * TILE)
+        start = jnp.where(rank == r, x0_ref[...], 0.0)
+        d_hi, d_lo = split(diags[r])
+        stack = [
+            *split(data[:, lanes]),
+            *split(moved[:, lanes] + start),
+            d_hi,
+            d_lo,
+            jnp.zeros((PAD - 2, TILE), jnp.bfloat16),
+        ]
+        at = g_rows + (r % per) * side_rows
+        for piece in stack[:4]:
+            all_ref[r // per, at : at + chans, :] = piece
+            at += chans
+        all_ref[r // per, at : at + PAD, :] = jnp.concatenate(stack[4:], axis=0)
+    for d, out in enumerate(outs):
+        out[...] = all_ref[base ^ d]
+
+
+def sum_body(g_rows, chans, per, *refs):
+    *parts, out = refs
+
+    def total(at, size):
+        value = parts[0][at : at + size].astype(jnp.float32)
+        for part in parts[1:]:
+            value = value + part[at : at + size].astype(jnp.float32)
+        return value
+
+    out[:g_rows] = total(0, g_rows).astype(jnp.bfloat16)
+    at = g_rows
+    for _ in range(per):
+        for _ in range(2):
+            high, low = split(total(at, chans) + total(at + chans, chans))
+            out[at : at + chans] = high
+            out[at + chans : at + 2 * chans] = low
+            at += 2 * chans
+        tail = total(at, PAD)
+        high, low = split(tail[0:1] + tail[1:2])
+        rest = jnp.zeros((PAD - 2, TILE), jnp.bfloat16)
+        out[at : at + PAD] = jnp.concatenate([high, low, rest], axis=0)
+        at += PAD
+
+
+def iterate_body(slots, n_base, g_rows, chans, where_ref, ranks_ref, *refs):
+    base = where_ref[1]
+    per = slots // n_base
+    side_rows = 4 * chans + PAD
+    chunks = [refs[:n_base], refs[n_base : 2 * n_base]]
+    out_ref, gram_ref, last_ref = refs[2 * n_base :]
+    states, datas, diags = [], [], []
+    for g in range(2):
+        full = in_order([ref[...] for ref in chunks[g]], base)
+        half = min(TILE, g_rows & -g_rows)
+        for i, (r, s) in enumerate(pairs(slots)):
+            pieces = []
+            for q in range(TILE // half):
+                at = i * TILE + q * half
+                pieces.append(full[at // g_rows][at % g_rows : at % g_rows + half])
+            block = jnp.concatenate(pieces, axis=0)
+            gram_ref[g, r * TILE : (r + 1) * TILE, s * TILE : (s + 1) * TILE] = block
+            if r != s:
+                gram_ref[g, s * TILE : (s + 1) * TILE, r * TILE : (r + 1) * TILE] = block.T
+        sides = [full[r // per][g_rows + (r % per) * side_rows :][:side_rows].astype(jnp.float32) for r in range(slots)]
+        wide = lambda at: jnp.concatenate([v[at : at + chans] + v[at + chans : at + 2 * chans] for v in sides], axis=1)
+        datas.append(wide(0))
+        states.append(wide(2 * chans))
+        tails = [v[4 * chans :] for v in sides]
+        diags.append(jnp.concatenate([t[0:1] + t[1:2] for t in tails], axis=1))
+    for step in range(ITERS):
+        factors = []
+        for r in range(slots):
+            lanes = slice(r * TILE, (r + 1) * TILE)
+            square = states[0][:, lanes] * states[0][:, lanes] + states[1][:, lanes] * states[1][:, lanes]
+            column = jnp.sum(square, axis=0, keepdims=True)
+            norm = jnp.sum(column, axis=1, keepdims=True)
+            rms = jnp.sqrt(norm / (CH * TILE) + eps_norm)
+            factors.append(jnp.broadcast_to(rms / (rms + lam_shrink), (1, TILE)))
+        factor = jnp.concatenate(factors, axis=1)
+        states = [state * factor for state in states]
+        if step == ITERS - 1:
+            break
+        for g in range(2):
+            high, low = split(states[g])
+            both = jnp.dot(
+                jnp.concatenate([high, low], axis=0), gram_ref[g], preferred_element_type=jnp.float32
+            )
+            product = both[:chans] + both[chans:] + states[g] * diags[g]
+            states[g] = states[g] + descent_stride * (datas[g] - product)
+    for r in range(slots):
+        last_ref[r] = states[0][:, r * TILE : (r + 1) * TILE]
+    rank = ranks_ref[0, base]
+    kept = last_ref[jnp.minimum(rank, slots - 1)]
+    out_ref[...] = jnp.where(rank < slots, kept, 0.0)
+
+
+def gram_plan(sensing_operator_parts, sampled_correlations, first_sky_estimate, patch_order_record):
+    a = sensing_operator_parts[0]
+    chans, m_dev = sampled_correlations.shape
+    n_base, n_pix = lax.axis_size("base"), lax.axis_size("pix")
+    slots = n_base * n_pix // 4
+    quarter = m_dev // n_pix
+    x0 = first_sky_estimate[:, 0, 0, :]
+    ranks = patch_order_record
+    where = jnp.stack([lax.axis_index("pix"), lax.axis_index("base")]).astype(jnp.int32)
+    shape = jax.ShapeDtypeStruct
+    bf16, f32 = jnp.bfloat16, jnp.float32
+
+    x0_round = x0.astype(bf16)
+    shares = [x0_round] + [swap(x0_round, "base", d) for d in range(1, n_base)]
+    packed = call(
+        functools.partial(pack_body, slots),
+        [shape((quarter, slots * TILE), bf16)] * n_pix,
+        (where, ranks, a),
+        smem=(0, 1),
+        name="pack",
+    )
+    parts = [packed[0]] + [swap(packed[d], "pix", d) for d in range(1, n_pix)]
+    firsts = call(
+        first_body,
+        [shape((chans, quarter), f32)] * n_pix,
+        (where, a, *shares),
+        scratch=[pltpu.VMEM((chans, n_base * TILE), bf16)],
+        smem=(0,),
+        name="first",
+    )
+    preds = [firsts[0]] + [swap(firsts[d], "pix", d) for d in range(1, n_pix)]
+
+    n_pairs = slots * (slots + 1) // 2
+    g_rows = n_pairs * TILE // n_base
+    per = slots // n_base
+    rows = g_rows + per * (4 * chans + PAD)
+    chunk = shape((rows, TILE), bf16)
+    outs = call(
+        functools.partial(gram_body, slots, n_pix),
+        [chunk] * n_base,
+        (where, ranks, sampled_correlations, x0, *parts, *preds),
+        scratch=[pltpu.VMEM((n_base, rows, TILE), bf16)],
+        smem=(0, 1),
+        name="gram",
+    )
+    add = functools.partial(sum_body, g_rows, chans, per)
+    part = call(add, chunk, [outs[0]] + [swap(outs[d], "base", d) for d in range(1, n_base)], name="sum_base")
+    total = call(add, chunk, [part] + [swap(part, "pix", d) for d in range(1, n_pix)], name="sum_pix")
+
+    axes = ("freq", "base")
+    got = {0: total}
+    for offset in range(2, 2 * n_base, 2):
+        got[offset] = swap(total, axes, offset)
+    got[1] = swap(total, axes, 1)
+    for offset in range(2, 2 * n_base, 2):
+        got[offset + 1] = swap(got[offset], axes, 1)
+    image = call(
+        functools.partial(iterate_body, slots, n_base, g_rows, chans),
+        shape((chans, TILE), f32),
+        (where, ranks, *[got[i] for i in range(2 * n_base)]),
+        scratch=[
+            pltpu.VMEM((2, slots * TILE, slots * TILE), bf16),
+            pltpu.VMEM((slots, chans, TILE), f32),
+        ],
+        smem=(0, 1),
+        name="iterate",
+    )
+    return image.reshape(chans, 1, 1, TILE)
+
+
+def on_device(sensing_operator_parts, sampled_correlations, first_sky_estimate, patch_order_record):
+    n_base, n_pix = lax.axis_size("base"), lax.axis_size("pix")
+    slots = n_base * n_pix // 4
+    chans, m_dev = sampled_correlations.shape
+    fits = (
+        first_sky_estimate.shape[3] == TILE
+        and (slots * TILE) ** 2 <= GRAM_LIMIT
+        and n_base & (n_base - 1) == 0
+        and n_pix & (n_pix - 1) == 0
+        and slots % n_base == 0
+        and slots * (slots + 1) // 2 * TILE % (n_base * 16) == 0
+        and m_dev % (n_pix * TILE) == 0
+        and lax.axis_size("freq") == 2
+        and chans % 16 == 0
+    )
+    plan = gram_plan if fits else streaming
+    return plan(sensing_operator_parts, sampled_correlations, first_sky_estimate, patch_order_record)
+
+
 def solution(mesh):
     in_specs = (
         P("freq", "base", "pix"),

time: 420 us -> 81.5 us (0.19)
  waiting for transfers between devices: 223 us -> 33.1 us
  blocking collectives: 144 us -> 0 us
  starting transfers between devices: 0.46 us -> 26.2 us
  between operations: 21.7 us -> 0.14 us
  other arithmetic: 17.7 us -> 0.61 us
  Pallas kernels: 0 us -> 14.9 us
  matrix products: 11.8 us -> 0 us
  local copies, waits for them, and re-layouts: 0.69 us -> 6.24 us
    reduce_scatter x12 -> x0, waiting for transfers between devices: 222 us -> none  [the longest x6 119 us: residual_of(): lax.psum_scatter(partial_value, 'pix', scatter_dimension=1, tiled=True)]
    all_gather x12 -> x0, blocking collectives: 111 us -> none  [the longest x6 78.7 us: residual_of(): lax.all_gather((own_rows - shares).astype(jnp.bfloat16), 'pix', axis=1, t...]
    psum x6 -> x0, blocking collectives: 33.2 us -> none  [on_device(): total = lax.psum(local_sum, 'freq')]
    ppermute x0 -> x22, waiting for transfers between devices: none -> 33.1 us  [swap(): return lax.ppermute(value, axis, [(i, i ^ offset) for i in range(size)])]
    ppermute x0 -> x22, starting transfers between devices: none -> 26.2 us  [swap(): return lax.ppermute(value, axis, [(i, i ^ offset) for i in range(size)])]
    pallas_call x0 -> x6, Pallas kernels: none -> 14.9 us  [call(): pl.pallas_call(body, out_shape=out_shape, in_specs=specs, out_specs=out_s...]
    dot_general x12 -> x0, matrix products: 11.8 us -> none  [the longest x6 6.32 us: project_rows(): lax.dot_general(rounded_amount, columns, (((1,), (1,)), ((), ())), prefer...]
    reduce_sum x6 -> x0, other arithmetic: 8.45 us -> none  [on_device(): local_sum = jnp.sum(tiles * tiles, axis=(0, 2))]
  transfers between devices with their start and end apart: 12 -> 22, of which waited for: 12 -> 14; matrix products, arithmetic and copies ran while one was open for 1% -> 0% of each run, Pallas kernels for 0% -> 3%
where the time goes in v1:
time: 81.5 us; the launch traced here: 81.2 us
  waiting for transfers between devices  33.1 us (41%)
  starting transfers between devices  26.2 us (32%)
  Pallas kernels  14.9 us (18%)
  local copies, waits for them, and re-layouts  6.24 us (8%)
    ppermute x22, waiting for transfers between devices, swap(): return lax.ppermute(value, axis, [(i, i ^ offset) for i in range(size)])  33.1 us
    ppermute x22, starting transfers between devices, swap(): return lax.ppermute(value, axis, [(i, i ^ offset) for i in range(size)])  26.2 us
    pallas_call x6, Pallas kernels, call(): pl.pallas_call(body, out_shape=out_shape, in_specs=specs, out_specs=out_s...  14.9 us
    unnamed x51, local copies, waits for them, and re-layouts  6.24 us
  transfers between devices with their start and end apart: 22, of which 14 were waited for; matrix products, arithmetic and copies ran while one was open for 0% of the time, Pallas kernels for 3%

profile of v1, /device:TPU:0, one launch (start us, length us, event | category | flops | bytes accessed | tf_op | source)
XLA Modules:
  0.0 81.2 jit_solution(9591282681283251538)
XLA Ops:
  0.0 0.7 copy-done.24
  0.7 0.7 copy.7.ranks_ref
  1.3 0.6 pad_add_fusion.where_ref
  2.0 2.5 %pack.1 = (bf16[256,512]{1,0:T(8,128)(2,1)}, bf16[256,512]{1,0:T(8,128)(2,1)}, bf16[256,512]{1,0:T(8,128)(2,1)}, bf16[256,512]{1,0:T(8,128)(2,1)}) custom-call(s32[2]{0:T(128)} %pad_add_fusion.where_ref, s32[6,4]{1,0:T(8,128)} %copy.7.ranks_ref, bf16[1024,512]{1,0:T(8,128)(2,1)} %bitcast.7), custom_call_target="tpu_custom_call" | custom-call | tf_op jit(solution)/shard_map/pack/pallas_call | solution.py:79
  4.5 3.1 %collective-permute-start = (bf16[256,512]{1,0:T(8,128)(2,1)}, bf16[256,512]{1,0:T(8,128)(2,1)S(1)}, u32[]{:S(2)}, u32[]{:S(2)}) collective-permute-start(bf16[256,512]{1,0:T(8,128)(2,1)} %get-tuple-element.18), channel_id=1, source_target_pairs={{0,1},{1,0},{2,3},{3,2},{4,5},{5,4},{6,7},{7,6},{8,9},{9,8},{10,11... | collective-permute-start | bytes 786440 | tf_op jit(solution)/shard_map/ppermute | solution.py:71
  7.5 2.6 %collective-permute-start.1 = (bf16[256,512]{1,0:T(8,128)(2,1)}, bf16[256,512]{1,0:T(8,128)(2,1)S(1)}, u32[]{:S(2)}, u32[]{:S(2)}) collective-permute-start(bf16[256,512]{1,0:T(8,128)(2,1)} %get-tuple-element.19), channel_id=1, source_target_pairs={{0,2},{1,3},{2,0},{3,1},{4,6},{5,7},{6,4},{7,5},{8,10},{9,11},{10,... | collective-permute-start | bytes 786440 | tf_op jit(solution)/shard_map/ppermute | solution.py:71
  10.1 0.5 collective-permute-start.5
  10.6 1.4 %collective-permute-start.4 = (bf16[32,128]{1,0:T(8,128)(2,1)S(1)}, bf16[32,128]{1,0:T(8,128)(2,1)S(1)}, u32[]{:S(2)}, u32[]{:S(2)}) collective-permute-start(bf16[32,128]{1,0:T(8,128)(2,1)S(1)} %convert_element_type.3.refs_0_), channel_id=1, source_target_pairs={{0,8},{4,12},{8,0},{12,4},{1,9},{5,13},{9,1},{13,5},{2,10},{6,14},... | collective-permute-start | bytes 24584 | tf_op jit(solution)/shard_map/ppermute | solution.py:71
  12.0 1.3 %collective-permute-done.5.refs_3_ = bf16[32,128]{1,0:T(8,128)(2,1)S(1)} collective-permute-done((bf16[32,128]{1,0:T(8,128)(2,1)S(1)}, bf16[32,128]{1,0:T(8,128)(2,1)S(1)}, u32[]{:S(2)}, u32[]{:S(2)}) %collective-permute-start.5) | collective-permute-done | bytes 8224 | tf_op jit(solution)/shard_map/ppermute | solution.py:71
  13.3 0.4 collective-permute-start.3
  13.7 0.6 collective-permute-done.4.refs_2_
  14.3 0.3 collective-permute-done.3.refs_1_
  14.5 0.3 copy-done.22
  14.9 0.6 copy-done.23
  15.4 2.3 %first.1 = (f32[32,256]{1,0:T(8,128)}, f32[32,256]{1,0:T(8,128)}, f32[32,256]{1,0:T(8,128)}, f32[32,256]{1,0:T(8,128)}) custom-call(s32[2]{0:T(128)} %pad_add_fusion.where_ref, bf16[1024,512]{1,0:T(8,128)(2,1)} %bitcast.8, bf16[32,128]{1,0:T(8,128)(2,1)} %copy-done.17, bf16[32,128]{1,0:T(8,128)(2,1)} %copy-done.23, bf16[32,128]{1,0:T(8,128)(2,1)} %copy-done.22, ...), custom_call_target="tpu_custom_call" | custom-call | tf_op jit(solution)/shard_map/first/pallas_call | solution.py:79
  17.8 0.6 collective-permute-start.6
  18.4 3.5 %collective-permute-start.7 = (f32[32,256]{1,0:T(8,128)}, f32[32,256]{1,0:T(8,128)S(1)}, u32[]{:S(2)}, u32[]{:S(2)}) collective-permute-start(f32[32,256]{1,0:T(8,128)} %get-tuple-element.23), channel_id=1, source_target_pairs={{0,2},{1,3},{2,0},{3,1},{4,6},{5,7},{6,4},{7,5},{8,10},{9,11},{10,... | collective-permute-start | bytes 98312 | tf_op jit(solution)/shard_map/ppermute | solution.py:71
  21.8 3.9 %collective-permute-done.6.refs_5_ = f32[32,256]{1,0:T(8,128)S(1)} collective-permute-done((f32[32,256]{1,0:T(8,128)}, f32[32,256]{1,0:T(8,128)S(1)}, u32[]{:S(2)}, u32[]{:S(2)}) %collective-permute-start.6) | collective-permute-done | bytes 32800 | tf_op jit(solution)/shard_map/ppermute | solution.py:71
  25.8 4.1 %collective-permute-start.8 = (f32[32,256]{1,0:T(8,128)}, f32[32,256]{1,0:T(8,128)S(1)}, u32[]{:S(2)}, u32[]{:S(2)}) collective-permute-start(f32[32,256]{1,0:T(8,128)} %get-tuple-element.24), channel_id=1, source_target_pairs={{0,3},{1,2},{2,1},{3,0},{4,7},{5,6},{6,5},{7,4},{8,11},{9,10},{10,... | collective-permute-start | bytes 98312 | tf_op jit(solution)/shard_map/ppermute | solution.py:71
  29.9 5.8 %collective-permute-done.7.refs_6_ = f32[32,256]{1,0:T(8,128)S(1)} collective-permute-done((f32[32,256]{1,0:T(8,128)}, f32[32,256]{1,0:T(8,128)S(1)}, u32[]{:S(2)}, u32[]{:S(2)}) %collective-permute-start.7) | collective-permute-done | bytes 32800 | tf_op jit(solution)/shard_map/ppermute | solution.py:71
  35.8 0.5 copy-done.19
  36.5 0.1 copy-done.1
  36.7 2.4 %gram.1 = (bf16[464,128]{1,0:T(8,128)(2,1)}, bf16[464,128]{1,0:T(8,128)(2,1)}, bf16[464,128]{1,0:T(8,128)(2,1)}, bf16[464,128]{1,0:T(8,128)(2,1)}) custom-call(s32[2]{0:T(128)} %pad_add_fusion.where_ref, s32[6,4]{1,0:T(8,128)} %copy.7.ranks_ref, f32[32,1024]{1,0:T(8,128)} %y_ref.1, f32[32,128]{1,0:T(8,128)} %bitcast.9, ...), custom_call_target="tpu_custom_call" | custom-call | tf_op jit(solution)/shard_map/gram/pallas_call | solution.py:79
  39.1 1.6 %collective-permute-start.10 = (bf16[464,128]{1,0:T(8,128)(2,1)}, bf16[464,128]{1,0:T(8,128)(2,1)S(1)}, u32[]{:S(2)}, u32[]{:S(2)}) collective-permute-start(bf16[464,128]{1,0:T(8,128)(2,1)} %get-tuple-element.27), channel_id=1, source_target_pairs={{0,8},{4,12},{8,0},{12,4},{1,9},{5,13},{9,1},{13,5},{2,10},{6,14},... | collective-permute-start | bytes 356360 | tf_op jit(solution)/shard_map/ppermute | solution.py:71
  40.7 0.3 collective-permute-start.11
  41.0 4.5 %collective-permute-done.10.refs_2_ = bf16[464,128]{1,0:T(8,128)(2,1)S(1)} collective-permute-done((bf16[464,128]{1,0:T(8,128)(2,1)}, bf16[464,128]{1,0:T(8,128)(2,1)S(1)}, u32[]{:S(2)}, u32[]{:S(2)}) %collective-permute-start.10) | collective-permute-done | bytes 118816 | tf_op jit(solution)/shard_map/ppermute | solution.py:71
  45.5 1.5 %collective-permute-done.11.refs_3_ = bf16[464,128]{1,0:T(8,128)(2,1)S(1)} collective-permute-done((bf16[464,128]{1,0:T(8,128)(2,1)}, bf16[464,128]{1,0:T(8,128)(2,1)S(1)}, u32[]{:S(2)}, u32[]{:S(2)}) %collective-permute-start.11) | collective-permute-done | bytes 118816 | tf_op jit(solution)/shard_map/ppermute | solution.py:71
  47.0 0.7 copy-done.6
  47.7 1.8 %sum_base.1.refs_0_ = bf16[464,128]{1,0:T(8,128)(2,1)} custom-call(bf16[464,128]{1,0:T(8,128)(2,1)} %get-tuple-element.25.refs_0_, bf16[464,128]{1,0:T(8,128)(2,1)} %copy-done.3, bf16[464,128]{1,0:T(8,128)(2,1)} %copy-done.4, bf16[464,128]{1,0:T(8,128)(2,1)} %copy-done.6), custom_call_target="tpu_custom_call" | custom-call | tf_op jit(solution)/shard_map/sum_base/pallas_call | solution.py:79
  49.5 2.5 %collective-permute-start.14 = (bf16[464,128]{1,0:T(8,128)(2,1)}, bf16[464,128]{1,0:T(8,128)(2,1)S(1)}, u32[]{:S(2)}, u32[]{:S(2)}) collective-permute-start(bf16[464,128]{1,0:T(8,128)(2,1)} %sum_base.1.refs_0_), channel_id=1, source_target_pairs={{0,3},{1,2},{2,1},{3,0},{4,7},{5,6},{6,5},{7,4},{8,11},{9,10},{10,... | collective-permute-start | bytes 356360 | tf_op jit(solution)/shard_map/ppermute | solution.py:71
  52.0 1.9 %collective-permute-start.12 = (bf16[464,128]{1,0:T(8,128)(2,1)}, bf16[464,128]{1,0:T(8,128)(2,1)S(1)}, u32[]{:S(2)}, u32[]{:S(2)}) collective-permute-start(bf16[464,128]{1,0:T(8,128)(2,1)} %sum_base.1.refs_0_), channel_id=1, source_target_pairs={{0,1},{1,0},{2,3},{3,2},{4,5},{5,4},{6,7},{7,6},{8,9},{9,8},{10,11... | collective-permute-start | bytes 356360 | tf_op jit(solution)/shard_map/ppermute | solution.py:71
  53.8 3.8 %collective-permute-done.14.refs_3_ = bf16[464,128]{1,0:T(8,128)(2,1)S(1)} collective-permute-done((bf16[464,128]{1,0:T(8,128)(2,1)}, bf16[464,128]{1,0:T(8,128)(2,1)S(1)}, u32[]{:S(2)}, u32[]{:S(2)}) %collective-permute-start.14) | collective-permute-done | bytes 118816 | tf_op jit(solution)/shard_map/ppermute | solution.py:71
  57.7 5.4 %collective-permute-done.13.refs_2_ = bf16[464,128]{1,0:T(8,128)(2,1)S(1)} collective-permute-done((bf16[464,128]{1,0:T(8,128)(2,1)}, bf16[464,128]{1,0:T(8,128)(2,1)S(1)}, u32[]{:S(2)}, u32[]{:S(2)}) %collective-permute-start.13) | collective-permute-done | bytes 118816 | tf_op jit(solution)/shard_map/ppermute | solution.py:71
  63.1 0.6 copy-done.7
  63.8 0.6 copy-done.8
  64.4 1.8 %sum_pix.1.refs_0_ = bf16[464,128]{1,0:T(8,128)(2,1)} custom-call(bf16[464,128]{1,0:T(8,128)(2,1)} %sum_base.1.refs_0_, bf16[464,128]{1,0:T(8,128)(2,1)} %copy-done.8, bf16[464,128]{1,0:T(8,128)(2,1)} %copy-done.7, bf16[464,128]{1,0:T(8,128)(2,1)} %copy-done.5), custom_call_target="tpu_custom_call" | custom-call | tf_op jit(solution)/shard_map/sum_pix/pallas_call | solution.py:79
  66.2 2.4 %collective-permute-start.20 = (bf16[464,128]{1,0:T(8,128)(2,1)}, bf16[464,128]{1,0:T(8,128)(2,1)S(1)}, u32[]{:S(2)}, u32[]{:S(2)}) collective-permute-start(bf16[464,128]{1,0:T(8,128)(2,1)} %sum_pix.1.refs_0_), channel_id=1, source_target_pairs={{0,24},{4,28},{8,16},{12,20},{16,8},{20,12},{24,0},{28,4},{1,25},{... | collective-permute-start | bytes 356360 | tf_op jit(solution)/shard_map/ppermute | solution.py:71
  68.7 0.5 collective-permute-start.18
  69.2 0.5 collective-permute-start.16
  69.7 3.6 %collective-permute-done.20.refs_6_ = bf16[464,128]{1,0:T(8,128)(2,1)S(1)} collective-permute-done((bf16[464,128]{1,0:T(8,128)(2,1)}, bf16[464,128]{1,0:T(8,128)(2,1)S(1)}, u32[]{:S(2)}, u32[]{:S(2)}) %collective-permute-start.20) | collective-permute-done | bytes 118816 | tf_op jit(solution)/shard_map/ppermute | solution.py:71
  73.3 1.2 %collective-permute-done.18.refs_4_ = bf16[464,128]{1,0:T(8,128)(2,1)S(1)} collective-permute-done((bf16[464,128]{1,0:T(8,128)(2,1)}, bf16[464,128]{1,0:T(8,128)(2,1)S(1)}, u32[]{:S(2)}, u32[]{:S(2)}) %collective-permute-start.18) | collective-permute-done | bytes 118816 | tf_op jit(solution)/shard_map/ppermute | solution.py:71
  74.6 0.2 collective-permute-done.16.refs_2_
  74.7 0.3 collective-permute-start.17
  75.1 0.8 collective-permute-done.19.refs_5_
  75.9 0.2 collective-permute-done.17.refs_3_
  76.1 0.4 copy-done.14
  76.5 0.7 copy-done.15
  77.2 4.0 %iterate.1 = f32[32,128]{1,0:T(8,128)} custom-call(s32[2]{0:T(128)} %pad_add_fusion.where_ref, s32[6,4]{1,0:T(8,128)} %copy.7.ranks_ref, bf16[464,128]{1,0:T(8,128)(2,1)} %sum_pix.1.refs_0_, bf16[464,128]{1,0:T(8,128)(2,1)} %copy-done.12, bf16[464,128]{1,0:T(8,128)(2,1)} %copy-done.11, bf16[464,128]{1,0:T(8,128)(2,1)} %copy-done.15, ...), custom_call_target="tpu_custom_call" | custom-call | tf_op jit(solution)/shard_map/iterate/pallas_call | solution.py:79
  (55 shorter events, 0.3 us)
Async XLA Ops:
  0.0 0.7 copy-start.24
  2.0 8.2 %copy-start.16 = (f32[32,1,1,128]{3,2,1,0:T(1,128)S(1)}, f32[32,1,1,128]{3,2,1,0:T(1,128)}, u32[]{:S(2)}) copy-start(f32[32,1,1,128]{3,2,1,0:T(1,128)} %param.6) | copy-start | bytes 49156
  4.5 31.3 %collective-permute-start = (bf16[256,512]{1,0:T(8,128)(2,1)}, bf16[256,512]{1,0:T(8,128)(2,1)S(1)}, u32[]{:S(2)}, u32[]{:S(2)}) collective-permute-start(bf16[256,512]{1,0:T(8,128)(2,1)} %get-tuple-element.18), channel_id=1, source_target_pairs={{0,1},{1,0},{2,3},{3,2},{4,5},{5,4},{6,7},{7,6},{8,9},{9,8},{10,11... | collective-permute-start | bytes 786440 | tf_op jit(solution)/shard_map/ppermute | solution.py:71
  7.5 28.3 %collective-permute-start.1 = (bf16[256,512]{1,0:T(8,128)(2,1)}, bf16[256,512]{1,0:T(8,128)(2,1)S(1)}, u32[]{:S(2)}, u32[]{:S(2)}) collective-permute-start(bf16[256,512]{1,0:T(8,128)(2,1)} %get-tuple-element.19), channel_id=1, source_target_pairs={{0,2},{1,3},{2,0},{3,1},{4,6},{5,7},{6,4},{7,5},{8,10},{9,11},{10,... | collective-permute-start | bytes 786440 | tf_op jit(solution)/shard_map/ppermute | solution.py:71
  10.1 25.7 %collective-permute-start.2 = (bf16[256,512]{1,0:T(8,128)(2,1)}, bf16[256,512]{1,0:T(8,128)(2,1)S(1)}, u32[]{:S(2)}, u32[]{:S(2)}) collective-permute-start(bf16[256,512]{1,0:T(8,128)(2,1)} %get-tuple-element.20), channel_id=1, source_target_pairs={{0,3},{1,2},{2,1},{3,0},{4,7},{5,6},{6,5},{7,4},{8,11},{9,10},{10,... | collective-permute-start | bytes 786440 | tf_op jit(solution)/shard_map/ppermute | solution.py:71
  10.1 4.4 %copy-start.17 = (bf16[32,128]{1,0:T(8,128)(2,1)}, bf16[32,128]{1,0:T(8,128)(2,1)S(1)}, u32[]{:S(2)}) copy-start(bf16[32,128]{1,0:T(8,128)(2,1)S(1)} %convert_element_type.3.refs_0_) | copy-start | bytes 24580
  10.1 3.1 %collective-permute-start.5 = (bf16[32,128]{1,0:T(8,128)(2,1)S(1)}, bf16[32,128]{1,0:T(8,128)(2,1)S(1)}, u32[]{:S(2)}, u32[]{:S(2)}) collective-permute-start(bf16[32,128]{1,0:T(8,128)(2,1)S(1)} %convert_element_type.3.refs_0_), channel_id=1, source_target_pairs={{0,12},{4,8},{8,4},{12,0},{1,13},{5,9},{9,5},{13,1},{2,14},{6,10},... | collective-permute-start | bytes 24584 | tf_op jit(solution)/shard_map/ppermute | solution.py:71
  10.6 3.7 %collective-permute-start.4 = (bf16[32,128]{1,0:T(8,128)(2,1)S(1)}, bf16[32,128]{1,0:T(8,128)(2,1)S(1)}, u32[]{:S(2)}, u32[]{:S(2)}) collective-permute-start(bf16[32,128]{1,0:T(8,128)(2,1)S(1)} %convert_element_type.3.refs_0_), channel_id=1, source_target_pairs={{0,8},{4,12},{8,0},{12,4},{1,9},{5,13},{9,1},{13,5},{2,10},{6,14},... | collective-permute-start | bytes 24584 | tf_op jit(solution)/shard_map/ppermute | solution.py:71
  13.3 1.2 %copy-start.21 = (bf16[32,128]{1,0:T(8,128)(2,1)}, bf16[32,128]{1,0:T(8,128)(2,1)S(1)}, u32[]{:S(2)}) copy-start(bf16[32,128]{1,0:T(8,128)(2,1)S(1)} %collective-permute-done.5.refs_3_) | copy-start | bytes 24580
  13.3 1.2 %collective-permute-start.3 = (bf16[32,128]{1,0:T(8,128)(2,1)S(1)}, bf16[32,128]{1,0:T(8,128)(2,1)S(1)}, u32[]{:S(2)}, u32[]{:S(2)}) collective-permute-start(bf16[32,128]{1,0:T(8,128)(2,1)S(1)} %convert_element_type.3.refs_0_), channel_id=1, source_target_pairs={{0,4},{4,0},{8,12},{12,8},{1,5},{5,1},{9,13},{13,9},{2,6},{6,2},{1... | collective-permute-start | bytes 24584 | tf_op jit(solution)/shard_map/ppermute | solution.py:71
  14.3 0.6 copy-start.22
  14.9 0.6 copy-start.23
  17.8 8.0 %collective-permute-start.6 = (f32[32,256]{1,0:T(8,128)}, f32[32,256]{1,0:T(8,128)S(1)}, u32[]{:S(2)}, u32[]{:S(2)}) collective-permute-start(f32[32,256]{1,0:T(8,128)} %get-tuple-element.22), channel_id=1, source_target_pairs={{0,1},{1,0},{2,3},{3,2},{4,5},{5,4},{6,7},{7,6},{8,9},{9,8},{10,11... | collective-permute-start | bytes 98312 | tf_op jit(solution)/shard_map/ppermute | solution.py:71
  18.4 17.4 %collective-permute-start.7 = (f32[32,256]{1,0:T(8,128)}, f32[32,256]{1,0:T(8,128)S(1)}, u32[]{:S(2)}, u32[]{:S(2)}) collective-permute-start(f32[32,256]{1,0:T(8,128)} %get-tuple-element.23), channel_id=1, source_target_pairs={{0,2},{1,3},{2,0},{3,1},{4,6},{5,7},{6,4},{7,5},{8,10},{9,11},{10,... | collective-permute-start | bytes 98312 | tf_op jit(solution)/shard_map/ppermute | solution.py:71
  25.8 10.0 %copy-start.18 = (f32[32,256]{1,0:T(8,128)}, f32[32,256]{1,0:T(8,128)S(1)}, u32[]{:S(2)}) copy-start(f32[32,256]{1,0:T(8,128)S(1)} %collective-permute-done.6.refs_5_) | copy-start | bytes 98308
  25.8 10.0 %collective-permute-start.8 = (f32[32,256]{1,0:T(8,128)}, f32[32,256]{1,0:T(8,128)S(1)}, u32[]{:S(2)}, u32[]{:S(2)}) collective-permute-start(f32[32,256]{1,0:T(8,128)} %get-tuple-element.24), channel_id=1, source_target_pairs={{0,3},{1,2},{2,1},{3,0},{4,7},{5,6},{6,5},{7,4},{8,11},{9,10},{10,... | collective-permute-start | bytes 98312 | tf_op jit(solution)/shard_map/ppermute | solution.py:71
  35.8 0.6 copy-start.19
  35.8 0.6 copy-start.20
  35.8 0.7 copy-start
  35.8 0.8 %copy-start.1 = (bf16[256,512]{1,0:T(8,128)(2,1)}, bf16[256,512]{1,0:T(8,128)(2,1)S(1)}, u32[]{:S(2)}) copy-start(bf16[256,512]{1,0:T(8,128)(2,1)S(1)} %collective-permute-done.1.refs_2_) | copy-start | bytes 786436
  35.8 0.9 %copy-start.2 = (bf16[256,512]{1,0:T(8,128)(2,1)}, bf16[256,512]{1,0:T(8,128)(2,1)S(1)}, u32[]{:S(2)}) copy-start(bf16[256,512]{1,0:T(8,128)(2,1)S(1)} %collective-permute-done.2.refs_3_) | copy-start | bytes 786436
  39.1 1.9 %collective-permute-start.9 = (bf16[464,128]{1,0:T(8,128)(2,1)}, bf16[464,128]{1,0:T(8,128)(2,1)S(1)}, u32[]{:S(2)}, u32[]{:S(2)}) collective-permute-start(bf16[464,128]{1,0:T(8,128)(2,1)} %get-tuple-element.26), channel_id=1, source_target_pairs={{0,4},{4,0},{8,12},{12,8},{1,5},{5,1},{9,13},{13,9},{2,6},{6,2},{1... | collective-permute-start | bytes 356360 | tf_op jit(solution)/shard_map/ppermute | solution.py:71
  39.1 6.4 %collective-permute-start.10 = (bf16[464,128]{1,0:T(8,128)(2,1)}, bf16[464,128]{1,0:T(8,128)(2,1)S(1)}, u32[]{:S(2)}, u32[]{:S(2)}) collective-permute-start(bf16[464,128]{1,0:T(8,128)(2,1)} %get-tuple-element.27), channel_id=1, source_target_pairs={{0,8},{4,12},{8,0},{12,4},{1,9},{5,13},{9,1},{13,5},{2,10},{6,14},... | collective-permute-start | bytes 356360 | tf_op jit(solution)/shard_map/ppermute | solution.py:71
  40.7 6.3 %collective-permute-start.11 = (bf16[464,128]{1,0:T(8,128)(2,1)}, bf16[464,128]{1,0:T(8,128)(2,1)S(1)}, u32[]{:S(2)}, u32[]{:S(2)}) collective-permute-start(bf16[464,128]{1,0:T(8,128)(2,1)} %get-tuple-element.28), channel_id=1, source_target_pairs={{0,12},{4,8},{8,4},{12,0},{1,13},{5,9},{9,5},{13,1},{2,14},{6,10},... | collective-permute-start | bytes 356360 | tf_op jit(solution)/shard_map/ppermute | solution.py:71
  41.0 6.0 %copy-start.3 = (bf16[464,128]{1,0:T(8,128)(2,1)}, bf16[464,128]{1,0:T(8,128)(2,1)S(1)}, u32[]{:S(2)}) copy-start(bf16[464,128]{1,0:T(8,128)(2,1)S(1)} %collective-permute-done.9.refs_1_) | copy-start | bytes 356356
  45.5 1.5 %copy-start.4 = (bf16[464,128]{1,0:T(8,128)(2,1)}, bf16[464,128]{1,0:T(8,128)(2,1)S(1)}, u32[]{:S(2)}) copy-start(bf16[464,128]{1,0:T(8,128)(2,1)S(1)} %collective-permute-done.10.refs_2_) | copy-start | bytes 356356
  47.0 0.7 copy-start.6
  49.5 8.2 %collective-permute-start.14 = (bf16[464,128]{1,0:T(8,128)(2,1)}, bf16[464,128]{1,0:T(8,128)(2,1)S(1)}, u32[]{:S(2)}, u32[]{:S(2)}) collective-permute-start(bf16[464,128]{1,0:T(8,128)(2,1)} %sum_base.1.refs_0_), channel_id=1, source_target_pairs={{0,3},{1,2},{2,1},{3,0},{4,7},{5,6},{6,5},{7,4},{8,11},{9,10},{10,... | collective-permute-start | bytes 356360 | tf_op jit(solution)/shard_map/ppermute | solution.py:71
  52.0 11.1 %collective-permute-start.13 = (bf16[464,128]{1,0:T(8,128)(2,1)}, bf16[464,128]{1,0:T(8,128)(2,1)S(1)}, u32[]{:S(2)}, u32[]{:S(2)}) collective-permute-start(bf16[464,128]{1,0:T(8,128)(2,1)} %sum_base.1.refs_0_), channel_id=1, source_target_pairs={{0,2},{1,3},{2,0},{3,1},{4,6},{5,7},{6,4},{7,5},{8,10},{9,11},{10,... | collective-permute-start | bytes 356360 | tf_op jit(solution)/shard_map/ppermute | solution.py:71
  52.0 11.1 %collective-permute-start.12 = (bf16[464,128]{1,0:T(8,128)(2,1)}, bf16[464,128]{1,0:T(8,128)(2,1)S(1)}, u32[]{:S(2)}, u32[]{:S(2)}) collective-permute-start(bf16[464,128]{1,0:T(8,128)(2,1)} %sum_base.1.refs_0_), channel_id=1, source_target_pairs={{0,1},{1,0},{2,3},{3,2},{4,5},{5,4},{6,7},{7,6},{8,9},{9,8},{10,11... | collective-permute-start | bytes 356360 | tf_op jit(solution)/shard_map/ppermute | solution.py:71
  57.7 5.4 %copy-start.5 = (bf16[464,128]{1,0:T(8,128)(2,1)}, bf16[464,128]{1,0:T(8,128)(2,1)S(1)}, u32[]{:S(2)}) copy-start(bf16[464,128]{1,0:T(8,128)(2,1)S(1)} %collective-permute-done.14.refs_3_) | copy-start | bytes 356356
  63.1 0.7 copy-start.7
  63.8 0.6 copy-start.8
  66.2 7.1 %collective-permute-start.20 = (bf16[464,128]{1,0:T(8,128)(2,1)}, bf16[464,128]{1,0:T(8,128)(2,1)S(1)}, u32[]{:S(2)}, u32[]{:S(2)}) collective-permute-start(bf16[464,128]{1,0:T(8,128)(2,1)} %sum_pix.1.refs_0_), channel_id=1, source_target_pairs={{0,24},{4,28},{8,16},{12,20},{16,8},{20,12},{24,0},{28,4},{1,25},{... | collective-permute-start | bytes 356360 | tf_op jit(solution)/shard_map/ppermute | solution.py:71
  68.7 5.9 %collective-permute-start.18 = (bf16[464,128]{1,0:T(8,128)(2,1)}, bf16[464,128]{1,0:T(8,128)(2,1)S(1)}, u32[]{:S(2)}, u32[]{:S(2)}) collective-permute-start(bf16[464,128]{1,0:T(8,128)(2,1)} %sum_pix.1.refs_0_), channel_id=1, source_target_pairs={{0,16},{4,20},{8,24},{12,28},{16,0},{20,4},{24,8},{28,12},{1,17},{... | collective-permute-start | bytes 356360 | tf_op jit(solution)/shard_map/ppermute | solution.py:71
  69.2 5.5 %collective-permute-start.16 = (bf16[464,128]{1,0:T(8,128)(2,1)}, bf16[464,128]{1,0:T(8,128)(2,1)S(1)}, u32[]{:S(2)}, u32[]{:S(2)}) collective-permute-start(bf16[464,128]{1,0:T(8,128)(2,1)} %sum_pix.1.refs_0_), channel_id=1, source_target_pairs={{0,8},{4,12},{8,0},{12,4},{16,24},{20,28},{24,16},{28,20},{1,9},{5... | collective-permute-start | bytes 356360 | tf_op jit(solution)/shard_map/ppermute | solution.py:71
  69.7 5.4 %collective-permute-start.15 = (bf16[464,128]{1,0:T(8,128)(2,1)}, bf16[464,128]{1,0:T(8,128)(2,1)S(1)}, u32[]{:S(2)}, u32[]{:S(2)}) collective-permute-start(bf16[464,128]{1,0:T(8,128)(2,1)} %sum_pix.1.refs_0_), channel_id=1, source_target_pairs={{0,4},{4,0},{8,12},{12,8},{16,20},{20,16},{24,28},{28,24},{1,5},{5... | collective-permute-start | bytes 356360 | tf_op jit(solution)/shard_map/ppermute | solution.py:71
  73.3 2.7 %copy-start.9 = (bf16[464,128]{1,0:T(8,128)(2,1)}, bf16[464,128]{1,0:T(8,128)(2,1)S(1)}, u32[]{:S(2)}) copy-start(bf16[464,128]{1,0:T(8,128)(2,1)S(1)} %collective-permute-done.20.refs_6_) | copy-start | bytes 356356
  73.3 1.8 %collective-permute-start.21 = (bf16[464,128]{1,0:T(8,128)(2,1)S(1)}, bf16[464,128]{1,0:T(8,128)(2,1)S(1)}, u32[]{:S(2)}, u32[]{:S(2)}) collective-permute-start(bf16[464,128]{1,0:T(8,128)(2,1)S(1)} %collective-permute-done.20.refs_6_), channel_id=1, source_target_pairs={{0,4},{4,0},{8,12},{12,8},{16,20},{20,16},{24,28},{28,24},{1,5},{5... | collective-permute-start | bytes 356360 | tf_op jit(solution)/shard_map/ppermute | solution.py:71
  74.6 1.5 %copy-start.10 = (bf16[464,128]{1,0:T(8,128)(2,1)}, bf16[464,128]{1,0:T(8,128)(2,1)S(1)}, u32[]{:S(2)}) copy-start(bf16[464,128]{1,0:T(8,128)(2,1)S(1)} %collective-permute-done.18.refs_4_) | copy-start | bytes 356356
  74.6 1.3 %collective-permute-start.19 = (bf16[464,128]{1,0:T(8,128)(2,1)S(1)}, bf16[464,128]{1,0:T(8,128)(2,1)S(1)}, u32[]{:S(2)}, u32[]{:S(2)}) collective-permute-start(bf16[464,128]{1,0:T(8,128)(2,1)S(1)} %collective-permute-done.18.refs_4_), channel_id=1, source_target_pairs={{0,4},{4,0},{8,12},{12,8},{16,20},{20,16},{24,28},{28,24},{1,5},{5... | collective-permute-start | bytes 356360 | tf_op jit(solution)/shard_map/ppermute | solution.py:71
  74.7 1.3 %copy-start.11 = (bf16[464,128]{1,0:T(8,128)(2,1)}, bf16[464,128]{1,0:T(8,128)(2,1)S(1)}, u32[]{:S(2)}) copy-start(bf16[464,128]{1,0:T(8,128)(2,1)S(1)} %collective-permute-done.16.refs_2_) | copy-start | bytes 356356
  74.7 1.3 %collective-permute-start.17 = (bf16[464,128]{1,0:T(8,128)(2,1)S(1)}, bf16[464,128]{1,0:T(8,128)(2,1)S(1)}, u32[]{:S(2)}, u32[]{:S(2)}) collective-permute-start(bf16[464,128]{1,0:T(8,128)(2,1)S(1)} %collective-permute-done.16.refs_2_), channel_id=1, source_target_pairs={{0,4},{4,0},{8,12},{12,8},{16,20},{20,16},{24,28},{28,24},{1,5},{5... | collective-permute-start | bytes 356360 | tf_op jit(solution)/shard_map/ppermute | solution.py:71
  75.1 1.0 %copy-start.12 = (bf16[464,128]{1,0:T(8,128)(2,1)}, bf16[464,128]{1,0:T(8,128)(2,1)S(1)}, u32[]{:S(2)}) copy-start(bf16[464,128]{1,0:T(8,128)(2,1)S(1)} %collective-permute-done.15.refs_1_) | copy-start | bytes 356356
  75.1 1.0 %copy-start.13 = (bf16[464,128]{1,0:T(8,128)(2,1)}, bf16[464,128]{1,0:T(8,128)(2,1)S(1)}, u32[]{:S(2)}) copy-start(bf16[464,128]{1,0:T(8,128)(2,1)S(1)} %collective-permute-done.21.refs_7_) | copy-start | bytes 356356
  75.9 0.6 copy-start.14
  76.5 0.7 copy-start.15

commit v2 on v1

--- a/solution.py
+++ b/solution.py
@@ -18,6 +18,7 @@
 
 GRAM_LIMIT = 1 << 20
 PAD = 16
+VMEM_LIMIT = 12 << 20
 
 
 def project_rows(rounded_amount, columns):
@@ -82,6 +83,7 @@
         in_specs=specs,
         out_specs=out_specs,
         scratch_shapes=list(scratch),
+        compiler_params=pltpu.CompilerParams(vmem_limit_bytes=VMEM_LIMIT),
         name=name,
     )(*args)
 

time: 81.5 us -> 69.9 us (0.86)
  Pallas kernels: 14.9 us -> 6.34 us
  local copies, waits for them, and re-layouts: 6.24 us -> 2.02 us
  waiting for transfers between devices: 33.1 us -> 36 us
  starting transfers between devices: 26.2 us -> 25.1 us
    pallas_call x6, Pallas kernels: 14.9 us -> 6.34 us  [call(): pl.pallas_call(body, out_shape=out_shape, in_specs=specs, out_specs=out_s...]
    unnamed x51 -> x9, local copies, waits for them, and re-layouts: 6.24 us -> 2.02 us
    ppermute x22, waiting for transfers between devices: 33.1 us -> 36 us  [swap(): return lax.ppermute(value, axis, [(i, i ^ offset) for i in range(size)])]
    ppermute x22, starting transfers between devices: 26.2 us -> 25.1 us  [swap(): return lax.ppermute(value, axis, [(i, i ^ offset) for i in range(size)])]
  transfers between devices with their start and end apart: 22 -> 22, of which waited for: 14 -> 14; matrix products, arithmetic and copies ran while one was open for 0% -> 0% of each run, Pallas kernels for 3% -> 1%
where the time goes in v2:
time: 69.9 us; the launch traced here: 69.7 us
  waiting for transfers between devices  36 us (52%)
  starting transfers between devices  25.1 us (36%)
  Pallas kernels  6.34 us (9%)
  local copies, waits for them, and re-layouts  2.02 us (3%)
    ppermute x22, waiting for transfers between devices, swap(): return lax.ppermute(value, axis, [(i, i ^ offset) for i in range(size)])  36 us
    ppermute x22, starting transfers between devices, swap(): return lax.ppermute(value, axis, [(i, i ^ offset) for i in range(size)])  25.1 us
    pallas_call x6, Pallas kernels, call(): pl.pallas_call(body, out_shape=out_shape, in_specs=specs, out_specs=out_s...  6.34 us
    unnamed x9, local copies, waits for them, and re-layouts  2.02 us
  transfers between devices with their start and end apart: 22, of which 14 were waited for; matrix products, arithmetic and copies ran while one was open for 0% of the time, Pallas kernels for 1%

profile of v2, /device:TPU:0, one launch (start us, length us, event | category | flops | bytes accessed | tf_op | source)
XLA Modules:
  0.0 69.7 jit_solution(1079168789744391755)
XLA Ops:
  0.0 0.8 %copy.7.ranks_ref = s32[6,4]{1,0:T(8,128)S(1)} copy(s32[6,4]{0,1:T(4,128)} %param.7) | data formatting | bytes 192 | tf_op args[3]
  0.8 0.1 pad_add_fusion.where_ref
  0.9 1.2 %copy-done = bf16[1,1024,512]{2,1,0:T(8,128)(2,1)S(1)} copy-done((bf16[1,1024,512]{2,1,0:T(8,128)(2,1)S(1)}, bf16[1,1024,512]{2,1,0:T(8,128)(2,1)}, u32[]{:S(2)}) %copy-start) | copy-done | bytes 1048600
  2.1 0.9 %pack.1 = (bf16[256,512]{1,0:T(8,128)(2,1)S(1)}, bf16[256,512]{1,0:T(8,128)(2,1)S(1)}, bf16[256,512]{1,0:T(8,128)(2,1)S(1)}, bf16[256,512]{1,0:T(8,128)(2,1)S(1)}) custom-call(s32[2]{0:T(128)S(1)} %pad_add_fusion.where_ref, s32[6,4]{1,0:T(8,128)S(1)} %copy.7.ranks_ref, bf16[1024,512]{1,0:T(8,128)(2,1)S(1)} %bitcast.7), custom_call_target="tpu_custom_call" | custom-call | tf_op jit(solution)/shard_map/pack/pallas_call | solution.py:80
  3.0 3.1 %collective-permute-start = (bf16[256,512]{1,0:T(8,128)(2,1)S(1)}, bf16[256,512]{1,0:T(8,128)(2,1)S(1)}, u32[]{:S(2)}, u32[]{:S(2)}) collective-permute-start(bf16[256,512]{1,0:T(8,128)(2,1)S(1)} %get-tuple-element.18), channel_id=1, source_target_pairs={{0,1},{1,0},{2,3},{3,2},{4,5},{5,4},{6,7},{7,6},{8,9},{9,8},{10,11... | collective-permute-start | bytes 786440 | tf_op jit(solution)/shard_map/ppermute | solution.py:72
  6.1 2.6 %collective-permute-start.1 = (bf16[256,512]{1,0:T(8,128)(2,1)S(1)}, bf16[256,512]{1,0:T(8,128)(2,1)S(1)}, u32[]{:S(2)}, u32[]{:S(2)}) collective-permute-start(bf16[256,512]{1,0:T(8,128)(2,1)S(1)} %get-tuple-element.19), channel_id=1, source_target_pairs={{0,2},{1,3},{2,0},{3,1},{4,6},{5,7},{6,4},{7,5},{8,10},{9,11},{10,... | collective-permute-start | bytes 786440 | tf_op jit(solution)/shard_map/ppermute | solution.py:72
  8.7 0.0 collective-permute-start.2
  8.7 0.0 copy-start.2
  8.7 0.5 collective-permute-start.5
  9.2 1.4 %collective-permute-start.4 = (bf16[32,128]{1,0:T(8,128)(2,1)S(1)}, bf16[32,128]{1,0:T(8,128)(2,1)S(1)}, u32[]{:S(2)}, u32[]{:S(2)}) collective-permute-start(bf16[32,128]{1,0:T(8,128)(2,1)S(1)} %convert_element_type.3.refs_0_), channel_id=1, source_target_pairs={{0,8},{4,12},{8,0},{12,4},{1,9},{5,13},{9,1},{13,5},{2,10},{6,14},... | collective-permute-start | bytes 24584 | tf_op jit(solution)/shard_map/ppermute | solution.py:72
  10.6 1.3 %collective-permute-done.5.refs_3_ = bf16[32,128]{1,0:T(8,128)(2,1)S(1)} collective-permute-done((bf16[32,128]{1,0:T(8,128)(2,1)S(1)}, bf16[32,128]{1,0:T(8,128)(2,1)S(1)}, u32[]{:S(2)}, u32[]{:S(2)}) %collective-permute-start.5) | collective-permute-done | bytes 8224 | tf_op jit(solution)/shard_map/ppermute | solution.py:72
  11.8 0.4 collective-permute-start.3
  12.2 0.6 collective-permute-done.4.refs_2_
  12.8 0.3 collective-permute-done.3.refs_1_
  13.1 0.9 %first.1 = (f32[32,256]{1,0:T(8,128)S(1)}, f32[32,256]{1,0:T(8,128)S(1)}, f32[32,256]{1,0:T(8,128)S(1)}, f32[32,256]{1,0:T(8,128)S(1)}) custom-call(s32[2]{0:T(128)S(1)} %pad_add_fusion.where_ref, bf16[1024,512]{1,0:T(8,128)(2,1)S(1)} %bitcast.8, bf16[32,128]{1,0:T(8,128)(2,1)S(1)} %convert_element_type.3.refs_0_, ...), custom_call_target="tpu_custom_call" | custom-call | tf_op jit(solution)/shard_map/first/pallas_call | solution.py:80
  14.0 0.9 %collective-permute-start.6 = (f32[32,256]{1,0:T(8,128)S(1)}, f32[32,256]{1,0:T(8,128)S(1)}, u32[]{:S(2)}, u32[]{:S(2)}) collective-permute-start(f32[32,256]{1,0:T(8,128)S(1)} %get-tuple-element.22), channel_id=1, source_target_pairs={{0,1},{1,0},{2,3},{3,2},{4,5},{5,4},{6,7},{7,6},{8,9},{9,8},{10,11... | collective-permute-start | bytes 98312 | tf_op jit(solution)/shard_map/ppermute | solution.py:72
  14.9 3.5 %collective-permute-start.7 = (f32[32,256]{1,0:T(8,128)S(1)}, f32[32,256]{1,0:T(8,128)S(1)}, u32[]{:S(2)}, u32[]{:S(2)}) collective-permute-start(f32[32,256]{1,0:T(8,128)S(1)} %get-tuple-element.23), channel_id=1, source_target_pairs={{0,2},{1,3},{2,0},{3,1},{4,6},{5,7},{6,4},{7,5},{8,10},{9,11},{10,... | collective-permute-start | bytes 98312 | tf_op jit(solution)/shard_map/ppermute | solution.py:72
  18.4 5.6 %collective-permute-done.6.refs_5_ = f32[32,256]{1,0:T(8,128)S(1)} collective-permute-done((f32[32,256]{1,0:T(8,128)S(1)}, f32[32,256]{1,0:T(8,128)S(1)}, u32[]{:S(2)}, u32[]{:S(2)}) %collective-permute-start.6) | collective-permute-done | bytes 32800 | tf_op jit(solution)/shard_map/ppermute | solution.py:72
  24.0 2.5 %collective-permute-start.8 = (f32[32,256]{1,0:T(8,128)S(1)}, f32[32,256]{1,0:T(8,128)S(1)}, u32[]{:S(2)}, u32[]{:S(2)}) collective-permute-start(f32[32,256]{1,0:T(8,128)S(1)} %get-tuple-element.24), channel_id=1, source_target_pairs={{0,3},{1,2},{2,1},{3,0},{4,7},{5,6},{6,5},{7,4},{8,11},{9,10},{10,... | collective-permute-start | bytes 98312 | tf_op jit(solution)/shard_map/ppermute | solution.py:72
  26.5 7.6 %collective-permute-done.7.refs_6_ = f32[32,256]{1,0:T(8,128)S(1)} collective-permute-done((f32[32,256]{1,0:T(8,128)S(1)}, f32[32,256]{1,0:T(8,128)S(1)}, u32[]{:S(2)}, u32[]{:S(2)}) %collective-permute-start.7) | collective-permute-done | bytes 32800 | tf_op jit(solution)/shard_map/ppermute | solution.py:72
  34.1 0.0 collective-permute-done.8.refs_7_
  34.1 0.0 collective-permute-done.refs_1_
  34.1 0.0 collective-permute-done.2.refs_3_
  34.2 1.0 %gram.1 = (bf16[464,128]{1,0:T(8,128)(2,1)S(1)}, bf16[464,128]{1,0:T(8,128)(2,1)S(1)}, bf16[464,128]{1,0:T(8,128)(2,1)S(1)}, bf16[464,128]{1,0:T(8,128)(2,1)S(1)}) custom-call(s32[2]{0:T(128)S(1)} %pad_add_fusion.where_ref, s32[6,4]{1,0:T(8,128)S(1)} %copy.7.ranks_ref, f32[32,1024]{1,0:T(8,128)S(1)} %copy-done.2, f32[32,128]{1,0:T(8,128)S(1)} %bitcast.10, ...), custom_call_target="tpu_custom_call" | custom-call | tf_op jit(solution)/shard_map/gram/pallas_call | solution.py:80
  35.2 0.1 collective-permute-start.9
  35.2 1.6 %collective-permute-start.10 = (bf16[464,128]{1,0:T(8,128)(2,1)S(1)}, bf16[464,128]{1,0:T(8,128)(2,1)S(1)}, u32[]{:S(2)}, u32[]{:S(2)}) collective-permute-start(bf16[464,128]{1,0:T(8,128)(2,1)S(1)} %get-tuple-element.27), channel_id=1, source_target_pairs={{0,8},{4,12},{8,0},{12,4},{1,9},{5,13},{9,1},{13,5},{2,10},{6,14},... | collective-permute-start | bytes 356360 | tf_op jit(solution)/shard_map/ppermute | solution.py:72
  36.8 0.3 collective-permute-start.11
  37.1 0.0 collective-permute-done.9.refs_1_
  37.1 4.3 %collective-permute-done.10.refs_2_ = bf16[464,128]{1,0:T(8,128)(2,1)S(1)} collective-permute-done((bf16[464,128]{1,0:T(8,128)(2,1)S(1)}, bf16[464,128]{1,0:T(8,128)(2,1)S(1)}, u32[]{:S(2)}, u32[]{:S(2)}) %collective-permute-start.10) | collective-permute-done | bytes 118816 | tf_op jit(solution)/shard_map/ppermute | solution.py:72
  41.4 1.5 %collective-permute-done.11.refs_3_ = bf16[464,128]{1,0:T(8,128)(2,1)S(1)} collective-permute-done((bf16[464,128]{1,0:T(8,128)(2,1)S(1)}, bf16[464,128]{1,0:T(8,128)(2,1)S(1)}, u32[]{:S(2)}, u32[]{:S(2)}) %collective-permute-start.11) | collective-permute-done | bytes 118816 | tf_op jit(solution)/shard_map/ppermute | solution.py:72
  42.9 0.1 sum_base.1.refs_0_
  43.0 2.5 %collective-permute-start.14 = (bf16[464,128]{1,0:T(8,128)(2,1)S(1)}, bf16[464,128]{1,0:T(8,128)(2,1)S(1)}, u32[]{:S(2)}, u32[]{:S(2)}) collective-permute-start(bf16[464,128]{1,0:T(8,128)(2,1)S(1)} %sum_base.1.refs_0_), channel_id=1, source_target_pairs={{0,3},{1,2},{2,1},{3,0},{4,7},{5,6},{6,5},{7,4},{8,11},{9,10},{10,... | collective-permute-start | bytes 356360 | tf_op jit(solution)/shard_map/ppermute | solution.py:72
  45.5 1.9 %collective-permute-start.12 = (bf16[464,128]{1,0:T(8,128)(2,1)S(1)}, bf16[464,128]{1,0:T(8,128)(2,1)S(1)}, u32[]{:S(2)}, u32[]{:S(2)}) collective-permute-start(bf16[464,128]{1,0:T(8,128)(2,1)S(1)} %sum_base.1.refs_0_), channel_id=1, source_target_pairs={{0,1},{1,0},{2,3},{3,2},{4,5},{5,4},{6,7},{7,6},{8,9},{9,8},{10,11... | collective-permute-start | bytes 356360 | tf_op jit(solution)/shard_map/ppermute | solution.py:72
  47.4 3.6 %collective-permute-done.14.refs_3_ = bf16[464,128]{1,0:T(8,128)(2,1)S(1)} collective-permute-done((bf16[464,128]{1,0:T(8,128)(2,1)S(1)}, bf16[464,128]{1,0:T(8,128)(2,1)S(1)}, u32[]{:S(2)}, u32[]{:S(2)}) %collective-permute-start.14) | collective-permute-done | bytes 118816 | tf_op jit(solution)/shard_map/ppermute | solution.py:72
  51.0 5.5 %collective-permute-done.13.refs_2_ = bf16[464,128]{1,0:T(8,128)(2,1)S(1)} collective-permute-done((bf16[464,128]{1,0:T(8,128)(2,1)S(1)}, bf16[464,128]{1,0:T(8,128)(2,1)S(1)}, u32[]{:S(2)}, u32[]{:S(2)}) %collective-permute-start.13) | collective-permute-done | bytes 118816 | tf_op jit(solution)/shard_map/ppermute | solution.py:72
  56.5 0.1 sum_pix.1.refs_0_
  56.6 2.5 %collective-permute-start.20 = (bf16[464,128]{1,0:T(8,128)(2,1)S(1)}, bf16[464,128]{1,0:T(8,128)(2,1)S(1)}, u32[]{:S(2)}, u32[]{:S(2)}) collective-permute-start(bf16[464,128]{1,0:T(8,128)(2,1)S(1)} %sum_pix.1.refs_0_), channel_id=1, source_target_pairs={{0,24},{4,28},{8,16},{12,20},{16,8},{20,12},{24,0},{28,4},{1,25},{... | collective-permute-start | bytes 356360 | tf_op jit(solution)/shard_map/ppermute | solution.py:72
  59.1 0.5 collective-permute-start.18
  59.6 0.5 collective-permute-start.16
  60.1 3.4 %collective-permute-done.20.refs_6_ = bf16[464,128]{1,0:T(8,128)(2,1)S(1)} collective-permute-done((bf16[464,128]{1,0:T(8,128)(2,1)S(1)}, bf16[464,128]{1,0:T(8,128)(2,1)S(1)}, u32[]{:S(2)}, u32[]{:S(2)}) %collective-permute-start.20) | collective-permute-done | bytes 118816 | tf_op jit(solution)/shard_map/ppermute | solution.py:72
  63.6 0.0 collective-permute-start.21
  63.6 1.2 %collective-permute-done.18.refs_4_ = bf16[464,128]{1,0:T(8,128)(2,1)S(1)} collective-permute-done((bf16[464,128]{1,0:T(8,128)(2,1)S(1)}, bf16[464,128]{1,0:T(8,128)(2,1)S(1)}, u32[]{:S(2)}, u32[]{:S(2)}) %collective-permute-start.18) | collective-permute-done | bytes 118816 | tf_op jit(solution)/shard_map/ppermute | solution.py:72
  64.8 0.2 collective-permute-done.16.refs_2_
  65.0 0.4 collective-permute-start.17
  65.3 0.0 collective-permute-done.21.refs_7_
  65.3 0.8 %collective-permute-done.19.refs_5_ = bf16[464,128]{1,0:T(8,128)(2,1)S(1)} collective-permute-done((bf16[464,128]{1,0:T(8,128)(2,1)S(1)}, bf16[464,128]{1,0:T(8,128)(2,1)S(1)}, u32[]{:S(2)}, u32[]{:S(2)}) %collective-permute-start.19) | collective-permute-done | bytes 118816 | tf_op jit(solution)/shard_map/ppermute | solution.py:72
  66.1 0.2 collective-permute-done.17.refs_3_
  66.3 3.4 %iterate.1 = f32[32,128]{1,0:T(8,128)} custom-call(s32[2]{0:T(128)S(1)} %pad_add_fusion.where_ref, s32[6,4]{1,0:T(8,128)S(1)} %copy.7.ranks_ref, bf16[464,128]{1,0:T(8,128)(2,1)S(1)} %sum_pix.1.refs_0_, bf16[464,128]{1,0:T(8,128)(2,1)S(1)} %collective-permute-done.15.refs_1_, bf16[464,128]{1,0:T(8,128)(2,1)S(1)} %collective-permute-done.16.refs_2_, ...), custom_call_target="tpu_custom_call" | custom-call | tf_op jit(solution)/shard_map/iterate/pallas_call | solution.py:80
  (13 shorter events, 0.0 us)
Async XLA Ops:
  0.0 8.7 %copy-start.3 = (f32[32,1,1,128]{3,2,1,0:T(1,128)S(1)}, f32[32,1,1,128]{3,2,1,0:T(1,128)}, u32[]{:S(2)}) copy-start(f32[32,1,1,128]{3,2,1,0:T(1,128)} %param.6) | copy-start | bytes 49156
  0.9 1.2 %copy-start = (bf16[1,1024,512]{2,1,0:T(8,128)(2,1)S(1)}, bf16[1,1024,512]{2,1,0:T(8,128)(2,1)}, u32[]{:S(2)}) copy-start(bf16[1,1024,512]{2,1,0:T(8,128)(2,1)} %param.4) | copy-start | bytes 3145732
  2.1 11.0 %copy-start.1 = (bf16[1,1024,512]{2,1,0:T(8,128)(2,1)S(1)}, bf16[1,1024,512]{2,1,0:T(8,128)(2,1)}, u32[]{:S(2)}) copy-start(bf16[1,1024,512]{2,1,0:T(8,128)(2,1)} %param.4) | copy-start | bytes 3145732
  3.0 31.1 %collective-permute-start = (bf16[256,512]{1,0:T(8,128)(2,1)S(1)}, bf16[256,512]{1,0:T(8,128)(2,1)S(1)}, u32[]{:S(2)}, u32[]{:S(2)}) collective-permute-start(bf16[256,512]{1,0:T(8,128)(2,1)S(1)} %get-tuple-element.18), channel_id=1, source_target_pairs={{0,1},{1,0},{2,3},{3,2},{4,5},{5,4},{6,7},{7,6},{8,9},{9,8},{10,11... | collective-permute-start | bytes 786440 | tf_op jit(solution)/shard_map/ppermute | solution.py:72
  6.1 28.0 %collective-permute-start.1 = (bf16[256,512]{1,0:T(8,128)(2,1)S(1)}, bf16[256,512]{1,0:T(8,128)(2,1)S(1)}, u32[]{:S(2)}, u32[]{:S(2)}) collective-permute-start(bf16[256,512]{1,0:T(8,128)(2,1)S(1)} %get-tuple-element.19), channel_id=1, source_target_pairs={{0,2},{1,3},{2,0},{3,1},{4,6},{5,7},{6,4},{7,5},{8,10},{9,11},{10,... | collective-permute-start | bytes 786440 | tf_op jit(solution)/shard_map/ppermute | solution.py:72
  8.7 25.4 %collective-permute-start.2 = (bf16[256,512]{1,0:T(8,128)(2,1)S(1)}, bf16[256,512]{1,0:T(8,128)(2,1)S(1)}, u32[]{:S(2)}, u32[]{:S(2)}) collective-permute-start(bf16[256,512]{1,0:T(8,128)(2,1)S(1)} %get-tuple-element.20), channel_id=1, source_target_pairs={{0,3},{1,2},{2,1},{3,0},{4,7},{5,6},{6,5},{7,4},{8,11},{9,10},{10,... | collective-permute-start | bytes 786440 | tf_op jit(solution)/shard_map/ppermute | solution.py:72
  8.7 25.4 %copy-start.2 = (f32[32,1024]{1,0:T(8,128)S(1)}, f32[32,1024]{1,0:T(8,128)}, u32[]{:S(2)}) copy-start(f32[32,1024]{1,0:T(8,128)} %y_ref.1) | copy-start | bytes 393220
  8.7 3.1 %collective-permute-start.5 = (bf16[32,128]{1,0:T(8,128)(2,1)S(1)}, bf16[32,128]{1,0:T(8,128)(2,1)S(1)}, u32[]{:S(2)}, u32[]{:S(2)}) collective-permute-start(bf16[32,128]{1,0:T(8,128)(2,1)S(1)} %convert_element_type.3.refs_0_), channel_id=1, source_target_pairs={{0,12},{4,8},{8,4},{12,0},{1,13},{5,9},{9,5},{13,1},{2,14},{6,10},... | collective-permute-start | bytes 24584 | tf_op jit(solution)/shard_map/ppermute | solution.py:72
  9.2 3.7 %collective-permute-start.4 = (bf16[32,128]{1,0:T(8,128)(2,1)S(1)}, bf16[32,128]{1,0:T(8,128)(2,1)S(1)}, u32[]{:S(2)}, u32[]{:S(2)}) collective-permute-start(bf16[32,128]{1,0:T(8,128)(2,1)S(1)} %convert_element_type.3.refs_0_), channel_id=1, source_target_pairs={{0,8},{4,12},{8,0},{12,4},{1,9},{5,13},{9,1},{13,5},{2,10},{6,14},... | collective-permute-start | bytes 24584 | tf_op jit(solution)/shard_map/ppermute | solution.py:72
  11.8 1.2 %collective-permute-start.3 = (bf16[32,128]{1,0:T(8,128)(2,1)S(1)}, bf16[32,128]{1,0:T(8,128)(2,1)S(1)}, u32[]{:S(2)}, u32[]{:S(2)}) collective-permute-start(bf16[32,128]{1,0:T(8,128)(2,1)S(1)} %convert_element_type.3.refs_0_), channel_id=1, source_target_pairs={{0,4},{4,0},{8,12},{12,8},{1,5},{5,1},{9,13},{13,9},{2,6},{6,2},{1... | collective-permute-start | bytes 24584 | tf_op jit(solution)/shard_map/ppermute | solution.py:72
  14.0 10.0 %collective-permute-start.6 = (f32[32,256]{1,0:T(8,128)S(1)}, f32[32,256]{1,0:T(8,128)S(1)}, u32[]{:S(2)}, u32[]{:S(2)}) collective-permute-start(f32[32,256]{1,0:T(8,128)S(1)} %get-tuple-element.22), channel_id=1, source_target_pairs={{0,1},{1,0},{2,3},{3,2},{4,5},{5,4},{6,7},{7,6},{8,9},{9,8},{10,11... | collective-permute-start | bytes 98312 | tf_op jit(solution)/shard_map/ppermute | solution.py:72
  14.9 19.2 %collective-permute-start.7 = (f32[32,256]{1,0:T(8,128)S(1)}, f32[32,256]{1,0:T(8,128)S(1)}, u32[]{:S(2)}, u32[]{:S(2)}) collective-permute-start(f32[32,256]{1,0:T(8,128)S(1)} %get-tuple-element.23), channel_id=1, source_target_pairs={{0,2},{1,3},{2,0},{3,1},{4,6},{5,7},{6,4},{7,5},{8,10},{9,11},{10,... | collective-permute-start | bytes 98312 | tf_op jit(solution)/shard_map/ppermute | solution.py:72
  24.0 10.1 %collective-permute-start.8 = (f32[32,256]{1,0:T(8,128)S(1)}, f32[32,256]{1,0:T(8,128)S(1)}, u32[]{:S(2)}, u32[]{:S(2)}) collective-permute-start(f32[32,256]{1,0:T(8,128)S(1)} %get-tuple-element.24), channel_id=1, source_target_pairs={{0,3},{1,2},{2,1},{3,0},{4,7},{5,6},{6,5},{7,4},{8,11},{9,10},{10,... | collective-permute-start | bytes 98312 | tf_op jit(solution)/shard_map/ppermute | solution.py:72
  35.2 1.9 %collective-permute-start.9 = (bf16[464,128]{1,0:T(8,128)(2,1)S(1)}, bf16[464,128]{1,0:T(8,128)(2,1)S(1)}, u32[]{:S(2)}, u32[]{:S(2)}) collective-permute-start(bf16[464,128]{1,0:T(8,128)(2,1)S(1)} %get-tuple-element.26), channel_id=1, source_target_pairs={{0,4},{4,0},{8,12},{12,8},{1,5},{5,1},{9,13},{13,9},{2,6},{6,2},{1... | collective-permute-start | bytes 356360 | tf_op jit(solution)/shard_map/ppermute | solution.py:72
  35.2 6.2 %collective-permute-start.10 = (bf16[464,128]{1,0:T(8,128)(2,1)S(1)}, bf16[464,128]{1,0:T(8,128)(2,1)S(1)}, u32[]{:S(2)}, u32[]{:S(2)}) collective-permute-start(bf16[464,128]{1,0:T(8,128)(2,1)S(1)} %get-tuple-element.27), channel_id=1, source_target_pairs={{0,8},{4,12},{8,0},{12,4},{1,9},{5,13},{9,1},{13,5},{2,10},{6,14},... | collective-permute-start | bytes 356360 | tf_op jit(solution)/shard_map/ppermute | solution.py:72
  36.8 6.1 %collective-permute-start.11 = (bf16[464,128]{1,0:T(8,128)(2,1)S(1)}, bf16[464,128]{1,0:T(8,128)(2,1)S(1)}, u32[]{:S(2)}, u32[]{:S(2)}) collective-permute-start(bf16[464,128]{1,0:T(8,128)(2,1)S(1)} %get-tuple-element.28), channel_id=1, source_target_pairs={{0,12},{4,8},{8,4},{12,0},{1,13},{5,9},{9,5},{13,1},{2,14},{6,10},... | collective-permute-start | bytes 356360 | tf_op jit(solution)/shard_map/ppermute | solution.py:72
  43.0 8.1 %collective-permute-start.14 = (bf16[464,128]{1,0:T(8,128)(2,1)S(1)}, bf16[464,128]{1,0:T(8,128)(2,1)S(1)}, u32[]{:S(2)}, u32[]{:S(2)}) collective-permute-start(bf16[464,128]{1,0:T(8,128)(2,1)S(1)} %sum_base.1.refs_0_), channel_id=1, source_target_pairs={{0,3},{1,2},{2,1},{3,0},{4,7},{5,6},{6,5},{7,4},{8,11},{9,10},{10,... | collective-permute-start | bytes 356360 | tf_op jit(solution)/shard_map/ppermute | solution.py:72
  45.5 11.0 %collective-permute-start.13 = (bf16[464,128]{1,0:T(8,128)(2,1)S(1)}, bf16[464,128]{1,0:T(8,128)(2,1)S(1)}, u32[]{:S(2)}, u32[]{:S(2)}) collective-permute-start(bf16[464,128]{1,0:T(8,128)(2,1)S(1)} %sum_base.1.refs_0_), channel_id=1, source_target_pairs={{0,2},{1,3},{2,0},{3,1},{4,6},{5,7},{6,4},{7,5},{8,10},{9,11},{10,... | collective-permute-start | bytes 356360 | tf_op jit(solution)/shard_map/ppermute | solution.py:72
  45.5 11.0 %collective-permute-start.12 = (bf16[464,128]{1,0:T(8,128)(2,1)S(1)}, bf16[464,128]{1,0:T(8,128)(2,1)S(1)}, u32[]{:S(2)}, u32[]{:S(2)}) collective-permute-start(bf16[464,128]{1,0:T(8,128)(2,1)S(1)} %sum_base.1.refs_0_), channel_id=1, source_target_pairs={{0,1},{1,0},{2,3},{3,2},{4,5},{5,4},{6,7},{7,6},{8,9},{9,8},{10,11... | collective-permute-start | bytes 356360 | tf_op jit(solution)/shard_map/ppermute | solution.py:72
  56.6 7.0 %collective-permute-start.20 = (bf16[464,128]{1,0:T(8,128)(2,1)S(1)}, bf16[464,128]{1,0:T(8,128)(2,1)S(1)}, u32[]{:S(2)}, u32[]{:S(2)}) collective-permute-start(bf16[464,128]{1,0:T(8,128)(2,1)S(1)} %sum_pix.1.refs_0_), channel_id=1, source_target_pairs={{0,24},{4,28},{8,16},{12,20},{16,8},{20,12},{24,0},{28,4},{1,25},{... | collective-permute-start | bytes 356360 | tf_op jit(solution)/shard_map/ppermute | solution.py:72
  59.1 5.7 %collective-permute-start.18 = (bf16[464,128]{1,0:T(8,128)(2,1)S(1)}, bf16[464,128]{1,0:T(8,128)(2,1)S(1)}, u32[]{:S(2)}, u32[]{:S(2)}) collective-permute-start(bf16[464,128]{1,0:T(8,128)(2,1)S(1)} %sum_pix.1.refs_0_), channel_id=1, source_target_pairs={{0,16},{4,20},{8,24},{12,28},{16,0},{20,4},{24,8},{28,12},{1,17},{... | collective-permute-start | bytes 356360 | tf_op jit(solution)/shard_map/ppermute | solution.py:72
  59.6 5.3 %collective-permute-start.16 = (bf16[464,128]{1,0:T(8,128)(2,1)S(1)}, bf16[464,128]{1,0:T(8,128)(2,1)S(1)}, u32[]{:S(2)}, u32[]{:S(2)}) collective-permute-start(bf16[464,128]{1,0:T(8,128)(2,1)S(1)} %sum_pix.1.refs_0_), channel_id=1, source_target_pairs={{0,8},{4,12},{8,0},{12,4},{16,24},{20,28},{24,16},{28,20},{1,9},{5... | collective-permute-start | bytes 356360 | tf_op jit(solution)/shard_map/ppermute | solution.py:72
  60.1 5.2 %collective-permute-start.15 = (bf16[464,128]{1,0:T(8,128)(2,1)S(1)}, bf16[464,128]{1,0:T(8,128)(2,1)S(1)}, u32[]{:S(2)}, u32[]{:S(2)}) collective-permute-start(bf16[464,128]{1,0:T(8,128)(2,1)S(1)} %sum_pix.1.refs_0_), channel_id=1, source_target_pairs={{0,4},{4,0},{8,12},{12,8},{16,20},{20,16},{24,28},{28,24},{1,5},{5... | collective-permute-start | bytes 356360 | tf_op jit(solution)/shard_map/ppermute | solution.py:72
  63.6 1.8 %collective-permute-start.21 = (bf16[464,128]{1,0:T(8,128)(2,1)S(1)}, bf16[464,128]{1,0:T(8,128)(2,1)S(1)}, u32[]{:S(2)}, u32[]{:S(2)}) collective-permute-start(bf16[464,128]{1,0:T(8,128)(2,1)S(1)} %collective-permute-done.20.refs_6_), channel_id=1, source_target_pairs={{0,4},{4,0},{8,12},{12,8},{16,20},{20,16},{24,28},{28,24},{1,5},{5... | collective-permute-start | bytes 356360 | tf_op jit(solution)/shard_map/ppermute | solution.py:72
  64.8 1.3 %collective-permute-start.19 = (bf16[464,128]{1,0:T(8,128)(2,1)S(1)}, bf16[464,128]{1,0:T(8,128)(2,1)S(1)}, u32[]{:S(2)}, u32[]{:S(2)}) collective-permute-start(bf16[464,128]{1,0:T(8,128)(2,1)S(1)} %collective-permute-done.18.refs_4_), channel_id=1, source_target_pairs={{0,4},{4,0},{8,12},{12,8},{16,20},{20,16},{24,28},{28,24},{1,5},{5... | collective-permute-start | bytes 356360 | tf_op jit(solution)/shard_map/ppermute | solution.py:72
  65.0 1.3 %collective-permute-start.17 = (bf16[464,128]{1,0:T(8,128)(2,1)S(1)}, bf16[464,128]{1,0:T(8,128)(2,1)S(1)}, u32[]{:S(2)}, u32[]{:S(2)}) collective-permute-start(bf16[464,128]{1,0:T(8,128)(2,1)S(1)} %collective-permute-done.16.refs_2_), channel_id=1, source_target_pairs={{0,4},{4,0},{8,12},{12,8},{16,20},{20,16},{24,28},{28,24},{1,5},{5... | collective-permute-start | bytes 356360 | tf_op jit(solution)/shard_map/ppermute | solution.py:72

commit v3 on v2

--- a/solution.py
+++ b/solution.py
@@ -18,6 +18,7 @@
 
 GRAM_LIMIT = 1 << 20
 PAD = 16
+CAPACITY = 2
 VMEM_LIMIT = 12 << 20
 
 
@@ -93,21 +94,37 @@
     return high, (value - high.astype(jnp.float32)).astype(jnp.bfloat16)
 
 
-def pack_body(slots, where_ref, ranks_ref, a_ref, *outs):
+def kept_tiles(ranks_ref, slots):
+    count = jnp.int32(0)
+    table = []
+    for j in range(ranks_ref.shape[0]):
+        rank = ranks_ref[j, 0]
+        kept = rank < slots
+        table.append((rank, kept, count))
+        count = count + jnp.where(kept, 1, 0)
+    return table, count
+
+
+def pack_body(slots, first, where_ref, ranks_ref, a_ref, *outs):
     pix = where_ref[0]
-    tiles = a_ref.shape[1] // TILE
-    quarter = outs[0].shape[0]
-    for d, out in enumerate(outs):
-        rows = pl.ds(pl.multiple_of((pix ^ d) * quarter, quarter), quarter)
-        for r in range(slots):
-            tile = jnp.int32(0)
-            owned = jnp.int32(0)
-            for j in range(tiles):
-                hit = ranks_ref[0, j] == r
-                tile = jnp.where(hit, j, tile)
-                owned = jnp.where(hit, 1, owned)
-            block = a_ref[rows, pl.ds(pl.multiple_of(tile * TILE, TILE), TILE)]
-            out[:, r * TILE : (r + 1) * TILE] = jnp.where(owned == 1, block, jnp.zeros_like(block))
+    quarter = a_ref.shape[0] // (len(outs) + 1)
+    places = (outs[0].shape[0] - PAD) // quarter
+    table, count = kept_tiles(ranks_ref, slots)
+    rows = lax.broadcasted_iota(jnp.int32, (PAD, TILE), 0)
+    notes = jnp.where(rows == PAD - 1, count, -1)
+    for i in range(places):
+        tile, slot = jnp.int32(0), jnp.int32(-1)
+        for j, (rank, kept, before) in enumerate(table):
+            hit = jnp.logical_and(kept, before == first + i)
+            tile = jnp.where(hit, j, tile)
+            slot = jnp.where(hit, rank, slot)
+        notes = jnp.where(rows == i, slot, notes)
+        lanes = pl.ds(pl.multiple_of(tile * TILE, TILE), TILE)
+        for d, out in enumerate(outs):
+            at = pl.ds(pl.multiple_of((pix ^ (d + 1)) * quarter, quarter), quarter)
+            out[i * quarter : (i + 1) * quarter, :] = a_ref[at, lanes]
+    for out in outs:
+        out[places * quarter :, :] = notes.astype(jnp.float32).astype(jnp.bfloat16)
 
 
 def first_body(where_ref, a_ref, *refs):
@@ -120,9 +137,10 @@
         x_ref[:, pl.ds(pl.multiple_of((base ^ d) * TILE, TILE), TILE)] = share[...]
     for d, out in enumerate(outs):
         rows = pl.ds(pl.multiple_of((pix ^ d) * quarter, quarter), quarter)
-        out[...] = lax.dot_general(
+        piece = lax.dot_general(
             x_ref[...], a_ref[rows, :], (((1,), (1,)), ((), ())), preferred_element_type=jnp.float32
         )
+        out[...] = piece.astype(out.dtype)
 
 
 def in_order(values, index):
@@ -138,18 +156,33 @@
     return [(r, s) for r in range(slots) for s in range(r, slots)]
 
 
-def gram_body(slots, n_pix, where_ref, ranks_ref, y_ref, x0_ref, *refs):
+def gram_body(slots, n_pix, n_parts, where_ref, ranks_ref, y_ref, x0_ref, a_ref, *refs):
     pix, base = where_ref[0], where_ref[1]
-    parts, preds = refs[:n_pix], refs[n_pix : 2 * n_pix]
-    *outs, all_ref = refs[2 * n_pix :]
+    parts, preds = refs[:n_parts], refs[n_parts : n_parts + n_pix]
+    *outs, all_ref = refs[n_parts + n_pix :]
     n_base = len(outs)
     chans, quarter = preds[0].shape
-    a = parts[0][...]
-    for part in parts[1:]:
-        a = a + part[...]
-    pred = preds[0][...]
+    table, _ = kept_tiles(ranks_ref, slots)
+    own_rows = pl.ds(pl.multiple_of(pix * quarter, quarter), quarter)
+    columns = []
+    for r in range(slots):
+        tile, owned = jnp.int32(0), jnp.int32(0)
+        for j, (rank, _, _) in enumerate(table):
+            tile = jnp.where(rank == r, j, tile)
+            owned = jnp.where(rank == r, 1, owned)
+        block = a_ref[own_rows, pl.ds(pl.multiple_of(tile * TILE, TILE), TILE)]
+        block = jnp.where(owned == 1, block, jnp.zeros_like(block))
+        for part in parts:
+            places = (part.shape[0] - PAD) // quarter
+            notes = part[places * quarter :, :].astype(jnp.float32)
+            for i in range(places):
+                hit = jnp.broadcast_to(notes[i : i + 1] == r, block.shape)
+                block = jnp.where(hit, part[i * quarter : (i + 1) * quarter, :], block)
+        columns.append(block)
+    a = jnp.concatenate(columns, axis=1)
+    pred = preds[0][...].astype(jnp.float32)
     for piece in preds[1:]:
-        pred = pred + piece[...]
+        pred = pred + piece[...].astype(jnp.float32)
     y = y_ref[:, pl.ds(pl.multiple_of(pix * quarter, quarter), quarter)]
     resid = (y - pred).astype(jnp.bfloat16)
     y_hi, y_lo = split(y)
@@ -157,7 +190,7 @@
     sides = jnp.dot(left, a, preferred_element_type=jnp.float32)
     data = sides[:chans] + sides[chans : 2 * chans]
     moved = descent_stride * sides[2 * chans :]
-    rank = ranks_ref[0, base]
+    rank = ranks_ref[base, 0]
     gram = lax.dot_general(a, a, (((0,), (0,)), ((), ())), preferred_element_type=jnp.float32)
     rows = lax.broadcasted_iota(jnp.int32, (TILE, TILE), 0)
     cols = lax.broadcasted_iota(jnp.int32, (TILE, TILE), 1)
@@ -268,7 +301,7 @@
             states[g] = states[g] + descent_stride * (datas[g] - product)
     for r in range(slots):
         last_ref[r] = states[0][:, r * TILE : (r + 1) * TILE]
-    rank = ranks_ref[0, base]
+    rank = ranks_ref[base, 0]
     kept = last_ref[jnp.minimum(rank, slots - 1)]
     out_ref[...] = jnp.where(rank < slots, kept, 0.0)
 
@@ -280,24 +313,28 @@
     slots = n_base * n_pix // 4
     quarter = m_dev // n_pix
     x0 = first_sky_estimate[:, 0, 0, :]
-    ranks = patch_order_record
+    ranks = patch_order_record.T
     where = jnp.stack([lax.axis_index("pix"), lax.axis_index("base")]).astype(jnp.int32)
     shape = jax.ShapeDtypeStruct
     bf16, f32 = jnp.bfloat16, jnp.float32
 
+    def exchange(first, places):
+        packed = call(
+            functools.partial(pack_body, slots, first),
+            [shape((places * quarter + PAD, TILE), bf16)] * (n_pix - 1),
+            (where, ranks, a),
+            smem=(0, 1),
+            name="pack",
+        )
+        return [swap(piece, "pix", d + 1) for d, piece in enumerate(packed)]
+
+    places = min(CAPACITY, ranks.shape[0])
+    parts = exchange(0, places)
     x0_round = x0.astype(bf16)
     shares = [x0_round] + [swap(x0_round, "base", d) for d in range(1, n_base)]
-    packed = call(
-        functools.partial(pack_body, slots),
-        [shape((quarter, slots * TILE), bf16)] * n_pix,
-        (where, ranks, a),
-        smem=(0, 1),
-        name="pack",
-    )
-    parts = [packed[0]] + [swap(packed[d], "pix", d) for d in range(1, n_pix)]
     firsts = call(
         first_body,
-        [shape((chans, quarter), f32)] * n_pix,
+        [shape((chans, quarter), bf16)] * n_pix,
         (where, a, *shares),
         scratch=[pltpu.VMEM((chans, n_base * TILE), bf16)],
         smem=(0,),
@@ -310,13 +347,24 @@
     per = slots // n_base
     rows = g_rows + per * (4 * chans + PAD)
     chunk = shape((rows, TILE), bf16)
-    outs = call(
-        functools.partial(gram_body, slots, n_pix),
-        [chunk] * n_base,
-        (where, ranks, sampled_correlations, x0, *parts, *preds),
-        scratch=[pltpu.VMEM((n_base, rows, TILE), bf16)],
-        smem=(0, 1),
-        name="gram",
+
+    def gram(parts):
+        return call(
+            functools.partial(gram_body, slots, n_pix, len(parts)),
+            [chunk] * n_base,
+            (where, ranks, sampled_correlations, x0, a, *parts, *preds),
+            scratch=[pltpu.VMEM((n_base, rows, TILE), bf16)],
+            smem=(0, 1),
+            name="gram",
+        )
+
+    counts = [part[-1, 0].astype(f32) for part in parts]
+    counts.append(jnp.sum((ranks[:, 0] < slots).astype(f32)))
+    crowded = functools.reduce(jnp.maximum, counts) > places
+    outs = lax.cond(
+        crowded,
+        lambda: gram(parts + exchange(places, ranks.shape[0] - places)),
+        lambda: gram(parts),
     )
     add = functools.partial(sum_body, g_rows, chans, per)
     part = call(add, chunk, [outs[0]] + [swap(outs[d], "base", d) for d in range(1, n_base)], name="sum_base")

time: 69.9 us -> 57.9 us (0.83)
  waiting for transfers between devices: 36 us -> 22.9 us
  between operations: 0.09 us -> 2.65 us
  starting transfers between devices: 25.1 us -> 22.9 us
    ppermute x22, waiting for transfers between devices: 36 us -> 22.9 us  [swap(): return lax.ppermute(value, axis, [(i, i ^ offset) for i in range(size)])]
    ppermute x22, starting transfers between devices: 25.1 us -> 22.9 us  [swap(): return lax.ppermute(value, axis, [(i, i ^ offset) for i in range(size)])]
    unnamed x9 -> x8, local copies, waits for them, and re-layouts: 2.02 us -> 0.03 us
    slice x0 -> x3, local copies, waits for them, and re-layouts: none -> 1.58 us  [gram_plan(): counts = [part[-1, 0].astype(f32) for part in parts]]
  transfers between devices with their start and end apart: 22 -> 22, of which waited for: 14 -> 12; matrix products, arithmetic and copies ran while one was open for 0% -> 4% of each run, Pallas kernels for 1% -> 2%
where the time goes in v3:
time: 57.9 us; the launch traced here: 57.7 us
  starting transfers between devices  22.9 us (40%)
  waiting for transfers between devices  22.9 us (40%)
  Pallas kernels  6.94 us (12%)
  between operations  2.65 us (5%)
  local copies, waits for them, and re-layouts  1.61 us (3%)
  other arithmetic  0.75 us (1%)
    ppermute x22, waiting for transfers between devices, swap(): return lax.ppermute(value, axis, [(i, i ^ offset) for i in range(size)])  22.9 us
    ppermute x22, starting transfers between devices, swap(): return lax.ppermute(value, axis, [(i, i ^ offset) for i in range(size)])  22.9 us
    pallas_call x6, Pallas kernels, call(): pl.pallas_call(body, out_shape=out_shape, in_specs=specs, out_specs=out_s...  6.94 us
    slice x3, local copies, waits for them, and re-layouts, gram_plan(): counts = [part[-1, 0].astype(f32) for part in parts]  1.58 us
  transfers between devices with their start and end apart: 22, of which 12 were waited for; matrix products, arithmetic and copies ran while one was open for 4% of the time, Pallas kernels for 2%

profile of v3, /device:TPU:0, one launch (start us, length us, event | category | flops | bytes accessed | tf_op | source)
XLA Modules:
  0.0 57.7 jit_solution(9678967636697049903)
XLA Ops:
  0.0 0.1 pad_add_fusion.where_ref
  0.1 1.4 %pack.3 = (bf16[528,128]{1,0:T(8,128)(2,1)S(1)}, bf16[528,128]{1,0:T(8,128)(2,1)S(1)}, bf16[528,128]{1,0:T(8,128)(2,1)S(1)}) custom-call(s32[2]{0:T(128)S(1)} %pad_add_fusion.where_ref, s32[4,6]{1,0:T(4,128)} %bitcast.16, bf16[1024,512]{1,0:T(8,128)(2,1)} %bitcast.9), custom_call_target="tpu_custom_call" | custom-call | tf_op jit(solution)/shard_map/pack/pallas_call | solution.py:81
  1.5 3.1 %collective-permute-start.3 = (bf16[528,128]{1,0:T(8,128)(2,1)S(1)}, bf16[528,128]{1,0:T(8,128)(2,1)S(1)}, u32[]{:S(2)}, u32[]{:S(2)}) collective-permute-start(bf16[528,128]{1,0:T(8,128)(2,1)S(1)} %get-tuple-element.91), channel_id=1, source_target_pairs={{0,1},{1,0},{2,3},{3,2},{4,5},{5,4},{6,7},{7,6},{8,9},{9,8},{10,11... | collective-permute-start | bytes 405512 | tf_op jit(solution)/shard_map/ppermute | solution.py:73
  4.6 2.6 %collective-permute-start.4 = (bf16[528,128]{1,0:T(8,128)(2,1)S(1)}, bf16[528,128]{1,0:T(8,128)(2,1)S(1)}, u32[]{:S(2)}, u32[]{:S(2)}) collective-permute-start(bf16[528,128]{1,0:T(8,128)(2,1)S(1)} %get-tuple-element.92), channel_id=1, source_target_pairs={{0,2},{1,3},{2,0},{3,1},{4,6},{5,7},{6,4},{7,5},{8,10},{9,11},{10,... | collective-permute-start | bytes 405512 | tf_op jit(solution)/shard_map/ppermute | solution.py:73
  7.2 0.0 collective-permute-start.5
  7.2 0.0 copy-start.1
  7.2 0.5 collective-permute-start.8
  7.7 1.4 %collective-permute-start.7 = (bf16[32,128]{1,0:T(8,128)(2,1)S(1)}, bf16[32,128]{1,0:T(8,128)(2,1)S(1)}, u32[]{:S(2)}, u32[]{:S(2)}) collective-permute-start(bf16[32,128]{1,0:T(8,128)(2,1)S(1)} %convert_element_type.27.refs_0_), channel_id=1, source_target_pairs={{0,8},{4,12},{8,0},{12,4},{1,9},{5,13},{9,1},{13,5},{2,10},{6,14},... | collective-permute-start | bytes 24584 | tf_op jit(solution)/shard_map/ppermute | solution.py:73
  9.1 1.3 %collective-permute-done.8.refs_3_ = bf16[32,128]{1,0:T(8,128)(2,1)S(1)} collective-permute-done((bf16[32,128]{1,0:T(8,128)(2,1)S(1)}, bf16[32,128]{1,0:T(8,128)(2,1)S(1)}, u32[]{:S(2)}, u32[]{:S(2)}) %collective-permute-start.8) | collective-permute-done | bytes 8224 | tf_op jit(solution)/shard_map/ppermute | solution.py:73
  10.4 0.4 collective-permute-start.6
  10.8 0.6 collective-permute-done.7.refs_2_
  11.3 0.3 collective-permute-done.6.refs_1_
  11.6 0.9 %first.1 = (bf16[32,256]{1,0:T(8,128)(2,1)S(1)}, bf16[32,256]{1,0:T(8,128)(2,1)S(1)}, bf16[32,256]{1,0:T(8,128)(2,1)S(1)}, bf16[32,256]{1,0:T(8,128)(2,1)S(1)}) custom-call(s32[2]{0:T(128)S(1)} %pad_add_fusion.where_ref, bf16[1024,512]{1,0:T(8,128)(2,1)S(1)} %bitcast.10, bf16[32,128]{1,0:T(8,128)(2,1)S(1)} %convert_element_type.27.refs_0_, ...), custom_call_target="tpu_custom_call" | custom-call | tf_op jit(solution)/shard_map/first/pallas_call | solution.py:81
  12.6 0.0 copy-start.3
  12.6 0.9 %collective-permute-start.9 = (bf16[32,256]{1,0:T(8,128)(2,1)S(1)}, bf16[32,256]{1,0:T(8,128)(2,1)S(1)}, u32[]{:S(2)}, u32[]{:S(2)}) collective-permute-start(bf16[32,256]{1,0:T(8,128)(2,1)S(1)} %get-tuple-element.95), channel_id=1, source_target_pairs={{0,1},{1,0},{2,3},{3,2},{4,5},{5,4},{6,7},{7,6},{8,9},{9,8},{10,11... | collective-permute-start | bytes 49160 | tf_op jit(solution)/shard_map/ppermute | solution.py:73
  13.5 3.5 %collective-permute-start.10 = (bf16[32,256]{1,0:T(8,128)(2,1)S(1)}, bf16[32,256]{1,0:T(8,128)(2,1)S(1)}, u32[]{:S(2)}, u32[]{:S(2)}) collective-permute-start(bf16[32,256]{1,0:T(8,128)(2,1)S(1)} %get-tuple-element.96), channel_id=1, source_target_pairs={{0,2},{1,3},{2,0},{3,1},{4,6},{5,7},{6,4},{7,5},{8,10},{9,11},{10,... | collective-permute-start | bytes 49160 | tf_op jit(solution)/shard_map/ppermute | solution.py:73
  17.0 0.0 collective-permute-done.3
  17.0 0.1 collective-permute-start.11
  17.0 0.7 %convert_reduce_fusion = f32[]{:T(128)} fusion(s32[4,6]{1,0:T(4,128)S(1)} %bitcast.17), kind=kLoop, calls=%fused_computation | loop fusion | flops 11 | bytes 20 | tf_op jit(solution)/shard_map/reduce_sum | solution.py:362
  17.7 0.5 slice.16
  18.2 0.0 collective-permute-done.4
  18.2 0.5 slice.17
  20.0 0.0 collective-permute-done.5
  20.0 0.5 slice.18
  21.8 0.0 collective-permute-done.9
  21.9 0.6 %collective-permute-done.11 = bf16[32,256]{1,0:T(8,128)(2,1)S(1)} collective-permute-done((bf16[32,256]{1,0:T(8,128)(2,1)S(1)}, bf16[32,256]{1,0:T(8,128)(2,1)S(1)}, u32[]{:S(2)}, u32[]{:S(2)}) %collective-permute-start.11) | collective-permute-done | bytes 16416 | tf_op jit(solution)/shard_map/ppermute | solution.py:73
  22.5 1.1 %conditional.1 = ((bf16[464,128]{1,0:T(8,128)(2,1)S(1)}, bf16[464,128]{1,0:T(8,128)(2,1)S(1)}, bf16[464,128]{1,0:T(8,128)(2,1)S(1)}, bf16[464,128]{1,0:T(8,128)(2,1)S(1)})) conditional(s32[]{:T(128)} %convert_element_type.26, (s32[2]{0:T(128)S(1)}, s32[4,6]{1,0:T(4,128)S(1)}, f32[32,1024]{1,0:T(8,128)S(1)}, f32[32,128]{1,0:T(8,128)S(1)}, ...), branch_computations={%region_1.0_spmd, %region_2.0_spmd} | conditional | bytes 1622144 | solution.py:364
  22.5 1.1 %gram.2 = (bf16[464,128]{1,0:T(8,128)(2,1)S(1)}, bf16[464,128]{1,0:T(8,128)(2,1)S(1)}, bf16[464,128]{1,0:T(8,128)(2,1)S(1)}, bf16[464,128]{1,0:T(8,128)(2,1)S(1)}) custom-call(s32[2]{0:T(128)S(1)} %get-tuple-element.53.where_ref, s32[4,6]{1,0:T(4,128)S(1)} %get-tuple-element.54.ranks_ref, f32[32,1024]{1,0:T(8,128)S(1)} %get-tuple-element.55.y_ref, ...), custom_call_target="tpu_custom_call" | custom-call | tf_op jit(solution)/shard_map/cond/branch_0_fun/gram/pallas_call | solution.py:81
  23.6 0.1 collective-permute-start.12
  23.7 1.6 %collective-permute-start.13 = (bf16[464,128]{1,0:T(8,128)(2,1)S(1)}, bf16[464,128]{1,0:T(8,128)(2,1)S(1)}, u32[]{:S(2)}, u32[]{:S(2)}) collective-permute-start(bf16[464,128]{1,0:T(8,128)(2,1)S(1)} %get-tuple-element.100), channel_id=1, source_target_pairs={{0,8},{4,12},{8,0},{12,4},{1,9},{5,13},{9,1},{13,5},{2,10},{6,14},... | collective-permute-start | bytes 356360 | tf_op jit(solution)/shard_map/ppermute | solution.py:73
  25.3 0.3 collective-permute-start.14
  25.6 4.3 %collective-permute-done.13.refs_2_ = bf16[464,128]{1,0:T(8,128)(2,1)S(1)} collective-permute-done((bf16[464,128]{1,0:T(8,128)(2,1)S(1)}, bf16[464,128]{1,0:T(8,128)(2,1)S(1)}, u32[]{:S(2)}, u32[]{:S(2)}) %collective-permute-start.13) | collective-permute-done | bytes 118816 | tf_op jit(solution)/shard_map/ppermute | solution.py:73
  29.9 1.5 %collective-permute-done.14.refs_3_ = bf16[464,128]{1,0:T(8,128)(2,1)S(1)} collective-permute-done((bf16[464,128]{1,0:T(8,128)(2,1)S(1)}, bf16[464,128]{1,0:T(8,128)(2,1)S(1)}, u32[]{:S(2)}, u32[]{:S(2)}) %collective-permute-start.14) | collective-permute-done | bytes 118816 | tf_op jit(solution)/shard_map/ppermute | solution.py:73
  31.3 0.1 sum_base.1.refs_0_
  31.4 3.2 %collective-permute-start.17 = (bf16[464,128]{1,0:T(8,128)(2,1)S(1)}, bf16[464,128]{1,0:T(8,128)(2,1)S(1)}, u32[]{:S(2)}, u32[]{:S(2)}) collective-permute-start(bf16[464,128]{1,0:T(8,128)(2,1)S(1)} %sum_base.1.refs_0_), channel_id=1, source_target_pairs={{0,3},{1,2},{2,1},{3,0},{4,7},{5,6},{6,5},{7,4},{8,11},{9,10},{10,... | collective-permute-start | bytes 356360 | tf_op jit(solution)/shard_map/ppermute | solution.py:73
  34.7 1.2 %collective-permute-start.15 = (bf16[464,128]{1,0:T(8,128)(2,1)S(1)}, bf16[464,128]{1,0:T(8,128)(2,1)S(1)}, u32[]{:S(2)}, u32[]{:S(2)}) collective-permute-start(bf16[464,128]{1,0:T(8,128)(2,1)S(1)} %sum_base.1.refs_0_), channel_id=1, source_target_pairs={{0,1},{1,0},{2,3},{3,2},{4,5},{5,4},{6,7},{7,6},{8,9},{9,8},{10,11... | collective-permute-start | bytes 356360 | tf_op jit(solution)/shard_map/ppermute | solution.py:73
  35.9 3.6 %collective-permute-done.17.refs_3_ = bf16[464,128]{1,0:T(8,128)(2,1)S(1)} collective-permute-done((bf16[464,128]{1,0:T(8,128)(2,1)S(1)}, bf16[464,128]{1,0:T(8,128)(2,1)S(1)}, u32[]{:S(2)}, u32[]{:S(2)}) %collective-permute-start.17) | collective-permute-done | bytes 118816 | tf_op jit(solution)/shard_map/ppermute | solution.py:73
  39.5 4.7 %collective-permute-done.16.refs_2_ = bf16[464,128]{1,0:T(8,128)(2,1)S(1)} collective-permute-done((bf16[464,128]{1,0:T(8,128)(2,1)S(1)}, bf16[464,128]{1,0:T(8,128)(2,1)S(1)}, u32[]{:S(2)}, u32[]{:S(2)}) %collective-permute-start.16) | collective-permute-done | bytes 118816 | tf_op jit(solution)/shard_map/ppermute | solution.py:73
  44.2 0.1 sum_pix.1.refs_0_
  44.2 2.5 %collective-permute-start.23 = (bf16[464,128]{1,0:T(8,128)(2,1)S(1)}, bf16[464,128]{1,0:T(8,128)(2,1)S(1)}, u32[]{:S(2)}, u32[]{:S(2)}) collective-permute-start(bf16[464,128]{1,0:T(8,128)(2,1)S(1)} %sum_pix.1.refs_0_), channel_id=1, source_target_pairs={{0,24},{4,28},{8,16},{12,20},{16,8},{20,12},{24,0},{28,4},{1,25},{... | collective-permute-start | bytes 356360 | tf_op jit(solution)/shard_map/ppermute | solution.py:73
  46.8 0.5 collective-permute-start.21
  47.3 0.5 collective-permute-start.19
  47.8 3.5 %collective-permute-done.23.refs_6_ = bf16[464,128]{1,0:T(8,128)(2,1)S(1)} collective-permute-done((bf16[464,128]{1,0:T(8,128)(2,1)S(1)}, bf16[464,128]{1,0:T(8,128)(2,1)S(1)}, u32[]{:S(2)}, u32[]{:S(2)}) %collective-permute-start.23) | collective-permute-done | bytes 118816 | tf_op jit(solution)/shard_map/ppermute | solution.py:73
  51.3 1.5 %collective-permute-done.21.refs_4_ = bf16[464,128]{1,0:T(8,128)(2,1)S(1)} collective-permute-done((bf16[464,128]{1,0:T(8,128)(2,1)S(1)}, bf16[464,128]{1,0:T(8,128)(2,1)S(1)}, u32[]{:S(2)}, u32[]{:S(2)}) %collective-permute-start.21) | collective-permute-done | bytes 118816 | tf_op jit(solution)/shard_map/ppermute | solution.py:73
  52.9 0.5 collective-permute-start.20
  53.4 0.8 %collective-permute-done.22.refs_5_ = bf16[464,128]{1,0:T(8,128)(2,1)S(1)} collective-permute-done((bf16[464,128]{1,0:T(8,128)(2,1)S(1)}, bf16[464,128]{1,0:T(8,128)(2,1)S(1)}, u32[]{:S(2)}, u32[]{:S(2)}) %collective-permute-start.22) | collective-permute-done | bytes 118816 | tf_op jit(solution)/shard_map/ppermute | solution.py:73
  54.2 0.2 collective-permute-done.20.refs_3_
  54.4 3.3 %iterate.1 = f32[32,128]{1,0:T(8,128)} custom-call(s32[2]{0:T(128)S(1)} %pad_add_fusion.where_ref, s32[4,6]{1,0:T(4,128)S(1)} %bitcast.20, bf16[464,128]{1,0:T(8,128)(2,1)S(1)} %sum_pix.1.refs_0_, bf16[464,128]{1,0:T(8,128)(2,1)S(1)} %collective-permute-done.18.refs_1_, bf16[464,128]{1,0:T(8,128)(2,1)S(1)} %collective-permute-done.19.refs_2_, ...), custom_call_target="tpu_custom_call" | custom-call | tf_op jit(solution)/shard_map/iterate/pallas_call | solution.py:81
  (17 shorter events, 0.0 us)
Async XLA Ops:
  0.0 11.6 %copy-start = (bf16[1,1024,512]{2,1,0:T(8,128)(2,1)S(1)}, bf16[1,1024,512]{2,1,0:T(8,128)(2,1)}, u32[]{:S(2)}) copy-start(bf16[1,1024,512]{2,1,0:T(8,128)(2,1)} %param.6) | copy-start | bytes 3145732
  0.1 7.1 %copy-start.2 = (f32[32,1,1,128]{3,2,1,0:T(1,128)S(1)}, f32[32,1,1,128]{3,2,1,0:T(1,128)}, u32[]{:S(2)}) copy-start(f32[32,1,1,128]{3,2,1,0:T(1,128)} %param.8) | copy-start | bytes 49156
  1.5 15.5 %collective-permute-start.3 = (bf16[528,128]{1,0:T(8,128)(2,1)S(1)}, bf16[528,128]{1,0:T(8,128)(2,1)S(1)}, u32[]{:S(2)}, u32[]{:S(2)}) collective-permute-start(bf16[528,128]{1,0:T(8,128)(2,1)S(1)} %get-tuple-element.91), channel_id=1, source_target_pairs={{0,1},{1,0},{2,3},{3,2},{4,5},{5,4},{6,7},{7,6},{8,9},{9,8},{10,11... | collective-permute-start | bytes 405512 | tf_op jit(solution)/shard_map/ppermute | solution.py:73
  4.6 13.6 %collective-permute-start.4 = (bf16[528,128]{1,0:T(8,128)(2,1)S(1)}, bf16[528,128]{1,0:T(8,128)(2,1)S(1)}, u32[]{:S(2)}, u32[]{:S(2)}) collective-permute-start(bf16[528,128]{1,0:T(8,128)(2,1)S(1)} %get-tuple-element.92), channel_id=1, source_target_pairs={{0,2},{1,3},{2,0},{3,1},{4,6},{5,7},{6,4},{7,5},{8,10},{9,11},{10,... | collective-permute-start | bytes 405512 | tf_op jit(solution)/shard_map/ppermute | solution.py:73
  7.2 12.8 %collective-permute-start.5 = (bf16[528,128]{1,0:T(8,128)(2,1)S(1)}, bf16[528,128]{1,0:T(8,128)(2,1)S(1)}, u32[]{:S(2)}, u32[]{:S(2)}) collective-permute-start(bf16[528,128]{1,0:T(8,128)(2,1)S(1)} %get-tuple-element.93), channel_id=1, source_target_pairs={{0,3},{1,2},{2,1},{3,0},{4,7},{5,6},{6,5},{7,4},{8,11},{9,10},{10,... | collective-permute-start | bytes 405512 | tf_op jit(solution)/shard_map/ppermute | solution.py:73
  7.2 15.3 %copy-start.1 = (f32[32,1024]{1,0:T(8,128)S(1)}, f32[32,1024]{1,0:T(8,128)}, u32[]{:S(2)}) copy-start(f32[32,1024]{1,0:T(8,128)} %param.7) | copy-start | bytes 393220
  7.2 3.1 %collective-permute-start.8 = (bf16[32,128]{1,0:T(8,128)(2,1)S(1)}, bf16[32,128]{1,0:T(8,128)(2,1)S(1)}, u32[]{:S(2)}, u32[]{:S(2)}) collective-permute-start(bf16[32,128]{1,0:T(8,128)(2,1)S(1)} %convert_element_type.27.refs_0_), channel_id=1, source_target_pairs={{0,12},{4,8},{8,4},{12,0},{1,13},{5,9},{9,5},{13,1},{2,14},{6,10},... | collective-permute-start | bytes 24584 | tf_op jit(solution)/shard_map/ppermute | solution.py:73
  7.7 3.7 %collective-permute-start.7 = (bf16[32,128]{1,0:T(8,128)(2,1)S(1)}, bf16[32,128]{1,0:T(8,128)(2,1)S(1)}, u32[]{:S(2)}, u32[]{:S(2)}) collective-permute-start(bf16[32,128]{1,0:T(8,128)(2,1)S(1)} %convert_element_type.27.refs_0_), channel_id=1, source_target_pairs={{0,8},{4,12},{8,0},{12,4},{1,9},{5,13},{9,1},{13,5},{2,10},{6,14},... | collective-permute-start | bytes 24584 | tf_op jit(solution)/shard_map/ppermute | solution.py:73
  10.4 1.2 %collective-permute-start.6 = (bf16[32,128]{1,0:T(8,128)(2,1)S(1)}, bf16[32,128]{1,0:T(8,128)(2,1)S(1)}, u32[]{:S(2)}, u32[]{:S(2)}) collective-permute-start(bf16[32,128]{1,0:T(8,128)(2,1)S(1)} %convert_element_type.27.refs_0_), channel_id=1, source_target_pairs={{0,4},{4,0},{8,12},{12,8},{1,5},{5,1},{9,13},{13,9},{2,6},{6,2},{1... | collective-permute-start | bytes 24584 | tf_op jit(solution)/shard_map/ppermute | solution.py:73
  12.6 4.5 %copy-start.3 = (s32[6,4]{0,1:T(4,128)S(1)}, s32[6,4]{0,1:T(4,128)}, u32[]{:S(2)}) copy-start(s32[6,4]{0,1:T(4,128)} %param.9) | copy-start | bytes 292
  12.6 9.3 %collective-permute-start.9 = (bf16[32,256]{1,0:T(8,128)(2,1)S(1)}, bf16[32,256]{1,0:T(8,128)(2,1)S(1)}, u32[]{:S(2)}, u32[]{:S(2)}) collective-permute-start(bf16[32,256]{1,0:T(8,128)(2,1)S(1)} %get-tuple-element.95), channel_id=1, source_target_pairs={{0,1},{1,0},{2,3},{3,2},{4,5},{5,4},{6,7},{7,6},{8,9},{9,8},{10,11... | collective-permute-start | bytes 49160 | tf_op jit(solution)/shard_map/ppermute | solution.py:73
  13.5 8.4 %collective-permute-start.10 = (bf16[32,256]{1,0:T(8,128)(2,1)S(1)}, bf16[32,256]{1,0:T(8,128)(2,1)S(1)}, u32[]{:S(2)}, u32[]{:S(2)}) collective-permute-start(bf16[32,256]{1,0:T(8,128)(2,1)S(1)} %get-tuple-element.96), channel_id=1, source_target_pairs={{0,2},{1,3},{2,0},{3,1},{4,6},{5,7},{6,4},{7,5},{8,10},{9,11},{10,... | collective-permute-start | bytes 49160 | tf_op jit(solution)/shard_map/ppermute | solution.py:73
  17.0 5.5 %collective-permute-start.11 = (bf16[32,256]{1,0:T(8,128)(2,1)S(1)}, bf16[32,256]{1,0:T(8,128)(2,1)S(1)}, u32[]{:S(2)}, u32[]{:S(2)}) collective-permute-start(bf16[32,256]{1,0:T(8,128)(2,1)S(1)} %get-tuple-element.97), channel_id=1, source_target_pairs={{0,3},{1,2},{2,1},{3,0},{4,7},{5,6},{6,5},{7,4},{8,11},{9,10},{10,... | collective-permute-start | bytes 49160 | tf_op jit(solution)/shard_map/ppermute | solution.py:73
  23.6 1.9 %collective-permute-start.12 = (bf16[464,128]{1,0:T(8,128)(2,1)S(1)}, bf16[464,128]{1,0:T(8,128)(2,1)S(1)}, u32[]{:S(2)}, u32[]{:S(2)}) collective-permute-start(bf16[464,128]{1,0:T(8,128)(2,1)S(1)} %get-tuple-element.99), channel_id=1, source_target_pairs={{0,4},{4,0},{8,12},{12,8},{1,5},{5,1},{9,13},{13,9},{2,6},{6,2},{1... | collective-permute-start | bytes 356360 | tf_op jit(solution)/shard_map/ppermute | solution.py:73
  23.7 6.2 %collective-permute-start.13 = (bf16[464,128]{1,0:T(8,128)(2,1)S(1)}, bf16[464,128]{1,0:T(8,128)(2,1)S(1)}, u32[]{:S(2)}, u32[]{:S(2)}) collective-permute-start(bf16[464,128]{1,0:T(8,128)(2,1)S(1)} %get-tuple-element.100), channel_id=1, source_target_pairs={{0,8},{4,12},{8,0},{12,4},{1,9},{5,13},{9,1},{13,5},{2,10},{6,14},... | collective-permute-start | bytes 356360 | tf_op jit(solution)/shard_map/ppermute | solution.py:73
  25.3 6.1 %collective-permute-start.14 = (bf16[464,128]{1,0:T(8,128)(2,1)S(1)}, bf16[464,128]{1,0:T(8,128)(2,1)S(1)}, u32[]{:S(2)}, u32[]{:S(2)}) collective-permute-start(bf16[464,128]{1,0:T(8,128)(2,1)S(1)} %get-tuple-element.101), channel_id=1, source_target_pairs={{0,12},{4,8},{8,4},{12,0},{1,13},{5,9},{9,5},{13,1},{2,14},{6,10},... | collective-permute-start | bytes 356360 | tf_op jit(solution)/shard_map/ppermute | solution.py:73
  31.4 8.1 %collective-permute-start.17 = (bf16[464,128]{1,0:T(8,128)(2,1)S(1)}, bf16[464,128]{1,0:T(8,128)(2,1)S(1)}, u32[]{:S(2)}, u32[]{:S(2)}) collective-permute-start(bf16[464,128]{1,0:T(8,128)(2,1)S(1)} %sum_base.1.refs_0_), channel_id=1, source_target_pairs={{0,3},{1,2},{2,1},{3,0},{4,7},{5,6},{6,5},{7,4},{8,11},{9,10},{10,... | collective-permute-start | bytes 356360 | tf_op jit(solution)/shard_map/ppermute | solution.py:73
  34.7 9.5 %collective-permute-start.16 = (bf16[464,128]{1,0:T(8,128)(2,1)S(1)}, bf16[464,128]{1,0:T(8,128)(2,1)S(1)}, u32[]{:S(2)}, u32[]{:S(2)}) collective-permute-start(bf16[464,128]{1,0:T(8,128)(2,1)S(1)} %sum_base.1.refs_0_), channel_id=1, source_target_pairs={{0,2},{1,3},{2,0},{3,1},{4,6},{5,7},{6,4},{7,5},{8,10},{9,11},{10,... | collective-permute-start | bytes 356360 | tf_op jit(solution)/shard_map/ppermute | solution.py:73
  34.7 9.5 %collective-permute-start.15 = (bf16[464,128]{1,0:T(8,128)(2,1)S(1)}, bf16[464,128]{1,0:T(8,128)(2,1)S(1)}, u32[]{:S(2)}, u32[]{:S(2)}) collective-permute-start(bf16[464,128]{1,0:T(8,128)(2,1)S(1)} %sum_base.1.refs_0_), channel_id=1, source_target_pairs={{0,1},{1,0},{2,3},{3,2},{4,5},{5,4},{6,7},{7,6},{8,9},{9,8},{10,11... | collective-permute-start | bytes 356360 | tf_op jit(solution)/shard_map/ppermute | solution.py:73
  44.2 7.1 %collective-permute-start.23 = (bf16[464,128]{1,0:T(8,128)(2,1)S(1)}, bf16[464,128]{1,0:T(8,128)(2,1)S(1)}, u32[]{:S(2)}, u32[]{:S(2)}) collective-permute-start(bf16[464,128]{1,0:T(8,128)(2,1)S(1)} %sum_pix.1.refs_0_), channel_id=1, source_target_pairs={{0,24},{4,28},{8,16},{12,20},{16,8},{20,12},{24,0},{28,4},{1,25},{... | collective-permute-start | bytes 356360 | tf_op jit(solution)/shard_map/ppermute | solution.py:73
  46.8 6.1 %collective-permute-start.21 = (bf16[464,128]{1,0:T(8,128)(2,1)S(1)}, bf16[464,128]{1,0:T(8,128)(2,1)S(1)}, u32[]{:S(2)}, u32[]{:S(2)}) collective-permute-start(bf16[464,128]{1,0:T(8,128)(2,1)S(1)} %sum_pix.1.refs_0_), channel_id=1, source_target_pairs={{0,16},{4,20},{8,24},{12,28},{16,0},{20,4},{24,8},{28,12},{1,17},{... | collective-permute-start | bytes 356360 | tf_op jit(solution)/shard_map/ppermute | solution.py:73
  47.3 5.6 %collective-permute-start.19 = (bf16[464,128]{1,0:T(8,128)(2,1)S(1)}, bf16[464,128]{1,0:T(8,128)(2,1)S(1)}, u32[]{:S(2)}, u32[]{:S(2)}) collective-permute-start(bf16[464,128]{1,0:T(8,128)(2,1)S(1)} %sum_pix.1.refs_0_), channel_id=1, source_target_pairs={{0,8},{4,12},{8,0},{12,4},{16,24},{20,28},{24,16},{28,20},{1,9},{5... | collective-permute-start | bytes 356360 | tf_op jit(solution)/shard_map/ppermute | solution.py:73
  47.8 5.6 %collective-permute-start.18 = (bf16[464,128]{1,0:T(8,128)(2,1)S(1)}, bf16[464,128]{1,0:T(8,128)(2,1)S(1)}, u32[]{:S(2)}, u32[]{:S(2)}) collective-permute-start(bf16[464,128]{1,0:T(8,128)(2,1)S(1)} %sum_pix.1.refs_0_), channel_id=1, source_target_pairs={{0,4},{4,0},{8,12},{12,8},{16,20},{20,16},{24,28},{28,24},{1,5},{5... | collective-permute-start | bytes 356360 | tf_op jit(solution)/shard_map/ppermute | solution.py:73
  51.3 2.1 %collective-permute-start.24 = (bf16[464,128]{1,0:T(8,128)(2,1)S(1)}, bf16[464,128]{1,0:T(8,128)(2,1)S(1)}, u32[]{:S(2)}, u32[]{:S(2)}) collective-permute-start(bf16[464,128]{1,0:T(8,128)(2,1)S(1)} %collective-permute-done.23.refs_6_), channel_id=1, source_target_pairs={{0,4},{4,0},{8,12},{12,8},{16,20},{20,16},{24,28},{28,24},{1,5},{5... | collective-permute-start | bytes 356360 | tf_op jit(solution)/shard_map/ppermute | solution.py:73
  52.9 1.3 %collective-permute-start.22 = (bf16[464,128]{1,0:T(8,128)(2,1)S(1)}, bf16[464,128]{1,0:T(8,128)(2,1)S(1)}, u32[]{:S(2)}, u32[]{:S(2)}) collective-permute-start(bf16[464,128]{1,0:T(8,128)(2,1)S(1)} %collective-permute-done.21.refs_4_), channel_id=1, source_target_pairs={{0,4},{4,0},{8,12},{12,8},{16,20},{20,16},{24,28},{28,24},{1,5},{5... | collective-permute-start | bytes 356360 | tf_op jit(solution)/shard_map/ppermute | solution.py:73
  52.9 1.5 %collective-permute-start.20 = (bf16[464,128]{1,0:T(8,128)(2,1)S(1)}, bf16[464,128]{1,0:T(8,128)(2,1)S(1)}, u32[]{:S(2)}, u32[]{:S(2)}) collective-permute-start(bf16[464,128]{1,0:T(8,128)(2,1)S(1)} %collective-permute-done.19.refs_2_), channel_id=1, source_target_pairs={{0,4},{4,0},{8,12},{12,8},{16,20},{20,16},{24,28},{28,24},{1,5},{5... | collective-permute-start | bytes 356360 | tf_op jit(solution)/shard_map/ppermute | solution.py:73

commit v4 on v3

--- a/solution.py
+++ b/solution.py
@@ -73,11 +73,10 @@
     return lax.ppermute(value, axis, [(i, i ^ offset) for i in range(size)])
 
 
-def call(body, out_shape, args, scratch=(), smem=(), name=None):
-    specs = [
-        pl.BlockSpec(memory_space=pltpu.SMEM if i in smem else pltpu.VMEM) for i in range(len(args))
-    ]
-    out_specs = jax.tree.map(lambda _: pl.BlockSpec(memory_space=pltpu.VMEM), out_shape)
+def call(body, out_shape, args, scratch=(), smem=(), hbm=(), out_space=pltpu.VMEM, name=None):
+    places = [pltpu.SMEM if i in smem else pl.ANY if i in hbm else pltpu.VMEM for i in range(len(args))]
+    specs = [pl.BlockSpec(memory_space=place) for place in places]
+    out_specs = jax.tree.map(lambda _: pl.BlockSpec(memory_space=out_space), out_shape)
     return pl.pallas_call(
         body,
         out_shape=out_shape,
@@ -127,6 +126,18 @@
         out[places * quarter :, :] = notes.astype(jnp.float32).astype(jnp.bfloat16)
 
 
+def crowd_body(slots, places, ranks_ref, *refs):
+    *parts, out_ref = refs
+    _, count = kept_tiles(ranks_ref, slots)
+    most = parts[0][-PAD:, :].astype(jnp.float32)
+    for part in parts[1:]:
+        most = jnp.maximum(most, part[-PAD:, :].astype(jnp.float32))
+    rows = lax.broadcasted_iota(jnp.int32, (PAD, TILE), 0)
+    others = jnp.max(jnp.where(rows == PAD - 1, most, -1.0))
+    over = jnp.logical_or(others > places, count > places)
+    out_ref[0] = jnp.where(over, 1, 0)
+
+
 def first_body(where_ref, a_ref, *refs):
     pix, base = where_ref[0], where_ref[1]
     n_base = a_ref.shape[1] // TILE
@@ -153,7 +164,17 @@
 
 
 def pairs(slots):
-    return [(r, s) for r in range(slots) for s in range(r, slots)]
+    return [(r, s) for r in range(slots) for s in range(r + 1, slots)] + [(r, r + 1) for r in range(0, slots, 2)]
+
+
+def pack_rows(slots, n_base):
+    return len(pairs(slots)) * TILE // n_base
+
+
+def corner():
+    rows = lax.broadcasted_iota(jnp.int32, (TILE, TILE), 0)
+    cols = lax.broadcasted_iota(jnp.int32, (TILE, TILE), 1)
+    return rows, cols
 
 
 def gram_body(slots, n_pix, n_parts, where_ref, ranks_ref, y_ref, x0_ref, a_ref, *refs):
@@ -192,20 +213,19 @@
     moved = descent_stride * sides[2 * chans :]
     rank = ranks_ref[base, 0]
     gram = lax.dot_general(a, a, (((0,), (0,)), ((), ())), preferred_element_type=jnp.float32)
-    rows = lax.broadcasted_iota(jnp.int32, (TILE, TILE), 0)
-    cols = lax.broadcasted_iota(jnp.int32, (TILE, TILE), 1)
-    here = rows == cols
-    n_pairs = len(pairs(slots))
-    g_rows = n_pairs * TILE // n_base
+    rows, cols = corner()
+    g_rows = pack_rows(slots, n_base)
     per = slots // n_base
     side_rows = 4 * chans + PAD
     half = min(TILE, g_rows & -g_rows)
-    diags = {}
+
+    def block_of(r, s):
+        return gram[r * TILE : (r + 1) * TILE, s * TILE : (s + 1) * TILE]
+
+    diags = [jnp.sum(jnp.where(rows == cols, block_of(r, r), 0.0), axis=0, keepdims=True) for r in range(slots)]
+    n_off = slots * (slots - 1) // 2
     for i, (r, s) in enumerate(pairs(slots)):
-        block = gram[r * TILE : (r + 1) * TILE, s * TILE : (s + 1) * TILE]
-        if r == s:
-            diags[r] = jnp.sum(jnp.where(here, block, 0.0), axis=0, keepdims=True)
-            block = jnp.where(here, 0.0, block)
+        block = block_of(r, s) if i < n_off else jnp.where(rows < cols, block_of(r, r), block_of(s, s))
         block = block.astype(jnp.bfloat16)
         for q in range(TILE // half):
             at = i * TILE + q * half
@@ -261,6 +281,12 @@
     chunks = [refs[:n_base], refs[n_base : 2 * n_base]]
     out_ref, gram_ref, last_ref = refs[2 * n_base :]
     states, datas, diags = [], [], []
+    rows, cols = corner()
+    n_off = slots * (slots - 1) // 2
+
+    def put(g, r, s, block):
+        gram_ref[g, r * TILE : (r + 1) * TILE, s * TILE : (s + 1) * TILE] = block
+
     for g in range(2):
         full = in_order([ref[...] for ref in chunks[g]], base)
         half = min(TILE, g_rows & -g_rows)
@@ -270,9 +296,14 @@
                 at = i * TILE + q * half
                 pieces.append(full[at // g_rows][at % g_rows : at % g_rows + half])
             block = jnp.concatenate(pieces, axis=0)
-            gram_ref[g, r * TILE : (r + 1) * TILE, s * TILE : (s + 1) * TILE] = block
-            if r != s:
-                gram_ref[g, s * TILE : (s + 1) * TILE, r * TILE : (r + 1) * TILE] = block.T
+            if i < n_off:
+                put(g, r, s, block)
+                put(g, s, r, block.T)
+            else:
+                upper = jnp.where(rows < cols, block, jnp.zeros_like(block))
+                lower = jnp.where(rows > cols, block, jnp.zeros_like(block))
+                put(g, r, r, upper + upper.T)
+                put(g, s, s, lower + lower.T)
         sides = [full[r // per][g_rows + (r % per) * side_rows :][:side_rows].astype(jnp.float32) for r in range(slots)]
         wide = lambda at: jnp.concatenate([v[at : at + chans] + v[at + chans : at + 2 * chans] for v in sides], axis=1)
         datas.append(wide(0))
@@ -342,8 +373,7 @@
     )
     preds = [firsts[0]] + [swap(firsts[d], "pix", d) for d in range(1, n_pix)]
 
-    n_pairs = slots * (slots + 1) // 2
-    g_rows = n_pairs * TILE // n_base
+    g_rows = pack_rows(slots, n_base)
     per = slots // n_base
     rows = g_rows + per * (4 * chans + PAD)
     chunk = shape((rows, TILE), bf16)
@@ -358,11 +388,16 @@
             name="gram",
         )
 
-    counts = [part[-1, 0].astype(f32) for part in parts]
-    counts.append(jnp.sum((ranks[:, 0] < slots).astype(f32)))
-    crowded = functools.reduce(jnp.maximum, counts) > places
+    crowded = call(
+        functools.partial(crowd_body, slots, places),
+        shape((1,), jnp.int32),
+        (ranks, *parts),
+        smem=(0,),
+        out_space=pltpu.SMEM,
+        name="crowd",
+    )[0]
     outs = lax.cond(
-        crowded,
+        crowded != 0,
         lambda: gram(parts + exchange(places, ranks.shape[0] - places)),
         lambda: gram(parts),
     )
@@ -401,7 +436,8 @@
         and n_base & (n_base - 1) == 0
         and n_pix & (n_pix - 1) == 0
         and slots % n_base == 0
-        and slots * (slots + 1) // 2 * TILE % (n_base * 16) == 0
+        and slots % 2 == 0
+        and len(pairs(slots)) * TILE % (n_base * 16) == 0
         and m_dev % (n_pix * TILE) == 0
         and lax.axis_size("freq") == 2
         and chans % 16 == 0

time: 57.9 us -> 55.1 us (0.952)
  between operations: 2.65 us -> 0.73 us
  local copies, waits for them, and re-layouts: 1.61 us -> 0.03 us
  Pallas kernels: 6.94 us -> 8.28 us
  other arithmetic: 0.75 us -> 0.08 us
    slice x3 -> x0, local copies, waits for them, and re-layouts: 1.58 us -> none  [gram_plan(): counts = [part[-1, 0].astype(f32) for part in parts]]
    pallas_call x6 -> x7, Pallas kernels: 6.94 us -> 8.28 us  [call(): pl.pallas_call(body, out_shape=out_shape, in_specs=specs, out_specs=out_s...]
    reduce_sum x1 -> x0, other arithmetic: 0.67 us -> none  [gram_plan(): counts.append(jnp.sum((ranks[:, 0] < slots).astype(f32)))]
  transfers between devices with their start and end apart: 22 -> 22, of which waited for: 12 -> 15; matrix products, arithmetic and copies ran while one was open for 4% -> 0% of each run, Pallas kernels for 2% -> 4%
where the time goes in v4:
time: 55.1 us; the launch traced here: 54.9 us
  waiting for transfers between devices  23.2 us (42%)
  starting transfers between devices  22.6 us (41%)
  Pallas kernels  8.28 us (15%)
  between operations  0.73 us (1%)
    ppermute x22, waiting for transfers between devices, swap(): return lax.ppermute(value, axis, [(i, i ^ offset) for i in range(size)])  23.2 us
    ppermute x22, starting transfers between devices, swap(): return lax.ppermute(value, axis, [(i, i ^ offset) for i in range(size)])  22.6 us
    pallas_call x7, Pallas kernels, call(): pl.pallas_call(body, out_shape=out_shape, in_specs=specs, out_specs=out_s...  8.28 us
  transfers between devices with their start and end apart: 22, of which 15 were waited for; matrix products, arithmetic and copies ran while one was open for 0% of the time, Pallas kernels for 4%

profile of v4, /device:TPU:0, one launch (start us, length us, event | category | flops | bytes accessed | tf_op | source)
XLA Modules:
  0.0 54.9 jit_solution(18241735547261678662)
XLA Ops:
  0.0 0.1 pad_add_fusion.where_ref
  0.1 1.4 %pack.3 = (bf16[528,128]{1,0:T(8,128)(2,1)S(1)}, bf16[528,128]{1,0:T(8,128)(2,1)S(1)}, bf16[528,128]{1,0:T(8,128)(2,1)S(1)}) custom-call(s32[2]{0:T(128)S(1)} %pad_add_fusion.where_ref, s32[4,6]{1,0:T(4,128)} %bitcast.16, bf16[1024,512]{1,0:T(8,128)(2,1)} %bitcast.9), custom_call_target="tpu_custom_call" | custom-call | tf_op jit(solution)/shard_map/pack/pallas_call | solution.py:80
  1.5 3.1 %collective-permute-start.3 = (bf16[528,128]{1,0:T(8,128)(2,1)S(1)}, bf16[528,128]{1,0:T(8,128)(2,1)S(1)}, u32[]{:S(2)}, u32[]{:S(2)}) collective-permute-start(bf16[528,128]{1,0:T(8,128)(2,1)S(1)} %get-tuple-element.91), channel_id=1, source_target_pairs={{0,1},{1,0},{2,3},{3,2},{4,5},{5,4},{6,7},{7,6},{8,9},{9,8},{10,11... | collective-permute-start | bytes 405512 | tf_op jit(solution)/shard_map/ppermute | solution.py:73
  4.6 2.6 %collective-permute-start.4 = (bf16[528,128]{1,0:T(8,128)(2,1)S(1)}, bf16[528,128]{1,0:T(8,128)(2,1)S(1)}, u32[]{:S(2)}, u32[]{:S(2)}) collective-permute-start(bf16[528,128]{1,0:T(8,128)(2,1)S(1)} %get-tuple-element.92), channel_id=1, source_target_pairs={{0,2},{1,3},{2,0},{3,1},{4,6},{5,7},{6,4},{7,5},{8,10},{9,11},{10,... | collective-permute-start | bytes 405512 | tf_op jit(solution)/shard_map/ppermute | solution.py:73
  7.2 0.5 collective-permute-start.8
  7.7 1.3 %collective-permute-start.7 = (bf16[32,128]{1,0:T(8,128)(2,1)S(1)}, bf16[32,128]{1,0:T(8,128)(2,1)S(1)}, u32[]{:S(2)}, u32[]{:S(2)}) collective-permute-start(bf16[32,128]{1,0:T(8,128)(2,1)S(1)} %convert_element_type.11.refs_0_), channel_id=1, source_target_pairs={{0,8},{4,12},{8,0},{12,4},{1,9},{5,13},{9,1},{13,5},{2,10},{6,14},... | collective-permute-start | bytes 24584 | tf_op jit(solution)/shard_map/ppermute | solution.py:73
  9.0 1.3 %collective-permute-done.8.refs_3_ = bf16[32,128]{1,0:T(8,128)(2,1)S(1)} collective-permute-done((bf16[32,128]{1,0:T(8,128)(2,1)S(1)}, bf16[32,128]{1,0:T(8,128)(2,1)S(1)}, u32[]{:S(2)}, u32[]{:S(2)}) %collective-permute-start.8) | collective-permute-done | bytes 8224 | tf_op jit(solution)/shard_map/ppermute | solution.py:73
  10.4 0.3 collective-permute-start.6
  10.7 0.6 %collective-permute-done.7.refs_2_ = bf16[32,128]{1,0:T(8,128)(2,1)S(1)} collective-permute-done((bf16[32,128]{1,0:T(8,128)(2,1)S(1)}, bf16[32,128]{1,0:T(8,128)(2,1)S(1)}, u32[]{:S(2)}, u32[]{:S(2)}) %collective-permute-start.7) | collective-permute-done | bytes 8224 | tf_op jit(solution)/shard_map/ppermute | solution.py:73
  11.3 0.2 collective-permute-done.6.refs_1_
  11.5 0.9 %first.1 = (bf16[32,256]{1,0:T(8,128)(2,1)S(1)}, bf16[32,256]{1,0:T(8,128)(2,1)S(1)}, bf16[32,256]{1,0:T(8,128)(2,1)S(1)}, bf16[32,256]{1,0:T(8,128)(2,1)S(1)}) custom-call(s32[2]{0:T(128)S(1)} %pad_add_fusion.where_ref, bf16[1024,512]{1,0:T(8,128)(2,1)S(1)} %bitcast.10, bf16[32,128]{1,0:T(8,128)(2,1)S(1)} %convert_element_type.11.refs_0_, ...), custom_call_target="tpu_custom_call" | custom-call | tf_op jit(solution)/shard_map/first/pallas_call | solution.py:80
  12.5 0.0 copy-start.3
  12.5 0.9 %collective-permute-start.9 = (bf16[32,256]{1,0:T(8,128)(2,1)S(1)}, bf16[32,256]{1,0:T(8,128)(2,1)S(1)}, u32[]{:S(2)}, u32[]{:S(2)}) collective-permute-start(bf16[32,256]{1,0:T(8,128)(2,1)S(1)} %get-tuple-element.95), channel_id=1, source_target_pairs={{0,1},{1,0},{2,3},{3,2},{4,5},{5,4},{6,7},{7,6},{8,9},{9,8},{10,11... | collective-permute-start | bytes 49160 | tf_op jit(solution)/shard_map/ppermute | solution.py:73
  13.4 3.5 %collective-permute-start.10 = (bf16[32,256]{1,0:T(8,128)(2,1)S(1)}, bf16[32,256]{1,0:T(8,128)(2,1)S(1)}, u32[]{:S(2)}, u32[]{:S(2)}) collective-permute-start(bf16[32,256]{1,0:T(8,128)(2,1)S(1)} %get-tuple-element.96), channel_id=1, source_target_pairs={{0,2},{1,3},{2,0},{3,1},{4,6},{5,7},{6,4},{7,5},{8,10},{9,11},{10,... | collective-permute-start | bytes 49160 | tf_op jit(solution)/shard_map/ppermute | solution.py:73
  16.9 0.0 collective-permute-done.3.refs_0_
  16.9 0.1 collective-permute-start.11
  17.0 1.0 %collective-permute-done.4.refs_1_ = bf16[528,128]{1,0:T(8,128)(2,1)S(1)} collective-permute-done((bf16[528,128]{1,0:T(8,128)(2,1)S(1)}, bf16[528,128]{1,0:T(8,128)(2,1)S(1)}, u32[]{:S(2)}, u32[]{:S(2)}) %collective-permute-start.4) | collective-permute-done | bytes 135200 | tf_op jit(solution)/shard_map/ppermute | solution.py:73
  18.0 1.2 %crowd.1 = s32[1]{0:T(128)} custom-call(s32[4,6]{1,0:T(4,128)S(1)} %bitcast.17, bf16[528,128]{1,0:T(8,128)(2,1)S(1)} %collective-permute-done.3.refs_0_, bf16[528,128]{1,0:T(8,128)(2,1)S(1)} %collective-permute-done.4.refs_1_, bf16[528,128]{1,0:T(8,128)(2,1)S(1)} %collective-permute-done.5.refs_2_), custom_call_target="tpu_custom_call" | custom-call | tf_op jit(solution)/shard_map/crowd/pallas_call | solution.py:80
  19.8 0.4 collective-permute-done.10
  20.2 2.3 %collective-permute-done.11 = bf16[32,256]{1,0:T(8,128)(2,1)S(1)} collective-permute-done((bf16[32,256]{1,0:T(8,128)(2,1)S(1)}, bf16[32,256]{1,0:T(8,128)(2,1)S(1)}, u32[]{:S(2)}, u32[]{:S(2)}) %collective-permute-start.11) | collective-permute-done | bytes 16416 | tf_op jit(solution)/shard_map/ppermute | solution.py:73
  22.4 1.1 %conditional.1 = ((bf16[400,128]{1,0:T(8,128)(2,1)S(1)}, bf16[400,128]{1,0:T(8,128)(2,1)S(1)}, bf16[400,128]{1,0:T(8,128)(2,1)S(1)}, bf16[400,128]{1,0:T(8,128)(2,1)S(1)})) conditional(s32[]{:T(128)} %bitcast.4, (s32[2]{0:T(128)S(1)}, s32[4,6]{1,0:T(4,128)S(1)}, f32[32,1024]{1,0:T(8,128)S(1)}, f32[32,128]{1,0:T(8,128)S(1)}, ...), branch_computations={%region_0.0_spmd, %region_1.0_spmd} | conditional | bytes 1622144 | solution.py:399
  22.4 1.1 %gram.2 = (bf16[400,128]{1,0:T(8,128)(2,1)S(1)}, bf16[400,128]{1,0:T(8,128)(2,1)S(1)}, bf16[400,128]{1,0:T(8,128)(2,1)S(1)}, bf16[400,128]{1,0:T(8,128)(2,1)S(1)}) custom-call(s32[2]{0:T(128)S(1)} %get-tuple-element.53.where_ref, s32[4,6]{1,0:T(4,128)S(1)} %get-tuple-element.54.ranks_ref, f32[32,1024]{1,0:T(8,128)S(1)} %get-tuple-element.55.y_ref, ...), custom_call_target="tpu_custom_call" | custom-call | tf_op jit(solution)/shard_map/cond/branch_0_fun/gram/pallas_call | solution.py:80
  23.6 0.1 collective-permute-start.12
  23.6 1.6 %collective-permute-start.13 = (bf16[400,128]{1,0:T(8,128)(2,1)S(1)}, bf16[400,128]{1,0:T(8,128)(2,1)S(1)}, u32[]{:S(2)}, u32[]{:S(2)}) collective-permute-start(bf16[400,128]{1,0:T(8,128)(2,1)S(1)} %get-tuple-element.100), channel_id=1, source_target_pairs={{0,8},{4,12},{8,0},{12,4},{1,9},{5,13},{9,1},{13,5},{2,10},{6,14},... | collective-permute-start | bytes 307208 | tf_op jit(solution)/shard_map/ppermute | solution.py:73
  25.2 0.3 collective-permute-start.14
  25.5 0.0 collective-permute-done.12.refs_1_
  25.5 4.0 %collective-permute-done.13.refs_2_ = bf16[400,128]{1,0:T(8,128)(2,1)S(1)} collective-permute-done((bf16[400,128]{1,0:T(8,128)(2,1)S(1)}, bf16[400,128]{1,0:T(8,128)(2,1)S(1)}, u32[]{:S(2)}, u32[]{:S(2)}) %collective-permute-start.13) | collective-permute-done | bytes 102432 | tf_op jit(solution)/shard_map/ppermute | solution.py:73
  29.5 1.1 %collective-permute-done.14.refs_3_ = bf16[400,128]{1,0:T(8,128)(2,1)S(1)} collective-permute-done((bf16[400,128]{1,0:T(8,128)(2,1)S(1)}, bf16[400,128]{1,0:T(8,128)(2,1)S(1)}, u32[]{:S(2)}, u32[]{:S(2)}) %collective-permute-start.14) | collective-permute-done | bytes 102432 | tf_op jit(solution)/shard_map/ppermute | solution.py:73
  30.6 0.1 sum_base.1.refs_0_
  30.6 0.6 %collective-permute-start.17 = (bf16[400,128]{1,0:T(8,128)(2,1)S(1)}, bf16[400,128]{1,0:T(8,128)(2,1)S(1)}, u32[]{:S(2)}, u32[]{:S(2)}) collective-permute-start(bf16[400,128]{1,0:T(8,128)(2,1)S(1)} %sum_base.1.refs_0_), channel_id=1, source_target_pairs={{0,3},{1,2},{2,1},{3,0},{4,7},{5,6},{6,5},{7,4},{8,11},{9,10},{10,... | collective-permute-start | bytes 307208 | tf_op jit(solution)/shard_map/ppermute | solution.py:73
  31.3 0.9 %collective-permute-start.16 = (bf16[400,128]{1,0:T(8,128)(2,1)S(1)}, bf16[400,128]{1,0:T(8,128)(2,1)S(1)}, u32[]{:S(2)}, u32[]{:S(2)}) collective-permute-start(bf16[400,128]{1,0:T(8,128)(2,1)S(1)} %sum_base.1.refs_0_), channel_id=1, source_target_pairs={{0,2},{1,3},{2,0},{3,1},{4,6},{5,7},{6,4},{7,5},{8,10},{9,11},{10,... | collective-permute-start | bytes 307208 | tf_op jit(solution)/shard_map/ppermute | solution.py:73
  32.2 2.9 %collective-permute-start.15 = (bf16[400,128]{1,0:T(8,128)(2,1)S(1)}, bf16[400,128]{1,0:T(8,128)(2,1)S(1)}, u32[]{:S(2)}, u32[]{:S(2)}) collective-permute-start(bf16[400,128]{1,0:T(8,128)(2,1)S(1)} %sum_base.1.refs_0_), channel_id=1, source_target_pairs={{0,1},{1,0},{2,3},{3,2},{4,5},{5,4},{6,7},{7,6},{8,9},{9,8},{10,11... | collective-permute-start | bytes 307208 | tf_op jit(solution)/shard_map/ppermute | solution.py:73
  35.1 3.3 %collective-permute-done.17.refs_3_ = bf16[400,128]{1,0:T(8,128)(2,1)S(1)} collective-permute-done((bf16[400,128]{1,0:T(8,128)(2,1)S(1)}, bf16[400,128]{1,0:T(8,128)(2,1)S(1)}, u32[]{:S(2)}, u32[]{:S(2)}) %collective-permute-start.17) | collective-permute-done | bytes 102432 | tf_op jit(solution)/shard_map/ppermute | solution.py:73
  38.4 3.7 %collective-permute-done.16.refs_2_ = bf16[400,128]{1,0:T(8,128)(2,1)S(1)} collective-permute-done((bf16[400,128]{1,0:T(8,128)(2,1)S(1)}, bf16[400,128]{1,0:T(8,128)(2,1)S(1)}, u32[]{:S(2)}, u32[]{:S(2)}) %collective-permute-start.16) | collective-permute-done | bytes 102432 | tf_op jit(solution)/shard_map/ppermute | solution.py:73
  42.1 0.1 sum_pix.1.refs_0_
  42.2 2.5 %collective-permute-start.23 = (bf16[400,128]{1,0:T(8,128)(2,1)S(1)}, bf16[400,128]{1,0:T(8,128)(2,1)S(1)}, u32[]{:S(2)}, u32[]{:S(2)}) collective-permute-start(bf16[400,128]{1,0:T(8,128)(2,1)S(1)} %sum_pix.1.refs_0_), channel_id=1, source_target_pairs={{0,24},{4,28},{8,16},{12,20},{16,8},{20,12},{24,0},{28,4},{1,25},{... | collective-permute-start | bytes 307208 | tf_op jit(solution)/shard_map/ppermute | solution.py:73
  44.7 0.5 collective-permute-start.21
  45.2 0.5 collective-permute-start.19
  45.7 0.0 collective-permute-start.18
  45.7 3.2 %collective-permute-done.23.refs_6_ = bf16[400,128]{1,0:T(8,128)(2,1)S(1)} collective-permute-done((bf16[400,128]{1,0:T(8,128)(2,1)S(1)}, bf16[400,128]{1,0:T(8,128)(2,1)S(1)}, u32[]{:S(2)}, u32[]{:S(2)}) %collective-permute-start.23) | collective-permute-done | bytes 102432 | tf_op jit(solution)/shard_map/ppermute | solution.py:73
  48.9 0.0 collective-permute-start.24
  48.9 1.1 %collective-permute-done.21.refs_4_ = bf16[400,128]{1,0:T(8,128)(2,1)S(1)} collective-permute-done((bf16[400,128]{1,0:T(8,128)(2,1)S(1)}, bf16[400,128]{1,0:T(8,128)(2,1)S(1)}, u32[]{:S(2)}, u32[]{:S(2)}) %collective-permute-start.21) | collective-permute-done | bytes 102432 | tf_op jit(solution)/shard_map/ppermute | solution.py:73
  50.0 0.0 collective-permute-start.22
  50.0 0.1 collective-permute-done.19.refs_2_
  50.1 0.4 collective-permute-start.20
  50.5 0.8 %collective-permute-done.22.refs_5_ = bf16[400,128]{1,0:T(8,128)(2,1)S(1)} collective-permute-done((bf16[400,128]{1,0:T(8,128)(2,1)S(1)}, bf16[400,128]{1,0:T(8,128)(2,1)S(1)}, u32[]{:S(2)}, u32[]{:S(2)}) %collective-permute-start.22) | collective-permute-done | bytes 102432 | tf_op jit(solution)/shard_map/ppermute | solution.py:73
  51.3 0.2 collective-permute-done.20.refs_3_
  51.4 3.5 %iterate.1 = f32[32,128]{1,0:T(8,128)} custom-call(s32[2]{0:T(128)S(1)} %pad_add_fusion.where_ref, s32[4,6]{1,0:T(4,128)S(1)} %bitcast.20, bf16[400,128]{1,0:T(8,128)(2,1)S(1)} %sum_pix.1.refs_0_, bf16[400,128]{1,0:T(8,128)(2,1)S(1)} %collective-permute-done.18.refs_1_, bf16[400,128]{1,0:T(8,128)(2,1)S(1)} %collective-permute-done.19.refs_2_, ...), custom_call_target="tpu_custom_call" | custom-call | tf_op jit(solution)/shard_map/iterate/pallas_call | solution.py:80
  (14 shorter events, 0.0 us)
Async XLA Ops:
  0.0 11.5 %copy-start = (bf16[1,1024,512]{2,1,0:T(8,128)(2,1)S(1)}, bf16[1,1024,512]{2,1,0:T(8,128)(2,1)}, u32[]{:S(2)}) copy-start(bf16[1,1024,512]{2,1,0:T(8,128)(2,1)} %param.6) | copy-start | bytes 3145732
  0.1 7.1 %copy-start.2 = (f32[32,1,1,128]{3,2,1,0:T(1,128)S(1)}, f32[32,1,1,128]{3,2,1,0:T(1,128)}, u32[]{:S(2)}) copy-start(f32[32,1,1,128]{3,2,1,0:T(1,128)} %param.8) | copy-start | bytes 49156
  1.5 15.4 %collective-permute-start.3 = (bf16[528,128]{1,0:T(8,128)(2,1)S(1)}, bf16[528,128]{1,0:T(8,128)(2,1)S(1)}, u32[]{:S(2)}, u32[]{:S(2)}) collective-permute-start(bf16[528,128]{1,0:T(8,128)(2,1)S(1)} %get-tuple-element.91), channel_id=1, source_target_pairs={{0,1},{1,0},{2,3},{3,2},{4,5},{5,4},{6,7},{7,6},{8,9},{9,8},{10,11... | collective-permute-start | bytes 405512 | tf_op jit(solution)/shard_map/ppermute | solution.py:73
  4.6 13.3 %collective-permute-start.4 = (bf16[528,128]{1,0:T(8,128)(2,1)S(1)}, bf16[528,128]{1,0:T(8,128)(2,1)S(1)}, u32[]{:S(2)}, u32[]{:S(2)}) collective-permute-start(bf16[528,128]{1,0:T(8,128)(2,1)S(1)} %get-tuple-element.92), channel_id=1, source_target_pairs={{0,2},{1,3},{2,0},{3,1},{4,6},{5,7},{6,4},{7,5},{8,10},{9,11},{10,... | collective-permute-start | bytes 405512 | tf_op jit(solution)/shard_map/ppermute | solution.py:73
  7.2 10.7 %collective-permute-start.5 = (bf16[528,128]{1,0:T(8,128)(2,1)S(1)}, bf16[528,128]{1,0:T(8,128)(2,1)S(1)}, u32[]{:S(2)}, u32[]{:S(2)}) collective-permute-start(bf16[528,128]{1,0:T(8,128)(2,1)S(1)} %get-tuple-element.93), channel_id=1, source_target_pairs={{0,3},{1,2},{2,1},{3,0},{4,7},{5,6},{6,5},{7,4},{8,11},{9,10},{10,... | collective-permute-start | bytes 405512 | tf_op jit(solution)/shard_map/ppermute | solution.py:73
  7.2 3.1 %collective-permute-start.8 = (bf16[32,128]{1,0:T(8,128)(2,1)S(1)}, bf16[32,128]{1,0:T(8,128)(2,1)S(1)}, u32[]{:S(2)}, u32[]{:S(2)}) collective-permute-start(bf16[32,128]{1,0:T(8,128)(2,1)S(1)} %convert_element_type.11.refs_0_), channel_id=1, source_target_pairs={{0,12},{4,8},{8,4},{12,0},{1,13},{5,9},{9,5},{13,1},{2,14},{6,10},... | collective-permute-start | bytes 24584 | tf_op jit(solution)/shard_map/ppermute | solution.py:73
  7.7 3.7 %collective-permute-start.7 = (bf16[32,128]{1,0:T(8,128)(2,1)S(1)}, bf16[32,128]{1,0:T(8,128)(2,1)S(1)}, u32[]{:S(2)}, u32[]{:S(2)}) collective-permute-start(bf16[32,128]{1,0:T(8,128)(2,1)S(1)} %convert_element_type.11.refs_0_), channel_id=1, source_target_pairs={{0,8},{4,12},{8,0},{12,4},{1,9},{5,13},{9,1},{13,5},{2,10},{6,14},... | collective-permute-start | bytes 24584 | tf_op jit(solution)/shard_map/ppermute | solution.py:73
  10.4 1.2 %collective-permute-start.6 = (bf16[32,128]{1,0:T(8,128)(2,1)S(1)}, bf16[32,128]{1,0:T(8,128)(2,1)S(1)}, u32[]{:S(2)}, u32[]{:S(2)}) collective-permute-start(bf16[32,128]{1,0:T(8,128)(2,1)S(1)} %convert_element_type.11.refs_0_), channel_id=1, source_target_pairs={{0,4},{4,0},{8,12},{12,8},{1,5},{5,1},{9,13},{13,9},{2,6},{6,2},{1... | collective-permute-start | bytes 24584 | tf_op jit(solution)/shard_map/ppermute | solution.py:73
  12.5 5.5 %copy-start.3 = (s32[6,4]{0,1:T(4,128)S(1)}, s32[6,4]{0,1:T(4,128)}, u32[]{:S(2)}) copy-start(s32[6,4]{0,1:T(4,128)} %param.9) | copy-start | bytes 292
  12.5 7.3 %collective-permute-start.9 = (bf16[32,256]{1,0:T(8,128)(2,1)S(1)}, bf16[32,256]{1,0:T(8,128)(2,1)S(1)}, u32[]{:S(2)}, u32[]{:S(2)}) collective-permute-start(bf16[32,256]{1,0:T(8,128)(2,1)S(1)} %get-tuple-element.95), channel_id=1, source_target_pairs={{0,1},{1,0},{2,3},{3,2},{4,5},{5,4},{6,7},{7,6},{8,9},{9,8},{10,11... | collective-permute-start | bytes 49160 | tf_op jit(solution)/shard_map/ppermute | solution.py:73
  13.4 6.8 %collective-permute-start.10 = (bf16[32,256]{1,0:T(8,128)(2,1)S(1)}, bf16[32,256]{1,0:T(8,128)(2,1)S(1)}, u32[]{:S(2)}, u32[]{:S(2)}) collective-permute-start(bf16[32,256]{1,0:T(8,128)(2,1)S(1)} %get-tuple-element.96), channel_id=1, source_target_pairs={{0,2},{1,3},{2,0},{3,1},{4,6},{5,7},{6,4},{7,5},{8,10},{9,11},{10,... | collective-permute-start | bytes 49160 | tf_op jit(solution)/shard_map/ppermute | solution.py:73
  16.9 5.5 %copy-start.1 = (f32[32,1024]{1,0:T(8,128)S(1)}, f32[32,1024]{1,0:T(8,128)}, u32[]{:S(2)}) copy-start(f32[32,1024]{1,0:T(8,128)} %param.7) | copy-start | bytes 393220
  16.9 5.5 %collective-permute-start.11 = (bf16[32,256]{1,0:T(8,128)(2,1)S(1)}, bf16[32,256]{1,0:T(8,128)(2,1)S(1)}, u32[]{:S(2)}, u32[]{:S(2)}) collective-permute-start(bf16[32,256]{1,0:T(8,128)(2,1)S(1)} %get-tuple-element.97), channel_id=1, source_target_pairs={{0,3},{1,2},{2,1},{3,0},{4,7},{5,6},{6,5},{7,4},{8,11},{9,10},{10,... | collective-permute-start | bytes 49160 | tf_op jit(solution)/shard_map/ppermute | solution.py:73
  23.6 1.9 %collective-permute-start.12 = (bf16[400,128]{1,0:T(8,128)(2,1)S(1)}, bf16[400,128]{1,0:T(8,128)(2,1)S(1)}, u32[]{:S(2)}, u32[]{:S(2)}) collective-permute-start(bf16[400,128]{1,0:T(8,128)(2,1)S(1)} %get-tuple-element.99), channel_id=1, source_target_pairs={{0,4},{4,0},{8,12},{12,8},{1,5},{5,1},{9,13},{13,9},{2,6},{6,2},{1... | collective-permute-start | bytes 307208 | tf_op jit(solution)/shard_map/ppermute | solution.py:73
  23.6 5.8 %collective-permute-start.13 = (bf16[400,128]{1,0:T(8,128)(2,1)S(1)}, bf16[400,128]{1,0:T(8,128)(2,1)S(1)}, u32[]{:S(2)}, u32[]{:S(2)}) collective-permute-start(bf16[400,128]{1,0:T(8,128)(2,1)S(1)} %get-tuple-element.100), channel_id=1, source_target_pairs={{0,8},{4,12},{8,0},{12,4},{1,9},{5,13},{9,1},{13,5},{2,10},{6,14},... | collective-permute-start | bytes 307208 | tf_op jit(solution)/shard_map/ppermute | solution.py:73
  25.2 5.4 %collective-permute-start.14 = (bf16[400,128]{1,0:T(8,128)(2,1)S(1)}, bf16[400,128]{1,0:T(8,128)(2,1)S(1)}, u32[]{:S(2)}, u32[]{:S(2)}) collective-permute-start(bf16[400,128]{1,0:T(8,128)(2,1)S(1)} %get-tuple-element.101), channel_id=1, source_target_pairs={{0,12},{4,8},{8,4},{12,0},{1,13},{5,9},{9,5},{13,1},{2,14},{6,10},... | collective-permute-start | bytes 307208 | tf_op jit(solution)/shard_map/ppermute | solution.py:73
  30.6 7.7 %collective-permute-start.17 = (bf16[400,128]{1,0:T(8,128)(2,1)S(1)}, bf16[400,128]{1,0:T(8,128)(2,1)S(1)}, u32[]{:S(2)}, u32[]{:S(2)}) collective-permute-start(bf16[400,128]{1,0:T(8,128)(2,1)S(1)} %sum_base.1.refs_0_), channel_id=1, source_target_pairs={{0,3},{1,2},{2,1},{3,0},{4,7},{5,6},{6,5},{7,4},{8,11},{9,10},{10,... | collective-permute-start | bytes 307208 | tf_op jit(solution)/shard_map/ppermute | solution.py:73
  31.3 10.8 %collective-permute-start.16 = (bf16[400,128]{1,0:T(8,128)(2,1)S(1)}, bf16[400,128]{1,0:T(8,128)(2,1)S(1)}, u32[]{:S(2)}, u32[]{:S(2)}) collective-permute-start(bf16[400,128]{1,0:T(8,128)(2,1)S(1)} %sum_base.1.refs_0_), channel_id=1, source_target_pairs={{0,2},{1,3},{2,0},{3,1},{4,6},{5,7},{6,4},{7,5},{8,10},{9,11},{10,... | collective-permute-start | bytes 307208 | tf_op jit(solution)/shard_map/ppermute | solution.py:73
  32.2 9.9 %collective-permute-start.15 = (bf16[400,128]{1,0:T(8,128)(2,1)S(1)}, bf16[400,128]{1,0:T(8,128)(2,1)S(1)}, u32[]{:S(2)}, u32[]{:S(2)}) collective-permute-start(bf16[400,128]{1,0:T(8,128)(2,1)S(1)} %sum_base.1.refs_0_), channel_id=1, source_target_pairs={{0,1},{1,0},{2,3},{3,2},{4,5},{5,4},{6,7},{7,6},{8,9},{9,8},{10,11... | collective-permute-start | bytes 307208 | tf_op jit(solution)/shard_map/ppermute | solution.py:73
  42.2 6.7 %collective-permute-start.23 = (bf16[400,128]{1,0:T(8,128)(2,1)S(1)}, bf16[400,128]{1,0:T(8,128)(2,1)S(1)}, u32[]{:S(2)}, u32[]{:S(2)}) collective-permute-start(bf16[400,128]{1,0:T(8,128)(2,1)S(1)} %sum_pix.1.refs_0_), channel_id=1, source_target_pairs={{0,24},{4,28},{8,16},{12,20},{16,8},{20,12},{24,0},{28,4},{1,25},{... | collective-permute-start | bytes 307208 | tf_op jit(solution)/shard_map/ppermute | solution.py:73
  44.7 5.3 %collective-permute-start.21 = (bf16[400,128]{1,0:T(8,128)(2,1)S(1)}, bf16[400,128]{1,0:T(8,128)(2,1)S(1)}, u32[]{:S(2)}, u32[]{:S(2)}) collective-permute-start(bf16[400,128]{1,0:T(8,128)(2,1)S(1)} %sum_pix.1.refs_0_), channel_id=1, source_target_pairs={{0,16},{4,20},{8,24},{12,28},{16,0},{20,4},{24,8},{28,12},{1,17},{... | collective-permute-start | bytes 307208 | tf_op jit(solution)/shard_map/ppermute | solution.py:73
  45.2 4.9 %collective-permute-start.19 = (bf16[400,128]{1,0:T(8,128)(2,1)S(1)}, bf16[400,128]{1,0:T(8,128)(2,1)S(1)}, u32[]{:S(2)}, u32[]{:S(2)}) collective-permute-start(bf16[400,128]{1,0:T(8,128)(2,1)S(1)} %sum_pix.1.refs_0_), channel_id=1, source_target_pairs={{0,8},{4,12},{8,0},{12,4},{16,24},{20,28},{24,16},{28,20},{1,9},{5... | collective-permute-start | bytes 307208 | tf_op jit(solution)/shard_map/ppermute | solution.py:73
  45.7 4.8 %collective-permute-start.18 = (bf16[400,128]{1,0:T(8,128)(2,1)S(1)}, bf16[400,128]{1,0:T(8,128)(2,1)S(1)}, u32[]{:S(2)}, u32[]{:S(2)}) collective-permute-start(bf16[400,128]{1,0:T(8,128)(2,1)S(1)} %sum_pix.1.refs_0_), channel_id=1, source_target_pairs={{0,4},{4,0},{8,12},{12,8},{16,20},{20,16},{24,28},{28,24},{1,5},{5... | collective-permute-start | bytes 307208 | tf_op jit(solution)/shard_map/ppermute | solution.py:73
  48.9 1.6 %collective-permute-start.24 = (bf16[400,128]{1,0:T(8,128)(2,1)S(1)}, bf16[400,128]{1,0:T(8,128)(2,1)S(1)}, u32[]{:S(2)}, u32[]{:S(2)}) collective-permute-start(bf16[400,128]{1,0:T(8,128)(2,1)S(1)} %collective-permute-done.23.refs_6_), channel_id=1, source_target_pairs={{0,4},{4,0},{8,12},{12,8},{16,20},{20,16},{24,28},{28,24},{1,5},{5... | collective-permute-start | bytes 307208 | tf_op jit(solution)/shard_map/ppermute | solution.py:73
  50.0 1.3 %collective-permute-start.22 = (bf16[400,128]{1,0:T(8,128)(2,1)S(1)}, bf16[400,128]{1,0:T(8,128)(2,1)S(1)}, u32[]{:S(2)}, u32[]{:S(2)}) collective-permute-start(bf16[400,128]{1,0:T(8,128)(2,1)S(1)} %collective-permute-done.21.refs_4_), channel_id=1, source_target_pairs={{0,4},{4,0},{8,12},{12,8},{16,20},{20,16},{24,28},{28,24},{1,5},{5... | collective-permute-start | bytes 307208 | tf_op jit(solution)/shard_map/ppermute | solution.py:73
  50.1 1.3 %collective-permute-start.20 = (bf16[400,128]{1,0:T(8,128)(2,1)S(1)}, bf16[400,128]{1,0:T(8,128)(2,1)S(1)}, u32[]{:S(2)}, u32[]{:S(2)}) collective-permute-start(bf16[400,128]{1,0:T(8,128)(2,1)S(1)} %collective-permute-done.19.refs_2_), channel_id=1, source_target_pairs={{0,4},{4,0},{8,12},{12,8},{16,20},{20,16},{24,28},{28,24},{1,5},{5... | collective-permute-start | bytes 307208 | tf_op jit(solution)/shard_map/ppermute | solution.py:73

commit v5 on v4

--- a/solution.py
+++ b/solution.py
@@ -16,6 +16,7 @@
 lam_shrink = 0.3
 eps_norm = 1e-06
 
+
 GRAM_LIMIT = 1 << 20
 PAD = 16
 CAPACITY = 2
@@ -39,7 +40,7 @@
 
 def streaming(sensing_operator_parts, sampled_correlations, first_sky_estimate, patch_order_record):
     sensing_operator = sensing_operator_parts[0]
-    chans, m_dev = sampled_correlations.shape
+    chans, _ = sampled_correlations.shape
     share_width = first_sky_estimate.shape[3]
     tiles_share = share_width // TILE
     keep_count = tiles_share * lax.axis_size("base") * lax.axis_size("pix") // 4
@@ -73,7 +74,7 @@
     return lax.ppermute(value, axis, [(i, i ^ offset) for i in range(size)])
 
 
-def call(body, out_shape, args, scratch=(), smem=(), hbm=(), out_space=pltpu.VMEM, name=None):
+def call(body, out_shape, args, scratch=(), smem=(), hbm=(), out_space=pltpu.VMEM):
     places = [pltpu.SMEM if i in smem else pl.ANY if i in hbm else pltpu.VMEM for i in range(len(args))]
     specs = [pl.BlockSpec(memory_space=place) for place in places]
     out_specs = jax.tree.map(lambda _: pl.BlockSpec(memory_space=out_space), out_shape)
@@ -84,7 +85,6 @@
         out_specs=out_specs,
         scratch_shapes=list(scratch),
         compiler_params=pltpu.CompilerParams(vmem_limit_bytes=VMEM_LIMIT),
-        name=name,
     )(*args)
 
 
@@ -177,12 +177,12 @@
     return rows, cols
 
 
-def gram_body(slots, n_pix, n_parts, where_ref, ranks_ref, y_ref, x0_ref, a_ref, *refs):
+def gram_body(slots, n_parts, where_ref, ranks_ref, y_ref, a_ref, *refs):
     pix, base = where_ref[0], where_ref[1]
-    parts, preds = refs[:n_parts], refs[n_parts : n_parts + n_pix]
-    *outs, all_ref = refs[n_parts + n_pix :]
+    parts = refs[:n_parts]
+    cols_ref, *outs, all_ref = refs[n_parts:]
     n_base = len(outs)
-    chans, quarter = preds[0].shape
+    chans, quarter = y_ref.shape[0], cols_ref.shape[0]
     table, _ = kept_tiles(ranks_ref, slots)
     own_rows = pl.ds(pl.multiple_of(pix * quarter, quarter), quarter)
     columns = []
@@ -201,28 +201,19 @@
                 block = jnp.where(hit, part[i * quarter : (i + 1) * quarter, :], block)
         columns.append(block)
     a = jnp.concatenate(columns, axis=1)
-    pred = preds[0][...].astype(jnp.float32)
-    for piece in preds[1:]:
-        pred = pred + piece[...].astype(jnp.float32)
+    cols_ref[...] = a
     y = y_ref[:, pl.ds(pl.multiple_of(pix * quarter, quarter), quarter)]
-    resid = (y - pred).astype(jnp.bfloat16)
-    y_hi, y_lo = split(y)
-    left = jnp.concatenate([y_hi, y_lo, resid], axis=0)
-    sides = jnp.dot(left, a, preferred_element_type=jnp.float32)
-    data = sides[:chans] + sides[chans : 2 * chans]
-    moved = descent_stride * sides[2 * chans :]
-    rank = ranks_ref[base, 0]
+    both = jnp.dot(jnp.concatenate(split(y), axis=0), a, preferred_element_type=jnp.float32)
+    data = both[:chans] + both[chans:]
     gram = lax.dot_general(a, a, (((0,), (0,)), ((), ())), preferred_element_type=jnp.float32)
     rows, cols = corner()
     g_rows = pack_rows(slots, n_base)
     per = slots // n_base
-    side_rows = 4 * chans + PAD
     half = min(TILE, g_rows & -g_rows)
 
     def block_of(r, s):
         return gram[r * TILE : (r + 1) * TILE, s * TILE : (s + 1) * TILE]
 
-    diags = [jnp.sum(jnp.where(rows == cols, block_of(r, r), 0.0), axis=0, keepdims=True) for r in range(slots)]
     n_off = slots * (slots - 1) // 2
     for i, (r, s) in enumerate(pairs(slots)):
         block = block_of(r, s) if i < n_off else jnp.where(rows < cols, block_of(r, r), block_of(s, s))
@@ -231,53 +222,70 @@
             at = i * TILE + q * half
             all_ref[at // g_rows, at % g_rows : at % g_rows + half, :] = block[q * half : (q + 1) * half]
     for r in range(slots):
-        lanes = slice(r * TILE, (r + 1) * TILE)
-        start = jnp.where(rank == r, x0_ref[...], 0.0)
-        d_hi, d_lo = split(diags[r])
-        stack = [
-            *split(data[:, lanes]),
-            *split(moved[:, lanes] + start),
-            d_hi,
-            d_lo,
-            jnp.zeros((PAD - 2, TILE), jnp.bfloat16),
-        ]
-        at = g_rows + (r % per) * side_rows
-        for piece in stack[:4]:
-            all_ref[r // per, at : at + chans, :] = piece
-            at += chans
-        all_ref[r // per, at : at + PAD, :] = jnp.concatenate(stack[4:], axis=0)
+        diag = jnp.sum(jnp.where(rows == cols, block_of(r, r), 0.0), axis=0, keepdims=True)
+        at = g_rows + (r % per) * (2 * chans + PAD)
+        wide = jnp.concatenate(split(data[:, r * TILE : (r + 1) * TILE]), axis=0)
+        all_ref[r // per, at : at + 2 * chans, :] = wide
+        all_ref[r // per, at + 2 * chans : at + 2 * chans + PAD, :] = tail_of(diag)
     for d, out in enumerate(outs):
         out[...] = all_ref[base ^ d]
 
 
-def sum_body(g_rows, chans, per, *refs):
+def tail_of(row):
+    return jnp.concatenate([*split(row), jnp.zeros((PAD - 2, TILE), jnp.bfloat16)], axis=0)
+
+
+def start_body(slots, n_pix, where_ref, ranks_ref, y_ref, x0_ref, cols_ref, *refs):
+    pix, base = where_ref[0], where_ref[1]
+    preds = refs[:n_pix]
+    *outs, all_ref = refs[n_pix:]
+    per = slots // len(outs)
+    chans, quarter = preds[0].shape
+    pred = preds[0][...].astype(jnp.float32)
+    for piece in preds[1:]:
+        pred = pred + piece[...].astype(jnp.float32)
+    y = y_ref[:, pl.ds(pl.multiple_of(pix * quarter, quarter), quarter)]
+    resid = (y - pred).astype(jnp.bfloat16)
+    moved = descent_stride * jnp.dot(resid, cols_ref[...], preferred_element_type=jnp.float32)
+    rank = ranks_ref[base, 0]
+    for r in range(slots):
+        start = moved[:, r * TILE : (r + 1) * TILE] + jnp.where(rank == r, x0_ref[...], 0.0)
+        at = (r % per) * 2 * chans
+        all_ref[r // per, at : at + 2 * chans, :] = jnp.concatenate(split(start), axis=0)
+    for d, out in enumerate(outs):
+        out[...] = all_ref[base ^ d]
+
+
+def sections(g_rows, chans, per):
+    first = [(g_rows, 0)] + [(2 * chans, chans), (PAD, 1)] * per
+    return first, [(2 * chans, chans)] * per
+
+
+def sum_body(layouts, *refs):
     *parts, out = refs
-
-    def total(at, size):
-        value = parts[0][at : at + size].astype(jnp.float32)
-        for part in parts[1:]:
-            value = value + part[at : at + size].astype(jnp.float32)
-        return value
-
-    out[:g_rows] = total(0, g_rows).astype(jnp.bfloat16)
-    at = g_rows
-    for _ in range(per):
-        for _ in range(2):
-            high, low = split(total(at, chans) + total(at + chans, chans))
-            out[at : at + chans] = high
-            out[at + chans : at + 2 * chans] = low
-            at += 2 * chans
-        tail = total(at, PAD)
-        high, low = split(tail[0:1] + tail[1:2])
-        rest = jnp.zeros((PAD - 2, TILE), jnp.bfloat16)
-        out[at : at + PAD] = jnp.concatenate([high, low, rest], axis=0)
-        at += PAD
+    groups = [parts[i :: len(layouts)] for i in range(len(layouts))]
+    to = 0
+    for group, layout in zip(groups, layouts):
+        at = 0
+        for size, pair in layout:
+            value = group[0][at : at + size].astype(jnp.float32)
+            for part in group[1:]:
+                value = value + part[at : at + size].astype(jnp.float32)
+            if pair == 0:
+                out[to : to + size] = value.astype(jnp.bfloat16)
+            elif pair == 1:
+                out[to : to + size] = tail_of(value[0:1] + value[1:2])
+            else:
+                out[to : to + size] = jnp.concatenate(split(value[:pair] + value[pair:]), axis=0)
+            at += size
+            to += size
 
 
 def iterate_body(slots, n_base, g_rows, chans, where_ref, ranks_ref, *refs):
     base = where_ref[1]
     per = slots // n_base
-    side_rows = 4 * chans + PAD
+    data_rows = 2 * chans + PAD
+    image_at = g_rows + per * data_rows
     chunks = [refs[:n_base], refs[n_base : 2 * n_base]]
     out_ref, gram_ref, last_ref = refs[2 * n_base :]
     states, datas, diags = [], [], []
@@ -304,11 +312,11 @@
                 lower = jnp.where(rows > cols, block, jnp.zeros_like(block))
                 put(g, r, r, upper + upper.T)
                 put(g, s, s, lower + lower.T)
-        sides = [full[r // per][g_rows + (r % per) * side_rows :][:side_rows].astype(jnp.float32) for r in range(slots)]
-        wide = lambda at: jnp.concatenate([v[at : at + chans] + v[at + chans : at + 2 * chans] for v in sides], axis=1)
-        datas.append(wide(0))
-        states.append(wide(2 * chans))
-        tails = [v[4 * chans :] for v in sides]
+        sides = [full[r // per][g_rows + (r % per) * data_rows :][:data_rows].astype(jnp.float32) for r in range(slots)]
+        images = [full[r // per][image_at + (r % per) * 2 * chans :][: 2 * chans].astype(jnp.float32) for r in range(slots)]
+        datas.append(jnp.concatenate([v[:chans] + v[chans : 2 * chans] for v in sides], axis=1))
+        states.append(jnp.concatenate([v[:chans] + v[chans:] for v in images], axis=1))
+        tails = [v[2 * chans :] for v in sides]
         diags.append(jnp.concatenate([t[0:1] + t[1:2] for t in tails], axis=1))
     for step in range(ITERS):
         factors = []
@@ -355,9 +363,8 @@
             [shape((places * quarter + PAD, TILE), bf16)] * (n_pix - 1),
             (where, ranks, a),
             smem=(0, 1),
-            name="pack",
-        )
-        return [swap(piece, "pix", d + 1) for d, piece in enumerate(packed)]
+        )
+        return [swap(packed[d - 1], "pix", d) for d in range(n_pix - 1, 0, -1)]
 
     places = min(CAPACITY, ranks.shape[0])
     parts = exchange(0, places)
@@ -369,24 +376,36 @@
         (where, a, *shares),
         scratch=[pltpu.VMEM((chans, n_base * TILE), bf16)],
         smem=(0,),
-        name="first",
-    )
-    preds = [firsts[0]] + [swap(firsts[d], "pix", d) for d in range(1, n_pix)]
+    )
+    preds = [firsts[0]] + [swap(firsts[d], "pix", d) for d in range(n_pix - 1, 0, -1)]
 
     g_rows = pack_rows(slots, n_base)
     per = slots // n_base
-    rows = g_rows + per * (4 * chans + PAD)
-    chunk = shape((rows, TILE), bf16)
-
-    def gram(parts):
-        return call(
-            functools.partial(gram_body, slots, n_pix, len(parts)),
-            [chunk] * n_base,
-            (where, ranks, sampled_correlations, x0, a, *parts, *preds),
-            scratch=[pltpu.VMEM((n_base, rows, TILE), bf16)],
+    layouts = sections(g_rows, chans, per)
+    gram_chunk, image_chunk = [shape((sum(size for size, _ in layout), TILE), bf16) for layout in layouts]
+    chunk = shape((gram_chunk.shape[0] + image_chunk.shape[0], TILE), bf16)
+
+    def spread(parts):
+        columns, *grams = call(
+            functools.partial(gram_body, slots, len(parts)),
+            [shape((quarter, slots * TILE), bf16)] + [gram_chunk] * n_base,
+            (where, ranks, sampled_correlations, a, *parts),
+            scratch=[pltpu.VMEM((n_base, *gram_chunk.shape), bf16)],
             smem=(0, 1),
-            name="gram",
-        )
+        )
+        grams = [grams[0]] + [swap(grams[d], "base", d) for d in range(1, n_base)]
+        images = call(
+            functools.partial(start_body, slots, n_pix),
+            [image_chunk] * n_base,
+            (where, ranks, sampled_correlations, x0, columns, *preds),
+            scratch=[pltpu.VMEM((n_base, *image_chunk.shape), bf16)],
+            smem=(0, 1),
+        )
+        images = [images[0]] + [swap(images[d], "base", d) for d in range(1, n_base)]
+        return [piece for pair in zip(grams, images) for piece in pair]
+
+    def add(layouts, pieces):
+        return call(functools.partial(sum_body, layouts), chunk, pieces)
 
     crowded = call(
         functools.partial(crowd_body, slots, places),
@@ -394,16 +413,14 @@
         (ranks, *parts),
         smem=(0,),
         out_space=pltpu.SMEM,
-        name="crowd",
     )[0]
-    outs = lax.cond(
+    pieces = spread(parts)
+    part = lax.cond(
         crowded != 0,
-        lambda: gram(parts + exchange(places, ranks.shape[0] - places)),
-        lambda: gram(parts),
-    )
-    add = functools.partial(sum_body, g_rows, chans, per)
-    part = call(add, chunk, [outs[0]] + [swap(outs[d], "base", d) for d in range(1, n_base)], name="sum_base")
-    total = call(add, chunk, [part] + [swap(part, "pix", d) for d in range(1, n_pix)], name="sum_pix")
+        lambda: add(layouts, spread(parts + exchange(places, ranks.shape[0] - places))),
+        lambda: add(layouts, pieces),
+    )
+    total = add([layouts[0] + layouts[1]], [part] + [swap(part, "pix", d) for d in range(n_pix - 1, 0, -1)])
 
     axes = ("freq", "base")
     got = {0: total}
@@ -421,7 +438,6 @@
             pltpu.VMEM((slots, chans, TILE), f32),
         ],
         smem=(0, 1),
-        name="iterate",
     )
     return image.reshape(chans, 1, 1, TILE)
 

time: 55.1 us -> 66.8 us (1.21)
  waiting for transfers between devices: 23.2 us -> 33.4 us
  Pallas kernels: 8.28 us -> 9.36 us
    ppermute x22 -> x25, waiting for transfers between devices: 23.2 us -> 33.4 us  [swap(): return lax.ppermute(value, axis, [(i, i ^ offset) for i in range(size)])]
    pallas_call x7 -> x8, Pallas kernels: 8.28 us -> 9.36 us  [call(): pl.pallas_call(body, out_shape=out_shape, in_specs=specs, out_specs=out_s...]
    ppermute x22 -> x25, starting transfers between devices: 22.6 us -> 23 us  [swap(): return lax.ppermute(value, axis, [(i, i ^ offset) for i in range(size)])]
  transfers between devices with their start and end apart: 22 -> 25, of which waited for: 15 -> 16; matrix products, arithmetic and copies ran while one was open for 0% -> 0% of each run, Pallas kernels for 4% -> 4%
where the time goes in v5:
time: 66.8 us; the launch traced here: 66.7 us
  waiting for transfers between devices  33.4 us (50%)
  starting transfers between devices  23 us (34%)
  Pallas kernels  9.36 us (14%)
  between operations  0.78 us (1%)
    ppermute x25, waiting for transfers between devices, swap(): return lax.ppermute(value, axis, [(i, i ^ offset) for i in range(size)])  33.4 us
    ppermute x25, starting transfers between devices, swap(): return lax.ppermute(value, axis, [(i, i ^ offset) for i in range(size)])  23 us
    pallas_call x8, Pallas kernels, call(): pl.pallas_call(body, out_shape=out_shape, in_specs=specs, out_specs=out_s...  9.36 us
  transfers between devices with their start and end apart: 25, of which 16 were waited for; matrix products, arithmetic and copies ran while one was open for 0% of the time, Pallas kernels for 4%

profile of v5, /device:TPU:0, one launch (start us, length us, event | category | flops | bytes accessed | tf_op | source)
XLA Modules:
  0.0 66.7 jit_solution(17402638032502020005)
XLA Ops:
  0.0 0.1 pad_add_fusion.where_ref
  0.1 1.4 %shard_map.46 = (bf16[528,128]{1,0:T(8,128)(2,1)S(1)}, bf16[528,128]{1,0:T(8,128)(2,1)S(1)}, bf16[528,128]{1,0:T(8,128)(2,1)S(1)}) custom-call(s32[2]{0:T(128)S(1)} %pad_add_fusion.where_ref, s32[4,6]{1,0:T(4,128)} %bitcast.16, bf16[1024,512]{1,0:T(8,128)(2,1)} %bitcast.9), custom_call_target="tpu_custom_call" | custom-call | tf_op jit(solution)/shard_map/pallas_call | solution.py:81
  1.5 0.0 copy-start.3
  1.5 5.1 %collective-permute-start.9 = (bf16[528,128]{1,0:T(8,128)(2,1)S(1)}, bf16[528,128]{1,0:T(8,128)(2,1)S(1)}, u32[]{:S(2)}, u32[]{:S(2)}) collective-permute-start(bf16[528,128]{1,0:T(8,128)(2,1)S(1)} %get-tuple-element.96), channel_id=1, source_target_pairs={{0,3},{1,2},{2,1},{3,0},{4,7},{5,6},{6,5},{7,4},{8,11},{9,10},{10,... | collective-permute-start | bytes 405512 | tf_op jit(solution)/shard_map/ppermute | solution.py:74
  6.6 0.0 collective-permute-start.10
  6.6 0.6 collective-permute-start.11
  7.3 3.9 %collective-permute-done.9.refs_0_ = bf16[528,128]{1,0:T(8,128)(2,1)S(1)} collective-permute-done((bf16[528,128]{1,0:T(8,128)(2,1)S(1)}, bf16[528,128]{1,0:T(8,128)(2,1)S(1)}, u32[]{:S(2)}, u32[]{:S(2)}) %collective-permute-start.9) | collective-permute-done | bytes 135200 | tf_op jit(solution)/shard_map/ppermute | solution.py:74
  11.2 6.9 %collective-permute-done.10.refs_1_ = bf16[528,128]{1,0:T(8,128)(2,1)S(1)} collective-permute-done((bf16[528,128]{1,0:T(8,128)(2,1)S(1)}, bf16[528,128]{1,0:T(8,128)(2,1)S(1)}, u32[]{:S(2)}, u32[]{:S(2)}) %collective-permute-start.10) | collective-permute-done | bytes 135200 | tf_op jit(solution)/shard_map/ppermute | solution.py:74
  18.1 0.0 copy-start.2
  18.1 1.5 %shard_map.48 = (bf16[256,512]{1,0:T(8,128)(2,1)S(1)}, bf16[336,128]{1,0:T(8,128)(2,1)S(1)}, bf16[336,128]{1,0:T(8,128)(2,1)S(1)}, bf16[336,128]{1,0:T(8,128)(2,1)S(1)}, bf16[336,128]{1,0:T(8,128)(2,1)S(1)}) custom-call(s32[2]{0:T(128)S(1)} %pad_add_fusion.where_ref, s32[4,6]{1,0:T(4,128)S(1)} %bitcast.17, f32[32,1024]{1,0:T(8,128)} %y_ref.3, ...), custom_call_target="tpu_custom_call" | custom-call | tf_op jit(solution)/shard_map/pallas_call | solution.py:81
  19.6 0.1 collective-permute-start.18
  19.6 1.6 %collective-permute-start.20 = (bf16[336,128]{1,0:T(8,128)(2,1)S(1)}, bf16[336,128]{1,0:T(8,128)(2,1)S(1)}, u32[]{:S(2)}, u32[]{:S(2)}) collective-permute-start(bf16[336,128]{1,0:T(8,128)(2,1)S(1)} %get-tuple-element.108), channel_id=1, source_target_pairs={{0,8},{4,12},{8,0},{12,4},{1,9},{5,13},{9,1},{13,5},{2,10},{6,14},... | collective-permute-start | bytes 258056 | tf_op jit(solution)/shard_map/ppermute | solution.py:74
  21.2 0.3 collective-permute-start.22
  21.5 1.5 %collective-permute-start.14 = (bf16[32,128]{1,0:T(8,128)(2,1)S(1)}, bf16[32,128]{1,0:T(8,128)(2,1)S(1)}, u32[]{:S(2)}, u32[]{:S(2)}) collective-permute-start(bf16[32,128]{1,0:T(8,128)(2,1)S(1)} %convert_element_type.11.refs_0_), channel_id=1, source_target_pairs={{0,12},{4,8},{8,4},{12,0},{1,13},{5,9},{9,5},{13,1},{2,14},{6,10},... | collective-permute-start | bytes 24584 | tf_op jit(solution)/shard_map/ppermute | solution.py:74
  23.1 0.5 collective-permute-start.13
  23.6 2.7 %collective-permute-done.14.refs_3_ = bf16[32,128]{1,0:T(8,128)(2,1)S(1)} collective-permute-done((bf16[32,128]{1,0:T(8,128)(2,1)S(1)}, bf16[32,128]{1,0:T(8,128)(2,1)S(1)}, u32[]{:S(2)}, u32[]{:S(2)}) %collective-permute-start.14) | collective-permute-done | bytes 8224 | tf_op jit(solution)/shard_map/ppermute | solution.py:74
  26.2 0.3 collective-permute-start.12
  26.5 0.3 collective-permute-done.13.refs_2_
  26.8 0.6 collective-permute-done.12.refs_1_
  27.4 0.9 %shard_map.49 = (bf16[32,256]{1,0:T(8,128)(2,1)S(1)}, bf16[32,256]{1,0:T(8,128)(2,1)S(1)}, bf16[32,256]{1,0:T(8,128)(2,1)S(1)}, bf16[32,256]{1,0:T(8,128)(2,1)S(1)}) custom-call(s32[2]{0:T(128)S(1)} %pad_add_fusion.where_ref, bf16[1024,512]{1,0:T(8,128)(2,1)S(1)} %bitcast.11, bf16[32,128]{1,0:T(8,128)(2,1)S(1)} %convert_element_type.11.refs_0_, ...), custom_call_target="tpu_custom_call" | custom-call | tf_op jit(solution)/shard_map/pallas_call | solution.py:81
  28.4 2.5 %collective-permute-start.15 = (bf16[32,256]{1,0:T(8,128)(2,1)S(1)}, bf16[32,256]{1,0:T(8,128)(2,1)S(1)}, u32[]{:S(2)}, u32[]{:S(2)}) collective-permute-start(bf16[32,256]{1,0:T(8,128)(2,1)S(1)} %get-tuple-element.102), channel_id=1, source_target_pairs={{0,3},{1,2},{2,1},{3,0},{4,7},{5,6},{6,5},{7,4},{8,11},{9,10},{10,... | collective-permute-start | bytes 49160 | tf_op jit(solution)/shard_map/ppermute | solution.py:74
  30.9 0.0 collective-permute-start.16
  30.9 3.0 %collective-permute-done.15.refs_1_ = bf16[32,256]{1,0:T(8,128)(2,1)S(1)} collective-permute-done((bf16[32,256]{1,0:T(8,128)(2,1)S(1)}, bf16[32,256]{1,0:T(8,128)(2,1)S(1)}, u32[]{:S(2)}, u32[]{:S(2)}) %collective-permute-start.15) | collective-permute-done | bytes 16416 | tf_op jit(solution)/shard_map/ppermute | solution.py:74
  33.9 1.6 %collective-permute-done.16.refs_2_ = bf16[32,256]{1,0:T(8,128)(2,1)S(1)} collective-permute-done((bf16[32,256]{1,0:T(8,128)(2,1)S(1)}, bf16[32,256]{1,0:T(8,128)(2,1)S(1)}, u32[]{:S(2)}, u32[]{:S(2)}) %collective-permute-start.16) | collective-permute-done | bytes 16416 | tf_op jit(solution)/shard_map/ppermute | solution.py:74
  35.5 2.2 %collective-permute-done.17.refs_3_ = bf16[32,256]{1,0:T(8,128)(2,1)S(1)} collective-permute-done((bf16[32,256]{1,0:T(8,128)(2,1)S(1)}, bf16[32,256]{1,0:T(8,128)(2,1)S(1)}, u32[]{:S(2)}, u32[]{:S(2)}) %collective-permute-start.17) | collective-permute-done | bytes 16416 | tf_op jit(solution)/shard_map/ppermute | solution.py:74
  37.7 0.7 %shard_map.50 = (bf16[64,128]{1,0:T(8,128)(2,1)S(1)}, bf16[64,128]{1,0:T(8,128)(2,1)S(1)}, bf16[64,128]{1,0:T(8,128)(2,1)S(1)}, bf16[64,128]{1,0:T(8,128)(2,1)S(1)}) custom-call(s32[2]{0:T(128)S(1)} %pad_add_fusion.where_ref, s32[4,6]{1,0:T(4,128)S(1)} %bitcast.18, f32[32,1024]{1,0:T(8,128)S(1)} %copy-done.1, f32[32,128]{1,0:T(8,128)S(1)} %bitcast.14, ...), custom_call_target="tpu_custom_call" | custom-call | tf_op jit(solution)/shard_map/pallas_call | solution.py:81
  38.4 0.1 collective-permute-start.19
  38.5 1.5 %collective-permute-start.21 = (bf16[64,128]{1,0:T(8,128)(2,1)S(1)}, bf16[64,128]{1,0:T(8,128)(2,1)S(1)}, u32[]{:S(2)}, u32[]{:S(2)}) collective-permute-start(bf16[64,128]{1,0:T(8,128)(2,1)S(1)} %get-tuple-element.109), channel_id=1, source_target_pairs={{0,8},{4,12},{8,0},{12,4},{1,9},{5,13},{9,1},{13,5},{2,10},{6,14},... | collective-permute-start | bytes 49160 | tf_op jit(solution)/shard_map/ppermute | solution.py:74
  40.0 0.9 %collective-permute-start.23 = (bf16[64,128]{1,0:T(8,128)(2,1)S(1)}, bf16[64,128]{1,0:T(8,128)(2,1)S(1)}, u32[]{:S(2)}, u32[]{:S(2)}) collective-permute-start(bf16[64,128]{1,0:T(8,128)(2,1)S(1)} %get-tuple-element.111), channel_id=1, source_target_pairs={{0,12},{4,8},{8,4},{12,0},{1,13},{5,9},{9,5},{13,1},{2,14},{6,10},... | collective-permute-start | bytes 49160 | tf_op jit(solution)/shard_map/ppermute | solution.py:74
  40.9 1.2 %shard_map.47 = s32[1]{0:T(128)} custom-call(s32[4,6]{1,0:T(4,128)S(1)} %bitcast.19, bf16[528,128]{1,0:T(8,128)(2,1)S(1)} %collective-permute-done.9.refs_0_, bf16[528,128]{1,0:T(8,128)(2,1)S(1)} %collective-permute-done.10.refs_1_, bf16[528,128]{1,0:T(8,128)(2,1)S(1)} %collective-permute-done.11.refs_2_), custom_call_target="tpu_custom_call" | custom-call | tf_op jit(solution)/shard_map/pallas_call | solution.py:81
  42.7 0.4 collective-permute-done.23
  43.2 0.1 conditional.1
  43.2 0.1 branch_0_fun.1
  43.3 0.1 collective-permute-start.26
  43.3 3.0 %collective-permute-start.25 = (bf16[400,128]{1,0:T(8,128)(2,1)S(1)}, bf16[400,128]{1,0:T(8,128)(2,1)S(1)}, u32[]{:S(2)}, u32[]{:S(2)}) collective-permute-start(bf16[400,128]{1,0:T(8,128)(2,1)S(1)} %get-tuple-element.112.refs_0_), channel_id=1, source_target_pairs={{0,2},{1,3},{2,0},{3,1},{4,6},{5,7},{6,4},{7,5},{8,10},{9,11},{10,... | collective-permute-start | bytes 307208 | tf_op jit(solution)/shard_map/ppermute | solution.py:74
  46.4 1.3 %collective-permute-start.24 = (bf16[400,128]{1,0:T(8,128)(2,1)S(1)}, bf16[400,128]{1,0:T(8,128)(2,1)S(1)}, u32[]{:S(2)}, u32[]{:S(2)}) collective-permute-start(bf16[400,128]{1,0:T(8,128)(2,1)S(1)} %get-tuple-element.112.refs_0_), channel_id=1, source_target_pairs={{0,3},{1,2},{2,1},{3,0},{4,7},{5,6},{6,5},{7,4},{8,11},{9,10},{10,... | collective-permute-start | bytes 307208 | tf_op jit(solution)/shard_map/ppermute | solution.py:74
  47.7 2.2 %collective-permute-done.26.refs_3_ = bf16[400,128]{1,0:T(8,128)(2,1)S(1)} collective-permute-done((bf16[400,128]{1,0:T(8,128)(2,1)S(1)}, bf16[400,128]{1,0:T(8,128)(2,1)S(1)}, u32[]{:S(2)}, u32[]{:S(2)}) %collective-permute-start.26) | collective-permute-done | bytes 102432 | tf_op jit(solution)/shard_map/ppermute | solution.py:74
  49.9 4.6 %collective-permute-done.25.refs_2_ = bf16[400,128]{1,0:T(8,128)(2,1)S(1)} collective-permute-done((bf16[400,128]{1,0:T(8,128)(2,1)S(1)}, bf16[400,128]{1,0:T(8,128)(2,1)S(1)}, u32[]{:S(2)}, u32[]{:S(2)}) %collective-permute-start.25) | collective-permute-done | bytes 102432 | tf_op jit(solution)/shard_map/ppermute | solution.py:74
  54.5 0.1 shard_map.51.refs_0_
  54.6 2.1 %collective-permute-start.32 = (bf16[400,128]{1,0:T(8,128)(2,1)S(1)}, bf16[400,128]{1,0:T(8,128)(2,1)S(1)}, u32[]{:S(2)}, u32[]{:S(2)}) collective-permute-start(bf16[400,128]{1,0:T(8,128)(2,1)S(1)} %shard_map.51.refs_0_), channel_id=1, source_target_pairs={{0,24},{4,28},{8,16},{12,20},{16,8},{20,12},{24,0},{28,4},{1,25},{... | collective-permute-start | bytes 307208 | tf_op jit(solution)/shard_map/ppermute | solution.py:74
  56.7 0.5 collective-permute-start.30
  57.2 0.9 %collective-permute-start.28 = (bf16[400,128]{1,0:T(8,128)(2,1)S(1)}, bf16[400,128]{1,0:T(8,128)(2,1)S(1)}, u32[]{:S(2)}, u32[]{:S(2)}) collective-permute-start(bf16[400,128]{1,0:T(8,128)(2,1)S(1)} %shard_map.51.refs_0_), channel_id=1, source_target_pairs={{0,8},{4,12},{8,0},{12,4},{16,24},{20,28},{24,16},{28,20},{1,9},{5... | collective-permute-start | bytes 307208 | tf_op jit(solution)/shard_map/ppermute | solution.py:74
  58.2 2.1 %collective-permute-done.32.refs_6_ = bf16[400,128]{1,0:T(8,128)(2,1)S(1)} collective-permute-done((bf16[400,128]{1,0:T(8,128)(2,1)S(1)}, bf16[400,128]{1,0:T(8,128)(2,1)S(1)}, u32[]{:S(2)}, u32[]{:S(2)}) %collective-permute-start.32) | collective-permute-done | bytes 102432 | tf_op jit(solution)/shard_map/ppermute | solution.py:74
  60.2 1.1 %collective-permute-done.30.refs_4_ = bf16[400,128]{1,0:T(8,128)(2,1)S(1)} collective-permute-done((bf16[400,128]{1,0:T(8,128)(2,1)S(1)}, bf16[400,128]{1,0:T(8,128)(2,1)S(1)}, u32[]{:S(2)}, u32[]{:S(2)}) %collective-permute-start.30) | collective-permute-done | bytes 102432 | tf_op jit(solution)/shard_map/ppermute | solution.py:74
  61.4 0.5 collective-permute-done.28.refs_2_
  61.9 0.8 %collective-permute-done.31.refs_5_ = bf16[400,128]{1,0:T(8,128)(2,1)S(1)} collective-permute-done((bf16[400,128]{1,0:T(8,128)(2,1)S(1)}, bf16[400,128]{1,0:T(8,128)(2,1)S(1)}, u32[]{:S(2)}, u32[]{:S(2)}) %collective-permute-start.31) | collective-permute-done | bytes 102432 | tf_op jit(solution)/shard_map/ppermute | solution.py:74
  62.7 0.5 collective-permute-done.29.refs_3_
  63.2 3.5 %shard_map.52 = f32[32,128]{1,0:T(8,128)} custom-call(s32[2]{0:T(128)S(1)} %pad_add_fusion.where_ref, s32[4,6]{1,0:T(4,128)S(1)} %bitcast.21, bf16[400,128]{1,0:T(8,128)(2,1)S(1)} %shard_map.51.refs_0_, bf16[400,128]{1,0:T(8,128)(2,1)S(1)} %collective-permute-done.27.refs_1_, bf16[400,128]{1,0:T(8,128)(2,1)S(1)} %collective-permute-done.28.refs_2_, ...), custom_call_target="tpu_custom_call" | custom-call | tf_op jit(solution)/shard_map/pallas_call | solution.py:81
  (21 shorter events, 0.1 us)
Async XLA Ops:
  0.0 18.1 %copy-start = (bf16[1,1024,512]{2,1,0:T(8,128)(2,1)S(1)}, bf16[1,1024,512]{2,1,0:T(8,128)(2,1)}, u32[]{:S(2)}) copy-start(bf16[1,1024,512]{2,1,0:T(8,128)(2,1)} %param.6) | copy-start | bytes 3145732
  1.5 16.6 %copy-start.3 = (s32[6,4]{0,1:T(4,128)S(1)}, s32[6,4]{0,1:T(4,128)}, u32[]{:S(2)}) copy-start(s32[6,4]{0,1:T(4,128)} %param.9) | copy-start | bytes 292
  1.5 9.7 %collective-permute-start.9 = (bf16[528,128]{1,0:T(8,128)(2,1)S(1)}, bf16[528,128]{1,0:T(8,128)(2,1)S(1)}, u32[]{:S(2)}, u32[]{:S(2)}) collective-permute-start(bf16[528,128]{1,0:T(8,128)(2,1)S(1)} %get-tuple-element.96), channel_id=1, source_target_pairs={{0,3},{1,2},{2,1},{3,0},{4,7},{5,6},{6,5},{7,4},{8,11},{9,10},{10,... | collective-permute-start | bytes 405512 | tf_op jit(solution)/shard_map/ppermute | solution.py:74
  6.6 11.4 %collective-permute-start.10 = (bf16[528,128]{1,0:T(8,128)(2,1)S(1)}, bf16[528,128]{1,0:T(8,128)(2,1)S(1)}, u32[]{:S(2)}, u32[]{:S(2)}) collective-permute-start(bf16[528,128]{1,0:T(8,128)(2,1)S(1)} %get-tuple-element.97), channel_id=1, source_target_pairs={{0,2},{1,3},{2,0},{3,1},{4,6},{5,7},{6,4},{7,5},{8,10},{9,11},{10,... | collective-permute-start | bytes 405512 | tf_op jit(solution)/shard_map/ppermute | solution.py:74
  6.6 11.4 %collective-permute-start.11 = (bf16[528,128]{1,0:T(8,128)(2,1)S(1)}, bf16[528,128]{1,0:T(8,128)(2,1)S(1)}, u32[]{:S(2)}, u32[]{:S(2)}) collective-permute-start(bf16[528,128]{1,0:T(8,128)(2,1)S(1)} %get-tuple-element.98), channel_id=1, source_target_pairs={{0,1},{1,0},{2,3},{3,2},{4,5},{5,4},{6,7},{7,6},{8,9},{9,8},{10,11... | collective-permute-start | bytes 405512 | tf_op jit(solution)/shard_map/ppermute | solution.py:74
  18.1 3.4 %copy-start.2 = (f32[32,1,1,128]{3,2,1,0:T(1,128)S(1)}, f32[32,1,1,128]{3,2,1,0:T(1,128)}, u32[]{:S(2)}) copy-start(f32[32,1,1,128]{3,2,1,0:T(1,128)} %param.8) | copy-start | bytes 49156
  19.6 23.6 %collective-permute-start.18 = (bf16[336,128]{1,0:T(8,128)(2,1)S(1)}, bf16[336,128]{1,0:T(8,128)(2,1)S(1)}, u32[]{:S(2)}, u32[]{:S(2)}) collective-permute-start(bf16[336,128]{1,0:T(8,128)(2,1)S(1)} %get-tuple-element.106), channel_id=1, source_target_pairs={{0,4},{4,0},{8,12},{12,8},{1,5},{5,1},{9,13},{13,9},{2,6},{6,2},{1... | collective-permute-start | bytes 258056 | tf_op jit(solution)/shard_map/ppermute | solution.py:74
  19.6 23.5 %collective-permute-start.20 = (bf16[336,128]{1,0:T(8,128)(2,1)S(1)}, bf16[336,128]{1,0:T(8,128)(2,1)S(1)}, u32[]{:S(2)}, u32[]{:S(2)}) collective-permute-start(bf16[336,128]{1,0:T(8,128)(2,1)S(1)} %get-tuple-element.108), channel_id=1, source_target_pairs={{0,8},{4,12},{8,0},{12,4},{1,9},{5,13},{9,1},{13,5},{2,10},{6,14},... | collective-permute-start | bytes 258056 | tf_op jit(solution)/shard_map/ppermute | solution.py:74
  21.2 21.9 %collective-permute-start.22 = (bf16[336,128]{1,0:T(8,128)(2,1)S(1)}, bf16[336,128]{1,0:T(8,128)(2,1)S(1)}, u32[]{:S(2)}, u32[]{:S(2)}) collective-permute-start(bf16[336,128]{1,0:T(8,128)(2,1)S(1)} %get-tuple-element.110), channel_id=1, source_target_pairs={{0,12},{4,8},{8,4},{12,0},{1,13},{5,9},{9,5},{13,1},{2,14},{6,10},... | collective-permute-start | bytes 258056 | tf_op jit(solution)/shard_map/ppermute | solution.py:74
  21.5 16.2 %copy-start.1 = (f32[32,1024]{1,0:T(8,128)S(1)}, f32[32,1024]{1,0:T(8,128)}, u32[]{:S(2)}) copy-start(f32[32,1024]{1,0:T(8,128)} %y_ref.3) | copy-start | bytes 393220
  21.5 4.7 %collective-permute-start.14 = (bf16[32,128]{1,0:T(8,128)(2,1)S(1)}, bf16[32,128]{1,0:T(8,128)(2,1)S(1)}, u32[]{:S(2)}, u32[]{:S(2)}) collective-permute-start(bf16[32,128]{1,0:T(8,128)(2,1)S(1)} %convert_element_type.11.refs_0_), channel_id=1, source_target_pairs={{0,12},{4,8},{8,4},{12,0},{1,13},{5,9},{9,5},{13,1},{2,14},{6,10},... | collective-permute-start | bytes 24584 | tf_op jit(solution)/shard_map/ppermute | solution.py:74
  23.1 3.7 %collective-permute-start.13 = (bf16[32,128]{1,0:T(8,128)(2,1)S(1)}, bf16[32,128]{1,0:T(8,128)(2,1)S(1)}, u32[]{:S(2)}, u32[]{:S(2)}) collective-permute-start(bf16[32,128]{1,0:T(8,128)(2,1)S(1)} %convert_element_type.11.refs_0_), channel_id=1, source_target_pairs={{0,8},{4,12},{8,0},{12,4},{1,9},{5,13},{9,1},{13,5},{2,10},{6,14},... | collective-permute-start | bytes 24584 | tf_op jit(solution)/shard_map/ppermute | solution.py:74
  26.2 1.2 %collective-permute-start.12 = (bf16[32,128]{1,0:T(8,128)(2,1)S(1)}, bf16[32,128]{1,0:T(8,128)(2,1)S(1)}, u32[]{:S(2)}, u32[]{:S(2)}) collective-permute-start(bf16[32,128]{1,0:T(8,128)(2,1)S(1)} %convert_element_type.11.refs_0_), channel_id=1, source_target_pairs={{0,4},{4,0},{8,12},{12,8},{1,5},{5,1},{9,13},{13,9},{2,6},{6,2},{1... | collective-permute-start | bytes 24584 | tf_op jit(solution)/shard_map/ppermute | solution.py:74
  28.4 5.6 %collective-permute-start.15 = (bf16[32,256]{1,0:T(8,128)(2,1)S(1)}, bf16[32,256]{1,0:T(8,128)(2,1)S(1)}, u32[]{:S(2)}, u32[]{:S(2)}) collective-permute-start(bf16[32,256]{1,0:T(8,128)(2,1)S(1)} %get-tuple-element.102), channel_id=1, source_target_pairs={{0,3},{1,2},{2,1},{3,0},{4,7},{5,6},{6,5},{7,4},{8,11},{9,10},{10,... | collective-permute-start | bytes 49160 | tf_op jit(solution)/shard_map/ppermute | solution.py:74
  30.9 4.6 %collective-permute-start.16 = (bf16[32,256]{1,0:T(8,128)(2,1)S(1)}, bf16[32,256]{1,0:T(8,128)(2,1)S(1)}, u32[]{:S(2)}, u32[]{:S(2)}) collective-permute-start(bf16[32,256]{1,0:T(8,128)(2,1)S(1)} %get-tuple-element.103), channel_id=1, source_target_pairs={{0,2},{1,3},{2,0},{3,1},{4,6},{5,7},{6,4},{7,5},{8,10},{9,11},{10,... | collective-permute-start | bytes 49160 | tf_op jit(solution)/shard_map/ppermute | solution.py:74
  33.9 3.7 %collective-permute-start.17 = (bf16[32,256]{1,0:T(8,128)(2,1)S(1)}, bf16[32,256]{1,0:T(8,128)(2,1)S(1)}, u32[]{:S(2)}, u32[]{:S(2)}) collective-permute-start(bf16[32,256]{1,0:T(8,128)(2,1)S(1)} %get-tuple-element.104), channel_id=1, source_target_pairs={{0,1},{1,0},{2,3},{3,2},{4,5},{5,4},{6,7},{7,6},{8,9},{9,8},{10,11... | collective-permute-start | bytes 49160 | tf_op jit(solution)/shard_map/ppermute | solution.py:74
  38.4 1.6 %collective-permute-start.19 = (bf16[64,128]{1,0:T(8,128)(2,1)S(1)}, bf16[64,128]{1,0:T(8,128)(2,1)S(1)}, u32[]{:S(2)}, u32[]{:S(2)}) collective-permute-start(bf16[64,128]{1,0:T(8,128)(2,1)S(1)} %get-tuple-element.107), channel_id=1, source_target_pairs={{0,4},{4,0},{8,12},{12,8},{1,5},{5,1},{9,13},{13,9},{2,6},{6,2},{1... | collective-permute-start | bytes 49160 | tf_op jit(solution)/shard_map/ppermute | solution.py:74
  38.5 4.3 %collective-permute-start.21 = (bf16[64,128]{1,0:T(8,128)(2,1)S(1)}, bf16[64,128]{1,0:T(8,128)(2,1)S(1)}, u32[]{:S(2)}, u32[]{:S(2)}) collective-permute-start(bf16[64,128]{1,0:T(8,128)(2,1)S(1)} %get-tuple-element.109), channel_id=1, source_target_pairs={{0,8},{4,12},{8,0},{12,4},{1,9},{5,13},{9,1},{13,5},{2,10},{6,14},... | collective-permute-start | bytes 49160 | tf_op jit(solution)/shard_map/ppermute | solution.py:74
  40.0 3.2 %collective-permute-start.23 = (bf16[64,128]{1,0:T(8,128)(2,1)S(1)}, bf16[64,128]{1,0:T(8,128)(2,1)S(1)}, u32[]{:S(2)}, u32[]{:S(2)}) collective-permute-start(bf16[64,128]{1,0:T(8,128)(2,1)S(1)} %get-tuple-element.111), channel_id=1, source_target_pairs={{0,12},{4,8},{8,4},{12,0},{1,13},{5,9},{9,5},{13,1},{2,14},{6,10},... | collective-permute-start | bytes 49160 | tf_op jit(solution)/shard_map/ppermute | solution.py:74
  43.3 6.7 %collective-permute-start.26 = (bf16[400,128]{1,0:T(8,128)(2,1)S(1)}, bf16[400,128]{1,0:T(8,128)(2,1)S(1)}, u32[]{:S(2)}, u32[]{:S(2)}) collective-permute-start(bf16[400,128]{1,0:T(8,128)(2,1)S(1)} %get-tuple-element.112.refs_0_), channel_id=1, source_target_pairs={{0,1},{1,0},{2,3},{3,2},{4,5},{5,4},{6,7},{7,6},{8,9},{9,8},{10,11... | collective-permute-start | bytes 307208 | tf_op jit(solution)/shard_map/ppermute | solution.py:74
  43.3 11.2 %collective-permute-start.25 = (bf16[400,128]{1,0:T(8,128)(2,1)S(1)}, bf16[400,128]{1,0:T(8,128)(2,1)S(1)}, u32[]{:S(2)}, u32[]{:S(2)}) collective-permute-start(bf16[400,128]{1,0:T(8,128)(2,1)S(1)} %get-tuple-element.112.refs_0_), channel_id=1, source_target_pairs={{0,2},{1,3},{2,0},{3,1},{4,6},{5,7},{6,4},{7,5},{8,10},{9,11},{10,... | collective-permute-start | bytes 307208 | tf_op jit(solution)/shard_map/ppermute | solution.py:74
  46.4 8.2 %collective-permute-start.24 = (bf16[400,128]{1,0:T(8,128)(2,1)S(1)}, bf16[400,128]{1,0:T(8,128)(2,1)S(1)}, u32[]{:S(2)}, u32[]{:S(2)}) collective-permute-start(bf16[400,128]{1,0:T(8,128)(2,1)S(1)} %get-tuple-element.112.refs_0_), channel_id=1, source_target_pairs={{0,3},{1,2},{2,1},{3,0},{4,7},{5,6},{6,5},{7,4},{8,11},{9,10},{10,... | collective-permute-start | bytes 307208 | tf_op jit(solution)/shard_map/ppermute | solution.py:74
  54.6 5.6 %collective-permute-start.32 = (bf16[400,128]{1,0:T(8,128)(2,1)S(1)}, bf16[400,128]{1,0:T(8,128)(2,1)S(1)}, u32[]{:S(2)}, u32[]{:S(2)}) collective-permute-start(bf16[400,128]{1,0:T(8,128)(2,1)S(1)} %shard_map.51.refs_0_), channel_id=1, source_target_pairs={{0,24},{4,28},{8,16},{12,20},{16,8},{20,12},{24,0},{28,4},{1,25},{... | collective-permute-start | bytes 307208 | tf_op jit(solution)/shard_map/ppermute | solution.py:74
  56.7 4.7 %collective-permute-start.30 = (bf16[400,128]{1,0:T(8,128)(2,1)S(1)}, bf16[400,128]{1,0:T(8,128)(2,1)S(1)}, u32[]{:S(2)}, u32[]{:S(2)}) collective-permute-start(bf16[400,128]{1,0:T(8,128)(2,1)S(1)} %shard_map.51.refs_0_), channel_id=1, source_target_pairs={{0,16},{4,20},{8,24},{12,28},{16,0},{20,4},{24,8},{28,12},{1,17},{... | collective-permute-start | bytes 307208 | tf_op jit(solution)/shard_map/ppermute | solution.py:74
  57.2 4.7 %collective-permute-start.28 = (bf16[400,128]{1,0:T(8,128)(2,1)S(1)}, bf16[400,128]{1,0:T(8,128)(2,1)S(1)}, u32[]{:S(2)}, u32[]{:S(2)}) collective-permute-start(bf16[400,128]{1,0:T(8,128)(2,1)S(1)} %shard_map.51.refs_0_), channel_id=1, source_target_pairs={{0,8},{4,12},{8,0},{12,4},{16,24},{20,28},{24,16},{28,20},{1,9},{5... | collective-permute-start | bytes 307208 | tf_op jit(solution)/shard_map/ppermute | solution.py:74
  58.2 3.7 %collective-permute-start.27 = (bf16[400,128]{1,0:T(8,128)(2,1)S(1)}, bf16[400,128]{1,0:T(8,128)(2,1)S(1)}, u32[]{:S(2)}, u32[]{:S(2)}) collective-permute-start(bf16[400,128]{1,0:T(8,128)(2,1)S(1)} %shard_map.51.refs_0_), channel_id=1, source_target_pairs={{0,4},{4,0},{8,12},{12,8},{16,20},{20,16},{24,28},{28,24},{1,5},{5... | collective-permute-start | bytes 307208 | tf_op jit(solution)/shard_map/ppermute | solution.py:74
  60.2 1.7 %collective-permute-start.33 = (bf16[400,128]{1,0:T(8,128)(2,1)S(1)}, bf16[400,128]{1,0:T(8,128)(2,1)S(1)}, u32[]{:S(2)}, u32[]{:S(2)}) collective-permute-start(bf16[400,128]{1,0:T(8,128)(2,1)S(1)} %collective-permute-done.32.refs_6_), channel_id=1, source_target_pairs={{0,4},{4,0},{8,12},{12,8},{16,20},{20,16},{24,28},{28,24},{1,5},{5... | collective-permute-start | bytes 307208 | tf_op jit(solution)/shard_map/ppermute | solution.py:74
  61.4 1.3 %collective-permute-start.31 = (bf16[400,128]{1,0:T(8,128)(2,1)S(1)}, bf16[400,128]{1,0:T(8,128)(2,1)S(1)}, u32[]{:S(2)}, u32[]{:S(2)}) collective-permute-start(bf16[400,128]{1,0:T(8,128)(2,1)S(1)} %collective-permute-done.30.refs_4_), channel_id=1, source_target_pairs={{0,4},{4,0},{8,12},{12,8},{16,20},{20,16},{24,28},{28,24},{1,5},{5... | collective-permute-start | bytes 307208 | tf_op jit(solution)/shard_map/ppermute | solution.py:74
  61.9 1.3 %collective-permute-start.29 = (bf16[400,128]{1,0:T(8,128)(2,1)S(1)}, bf16[400,128]{1,0:T(8,128)(2,1)S(1)}, u32[]{:S(2)}, u32[]{:S(2)}) collective-permute-start(bf16[400,128]{1,0:T(8,128)(2,1)S(1)} %collective-permute-done.28.refs_2_), channel_id=1, source_target_pairs={{0,4},{4,0},{8,12},{12,8},{16,20},{20,16},{24,28},{28,24},{1,5},{5... | collective-permute-start | bytes 307208 | tf_op jit(solution)/shard_map/ppermute | solution.py:74

commit v6 on v5

--- a/solution.py
+++ b/solution.py
@@ -74,10 +74,36 @@
     return lax.ppermute(value, axis, [(i, i ^ offset) for i in range(size)])
 
 
-def call(body, out_shape, args, scratch=(), smem=(), hbm=(), out_space=pltpu.VMEM):
-    places = [pltpu.SMEM if i in smem else pl.ANY if i in hbm else pltpu.VMEM for i in range(len(args))]
+def routes(size):
+    if size == 4:
+        return [(1, 3, 0, 2), (3, 2, 1, 0), (2, 0, 3, 1)]
+    return [tuple(i ^ d for i in range(size)) for d in range(1, size)]
+
+
+def send(pieces):
+    got = []
+    for piece, route in zip(pieces, routes(lax.axis_size("pix"))):
+        got.append(lax.ppermute(piece, "pix", list(enumerate(route))))
+    return got
+
+
+def target(pix, k, size):
+    if k == 0:
+        return pix
+    place = jnp.int32(0)
+    for i, to in enumerate(routes(size)[k - 1]):
+        place = jnp.where(pix == i, to, place)
+    return place
+
+
+def call(body, out_shape, args, scratch=(), smem=(), scalars=()):
+    places = [pltpu.SMEM if i in smem else pltpu.VMEM for i in range(len(args))]
     specs = [pl.BlockSpec(memory_space=place) for place in places]
-    out_specs = jax.tree.map(lambda _: pl.BlockSpec(memory_space=out_space), out_shape)
+    place = lambda i: pltpu.SMEM if i in scalars else pltpu.VMEM
+    if isinstance(out_shape, list):
+        out_specs = [pl.BlockSpec(memory_space=place(i)) for i in range(len(out_shape))]
+    else:
+        out_specs = pl.BlockSpec(memory_space=place(0))
     return pl.pallas_call(
         body,
         out_shape=out_shape,
@@ -120,7 +146,7 @@
         notes = jnp.where(rows == i, slot, notes)
         lanes = pl.ds(pl.multiple_of(tile * TILE, TILE), TILE)
         for d, out in enumerate(outs):
-            at = pl.ds(pl.multiple_of((pix ^ (d + 1)) * quarter, quarter), quarter)
+            at = pl.ds(pl.multiple_of(target(pix, d + 1, len(outs) + 1) * quarter, quarter), quarter)
             out[i * quarter : (i + 1) * quarter, :] = a_ref[at, lanes]
     for out in outs:
         out[places * quarter :, :] = notes.astype(jnp.float32).astype(jnp.bfloat16)
@@ -147,7 +173,7 @@
     for d, share in enumerate(shares):
         x_ref[:, pl.ds(pl.multiple_of((base ^ d) * TILE, TILE), TILE)] = share[...]
     for d, out in enumerate(outs):
-        rows = pl.ds(pl.multiple_of((pix ^ d) * quarter, quarter), quarter)
+        rows = pl.ds(pl.multiple_of(target(pix, d, len(outs)) * quarter, quarter), quarter)
         piece = lax.dot_general(
             x_ref[...], a_ref[rows, :], (((1,), (1,)), ((), ())), preferred_element_type=jnp.float32
         )
@@ -180,8 +206,8 @@
 def gram_body(slots, n_parts, where_ref, ranks_ref, y_ref, a_ref, *refs):
     pix, base = where_ref[0], where_ref[1]
     parts = refs[:n_parts]
-    cols_ref, *outs, all_ref = refs[n_parts:]
-    n_base = len(outs)
+    cols_ref, own_ref, sent_ref, all_ref = refs[n_parts:]
+    n_base = all_ref.shape[0]
     chans, quarter = y_ref.shape[0], cols_ref.shape[0]
     table, _ = kept_tiles(ranks_ref, slots)
     own_rows = pl.ds(pl.multiple_of(pix * quarter, quarter), quarter)
@@ -227,8 +253,14 @@
         wide = jnp.concatenate(split(data[:, r * TILE : (r + 1) * TILE]), axis=0)
         all_ref[r // per, at : at + 2 * chans, :] = wide
         all_ref[r // per, at + 2 * chans : at + 2 * chans + PAD, :] = tail_of(diag)
-    for d, out in enumerate(outs):
-        out[...] = all_ref[base ^ d]
+    by_core(base, all_ref, own_ref, sent_ref)
+
+
+def by_core(base, all_ref, own_ref, sent_ref):
+    size = all_ref.shape[1]
+    for k in range(all_ref.shape[0] // 2):
+        own_ref[k * size : (k + 1) * size, :] = all_ref[base ^ (2 * k)]
+        sent_ref[k * size : (k + 1) * size, :] = all_ref[base ^ (2 * k + 1)]
 
 
 def tail_of(row):
@@ -238,8 +270,8 @@
 def start_body(slots, n_pix, where_ref, ranks_ref, y_ref, x0_ref, cols_ref, *refs):
     pix, base = where_ref[0], where_ref[1]
     preds = refs[:n_pix]
-    *outs, all_ref = refs[n_pix:]
-    per = slots // len(outs)
+    own_ref, sent_ref, all_ref = refs[n_pix:]
+    per = slots // all_ref.shape[0]
     chans, quarter = preds[0].shape
     pred = preds[0][...].astype(jnp.float32)
     for piece in preds[1:]:
@@ -252,52 +284,68 @@
         start = moved[:, r * TILE : (r + 1) * TILE] + jnp.where(rank == r, x0_ref[...], 0.0)
         at = (r % per) * 2 * chans
         all_ref[r // per, at : at + 2 * chans, :] = jnp.concatenate(split(start), axis=0)
-    for d, out in enumerate(outs):
-        out[...] = all_ref[base ^ d]
-
-
-def sections(g_rows, chans, per):
-    first = [(g_rows, 0)] + [(2 * chans, chans), (PAD, 1)] * per
-    return first, [(2 * chans, chans)] * per
-
-
-def sum_body(layouts, *refs):
+    by_core(base, all_ref, own_ref, sent_ref)
+
+
+def summed(parts, at, size, pair):
+    value = parts[0][at : at + size].astype(jnp.float32)
+    for part in parts[1:]:
+        value = value + part[at : at + size].astype(jnp.float32)
+    if pair == 0:
+        return value.astype(jnp.bfloat16)
+    if pair == 1:
+        return tail_of(value[0:1] + value[1:2])
+    return jnp.concatenate(split(value[:pair] + value[pair:]), axis=0)
+
+
+def core_body(layout, own_ref, got_ref, *outs):
+    at = 0
+    for out in outs:
+        to = 0
+        for size, pair in layout:
+            out[to : to + size] = summed([own_ref, got_ref], at, size, pair)
+            at += size
+            to += size
+
+
+def join_body(layouts, *refs):
     *parts, out = refs
-    groups = [parts[i :: len(layouts)] for i in range(len(layouts))]
     to = 0
-    for group, layout in zip(groups, layouts):
+    for i, layout in enumerate(layouts):
         at = 0
         for size, pair in layout:
-            value = group[0][at : at + size].astype(jnp.float32)
-            for part in group[1:]:
-                value = value + part[at : at + size].astype(jnp.float32)
-            if pair == 0:
-                out[to : to + size] = value.astype(jnp.bfloat16)
-            elif pair == 1:
-                out[to : to + size] = tail_of(value[0:1] + value[1:2])
-            else:
-                out[to : to + size] = jnp.concatenate(split(value[:pair] + value[pair:]), axis=0)
+            out[to : to + size] = summed(parts[i :: len(layouts)], at, size, pair)
             at += size
             to += size
 
 
-def iterate_body(slots, n_base, g_rows, chans, where_ref, ranks_ref, *refs):
+def total_body(layout, *refs):
+    *parts, out, short = refs
+    at = to = 0
+    for size, pair in layout:
+        value = summed(parts, at, size, pair)
+        out[at : at + size] = value
+        kept = pair if pair > 1 else size
+        short[to : to + kept] = value[:kept]
+        at += size
+        to += kept
+
+
+def iterate_body(slots, n_base, where_ref, ranks_ref, *refs):
     base = where_ref[1]
-    per = slots // n_base
-    data_rows = 2 * chans + PAD
-    image_at = g_rows + per * data_rows
-    chunks = [refs[:n_base], refs[n_base : 2 * n_base]]
-    out_ref, gram_ref, last_ref = refs[2 * n_base :]
-    states, datas, diags = [], [], []
+    *chunks, out_ref, gram_ref, last_ref = refs
+    chans = out_ref.shape[0]
     rows, cols = corner()
     n_off = slots * (slots - 1) // 2
+    g_rows = pack_rows(slots, n_base)
+    half = min(TILE, g_rows & -g_rows)
+    states, datas, diags = [], [], []
 
     def put(g, r, s, block):
         gram_ref[g, r * TILE : (r + 1) * TILE, s * TILE : (s + 1) * TILE] = block
 
     for g in range(2):
-        full = in_order([ref[...] for ref in chunks[g]], base)
-        half = min(TILE, g_rows & -g_rows)
+        full = in_order([ref[...] for ref in chunks[g * n_base : (g + 1) * n_base]], base)
         for i, (r, s) in enumerate(pairs(slots)):
             pieces = []
             for q in range(TILE // half):
@@ -312,12 +360,23 @@
                 lower = jnp.where(rows > cols, block, jnp.zeros_like(block))
                 put(g, r, r, upper + upper.T)
                 put(g, s, s, lower + lower.T)
-        sides = [full[r // per][g_rows + (r % per) * data_rows :][:data_rows].astype(jnp.float32) for r in range(slots)]
-        images = [full[r // per][image_at + (r % per) * 2 * chans :][: 2 * chans].astype(jnp.float32) for r in range(slots)]
-        datas.append(jnp.concatenate([v[:chans] + v[chans : 2 * chans] for v in sides], axis=1))
-        states.append(jnp.concatenate([v[:chans] + v[chans:] for v in images], axis=1))
-        tails = [v[2 * chans :] for v in sides]
-        diags.append(jnp.concatenate([t[0:1] + t[1:2] for t in tails], axis=1))
+        per = slots // n_base
+        wide = (full[0].shape[0] - g_rows - per * PAD) // (2 * per)
+
+        def gather(at, pitch):
+            values = []
+            for r in range(slots):
+                v = full[r // per][at + (r % per) * pitch :][:wide].astype(jnp.float32)
+                values.append(v[:chans] + v[chans:] if wide > chans else v)
+            return jnp.concatenate(values, axis=1)
+
+        datas.append(gather(g_rows, wide + PAD))
+        states.append(gather(g_rows + per * (wide + PAD), wide))
+        tails = []
+        for r in range(slots):
+            v = full[r // per][g_rows + (r % per) * (wide + PAD) + wide :][:PAD].astype(jnp.float32)
+            tails.append(v[0:1] + v[1:2])
+        diags.append(jnp.concatenate(tails, axis=1))
     for step in range(ITERS):
         factors = []
         for r in range(slots):
@@ -333,10 +392,11 @@
             break
         for g in range(2):
             high, low = split(states[g])
-            both = jnp.dot(
-                jnp.concatenate([high, low], axis=0), gram_ref[g], preferred_element_type=jnp.float32
-            )
-            product = both[:chans] + both[chans:] + states[g] * diags[g]
+            left = jnp.concatenate([high, low], axis=0) if g == 0 else high
+            product = jnp.dot(left, gram_ref[g], preferred_element_type=jnp.float32)
+            if g == 0:
+                product = product[:chans] + product[chans:]
+            product = product + states[g] * diags[g]
             states[g] = states[g] + descent_stride * (datas[g] - product)
     for r in range(slots):
         last_ref[r] = states[0][:, r * TILE : (r + 1) * TILE]
@@ -364,7 +424,7 @@
             (where, ranks, a),
             smem=(0, 1),
         )
-        return [swap(packed[d - 1], "pix", d) for d in range(n_pix - 1, 0, -1)]
+        return send(packed)
 
     places = min(CAPACITY, ranks.shape[0])
     parts = exchange(0, places)
@@ -377,60 +437,70 @@
         scratch=[pltpu.VMEM((chans, n_base * TILE), bf16)],
         smem=(0,),
     )
-    preds = [firsts[0]] + [swap(firsts[d], "pix", d) for d in range(n_pix - 1, 0, -1)]
-
-    g_rows = pack_rows(slots, n_base)
+    preds = [firsts[0]] + send(firsts[1:])
+
     per = slots // n_base
-    layouts = sections(g_rows, chans, per)
-    gram_chunk, image_chunk = [shape((sum(size for size, _ in layout), TILE), bf16) for layout in layouts]
-    chunk = shape((gram_chunk.shape[0] + image_chunk.shape[0], TILE), bf16)
-
-    def spread(parts):
-        columns, *grams = call(
+    gram_layout = [(pack_rows(slots, n_base), 0)] + [(2 * chans, chans), (PAD, 1)] * per
+    side_layout = [(2 * chans, chans)] * per
+    layouts = [gram_layout, side_layout]
+    heights = [sum(size for size, _ in layout) for layout in layouts]
+    chunk = shape((sum(heights), TILE), bf16)
+    short = shape((chunk.shape[0] - 2 * chans * per, TILE), bf16)
+
+    def halves(height):
+        return [shape((n_base // 2 * height, TILE), bf16)] * 2
+
+    def base_sum(parts):
+        columns, *gram = call(
             functools.partial(gram_body, slots, len(parts)),
-            [shape((quarter, slots * TILE), bf16)] + [gram_chunk] * n_base,
+            [shape((quarter, slots * TILE), bf16)] + halves(heights[0]),
             (where, ranks, sampled_correlations, a, *parts),
-            scratch=[pltpu.VMEM((n_base, *gram_chunk.shape), bf16)],
+            scratch=[pltpu.VMEM((n_base, heights[0], TILE), bf16)],
             smem=(0, 1),
         )
-        grams = [grams[0]] + [swap(grams[d], "base", d) for d in range(1, n_base)]
-        images = call(
+        side = call(
             functools.partial(start_body, slots, n_pix),
-            [image_chunk] * n_base,
+            halves(heights[1]),
             (where, ranks, sampled_correlations, x0, columns, *preds),
-            scratch=[pltpu.VMEM((n_base, *image_chunk.shape), bf16)],
+            scratch=[pltpu.VMEM((n_base, heights[1], TILE), bf16)],
             smem=(0, 1),
         )
-        images = [images[0]] + [swap(images[d], "base", d) for d in range(1, n_base)]
-        return [piece for pair in zip(grams, images) for piece in pair]
-
-    def add(layouts, pieces):
-        return call(functools.partial(sum_body, layouts), chunk, pieces)
+        pieces = []
+        for (own, sent), layout in zip((gram, side), layouts):
+            height = sum(size for size, _ in layout)
+            sums = call(
+                functools.partial(core_body, layout),
+                [shape((height, TILE), bf16)] * (n_base // 2),
+                (own, swap(sent, "base", 1)),
+            )
+            far = [swap(sums[k], "base", 2 * k) for k in range(1, n_base // 2)]
+            pieces.append([sums[0], *far])
+        return [piece for pair in zip(*pieces) for piece in pair]
+
+    def join(pieces):
+        return call(functools.partial(join_body, layouts), chunk, pieces)
 
     crowded = call(
-        functools.partial(crowd_body, slots, places),
-        shape((1,), jnp.int32),
-        (ranks, *parts),
-        smem=(0,),
-        out_space=pltpu.SMEM,
+        functools.partial(crowd_body, slots, places), shape((1,), jnp.int32), (ranks, *parts), smem=(0,), scalars=(0,)
     )[0]
-    pieces = spread(parts)
+    pieces = base_sum(parts)
     part = lax.cond(
-        crowded != 0,
-        lambda: add(layouts, spread(parts + exchange(places, ranks.shape[0] - places))),
-        lambda: add(layouts, pieces),
-    )
-    total = add([layouts[0] + layouts[1]], [part] + [swap(part, "pix", d) for d in range(n_pix - 1, 0, -1)])
+        crowded != 0, lambda: join(base_sum(parts + exchange(places, ranks.shape[0] - places))), lambda: join(pieces)
+    )
+    total, brief = call(
+        functools.partial(total_body, gram_layout + side_layout), [chunk, short], [part] + send([part] * (n_pix - 1))
+    )
 
     axes = ("freq", "base")
-    got = {0: total}
-    for offset in range(2, 2 * n_base, 2):
+    got = {0: total, n_base: swap(brief, axes, n_base)}
+    for offset in range(2, n_base, 2):
+        got[n_base + offset] = swap(brief, axes, n_base + offset)
         got[offset] = swap(total, axes, offset)
     got[1] = swap(total, axes, 1)
     for offset in range(2, 2 * n_base, 2):
         got[offset + 1] = swap(got[offset], axes, 1)
     image = call(
-        functools.partial(iterate_body, slots, n_base, g_rows, chans),
+        functools.partial(iterate_body, slots, n_base),
         shape((chans, TILE), f32),
         (where, ranks, *[got[i] for i in range(2 * n_base)]),
         scratch=[

time: 66.8 us -> 64.9 us (0.972)
  waiting for transfers between devices: 33.4 us -> 28.8 us
  starting transfers between devices: 23 us -> 25.8 us
    ppermute x25 -> x14, waiting for transfers between devices: 33.4 us -> 10.5 us  [swap(): return lax.ppermute(value, axis, [(i, i ^ offset) for i in range(size)])]
    ppermute x0 -> x9, waiting for transfers between devices: none -> 18.3 us  [send(): got.append(lax.ppermute(piece, 'pix', list(enumerate(route))))]
    ppermute x0 -> x9, starting transfers between devices: none -> 17.2 us  [send(): got.append(lax.ppermute(piece, 'pix', list(enumerate(route))))]
    ppermute x25 -> x14, starting transfers between devices: 23 us -> 8.56 us  [swap(): return lax.ppermute(value, axis, [(i, i ^ offset) for i in range(size)])]
    pallas_call x8 -> x10, Pallas kernels: 9.36 us -> 9.34 us  [call(): pl.pallas_call(body, out_shape=out_shape, in_specs=specs, out_specs=out_s...]
  transfers between devices with their start and end apart: 25 -> 23, of which waited for: 16 -> 19; matrix products, arithmetic and copies ran while one was open for 0% -> 0% of each run, Pallas kernels for 4% -> 4%
where the time goes in v6:
time: 64.9 us; the launch traced here: 64.8 us
  waiting for transfers between devices  28.8 us (44%)
  starting transfers between devices  25.8 us (40%)
  Pallas kernels  9.34 us (14%)
  between operations  0.75 us (1%)
    ppermute x9, waiting for transfers between devices, send(): got.append(lax.ppermute(piece, 'pix', list(enumerate(route))))  18.3 us
    ppermute x9, starting transfers between devices, send(): got.append(lax.ppermute(piece, 'pix', list(enumerate(route))))  17.2 us
    ppermute x14, waiting for transfers between devices, swap(): return lax.ppermute(value, axis, [(i, i ^ offset) for i in range(size)])  10.5 us
    pallas_call x10, Pallas kernels, call(): pl.pallas_call(body, out_shape=out_shape, in_specs=specs, out_specs=out_s...  9.34 us
    ppermute x14, starting transfers between devices, swap(): return lax.ppermute(value, axis, [(i, i ^ offset) for i in range(size)])  8.56 us
  transfers between devices with their start and end apart: 23, of which 19 were waited for; matrix products, arithmetic and copies ran while one was open for 0% of the time, Pallas kernels for 4%

profile of v6, /device:TPU:0, one launch (start us, length us, event | category | flops | bytes accessed | tf_op | source)
XLA Modules:
  0.0 64.8 jit_solution(8917601237134082678)
XLA Ops:
  0.0 0.1 pad_add_fusion.where_ref
  0.1 1.4 %shard_map.46 = (bf16[528,128]{1,0:T(8,128)(2,1)S(1)}, bf16[528,128]{1,0:T(8,128)(2,1)S(1)}, bf16[528,128]{1,0:T(8,128)(2,1)S(1)}) custom-call(s32[2]{0:T(128)S(1)} %pad_add_fusion.where_ref, s32[4,6]{1,0:T(4,128)} %bitcast.16, bf16[1024,512]{1,0:T(8,128)(2,1)} %bitcast.9), custom_call_target="tpu_custom_call" | custom-call | tf_op jit(solution)/shard_map/pallas_call | solution.py:107
  1.5 0.0 copy-start.3
  1.5 3.1 %collective-permute-start.7 = (bf16[528,128]{1,0:T(8,128)(2,1)S(1)}, bf16[528,128]{1,0:T(8,128)(2,1)S(1)}, u32[]{:S(2)}, u32[]{:S(2)}) collective-permute-start(bf16[528,128]{1,0:T(8,128)(2,1)S(1)} %get-tuple-element.86), channel_id=1, source_target_pairs={{0,1},{1,3},{2,0},{3,2},{4,5},{5,7},{6,4},{7,6},{8,9},{9,11},{10,8... | collective-permute-start | bytes 405512 | tf_op jit(solution)/shard_map/ppermute | solution.py:86
  4.6 2.5 %collective-permute-start.8 = (bf16[528,128]{1,0:T(8,128)(2,1)S(1)}, bf16[528,128]{1,0:T(8,128)(2,1)S(1)}, u32[]{:S(2)}, u32[]{:S(2)}) collective-permute-start(bf16[528,128]{1,0:T(8,128)(2,1)S(1)} %get-tuple-element.87), channel_id=1, source_target_pairs={{0,3},{1,2},{2,1},{3,0},{4,7},{5,6},{6,5},{7,4},{8,11},{9,10},{10,... | collective-permute-start | bytes 405512 | tf_op jit(solution)/shard_map/ppermute | solution.py:86
  7.1 1.6 %collective-permute-start.9 = (bf16[528,128]{1,0:T(8,128)(2,1)S(1)}, bf16[528,128]{1,0:T(8,128)(2,1)S(1)}, u32[]{:S(2)}, u32[]{:S(2)}) collective-permute-start(bf16[528,128]{1,0:T(8,128)(2,1)S(1)} %get-tuple-element.88), channel_id=1, source_target_pairs={{0,2},{1,0},{2,3},{3,1},{4,6},{5,4},{6,7},{7,5},{8,10},{9,8},{10,1... | collective-permute-start | bytes 405512 | tf_op jit(solution)/shard_map/ppermute | solution.py:86
  8.7 1.3 %collective-permute-done.7.refs_0_ = bf16[528,128]{1,0:T(8,128)(2,1)S(1)} collective-permute-done((bf16[528,128]{1,0:T(8,128)(2,1)S(1)}, bf16[528,128]{1,0:T(8,128)(2,1)S(1)}, u32[]{:S(2)}, u32[]{:S(2)}) %collective-permute-start.7) | collective-permute-done | bytes 135200 | tf_op jit(solution)/shard_map/ppermute | solution.py:86
  10.0 4.5 %collective-permute-done.8.refs_1_ = bf16[528,128]{1,0:T(8,128)(2,1)S(1)} collective-permute-done((bf16[528,128]{1,0:T(8,128)(2,1)S(1)}, bf16[528,128]{1,0:T(8,128)(2,1)S(1)}, u32[]{:S(2)}, u32[]{:S(2)}) %collective-permute-start.8) | collective-permute-done | bytes 135200 | tf_op jit(solution)/shard_map/ppermute | solution.py:86
  14.5 0.6 collective-permute-done.9.refs_2_
  15.1 1.5 %shard_map.48 = (bf16[256,512]{1,0:T(8,128)(2,1)S(1)}, bf16[672,128]{1,0:T(8,128)(2,1)S(1)}, bf16[672,128]{1,0:T(8,128)(2,1)S(1)}) custom-call(s32[2]{0:T(128)S(1)} %pad_add_fusion.where_ref, s32[4,6]{1,0:T(4,128)S(1)} %bitcast.17, f32[32,1024]{1,0:T(8,128)} %y_ref.3, bf16[1024,512]{1,0:T(8,128)(2,1)S(1)} %bitcast.10, ...), custom_call_target="tpu_custom_call" | custom-call | tf_op jit(solution)/shard_map/pallas_call | solution.py:107
  16.6 0.1 collective-permute-start.10
  16.6 1.4 %collective-permute-done.10.got_ref = bf16[672,128]{1,0:T(8,128)(2,1)S(1)} collective-permute-done((bf16[672,128]{1,0:T(8,128)(2,1)S(1)}, bf16[672,128]{1,0:T(8,128)(2,1)S(1)}, u32[]{:S(2)}, u32[]{:S(2)}) %collective-permute-start.10) | collective-permute-done | bytes 172064 | tf_op jit(solution)/shard_map/ppermute | solution.py:74
  18.0 0.1 shard_map.49
  18.1 1.6 %collective-permute-start.18 = (bf16[336,128]{1,0:T(8,128)(2,1)S(1)}, bf16[336,128]{1,0:T(8,128)(2,1)S(1)}, u32[]{:S(2)}, u32[]{:S(2)}) collective-permute-start(bf16[336,128]{1,0:T(8,128)(2,1)S(1)} %get-tuple-element.100), channel_id=1, source_target_pairs={{0,8},{4,12},{8,0},{12,4},{1,9},{5,13},{9,1},{13,5},{2,10},{6,14},... | collective-permute-start | bytes 258056 | tf_op jit(solution)/shard_map/ppermute | solution.py:74
  19.7 0.3 collective-permute-start.13
  20.1 1.2 %collective-permute-start.12 = (bf16[32,128]{1,0:T(8,128)(2,1)S(1)}, bf16[32,128]{1,0:T(8,128)(2,1)S(1)}, u32[]{:S(2)}, u32[]{:S(2)}) collective-permute-start(bf16[32,128]{1,0:T(8,128)(2,1)S(1)} %convert_element_type.11.refs_0_), channel_id=1, source_target_pairs={{0,8},{4,12},{8,0},{12,4},{1,9},{5,13},{9,1},{13,5},{2,10},{6,14},... | collective-permute-start | bytes 24584 | tf_op jit(solution)/shard_map/ppermute | solution.py:74
  21.3 0.4 collective-permute-start.11
  21.7 1.3 %collective-permute-done.13.refs_3_ = bf16[32,128]{1,0:T(8,128)(2,1)S(1)} collective-permute-done((bf16[32,128]{1,0:T(8,128)(2,1)S(1)}, bf16[32,128]{1,0:T(8,128)(2,1)S(1)}, u32[]{:S(2)}, u32[]{:S(2)}) %collective-permute-start.13) | collective-permute-done | bytes 8224 | tf_op jit(solution)/shard_map/ppermute | solution.py:74
  22.9 0.8 %collective-permute-done.12.refs_2_ = bf16[32,128]{1,0:T(8,128)(2,1)S(1)} collective-permute-done((bf16[32,128]{1,0:T(8,128)(2,1)S(1)}, bf16[32,128]{1,0:T(8,128)(2,1)S(1)}, u32[]{:S(2)}, u32[]{:S(2)}) %collective-permute-start.12) | collective-permute-done | bytes 8224 | tf_op jit(solution)/shard_map/ppermute | solution.py:74
  23.7 0.0 collective-permute-done.11.refs_1_
  23.7 0.9 %shard_map.50 = (bf16[32,256]{1,0:T(8,128)(2,1)S(1)}, bf16[32,256]{1,0:T(8,128)(2,1)S(1)}, bf16[32,256]{1,0:T(8,128)(2,1)S(1)}, bf16[32,256]{1,0:T(8,128)(2,1)S(1)}) custom-call(s32[2]{0:T(128)S(1)} %pad_add_fusion.where_ref, bf16[1024,512]{1,0:T(8,128)(2,1)S(1)} %bitcast.11, bf16[32,128]{1,0:T(8,128)(2,1)S(1)} %convert_element_type.11.refs_0_, ...), custom_call_target="tpu_custom_call" | custom-call | tf_op jit(solution)/shard_map/pallas_call | solution.py:107
  24.7 3.7 %collective-permute-start.14 = (bf16[32,256]{1,0:T(8,128)(2,1)S(1)}, bf16[32,256]{1,0:T(8,128)(2,1)S(1)}, u32[]{:S(2)}, u32[]{:S(2)}) collective-permute-start(bf16[32,256]{1,0:T(8,128)(2,1)S(1)} %get-tuple-element.94), channel_id=1, source_target_pairs={{0,1},{1,3},{2,0},{3,2},{4,5},{5,7},{6,4},{7,6},{8,9},{9,11},{10,8... | collective-permute-start | bytes 49160 | tf_op jit(solution)/shard_map/ppermute | solution.py:86
  28.4 3.4 %collective-permute-start.15 = (bf16[32,256]{1,0:T(8,128)(2,1)S(1)}, bf16[32,256]{1,0:T(8,128)(2,1)S(1)}, u32[]{:S(2)}, u32[]{:S(2)}) collective-permute-start(bf16[32,256]{1,0:T(8,128)(2,1)S(1)} %get-tuple-element.95), channel_id=1, source_target_pairs={{0,3},{1,2},{2,1},{3,0},{4,7},{5,6},{6,5},{7,4},{8,11},{9,10},{10,... | collective-permute-start | bytes 49160 | tf_op jit(solution)/shard_map/ppermute | solution.py:86
  31.8 0.4 collective-permute-done.14.refs_1_
  32.2 1.7 %collective-permute-done.15.refs_2_ = bf16[32,256]{1,0:T(8,128)(2,1)S(1)} collective-permute-done((bf16[32,256]{1,0:T(8,128)(2,1)S(1)}, bf16[32,256]{1,0:T(8,128)(2,1)S(1)}, u32[]{:S(2)}, u32[]{:S(2)}) %collective-permute-start.15) | collective-permute-done | bytes 16416 | tf_op jit(solution)/shard_map/ppermute | solution.py:86
  33.9 1.6 %collective-permute-done.16.refs_3_ = bf16[32,256]{1,0:T(8,128)(2,1)S(1)} collective-permute-done((bf16[32,256]{1,0:T(8,128)(2,1)S(1)}, bf16[32,256]{1,0:T(8,128)(2,1)S(1)}, u32[]{:S(2)}, u32[]{:S(2)}) %collective-permute-start.16) | collective-permute-done | bytes 16416 | tf_op jit(solution)/shard_map/ppermute | solution.py:86
  35.5 0.7 %shard_map.51 = (bf16[128,128]{1,0:T(8,128)(2,1)S(1)}, bf16[128,128]{1,0:T(8,128)(2,1)S(1)}) custom-call(s32[2]{0:T(128)S(1)} %pad_add_fusion.where_ref, s32[4,6]{1,0:T(4,128)S(1)} %bitcast.18, f32[32,1024]{1,0:T(8,128)S(1)} %copy-done.1, f32[32,128]{1,0:T(8,128)S(1)} %bitcast.14, bf16[256,512]{1,0:T(8,128)(2,1)S(1)} %get-tuple-element.92.cols_ref, ...), custom_call_target="tpu_custom_call" | custom-call | tf_op jit(solution)/shard_map/pallas_call | solution.py:107
  36.2 0.1 collective-permute-start.17
  36.3 1.2 %collective-permute-done.17.got_ref = bf16[128,128]{1,0:T(8,128)(2,1)S(1)} collective-permute-done((bf16[128,128]{1,0:T(8,128)(2,1)S(1)}, bf16[128,128]{1,0:T(8,128)(2,1)S(1)}, u32[]{:S(2)}, u32[]{:S(2)}) %collective-permute-start.17) | collective-permute-done | bytes 32800 | tf_op jit(solution)/shard_map/ppermute | solution.py:74
  37.5 1.3 %collective-permute-start.19 = (bf16[64,128]{1,0:T(8,128)(2,1)S(1)}, bf16[64,128]{1,0:T(8,128)(2,1)S(1)}, u32[]{:S(2)}, u32[]{:S(2)}) collective-permute-start(bf16[64,128]{1,0:T(8,128)(2,1)S(1)} %get-tuple-element.101), channel_id=1, source_target_pairs={{0,8},{4,12},{8,0},{12,4},{1,9},{5,13},{9,1},{13,5},{2,10},{6,14},... | collective-permute-start | bytes 49160 | tf_op jit(solution)/shard_map/ppermute | solution.py:74
  38.8 1.2 %shard_map.47 = s32[1]{0:T(128)} custom-call(s32[4,6]{1,0:T(4,128)S(1)} %bitcast.19, bf16[528,128]{1,0:T(8,128)(2,1)S(1)} %collective-permute-done.7.refs_0_, bf16[528,128]{1,0:T(8,128)(2,1)S(1)} %collective-permute-done.8.refs_1_, bf16[528,128]{1,0:T(8,128)(2,1)S(1)} %collective-permute-done.9.refs_2_), custom_call_target="tpu_custom_call" | custom-call | tf_op jit(solution)/shard_map/pallas_call | solution.py:107
  40.7 0.7 %collective-permute-done.19 = bf16[64,128]{1,0:T(8,128)(2,1)S(1)} collective-permute-done((bf16[64,128]{1,0:T(8,128)(2,1)S(1)}, bf16[64,128]{1,0:T(8,128)(2,1)S(1)}, u32[]{:S(2)}, u32[]{:S(2)}) %collective-permute-start.19) | collective-permute-done | bytes 16416 | tf_op jit(solution)/shard_map/ppermute | solution.py:74
  41.4 1.1 %collective-permute-start.22 = (bf16[400,128]{1,0:T(8,128)(2,1)S(1)}, bf16[400,128]{1,0:T(8,128)(2,1)S(1)}, u32[]{:S(2)}, u32[]{:S(2)}) collective-permute-start(bf16[400,128]{1,0:T(8,128)(2,1)S(1)} %get-tuple-element.104.refs_0_), channel_id=1, source_target_pairs={{0,2},{1,0},{2,3},{3,1},{4,6},{5,4},{6,7},{7,5},{8,10},{9,8},{10,1... | collective-permute-start | bytes 307208 | tf_op jit(solution)/shard_map/ppermute | solution.py:86
  42.5 1.4 %collective-permute-start.21 = (bf16[400,128]{1,0:T(8,128)(2,1)S(1)}, bf16[400,128]{1,0:T(8,128)(2,1)S(1)}, u32[]{:S(2)}, u32[]{:S(2)}) collective-permute-start(bf16[400,128]{1,0:T(8,128)(2,1)S(1)} %get-tuple-element.104.refs_0_), channel_id=1, source_target_pairs={{0,3},{1,2},{2,1},{3,0},{4,7},{5,6},{6,5},{7,4},{8,11},{9,10},{10,... | collective-permute-start | bytes 307208 | tf_op jit(solution)/shard_map/ppermute | solution.py:86
  43.9 0.5 collective-permute-start.20
  44.4 1.8 %collective-permute-done.22.refs_3_ = bf16[400,128]{1,0:T(8,128)(2,1)S(1)} collective-permute-done((bf16[400,128]{1,0:T(8,128)(2,1)S(1)}, bf16[400,128]{1,0:T(8,128)(2,1)S(1)}, u32[]{:S(2)}, u32[]{:S(2)}) %collective-permute-start.22) | collective-permute-done | bytes 102432 | tf_op jit(solution)/shard_map/ppermute | solution.py:86
  46.2 3.6 %collective-permute-done.21.refs_2_ = bf16[400,128]{1,0:T(8,128)(2,1)S(1)} collective-permute-done((bf16[400,128]{1,0:T(8,128)(2,1)S(1)}, bf16[400,128]{1,0:T(8,128)(2,1)S(1)}, u32[]{:S(2)}, u32[]{:S(2)}) %collective-permute-start.21) | collective-permute-done | bytes 102432 | tf_op jit(solution)/shard_map/ppermute | solution.py:86
  49.9 2.6 %collective-permute-done.20.refs_1_ = bf16[400,128]{1,0:T(8,128)(2,1)S(1)} collective-permute-done((bf16[400,128]{1,0:T(8,128)(2,1)S(1)}, bf16[400,128]{1,0:T(8,128)(2,1)S(1)}, u32[]{:S(2)}, u32[]{:S(2)}) %collective-permute-start.20) | collective-permute-done | bytes 102432 | tf_op jit(solution)/shard_map/ppermute | solution.py:86
  52.5 0.1 shard_map.53
  52.6 1.0 %collective-permute-start.24 = (bf16[400,128]{1,0:T(8,128)(2,1)S(1)}, bf16[400,128]{1,0:T(8,128)(2,1)S(1)}, u32[]{:S(2)}, u32[]{:S(2)}) collective-permute-start(bf16[400,128]{1,0:T(8,128)(2,1)S(1)} %get-tuple-element.102.refs_0_), channel_id=1, source_target_pairs={{0,8},{4,12},{8,0},{12,4},{16,24},{20,28},{24,16},{28,20},{1,9},{5... | collective-permute-start | bytes 307208 | tf_op jit(solution)/shard_map/ppermute | solution.py:74
  53.6 2.0 %collective-permute-start.28 = (bf16[336,128]{1,0:T(8,128)(2,1)S(1)}, bf16[336,128]{1,0:T(8,128)(2,1)S(1)}, u32[]{:S(2)}, u32[]{:S(2)}) collective-permute-start(bf16[336,128]{1,0:T(8,128)(2,1)S(1)} %get-tuple-element.103), channel_id=1, source_target_pairs={{0,24},{4,28},{8,16},{12,20},{16,8},{20,12},{24,0},{28,4},{1,25},{... | collective-permute-start | bytes 258056 | tf_op jit(solution)/shard_map/ppermute | solution.py:74
  55.6 0.5 collective-permute-start.26
  56.1 1.9 %collective-permute-done.24.refs_2_ = bf16[400,128]{1,0:T(8,128)(2,1)S(1)} collective-permute-done((bf16[400,128]{1,0:T(8,128)(2,1)S(1)}, bf16[400,128]{1,0:T(8,128)(2,1)S(1)}, u32[]{:S(2)}, u32[]{:S(2)}) %collective-permute-start.24) | collective-permute-done | bytes 102432 | tf_op jit(solution)/shard_map/ppermute | solution.py:74
  58.0 1.0 %collective-permute-done.28.refs_6_ = bf16[336,128]{1,0:T(8,128)(2,1)S(1)} collective-permute-done((bf16[336,128]{1,0:T(8,128)(2,1)S(1)}, bf16[336,128]{1,0:T(8,128)(2,1)S(1)}, u32[]{:S(2)}, u32[]{:S(2)}) %collective-permute-start.28) | collective-permute-done | bytes 86048 | tf_op jit(solution)/shard_map/ppermute | solution.py:74
  59.0 1.0 %collective-permute-done.26.refs_4_ = bf16[336,128]{1,0:T(8,128)(2,1)S(1)} collective-permute-done((bf16[336,128]{1,0:T(8,128)(2,1)S(1)}, bf16[336,128]{1,0:T(8,128)(2,1)S(1)}, u32[]{:S(2)}, u32[]{:S(2)}) %collective-permute-start.26) | collective-permute-done | bytes 86048 | tf_op jit(solution)/shard_map/ppermute | solution.py:74
  60.1 0.2 collective-permute-done.29.refs_7_
  60.3 1.0 %collective-permute-done.27.refs_5_ = bf16[336,128]{1,0:T(8,128)(2,1)S(1)} collective-permute-done((bf16[336,128]{1,0:T(8,128)(2,1)S(1)}, bf16[336,128]{1,0:T(8,128)(2,1)S(1)}, u32[]{:S(2)}, u32[]{:S(2)}) %collective-permute-start.27) | collective-permute-done | bytes 86048 | tf_op jit(solution)/shard_map/ppermute | solution.py:74
  61.3 3.4 %shard_map.54 = f32[32,128]{1,0:T(8,128)} custom-call(s32[2]{0:T(128)S(1)} %pad_add_fusion.where_ref, s32[4,6]{1,0:T(4,128)S(1)} %bitcast.21, bf16[400,128]{1,0:T(8,128)(2,1)S(1)} %get-tuple-element.102.refs_0_, bf16[400,128]{1,0:T(8,128)(2,1)S(1)} %collective-permute-done.23.refs_1_, bf16[400,128]{1,0:T(8,128)(2,1)S(1)} %collective-permute-done.24.refs_2_, ...), custom_call_target="tpu_custom_call" | custom-call | tf_op jit(solution)/shard_map/pallas_call | solution.py:107
  (19 shorter events, 0.1 us)
Async XLA Ops:
  0.0 15.1 %copy-start = (bf16[1,1024,512]{2,1,0:T(8,128)(2,1)S(1)}, bf16[1,1024,512]{2,1,0:T(8,128)(2,1)}, u32[]{:S(2)}) copy-start(bf16[1,1024,512]{2,1,0:T(8,128)(2,1)} %param.6) | copy-start | bytes 3145732
  1.5 13.6 %copy-start.3 = (s32[6,4]{0,1:T(4,128)S(1)}, s32[6,4]{0,1:T(4,128)}, u32[]{:S(2)}) copy-start(s32[6,4]{0,1:T(4,128)} %param.9) | copy-start | bytes 292
  1.5 8.5 %collective-permute-start.7 = (bf16[528,128]{1,0:T(8,128)(2,1)S(1)}, bf16[528,128]{1,0:T(8,128)(2,1)S(1)}, u32[]{:S(2)}, u32[]{:S(2)}) collective-permute-start(bf16[528,128]{1,0:T(8,128)(2,1)S(1)} %get-tuple-element.86), channel_id=1, source_target_pairs={{0,1},{1,3},{2,0},{3,2},{4,5},{5,7},{6,4},{7,6},{8,9},{9,11},{10,8... | collective-permute-start | bytes 405512 | tf_op jit(solution)/shard_map/ppermute | solution.py:86
  4.6 9.9 %collective-permute-start.8 = (bf16[528,128]{1,0:T(8,128)(2,1)S(1)}, bf16[528,128]{1,0:T(8,128)(2,1)S(1)}, u32[]{:S(2)}, u32[]{:S(2)}) collective-permute-start(bf16[528,128]{1,0:T(8,128)(2,1)S(1)} %get-tuple-element.87), channel_id=1, source_target_pairs={{0,3},{1,2},{2,1},{3,0},{4,7},{5,6},{6,5},{7,4},{8,11},{9,10},{10,... | collective-permute-start | bytes 405512 | tf_op jit(solution)/shard_map/ppermute | solution.py:86
  7.1 8.0 %collective-permute-start.9 = (bf16[528,128]{1,0:T(8,128)(2,1)S(1)}, bf16[528,128]{1,0:T(8,128)(2,1)S(1)}, u32[]{:S(2)}, u32[]{:S(2)}) collective-permute-start(bf16[528,128]{1,0:T(8,128)(2,1)S(1)} %get-tuple-element.88), channel_id=1, source_target_pairs={{0,2},{1,0},{2,3},{3,1},{4,6},{5,4},{6,7},{7,5},{8,10},{9,8},{10,1... | collective-permute-start | bytes 405512 | tf_op jit(solution)/shard_map/ppermute | solution.py:86
  16.6 1.5 %collective-permute-start.10 = (bf16[672,128]{1,0:T(8,128)(2,1)S(1)}, bf16[672,128]{1,0:T(8,128)(2,1)S(1)}, u32[]{:S(2)}, u32[]{:S(2)}) collective-permute-start(bf16[672,128]{1,0:T(8,128)(2,1)S(1)} %get-tuple-element.90), channel_id=1, source_target_pairs={{0,4},{4,0},{8,12},{12,8},{1,5},{5,1},{9,13},{13,9},{2,6},{6,2},{1... | collective-permute-start | bytes 516104 | tf_op jit(solution)/shard_map/ppermute | solution.py:74
  18.0 1.7 %copy-start.2 = (f32[32,1,1,128]{3,2,1,0:T(1,128)S(1)}, f32[32,1,1,128]{3,2,1,0:T(1,128)}, u32[]{:S(2)}) copy-start(f32[32,1,1,128]{3,2,1,0:T(1,128)} %param.8) | copy-start | bytes 49156
  18.1 23.3 %collective-permute-start.18 = (bf16[336,128]{1,0:T(8,128)(2,1)S(1)}, bf16[336,128]{1,0:T(8,128)(2,1)S(1)}, u32[]{:S(2)}, u32[]{:S(2)}) collective-permute-start(bf16[336,128]{1,0:T(8,128)(2,1)S(1)} %get-tuple-element.100), channel_id=1, source_target_pairs={{0,8},{4,12},{8,0},{12,4},{1,9},{5,13},{9,1},{13,5},{2,10},{6,14},... | collective-permute-start | bytes 258056 | tf_op jit(solution)/shard_map/ppermute | solution.py:74
  19.7 15.8 %copy-start.1 = (f32[32,1024]{1,0:T(8,128)S(1)}, f32[32,1024]{1,0:T(8,128)}, u32[]{:S(2)}) copy-start(f32[32,1024]{1,0:T(8,128)} %y_ref.3) | copy-start | bytes 393220
  19.7 3.2 %collective-permute-start.13 = (bf16[32,128]{1,0:T(8,128)(2,1)S(1)}, bf16[32,128]{1,0:T(8,128)(2,1)S(1)}, u32[]{:S(2)}, u32[]{:S(2)}) collective-permute-start(bf16[32,128]{1,0:T(8,128)(2,1)S(1)} %convert_element_type.11.refs_0_), channel_id=1, source_target_pairs={{0,12},{4,8},{8,4},{12,0},{1,13},{5,9},{9,5},{13,1},{2,14},{6,10},... | collective-permute-start | bytes 24584 | tf_op jit(solution)/shard_map/ppermute | solution.py:74
  20.1 3.7 %collective-permute-start.12 = (bf16[32,128]{1,0:T(8,128)(2,1)S(1)}, bf16[32,128]{1,0:T(8,128)(2,1)S(1)}, u32[]{:S(2)}, u32[]{:S(2)}) collective-permute-start(bf16[32,128]{1,0:T(8,128)(2,1)S(1)} %convert_element_type.11.refs_0_), channel_id=1, source_target_pairs={{0,8},{4,12},{8,0},{12,4},{1,9},{5,13},{9,1},{13,5},{2,10},{6,14},... | collective-permute-start | bytes 24584 | tf_op jit(solution)/shard_map/ppermute | solution.py:74
  21.3 2.4 %collective-permute-start.11 = (bf16[32,128]{1,0:T(8,128)(2,1)S(1)}, bf16[32,128]{1,0:T(8,128)(2,1)S(1)}, u32[]{:S(2)}, u32[]{:S(2)}) collective-permute-start(bf16[32,128]{1,0:T(8,128)(2,1)S(1)} %convert_element_type.11.refs_0_), channel_id=1, source_target_pairs={{0,4},{4,0},{8,12},{12,8},{1,5},{5,1},{9,13},{13,9},{2,6},{6,2},{1... | collective-permute-start | bytes 24584 | tf_op jit(solution)/shard_map/ppermute | solution.py:74
  24.7 7.5 %collective-permute-start.14 = (bf16[32,256]{1,0:T(8,128)(2,1)S(1)}, bf16[32,256]{1,0:T(8,128)(2,1)S(1)}, u32[]{:S(2)}, u32[]{:S(2)}) collective-permute-start(bf16[32,256]{1,0:T(8,128)(2,1)S(1)} %get-tuple-element.94), channel_id=1, source_target_pairs={{0,1},{1,3},{2,0},{3,2},{4,5},{5,7},{6,4},{7,6},{8,9},{9,11},{10,8... | collective-permute-start | bytes 49160 | tf_op jit(solution)/shard_map/ppermute | solution.py:86
  28.4 5.5 %collective-permute-start.15 = (bf16[32,256]{1,0:T(8,128)(2,1)S(1)}, bf16[32,256]{1,0:T(8,128)(2,1)S(1)}, u32[]{:S(2)}, u32[]{:S(2)}) collective-permute-start(bf16[32,256]{1,0:T(8,128)(2,1)S(1)} %get-tuple-element.95), channel_id=1, source_target_pairs={{0,3},{1,2},{2,1},{3,0},{4,7},{5,6},{6,5},{7,4},{8,11},{9,10},{10,... | collective-permute-start | bytes 49160 | tf_op jit(solution)/shard_map/ppermute | solution.py:86
  31.8 3.7 %collective-permute-start.16 = (bf16[32,256]{1,0:T(8,128)(2,1)S(1)}, bf16[32,256]{1,0:T(8,128)(2,1)S(1)}, u32[]{:S(2)}, u32[]{:S(2)}) collective-permute-start(bf16[32,256]{1,0:T(8,128)(2,1)S(1)} %get-tuple-element.96), channel_id=1, source_target_pairs={{0,2},{1,0},{2,3},{3,1},{4,6},{5,4},{6,7},{7,5},{8,10},{9,8},{10,1... | collective-permute-start | bytes 49160 | tf_op jit(solution)/shard_map/ppermute | solution.py:86
  36.2 1.3 %collective-permute-start.17 = (bf16[128,128]{1,0:T(8,128)(2,1)S(1)}, bf16[128,128]{1,0:T(8,128)(2,1)S(1)}, u32[]{:S(2)}, u32[]{:S(2)}) collective-permute-start(bf16[128,128]{1,0:T(8,128)(2,1)S(1)} %get-tuple-element.98), channel_id=1, source_target_pairs={{0,4},{4,0},{8,12},{12,8},{1,5},{5,1},{9,13},{13,9},{2,6},{6,2},{1... | collective-permute-start | bytes 98312 | tf_op jit(solution)/shard_map/ppermute | solution.py:74
  37.5 3.8 %collective-permute-start.19 = (bf16[64,128]{1,0:T(8,128)(2,1)S(1)}, bf16[64,128]{1,0:T(8,128)(2,1)S(1)}, u32[]{:S(2)}, u32[]{:S(2)}) collective-permute-start(bf16[64,128]{1,0:T(8,128)(2,1)S(1)} %get-tuple-element.101), channel_id=1, source_target_pairs={{0,8},{4,12},{8,0},{12,4},{1,9},{5,13},{9,1},{13,5},{2,10},{6,14},... | collective-permute-start | bytes 49160 | tf_op jit(solution)/shard_map/ppermute | solution.py:74
  41.4 4.8 %collective-permute-start.22 = (bf16[400,128]{1,0:T(8,128)(2,1)S(1)}, bf16[400,128]{1,0:T(8,128)(2,1)S(1)}, u32[]{:S(2)}, u32[]{:S(2)}) collective-permute-start(bf16[400,128]{1,0:T(8,128)(2,1)S(1)} %get-tuple-element.104.refs_0_), channel_id=1, source_target_pairs={{0,2},{1,0},{2,3},{3,1},{4,6},{5,4},{6,7},{7,5},{8,10},{9,8},{10,1... | collective-permute-start | bytes 307208 | tf_op jit(solution)/shard_map/ppermute | solution.py:86
  42.5 7.3 %collective-permute-start.21 = (bf16[400,128]{1,0:T(8,128)(2,1)S(1)}, bf16[400,128]{1,0:T(8,128)(2,1)S(1)}, u32[]{:S(2)}, u32[]{:S(2)}) collective-permute-start(bf16[400,128]{1,0:T(8,128)(2,1)S(1)} %get-tuple-element.104.refs_0_), channel_id=1, source_target_pairs={{0,3},{1,2},{2,1},{3,0},{4,7},{5,6},{6,5},{7,4},{8,11},{9,10},{10,... | collective-permute-start | bytes 307208 | tf_op jit(solution)/shard_map/ppermute | solution.py:86
  43.9 8.6 %collective-permute-start.20 = (bf16[400,128]{1,0:T(8,128)(2,1)S(1)}, bf16[400,128]{1,0:T(8,128)(2,1)S(1)}, u32[]{:S(2)}, u32[]{:S(2)}) collective-permute-start(bf16[400,128]{1,0:T(8,128)(2,1)S(1)} %get-tuple-element.104.refs_0_), channel_id=1, source_target_pairs={{0,1},{1,3},{2,0},{3,2},{4,5},{5,7},{6,4},{7,6},{8,9},{9,11},{10,8... | collective-permute-start | bytes 307208 | tf_op jit(solution)/shard_map/ppermute | solution.py:86
  52.6 5.4 %collective-permute-start.24 = (bf16[400,128]{1,0:T(8,128)(2,1)S(1)}, bf16[400,128]{1,0:T(8,128)(2,1)S(1)}, u32[]{:S(2)}, u32[]{:S(2)}) collective-permute-start(bf16[400,128]{1,0:T(8,128)(2,1)S(1)} %get-tuple-element.102.refs_0_), channel_id=1, source_target_pairs={{0,8},{4,12},{8,0},{12,4},{16,24},{20,28},{24,16},{28,20},{1,9},{5... | collective-permute-start | bytes 307208 | tf_op jit(solution)/shard_map/ppermute | solution.py:74
  53.6 5.4 %collective-permute-start.28 = (bf16[336,128]{1,0:T(8,128)(2,1)S(1)}, bf16[336,128]{1,0:T(8,128)(2,1)S(1)}, u32[]{:S(2)}, u32[]{:S(2)}) collective-permute-start(bf16[336,128]{1,0:T(8,128)(2,1)S(1)} %get-tuple-element.103), channel_id=1, source_target_pairs={{0,24},{4,28},{8,16},{12,20},{16,8},{20,12},{24,0},{28,4},{1,25},{... | collective-permute-start | bytes 258056 | tf_op jit(solution)/shard_map/ppermute | solution.py:74
  55.6 4.5 %collective-permute-start.26 = (bf16[336,128]{1,0:T(8,128)(2,1)S(1)}, bf16[336,128]{1,0:T(8,128)(2,1)S(1)}, u32[]{:S(2)}, u32[]{:S(2)}) collective-permute-start(bf16[336,128]{1,0:T(8,128)(2,1)S(1)} %get-tuple-element.103), channel_id=1, source_target_pairs={{0,16},{4,20},{8,24},{12,28},{16,0},{20,4},{24,8},{28,12},{1,17},{... | collective-permute-start | bytes 258056 | tf_op jit(solution)/shard_map/ppermute | solution.py:74
  56.1 4.0 %collective-permute-start.23 = (bf16[400,128]{1,0:T(8,128)(2,1)S(1)}, bf16[400,128]{1,0:T(8,128)(2,1)S(1)}, u32[]{:S(2)}, u32[]{:S(2)}) collective-permute-start(bf16[400,128]{1,0:T(8,128)(2,1)S(1)} %get-tuple-element.102.refs_0_), channel_id=1, source_target_pairs={{0,4},{4,0},{8,12},{12,8},{16,20},{20,16},{24,28},{28,24},{1,5},{5... | collective-permute-start | bytes 307208 | tf_op jit(solution)/shard_map/ppermute | solution.py:74
  58.0 3.4 %collective-permute-start.25 = (bf16[400,128]{1,0:T(8,128)(2,1)S(1)}, bf16[400,128]{1,0:T(8,128)(2,1)S(1)}, u32[]{:S(2)}, u32[]{:S(2)}) collective-permute-start(bf16[400,128]{1,0:T(8,128)(2,1)S(1)} %collective-permute-done.24.refs_2_), channel_id=1, source_target_pairs={{0,4},{4,0},{8,12},{12,8},{16,20},{20,16},{24,28},{28,24},{1,5},{5... | collective-permute-start | bytes 307208 | tf_op jit(solution)/shard_map/ppermute | solution.py:74
  59.0 1.3 %collective-permute-start.29 = (bf16[336,128]{1,0:T(8,128)(2,1)S(1)}, bf16[336,128]{1,0:T(8,128)(2,1)S(1)}, u32[]{:S(2)}, u32[]{:S(2)}) collective-permute-start(bf16[336,128]{1,0:T(8,128)(2,1)S(1)} %collective-permute-done.28.refs_6_), channel_id=1, source_target_pairs={{0,4},{4,0},{8,12},{12,8},{16,20},{20,16},{24,28},{28,24},{1,5},{5... | collective-permute-start | bytes 258056 | tf_op jit(solution)/shard_map/ppermute | solution.py:74
  60.1 1.3 %collective-permute-start.27 = (bf16[336,128]{1,0:T(8,128)(2,1)S(1)}, bf16[336,128]{1,0:T(8,128)(2,1)S(1)}, u32[]{:S(2)}, u32[]{:S(2)}) collective-permute-start(bf16[336,128]{1,0:T(8,128)(2,1)S(1)} %collective-permute-done.26.refs_4_), channel_id=1, source_target_pairs={{0,4},{4,0},{8,12},{12,8},{16,20},{20,16},{24,28},{28,24},{1,5},{5... | collective-permute-start | bytes 258056 | tf_op jit(solution)/shard_map/ppermute | solution.py:74

commit v7 on v6

--- a/solution.py
+++ b/solution.py
@@ -97,8 +97,7 @@
 
 
 def call(body, out_shape, args, scratch=(), smem=(), scalars=()):
-    places = [pltpu.SMEM if i in smem else pltpu.VMEM for i in range(len(args))]
-    specs = [pl.BlockSpec(memory_space=place) for place in places]
+    specs = [pl.BlockSpec(memory_space=pltpu.SMEM if i in smem else pltpu.VMEM) for i in range(len(args))]
     place = lambda i: pltpu.SMEM if i in scalars else pltpu.VMEM
     if isinstance(out_shape, list):
         out_specs = [pl.BlockSpec(memory_space=place(i)) for i in range(len(out_shape))]
@@ -119,53 +118,80 @@
     return high, (value - high.astype(jnp.float32)).astype(jnp.bfloat16)
 
 
-def kept_tiles(ranks_ref, slots):
+def pack_body(slots, ranks_ref, a_ref, x0_ref, *outs):
+    *outs, notes_ref, round_ref = outs
+    round_ref[...] = x0_ref[...].astype(jnp.bfloat16)
+    pix, base = lax.axis_index("pix"), lax.axis_index("base")
+    tiles = ranks_ref.shape[0]
+    quarter = a_ref.shape[0] // (len(outs) + 1)
+    places = (outs[0].shape[0] - PAD) // quarter
+    rows = lax.broadcasted_iota(jnp.int32, (PAD, TILE), 0)
     count = jnp.int32(0)
     table = []
-    for j in range(ranks_ref.shape[0]):
+    notes = jnp.full((PAD, TILE), -1, jnp.int32)
+    for j in range(tiles):
         rank = ranks_ref[j, 0]
-        kept = rank < slots
-        table.append((rank, kept, count))
-        count = count + jnp.where(kept, 1, 0)
-    return table, count
-
-
-def pack_body(slots, first, where_ref, ranks_ref, a_ref, *outs):
-    pix = where_ref[0]
-    quarter = a_ref.shape[0] // (len(outs) + 1)
-    places = (outs[0].shape[0] - PAD) // quarter
-    table, count = kept_tiles(ranks_ref, slots)
-    rows = lax.broadcasted_iota(jnp.int32, (PAD, TILE), 0)
-    notes = jnp.where(rows == PAD - 1, count, -1)
+        slot = jnp.where(rank < slots, rank, -1)
+        table.append((slot, count))
+        notes = jnp.where(rows == j, slot, notes)
+        notes = jnp.where(jnp.logical_and(rows == PAD - 2, base == j), slot, notes)
+        count = count + jnp.where(rank < slots, 1, 0)
+    notes = jnp.where(rows == PAD - 1, count, notes)
+    notes_ref[...] = notes.astype(jnp.float32).astype(jnp.bfloat16)
+    sent = jnp.where(rows == PAD - 1, count, -1)
     for i in range(places):
-        tile, slot = jnp.int32(0), jnp.int32(-1)
-        for j, (rank, kept, before) in enumerate(table):
-            hit = jnp.logical_and(kept, before == first + i)
+        tile = jnp.int32(0)
+        for j, (slot, before) in enumerate(table):
+            hit = jnp.logical_and(slot >= 0, before == i)
             tile = jnp.where(hit, j, tile)
-            slot = jnp.where(hit, rank, slot)
-        notes = jnp.where(rows == i, slot, notes)
+            sent = jnp.where(jnp.logical_and(rows == i, hit), slot, sent)
         lanes = pl.ds(pl.multiple_of(tile * TILE, TILE), TILE)
         for d, out in enumerate(outs):
             at = pl.ds(pl.multiple_of(target(pix, d + 1, len(outs) + 1) * quarter, quarter), quarter)
             out[i * quarter : (i + 1) * quarter, :] = a_ref[at, lanes]
     for out in outs:
-        out[places * quarter :, :] = notes.astype(jnp.float32).astype(jnp.bfloat16)
-
-
-def crowd_body(slots, places, ranks_ref, *refs):
+        out[places * quarter :, :] = sent.astype(jnp.float32).astype(jnp.bfloat16)
+
+
+def rest_body(first, notes_ref, a_ref, *outs):
+    pix = lax.axis_index("pix")
+    quarter = a_ref.shape[0] // (len(outs) + 1)
+    places = (outs[0].shape[0] - PAD) // quarter
+    notes = notes_ref[...].astype(jnp.float32)
+    tiles = a_ref.shape[1] // TILE
+    rows = lax.broadcasted_iota(jnp.int32, (PAD, TILE), 0)
+    before = jnp.zeros((1, TILE), jnp.float32)
+    sent = jnp.full((PAD, TILE), -1.0, jnp.float32)
+    hits = []
+    for j in range(tiles):
+        slot = notes[j : j + 1]
+        hits.append([jnp.logical_and(slot >= 0, before == first + i) for i in range(places)])
+        for i in range(places):
+            sent = jnp.where(jnp.logical_and(rows == i, hits[j][i]), slot, sent)
+        before = before + jnp.where(slot >= 0, 1.0, 0.0)
+    for d, out in enumerate(outs):
+        at = pl.ds(pl.multiple_of(target(pix, d + 1, len(outs) + 1) * quarter, quarter), quarter)
+        for i in range(places):
+            block = a_ref[at, :TILE]
+            for j in range(1, tiles):
+                tile = a_ref[at, j * TILE : (j + 1) * TILE]
+                block = jnp.where(jnp.broadcast_to(hits[j][i], block.shape), tile, block)
+            out[i * quarter : (i + 1) * quarter, :] = block
+        out[places * quarter :, :] = sent.astype(jnp.bfloat16)
+
+
+def crowd_body(places, *refs):
     *parts, out_ref = refs
-    _, count = kept_tiles(ranks_ref, slots)
     most = parts[0][-PAD:, :].astype(jnp.float32)
     for part in parts[1:]:
         most = jnp.maximum(most, part[-PAD:, :].astype(jnp.float32))
     rows = lax.broadcasted_iota(jnp.int32, (PAD, TILE), 0)
-    others = jnp.max(jnp.where(rows == PAD - 1, most, -1.0))
-    over = jnp.logical_or(others > places, count > places)
-    out_ref[0] = jnp.where(over, 1, 0)
-
-
-def first_body(where_ref, a_ref, *refs):
-    pix, base = where_ref[0], where_ref[1]
+    most = jnp.max(jnp.where(rows == PAD - 1, most, -1.0))
+    out_ref[0] = jnp.where(most > places, 1, 0)
+
+
+def first_body(a_ref, *refs):
+    pix, base = lax.axis_index("pix"), lax.axis_index("base")
     n_base = a_ref.shape[1] // TILE
     shares, rest = refs[:n_base], refs[n_base:]
     outs, x_ref = rest[:-1], rest[-1]
@@ -203,29 +229,28 @@
     return rows, cols
 
 
-def gram_body(slots, n_parts, where_ref, ranks_ref, y_ref, a_ref, *refs):
-    pix, base = where_ref[0], where_ref[1]
+def gram_body(slots, n_parts, y_ref, a_ref, notes_ref, *refs):
+    pix, base = lax.axis_index("pix"), lax.axis_index("base")
     parts = refs[:n_parts]
     cols_ref, own_ref, sent_ref, all_ref = refs[n_parts:]
     n_base = all_ref.shape[0]
     chans, quarter = y_ref.shape[0], cols_ref.shape[0]
-    table, _ = kept_tiles(ranks_ref, slots)
     own_rows = pl.ds(pl.multiple_of(pix * quarter, quarter), quarter)
+    tiles = a_ref.shape[1] // TILE
+    blocks = [a_ref[own_rows, j * TILE : (j + 1) * TILE] for j in range(tiles)]
+    notes = notes_ref[...].astype(jnp.float32)
+    marks = [notes[j : j + 1] for j in range(tiles)]
+    for part in parts:
+        places = (part.shape[0] - PAD) // quarter
+        notes = part[places * quarter :, :].astype(jnp.float32)
+        blocks += [part[i * quarter : (i + 1) * quarter, :] for i in range(places)]
+        marks += [notes[i : i + 1] for i in range(places)]
     columns = []
     for r in range(slots):
-        tile, owned = jnp.int32(0), jnp.int32(0)
-        for j, (rank, _, _) in enumerate(table):
-            tile = jnp.where(rank == r, j, tile)
-            owned = jnp.where(rank == r, 1, owned)
-        block = a_ref[own_rows, pl.ds(pl.multiple_of(tile * TILE, TILE), TILE)]
-        block = jnp.where(owned == 1, block, jnp.zeros_like(block))
-        for part in parts:
-            places = (part.shape[0] - PAD) // quarter
-            notes = part[places * quarter :, :].astype(jnp.float32)
-            for i in range(places):
-                hit = jnp.broadcast_to(notes[i : i + 1] == r, block.shape)
-                block = jnp.where(hit, part[i * quarter : (i + 1) * quarter, :], block)
-        columns.append(block)
+        column = jnp.zeros((quarter, TILE), jnp.bfloat16)
+        for block, mark in zip(blocks, marks):
+            column = jnp.where(jnp.broadcast_to(mark == r, column.shape), block, column)
+        columns.append(column)
     a = jnp.concatenate(columns, axis=1)
     cols_ref[...] = a
     y = y_ref[:, pl.ds(pl.multiple_of(pix * quarter, quarter), quarter)]
@@ -267,8 +292,8 @@
     return jnp.concatenate([*split(row), jnp.zeros((PAD - 2, TILE), jnp.bfloat16)], axis=0)
 
 
-def start_body(slots, n_pix, where_ref, ranks_ref, y_ref, x0_ref, cols_ref, *refs):
-    pix, base = where_ref[0], where_ref[1]
+def start_body(slots, n_pix, y_ref, x0_ref, notes_ref, cols_ref, *refs):
+    pix, base = lax.axis_index("pix"), lax.axis_index("base")
     preds = refs[:n_pix]
     own_ref, sent_ref, all_ref = refs[n_pix:]
     per = slots // all_ref.shape[0]
@@ -279,9 +304,9 @@
     y = y_ref[:, pl.ds(pl.multiple_of(pix * quarter, quarter), quarter)]
     resid = (y - pred).astype(jnp.bfloat16)
     moved = descent_stride * jnp.dot(resid, cols_ref[...], preferred_element_type=jnp.float32)
-    rank = ranks_ref[base, 0]
+    mark = notes_ref[PAD - 2 : PAD - 1, :].astype(jnp.float32)
     for r in range(slots):
-        start = moved[:, r * TILE : (r + 1) * TILE] + jnp.where(rank == r, x0_ref[...], 0.0)
+        start = moved[:, r * TILE : (r + 1) * TILE] + jnp.where(mark == r, x0_ref[...], 0.0)
         at = (r % per) * 2 * chans
         all_ref[r // per, at : at + 2 * chans, :] = jnp.concatenate(split(start), axis=0)
     by_core(base, all_ref, own_ref, sent_ref)
@@ -331,9 +356,9 @@
         to += kept
 
 
-def iterate_body(slots, n_base, where_ref, ranks_ref, *refs):
-    base = where_ref[1]
-    *chunks, out_ref, gram_ref, last_ref = refs
+def iterate_body(slots, n_base, notes_ref, *refs):
+    base = lax.axis_index("base")
+    *chunks, out_ref, gram_ref = refs
     chans = out_ref.shape[0]
     rows, cols = corner()
     n_off = slots * (slots - 1) // 2
@@ -377,32 +402,38 @@
             v = full[r // per][g_rows + (r % per) * (wide + PAD) + wide :][:PAD].astype(jnp.float32)
             tails.append(v[0:1] + v[1:2])
         diags.append(jnp.concatenate(tails, axis=1))
+    tile = lambda v, r: v[:, r * TILE : (r + 1) * TILE]
     for step in range(ITERS):
+        parts = [[], []]
+        if step < ITERS - 1:
+            for g in range(2):
+                high, low = split(states[g])
+                left = jnp.concatenate([high, low], axis=0) if g == 0 else high
+                for r in range(slots):
+                    rows_r = gram_ref[g, r * TILE : (r + 1) * TILE, :]
+                    part = jnp.dot(tile(left, r), rows_r, preferred_element_type=jnp.float32)
+                    parts[g].append(part[:chans] + part[chans:] if g == 0 else part)
+        squares = states[0] * states[0] + states[1] * states[1]
+        column = jnp.sum(squares, axis=0, keepdims=True)
         factors = []
         for r in range(slots):
-            lanes = slice(r * TILE, (r + 1) * TILE)
-            square = states[0][:, lanes] * states[0][:, lanes] + states[1][:, lanes] * states[1][:, lanes]
-            column = jnp.sum(square, axis=0, keepdims=True)
-            norm = jnp.sum(column, axis=1, keepdims=True)
+            norm = jnp.sum(tile(column, r), axis=1, keepdims=True)
             rms = jnp.sqrt(norm / (CH * TILE) + eps_norm)
-            factors.append(jnp.broadcast_to(rms / (rms + lam_shrink), (1, TILE)))
-        factor = jnp.concatenate(factors, axis=1)
+            factors.append(rms / (rms + lam_shrink))
+        factor = jnp.concatenate([jnp.broadcast_to(f, (1, TILE)) for f in factors], axis=1)
         states = [state * factor for state in states]
         if step == ITERS - 1:
             break
         for g in range(2):
-            high, low = split(states[g])
-            left = jnp.concatenate([high, low], axis=0) if g == 0 else high
-            product = jnp.dot(left, gram_ref[g], preferred_element_type=jnp.float32)
-            if g == 0:
-                product = product[:chans] + product[chans:]
-            product = product + states[g] * diags[g]
+            product = states[g] * diags[g]
+            for f, part in zip(factors, parts[g]):
+                product = product + f * part
             states[g] = states[g] + descent_stride * (datas[g] - product)
+    mark = notes_ref[PAD - 2 : PAD - 1, :].astype(jnp.float32)
+    image = jnp.zeros(out_ref.shape, jnp.float32)
     for r in range(slots):
-        last_ref[r] = states[0][:, r * TILE : (r + 1) * TILE]
-    rank = ranks_ref[base, 0]
-    kept = last_ref[jnp.minimum(rank, slots - 1)]
-    out_ref[...] = jnp.where(rank < slots, kept, 0.0)
+        image = jnp.where(mark == r, states[0][:, r * TILE : (r + 1) * TILE], image)
+    out_ref[...] = image
 
 
 def gram_plan(sensing_operator_parts, sampled_correlations, first_sky_estimate, patch_order_record):
@@ -412,30 +443,33 @@
     slots = n_base * n_pix // 4
     quarter = m_dev // n_pix
     x0 = first_sky_estimate[:, 0, 0, :]
-    ranks = patch_order_record.T
-    where = jnp.stack([lax.axis_index("pix"), lax.axis_index("base")]).astype(jnp.int32)
+    ranks = pltpu.with_memory_space_constraint(patch_order_record.T, pltpu.HBM)
     shape = jax.ShapeDtypeStruct
     bf16, f32 = jnp.bfloat16, jnp.float32
 
-    def exchange(first, places):
-        packed = call(
-            functools.partial(pack_body, slots, first),
-            [shape((places * quarter + PAD, TILE), bf16)] * (n_pix - 1),
-            (where, ranks, a),
-            smem=(0, 1),
-        )
+    def pieces_of(places):
+        return [shape((places * quarter + PAD, TILE), bf16)] * (n_pix - 1)
+
+    tiles = ranks.shape[0]
+    places = min(CAPACITY, tiles)
+    *packed, notes, x0_round = call(
+        functools.partial(pack_body, slots),
+        pieces_of(places) + [shape((PAD, TILE), bf16), shape(x0.shape, bf16)],
+        (ranks, a, x0),
+        smem=(0,),
+    )
+    parts = send(packed)
+
+    def rest():
+        packed = call(functools.partial(rest_body, places), pieces_of(tiles - places), (notes, a))
         return send(packed)
 
-    places = min(CAPACITY, ranks.shape[0])
-    parts = exchange(0, places)
-    x0_round = x0.astype(bf16)
     shares = [x0_round] + [swap(x0_round, "base", d) for d in range(1, n_base)]
     firsts = call(
         first_body,
         [shape((chans, quarter), bf16)] * n_pix,
-        (where, a, *shares),
+        (a, *shares),
         scratch=[pltpu.VMEM((chans, n_base * TILE), bf16)],
-        smem=(0,),
     )
     preds = [firsts[0]] + send(firsts[1:])
 
@@ -454,16 +488,14 @@
         columns, *gram = call(
             functools.partial(gram_body, slots, len(parts)),
             [shape((quarter, slots * TILE), bf16)] + halves(heights[0]),
-            (where, ranks, sampled_correlations, a, *parts),
+            (sampled_correlations, a, notes, *parts),
             scratch=[pltpu.VMEM((n_base, heights[0], TILE), bf16)],
-            smem=(0, 1),
         )
         side = call(
             functools.partial(start_body, slots, n_pix),
             halves(heights[1]),
-            (where, ranks, sampled_correlations, x0, columns, *preds),
+            (sampled_correlations, x0, notes, columns, *preds),
             scratch=[pltpu.VMEM((n_base, heights[1], TILE), bf16)],
-            smem=(0, 1),
         )
         pieces = []
         for (own, sent), layout in zip((gram, side), layouts):
@@ -480,13 +512,9 @@
     def join(pieces):
         return call(functools.partial(join_body, layouts), chunk, pieces)
 
-    crowded = call(
-        functools.partial(crowd_body, slots, places), shape((1,), jnp.int32), (ranks, *parts), smem=(0,), scalars=(0,)
-    )[0]
+    crowded = call(functools.partial(crowd_body, places), shape((1,), jnp.int32), (notes, *parts), scalars=(0,))[0]
     pieces = base_sum(parts)
-    part = lax.cond(
-        crowded != 0, lambda: join(base_sum(parts + exchange(places, ranks.shape[0] - places))), lambda: join(pieces)
-    )
+    part = lax.cond(crowded != 0, lambda: join(base_sum(parts + rest())), lambda: join(pieces))
     total, brief = call(
         functools.partial(total_body, gram_layout + side_layout), [chunk, short], [part] + send([part] * (n_pix - 1))
     )
@@ -502,12 +530,10 @@
     image = call(
         functools.partial(iterate_body, slots, n_base),
         shape((chans, TILE), f32),
-        (where, ranks, *[got[i] for i in range(2 * n_base)]),
+        (notes, *[got[i] for i in range(2 * n_base)]),
         scratch=[
             pltpu.VMEM((2, slots * TILE, slots * TILE), bf16),
-            pltpu.VMEM((slots, chans, TILE), f32),
         ],
-        smem=(0, 1),
     )
     return image.reshape(chans, 1, 1, TILE)
 

time: 64.9 us -> 62.1 us (0.957)
  Pallas kernels: 9.34 us -> 6.62 us
    pallas_call x10, Pallas kernels: 9.34 us -> 6.62 us  [call(): pl.pallas_call(body, out_shape=out_shape, in_specs=specs, out_specs=out_s...]
  transfers between devices with their start and end apart: 23 -> 23, of which waited for: 19 -> 19; matrix products, arithmetic and copies ran while one was open for 0% -> 0% of each run, Pallas kernels for 4% -> 2%
where the time goes in v7:
time: 62.1 us; the launch traced here: 61.9 us
  waiting for transfers between devices  28.6 us (46%)
  starting transfers between devices  26 us (42%)
  Pallas kernels  6.62 us (11%)
  between operations  0.74 us (1%)
    ppermute x9, waiting for transfers between devices, send(): got.append(lax.ppermute(piece, 'pix', list(enumerate(route))))  18 us
    ppermute x9, starting transfers between devices, send(): got.append(lax.ppermute(piece, 'pix', list(enumerate(route))))  17.2 us
    ppermute x14, waiting for transfers between devices, swap(): return lax.ppermute(value, axis, [(i, i ^ offset) for i in range(size)])  10.6 us
    ppermute x14, starting transfers between devices, swap(): return lax.ppermute(value, axis, [(i, i ^ offset) for i in range(size)])  8.76 us
    pallas_call x10, Pallas kernels, call(): pl.pallas_call(body, out_shape=out_shape, in_specs=specs, out_specs=out_s...  6.62 us
  transfers between devices with their start and end apart: 23, of which 19 were waited for; matrix products, arithmetic and copies ran while one was open for 0% of the time, Pallas kernels for 2%

profile of v7, /device:TPU:0, one launch (start us, length us, event | category | flops | bytes accessed | tf_op | source)
XLA Modules:
  0.0 61.9 jit_solution(2767855400516365427)
XLA Ops:
  0.0 1.4 %shard_map.46 = (bf16[528,128]{1,0:T(8,128)(2,1)S(1)}, bf16[528,128]{1,0:T(8,128)(2,1)S(1)}, bf16[528,128]{1,0:T(8,128)(2,1)S(1)}, bf16[16,128]{1,0:T(8,128)(2,1)S(1)}, bf16[32,128]{1,0:T(8,128)(2,1)S(1)}) custom-call(s32[4,6]{1,0:T(4,128)} %bitcast.14, bf16[1024,512]{1,0:T(8,128)(2,1)} %bitcast.7, f32[32,128]{1,0:T(8,128)} %bitcast.11), custom_call_target="tpu_custom_call" | custom-call | tf_op jit(solution)/shard_map/pallas_call | solution.py:106
  1.4 3.1 %collective-permute-start.7 = (bf16[528,128]{1,0:T(8,128)(2,1)S(1)}, bf16[528,128]{1,0:T(8,128)(2,1)S(1)}, u32[]{:S(2)}, u32[]{:S(2)}) collective-permute-start(bf16[528,128]{1,0:T(8,128)(2,1)S(1)} %get-tuple-element.86), channel_id=1, source_target_pairs={{0,1},{1,3},{2,0},{3,2},{4,5},{5,7},{6,4},{7,6},{8,9},{9,11},{10,8... | collective-permute-start | bytes 405512 | tf_op jit(solution)/shard_map/ppermute | solution.py:86
  4.5 2.5 %collective-permute-start.8 = (bf16[528,128]{1,0:T(8,128)(2,1)S(1)}, bf16[528,128]{1,0:T(8,128)(2,1)S(1)}, u32[]{:S(2)}, u32[]{:S(2)}) collective-permute-start(bf16[528,128]{1,0:T(8,128)(2,1)S(1)} %get-tuple-element.87), channel_id=1, source_target_pairs={{0,3},{1,2},{2,1},{3,0},{4,7},{5,6},{6,5},{7,4},{8,11},{9,10},{10,... | collective-permute-start | bytes 405512 | tf_op jit(solution)/shard_map/ppermute | solution.py:86
  7.0 1.6 %collective-permute-start.9 = (bf16[528,128]{1,0:T(8,128)(2,1)S(1)}, bf16[528,128]{1,0:T(8,128)(2,1)S(1)}, u32[]{:S(2)}, u32[]{:S(2)}) collective-permute-start(bf16[528,128]{1,0:T(8,128)(2,1)S(1)} %get-tuple-element.88), channel_id=1, source_target_pairs={{0,2},{1,0},{2,3},{3,1},{4,6},{5,4},{6,7},{7,5},{8,10},{9,8},{10,1... | collective-permute-start | bytes 405512 | tf_op jit(solution)/shard_map/ppermute | solution.py:86
  8.6 1.3 %collective-permute-done.7.refs_1_.refs_0_ = bf16[528,128]{1,0:T(8,128)(2,1)S(1)} collective-permute-done((bf16[528,128]{1,0:T(8,128)(2,1)S(1)}, bf16[528,128]{1,0:T(8,128)(2,1)S(1)}, u32[]{:S(2)}, u32[]{:S(2)}) %collective-permute-start.7) | collective-permute-done | bytes 135200 | tf_op jit(solution)/shard_map/ppermute | solution.py:86
  9.9 4.5 %collective-permute-done.8.refs_2_.refs_1_ = bf16[528,128]{1,0:T(8,128)(2,1)S(1)} collective-permute-done((bf16[528,128]{1,0:T(8,128)(2,1)S(1)}, bf16[528,128]{1,0:T(8,128)(2,1)S(1)}, u32[]{:S(2)}, u32[]{:S(2)}) %collective-permute-start.8) | collective-permute-done | bytes 135200 | tf_op jit(solution)/shard_map/ppermute | solution.py:86
  14.5 0.6 collective-permute-done.9.refs_3_.refs_2_
  15.0 1.5 %shard_map.48 = (bf16[256,512]{1,0:T(8,128)(2,1)S(1)}, bf16[672,128]{1,0:T(8,128)(2,1)S(1)}, bf16[672,128]{1,0:T(8,128)(2,1)S(1)}) custom-call(f32[32,1024]{1,0:T(8,128)} %y_ref.3, bf16[1024,512]{1,0:T(8,128)(2,1)S(1)} %bitcast.8, bf16[16,128]{1,0:T(8,128)(2,1)S(1)} %get-tuple-element.85.refs_0_.notes_ref, ...), custom_call_target="tpu_custom_call" | custom-call | tf_op jit(solution)/shard_map/pallas_call | solution.py:106
  16.6 0.1 collective-permute-start.10
  16.6 1.4 %collective-permute-done.10.got_ref = bf16[672,128]{1,0:T(8,128)(2,1)S(1)} collective-permute-done((bf16[672,128]{1,0:T(8,128)(2,1)S(1)}, bf16[672,128]{1,0:T(8,128)(2,1)S(1)}, u32[]{:S(2)}, u32[]{:S(2)}) %collective-permute-start.10) | collective-permute-done | bytes 172064 | tf_op jit(solution)/shard_map/ppermute | solution.py:74
  18.0 0.1 shard_map.49
  18.1 1.6 %collective-permute-start.18 = (bf16[336,128]{1,0:T(8,128)(2,1)S(1)}, bf16[336,128]{1,0:T(8,128)(2,1)S(1)}, u32[]{:S(2)}, u32[]{:S(2)}) collective-permute-start(bf16[336,128]{1,0:T(8,128)(2,1)S(1)} %get-tuple-element.101), channel_id=1, source_target_pairs={{0,8},{4,12},{8,0},{12,4},{1,9},{5,13},{9,1},{13,5},{2,10},{6,14},... | collective-permute-start | bytes 258056 | tf_op jit(solution)/shard_map/ppermute | solution.py:74
  19.7 1.5 %collective-permute-start.12 = (bf16[32,128]{1,0:T(8,128)(2,1)S(1)}, bf16[32,128]{1,0:T(8,128)(2,1)S(1)}, u32[]{:S(2)}, u32[]{:S(2)}) collective-permute-start(bf16[32,128]{1,0:T(8,128)(2,1)S(1)} %get-tuple-element.93.refs_0_), channel_id=1, source_target_pairs={{0,8},{4,12},{8,0},{12,4},{1,9},{5,13},{9,1},{13,5},{2,10},{6,14},... | collective-permute-start | bytes 24584 | tf_op jit(solution)/shard_map/ppermute | solution.py:74
  21.2 0.4 collective-permute-start.11
  21.6 1.3 %collective-permute-done.13.refs_3_ = bf16[32,128]{1,0:T(8,128)(2,1)S(1)} collective-permute-done((bf16[32,128]{1,0:T(8,128)(2,1)S(1)}, bf16[32,128]{1,0:T(8,128)(2,1)S(1)}, u32[]{:S(2)}, u32[]{:S(2)}) %collective-permute-start.13) | collective-permute-done | bytes 8224 | tf_op jit(solution)/shard_map/ppermute | solution.py:74
  22.9 0.5 collective-permute-done.12.refs_2_
  23.4 0.0 collective-permute-done.11.refs_1_
  23.4 0.4 shard_map.50
  23.8 3.7 %collective-permute-start.14 = (bf16[32,256]{1,0:T(8,128)(2,1)S(1)}, bf16[32,256]{1,0:T(8,128)(2,1)S(1)}, u32[]{:S(2)}, u32[]{:S(2)}) collective-permute-start(bf16[32,256]{1,0:T(8,128)(2,1)S(1)} %get-tuple-element.95), channel_id=1, source_target_pairs={{0,1},{1,3},{2,0},{3,2},{4,5},{5,7},{6,4},{7,6},{8,9},{9,11},{10,8... | collective-permute-start | bytes 49160 | tf_op jit(solution)/shard_map/ppermute | solution.py:86
  27.5 3.4 %collective-permute-start.15 = (bf16[32,256]{1,0:T(8,128)(2,1)S(1)}, bf16[32,256]{1,0:T(8,128)(2,1)S(1)}, u32[]{:S(2)}, u32[]{:S(2)}) collective-permute-start(bf16[32,256]{1,0:T(8,128)(2,1)S(1)} %get-tuple-element.96), channel_id=1, source_target_pairs={{0,3},{1,2},{2,1},{3,0},{4,7},{5,6},{6,5},{7,4},{8,11},{9,10},{10,... | collective-permute-start | bytes 49160 | tf_op jit(solution)/shard_map/ppermute | solution.py:86
  30.9 0.0 collective-permute-start.16
  30.9 0.3 collective-permute-done.14.refs_1_
  31.1 1.9 %collective-permute-done.15.refs_2_ = bf16[32,256]{1,0:T(8,128)(2,1)S(1)} collective-permute-done((bf16[32,256]{1,0:T(8,128)(2,1)S(1)}, bf16[32,256]{1,0:T(8,128)(2,1)S(1)}, u32[]{:S(2)}, u32[]{:S(2)}) %collective-permute-start.15) | collective-permute-done | bytes 16416 | tf_op jit(solution)/shard_map/ppermute | solution.py:86
  33.0 1.6 %collective-permute-done.16.refs_3_ = bf16[32,256]{1,0:T(8,128)(2,1)S(1)} collective-permute-done((bf16[32,256]{1,0:T(8,128)(2,1)S(1)}, bf16[32,256]{1,0:T(8,128)(2,1)S(1)}, u32[]{:S(2)}, u32[]{:S(2)}) %collective-permute-start.16) | collective-permute-done | bytes 16416 | tf_op jit(solution)/shard_map/ppermute | solution.py:86
  34.6 0.2 shard_map.51
  34.8 0.1 collective-permute-start.17
  34.9 1.2 %collective-permute-done.17.got_ref = bf16[128,128]{1,0:T(8,128)(2,1)S(1)} collective-permute-done((bf16[128,128]{1,0:T(8,128)(2,1)S(1)}, bf16[128,128]{1,0:T(8,128)(2,1)S(1)}, u32[]{:S(2)}, u32[]{:S(2)}) %collective-permute-start.17) | collective-permute-done | bytes 32800 | tf_op jit(solution)/shard_map/ppermute | solution.py:74
  36.1 1.6 %collective-permute-start.19 = (bf16[64,128]{1,0:T(8,128)(2,1)S(1)}, bf16[64,128]{1,0:T(8,128)(2,1)S(1)}, u32[]{:S(2)}, u32[]{:S(2)}) collective-permute-start(bf16[64,128]{1,0:T(8,128)(2,1)S(1)} %get-tuple-element.102), channel_id=1, source_target_pairs={{0,8},{4,12},{8,0},{12,4},{1,9},{5,13},{9,1},{13,5},{2,10},{6,14},... | collective-permute-start | bytes 49160 | tf_op jit(solution)/shard_map/ppermute | solution.py:74
  37.7 0.6 %shard_map.47 = s32[1]{0:T(128)} custom-call(bf16[16,128]{1,0:T(8,128)(2,1)S(1)} %get-tuple-element.85.refs_0_.notes_ref, bf16[528,128]{1,0:T(8,128)(2,1)S(1)} %collective-permute-done.7.refs_1_.refs_0_, bf16[528,128]{1,0:T(8,128)(2,1)S(1)} %collective-permute-done.8.refs_2_.refs_1_, bf16[528,128]{1,0:T(8,128)(2,1)S(1)} %collective-permute-done.9.refs_3_.refs_2_), custom_call_target="tpu_custom_call" | custom-call | tf_op jit(solution)/shard_map/pallas_call | solution.py:106
  39.0 1.0 %collective-permute-done.19 = bf16[64,128]{1,0:T(8,128)(2,1)S(1)} collective-permute-done((bf16[64,128]{1,0:T(8,128)(2,1)S(1)}, bf16[64,128]{1,0:T(8,128)(2,1)S(1)}, u32[]{:S(2)}, u32[]{:S(2)}) %collective-permute-start.19) | collective-permute-done | bytes 16416 | tf_op jit(solution)/shard_map/ppermute | solution.py:74
  40.0 1.1 %collective-permute-start.22 = (bf16[400,128]{1,0:T(8,128)(2,1)S(1)}, bf16[400,128]{1,0:T(8,128)(2,1)S(1)}, u32[]{:S(2)}, u32[]{:S(2)}) collective-permute-start(bf16[400,128]{1,0:T(8,128)(2,1)S(1)} %get-tuple-element.105.refs_0_), channel_id=1, source_target_pairs={{0,2},{1,0},{2,3},{3,1},{4,6},{5,4},{6,7},{7,5},{8,10},{9,8},{10,1... | collective-permute-start | bytes 307208 | tf_op jit(solution)/shard_map/ppermute | solution.py:86
  41.1 1.4 %collective-permute-start.21 = (bf16[400,128]{1,0:T(8,128)(2,1)S(1)}, bf16[400,128]{1,0:T(8,128)(2,1)S(1)}, u32[]{:S(2)}, u32[]{:S(2)}) collective-permute-start(bf16[400,128]{1,0:T(8,128)(2,1)S(1)} %get-tuple-element.105.refs_0_), channel_id=1, source_target_pairs={{0,3},{1,2},{2,1},{3,0},{4,7},{5,6},{6,5},{7,4},{8,11},{9,10},{10,... | collective-permute-start | bytes 307208 | tf_op jit(solution)/shard_map/ppermute | solution.py:86
  42.4 0.5 collective-permute-start.20
  42.9 2.1 %collective-permute-done.22.refs_3_ = bf16[400,128]{1,0:T(8,128)(2,1)S(1)} collective-permute-done((bf16[400,128]{1,0:T(8,128)(2,1)S(1)}, bf16[400,128]{1,0:T(8,128)(2,1)S(1)}, u32[]{:S(2)}, u32[]{:S(2)}) %collective-permute-start.22) | collective-permute-done | bytes 102432 | tf_op jit(solution)/shard_map/ppermute | solution.py:86
  45.0 3.4 %collective-permute-done.21.refs_2_ = bf16[400,128]{1,0:T(8,128)(2,1)S(1)} collective-permute-done((bf16[400,128]{1,0:T(8,128)(2,1)S(1)}, bf16[400,128]{1,0:T(8,128)(2,1)S(1)}, u32[]{:S(2)}, u32[]{:S(2)}) %collective-permute-start.21) | collective-permute-done | bytes 102432 | tf_op jit(solution)/shard_map/ppermute | solution.py:86
  48.4 2.4 %collective-permute-done.20.refs_1_ = bf16[400,128]{1,0:T(8,128)(2,1)S(1)} collective-permute-done((bf16[400,128]{1,0:T(8,128)(2,1)S(1)}, bf16[400,128]{1,0:T(8,128)(2,1)S(1)}, u32[]{:S(2)}, u32[]{:S(2)}) %collective-permute-start.20) | collective-permute-done | bytes 102432 | tf_op jit(solution)/shard_map/ppermute | solution.py:86
  50.8 0.1 shard_map.53
  50.9 1.6 %collective-permute-start.24 = (bf16[400,128]{1,0:T(8,128)(2,1)S(1)}, bf16[400,128]{1,0:T(8,128)(2,1)S(1)}, u32[]{:S(2)}, u32[]{:S(2)}) collective-permute-start(bf16[400,128]{1,0:T(8,128)(2,1)S(1)} %get-tuple-element.103.refs_0_), channel_id=1, source_target_pairs={{0,8},{4,12},{8,0},{12,4},{16,24},{20,28},{24,16},{28,20},{1,9},{5... | collective-permute-start | bytes 307208 | tf_op jit(solution)/shard_map/ppermute | solution.py:74
  52.4 1.5 %collective-permute-start.28 = (bf16[336,128]{1,0:T(8,128)(2,1)S(1)}, bf16[336,128]{1,0:T(8,128)(2,1)S(1)}, u32[]{:S(2)}, u32[]{:S(2)}) collective-permute-start(bf16[336,128]{1,0:T(8,128)(2,1)S(1)} %get-tuple-element.104), channel_id=1, source_target_pairs={{0,24},{4,28},{8,16},{12,20},{16,8},{20,12},{24,0},{28,4},{1,25},{... | collective-permute-start | bytes 258056 | tf_op jit(solution)/shard_map/ppermute | solution.py:74
  53.9 0.5 collective-permute-start.26
  54.4 2.1 %collective-permute-done.24.refs_2_ = bf16[400,128]{1,0:T(8,128)(2,1)S(1)} collective-permute-done((bf16[400,128]{1,0:T(8,128)(2,1)S(1)}, bf16[400,128]{1,0:T(8,128)(2,1)S(1)}, u32[]{:S(2)}, u32[]{:S(2)}) %collective-permute-start.24) | collective-permute-done | bytes 102432 | tf_op jit(solution)/shard_map/ppermute | solution.py:74
  56.5 0.0 collective-permute-start.25
  56.5 1.3 %collective-permute-done.28.refs_6_ = bf16[336,128]{1,0:T(8,128)(2,1)S(1)} collective-permute-done((bf16[336,128]{1,0:T(8,128)(2,1)S(1)}, bf16[336,128]{1,0:T(8,128)(2,1)S(1)}, u32[]{:S(2)}, u32[]{:S(2)}) %collective-permute-start.28) | collective-permute-done | bytes 86048 | tf_op jit(solution)/shard_map/ppermute | solution.py:74
  57.8 0.0 collective-permute-start.29
  57.8 0.5 collective-permute-done.26.refs_4_
  58.4 0.7 %collective-permute-done.29.refs_7_ = bf16[336,128]{1,0:T(8,128)(2,1)S(1)} collective-permute-done((bf16[336,128]{1,0:T(8,128)(2,1)S(1)}, bf16[336,128]{1,0:T(8,128)(2,1)S(1)}, u32[]{:S(2)}, u32[]{:S(2)}) %collective-permute-start.29) | collective-permute-done | bytes 86048 | tf_op jit(solution)/shard_map/ppermute | solution.py:74
  59.1 0.5 collective-permute-done.27.refs_5_
  59.7 2.3 %shard_map.54 = f32[32,128]{1,0:T(8,128)} custom-call(bf16[16,128]{1,0:T(8,128)(2,1)S(1)} %get-tuple-element.85.refs_0_.notes_ref, bf16[400,128]{1,0:T(8,128)(2,1)S(1)} %get-tuple-element.103.refs_0_, bf16[400,128]{1,0:T(8,128)(2,1)S(1)} %collective-permute-done.23.refs_1_, bf16[400,128]{1,0:T(8,128)(2,1)S(1)} %collective-permute-done.24.refs_2_, ...), custom_call_target="tpu_custom_call" | custom-call | tf_op jit(solution)/shard_map/pallas_call | solution.py:106
  (15 shorter events, 0.1 us)
Async XLA Ops:
  0.0 15.0 %copy-start = (bf16[1,1024,512]{2,1,0:T(8,128)(2,1)S(1)}, bf16[1,1024,512]{2,1,0:T(8,128)(2,1)}, u32[]{:S(2)}) copy-start(bf16[1,1024,512]{2,1,0:T(8,128)(2,1)} %param.6) | copy-start | bytes 3145732
  1.4 8.5 %collective-permute-start.7 = (bf16[528,128]{1,0:T(8,128)(2,1)S(1)}, bf16[528,128]{1,0:T(8,128)(2,1)S(1)}, u32[]{:S(2)}, u32[]{:S(2)}) collective-permute-start(bf16[528,128]{1,0:T(8,128)(2,1)S(1)} %get-tuple-element.86), channel_id=1, source_target_pairs={{0,1},{1,3},{2,0},{3,2},{4,5},{5,7},{6,4},{7,6},{8,9},{9,11},{10,8... | collective-permute-start | bytes 405512 | tf_op jit(solution)/shard_map/ppermute | solution.py:86
  4.5 9.9 %collective-permute-start.8 = (bf16[528,128]{1,0:T(8,128)(2,1)S(1)}, bf16[528,128]{1,0:T(8,128)(2,1)S(1)}, u32[]{:S(2)}, u32[]{:S(2)}) collective-permute-start(bf16[528,128]{1,0:T(8,128)(2,1)S(1)} %get-tuple-element.87), channel_id=1, source_target_pairs={{0,3},{1,2},{2,1},{3,0},{4,7},{5,6},{6,5},{7,4},{8,11},{9,10},{10,... | collective-permute-start | bytes 405512 | tf_op jit(solution)/shard_map/ppermute | solution.py:86
  7.0 8.0 %collective-permute-start.9 = (bf16[528,128]{1,0:T(8,128)(2,1)S(1)}, bf16[528,128]{1,0:T(8,128)(2,1)S(1)}, u32[]{:S(2)}, u32[]{:S(2)}) collective-permute-start(bf16[528,128]{1,0:T(8,128)(2,1)S(1)} %get-tuple-element.88), channel_id=1, source_target_pairs={{0,2},{1,0},{2,3},{3,1},{4,6},{5,4},{6,7},{7,5},{8,10},{9,8},{10,1... | collective-permute-start | bytes 405512 | tf_op jit(solution)/shard_map/ppermute | solution.py:86
  16.6 1.5 %collective-permute-start.10 = (bf16[672,128]{1,0:T(8,128)(2,1)S(1)}, bf16[672,128]{1,0:T(8,128)(2,1)S(1)}, u32[]{:S(2)}, u32[]{:S(2)}) collective-permute-start(bf16[672,128]{1,0:T(8,128)(2,1)S(1)} %get-tuple-element.90), channel_id=1, source_target_pairs={{0,4},{4,0},{8,12},{12,8},{1,5},{5,1},{9,13},{13,9},{2,6},{6,2},{1... | collective-permute-start | bytes 516104 | tf_op jit(solution)/shard_map/ppermute | solution.py:74
  18.1 21.8 %collective-permute-start.18 = (bf16[336,128]{1,0:T(8,128)(2,1)S(1)}, bf16[336,128]{1,0:T(8,128)(2,1)S(1)}, u32[]{:S(2)}, u32[]{:S(2)}) collective-permute-start(bf16[336,128]{1,0:T(8,128)(2,1)S(1)} %get-tuple-element.101), channel_id=1, source_target_pairs={{0,8},{4,12},{8,0},{12,4},{1,9},{5,13},{9,1},{13,5},{2,10},{6,14},... | collective-permute-start | bytes 258056 | tf_op jit(solution)/shard_map/ppermute | solution.py:74
  19.7 14.9 %copy-start.1 = (f32[32,1024]{1,0:T(8,128)S(1)}, f32[32,1024]{1,0:T(8,128)}, u32[]{:S(2)}) copy-start(f32[32,1024]{1,0:T(8,128)} %y_ref.3) | copy-start | bytes 393220
  19.7 3.1 %collective-permute-start.13 = (bf16[32,128]{1,0:T(8,128)(2,1)S(1)}, bf16[32,128]{1,0:T(8,128)(2,1)S(1)}, u32[]{:S(2)}, u32[]{:S(2)}) collective-permute-start(bf16[32,128]{1,0:T(8,128)(2,1)S(1)} %get-tuple-element.93.refs_0_), channel_id=1, source_target_pairs={{0,12},{4,8},{8,4},{12,0},{1,13},{5,9},{9,5},{13,1},{2,14},{6,10},... | collective-permute-start | bytes 24584 | tf_op jit(solution)/shard_map/ppermute | solution.py:74
  19.7 3.7 %collective-permute-start.12 = (bf16[32,128]{1,0:T(8,128)(2,1)S(1)}, bf16[32,128]{1,0:T(8,128)(2,1)S(1)}, u32[]{:S(2)}, u32[]{:S(2)}) collective-permute-start(bf16[32,128]{1,0:T(8,128)(2,1)S(1)} %get-tuple-element.93.refs_0_), channel_id=1, source_target_pairs={{0,8},{4,12},{8,0},{12,4},{1,9},{5,13},{9,1},{13,5},{2,10},{6,14},... | collective-permute-start | bytes 24584 | tf_op jit(solution)/shard_map/ppermute | solution.py:74
  21.2 2.2 %collective-permute-start.11 = (bf16[32,128]{1,0:T(8,128)(2,1)S(1)}, bf16[32,128]{1,0:T(8,128)(2,1)S(1)}, u32[]{:S(2)}, u32[]{:S(2)}) collective-permute-start(bf16[32,128]{1,0:T(8,128)(2,1)S(1)} %get-tuple-element.93.refs_0_), channel_id=1, source_target_pairs={{0,4},{4,0},{8,12},{12,8},{1,5},{5,1},{9,13},{13,9},{2,6},{6,2},{1... | collective-permute-start | bytes 24584 | tf_op jit(solution)/shard_map/ppermute | solution.py:74
  23.4 11.2 %copy-start.2 = (f32[32,1,1,128]{3,2,1,0:T(1,128)S(1)}, f32[32,1,1,128]{3,2,1,0:T(1,128)}, u32[]{:S(2)}) copy-start(f32[32,1,1,128]{3,2,1,0:T(1,128)} %param.8) | copy-start | bytes 49156
  23.8 7.3 %collective-permute-start.14 = (bf16[32,256]{1,0:T(8,128)(2,1)S(1)}, bf16[32,256]{1,0:T(8,128)(2,1)S(1)}, u32[]{:S(2)}, u32[]{:S(2)}) collective-permute-start(bf16[32,256]{1,0:T(8,128)(2,1)S(1)} %get-tuple-element.95), channel_id=1, source_target_pairs={{0,1},{1,3},{2,0},{3,2},{4,5},{5,7},{6,4},{7,6},{8,9},{9,11},{10,8... | collective-permute-start | bytes 49160 | tf_op jit(solution)/shard_map/ppermute | solution.py:86
  27.5 5.5 %collective-permute-start.15 = (bf16[32,256]{1,0:T(8,128)(2,1)S(1)}, bf16[32,256]{1,0:T(8,128)(2,1)S(1)}, u32[]{:S(2)}, u32[]{:S(2)}) collective-permute-start(bf16[32,256]{1,0:T(8,128)(2,1)S(1)} %get-tuple-element.96), channel_id=1, source_target_pairs={{0,3},{1,2},{2,1},{3,0},{4,7},{5,6},{6,5},{7,4},{8,11},{9,10},{10,... | collective-permute-start | bytes 49160 | tf_op jit(solution)/shard_map/ppermute | solution.py:86
  30.9 3.7 %collective-permute-start.16 = (bf16[32,256]{1,0:T(8,128)(2,1)S(1)}, bf16[32,256]{1,0:T(8,128)(2,1)S(1)}, u32[]{:S(2)}, u32[]{:S(2)}) collective-permute-start(bf16[32,256]{1,0:T(8,128)(2,1)S(1)} %get-tuple-element.97), channel_id=1, source_target_pairs={{0,2},{1,0},{2,3},{3,1},{4,6},{5,4},{6,7},{7,5},{8,10},{9,8},{10,1... | collective-permute-start | bytes 49160 | tf_op jit(solution)/shard_map/ppermute | solution.py:86
  34.8 1.3 %collective-permute-start.17 = (bf16[128,128]{1,0:T(8,128)(2,1)S(1)}, bf16[128,128]{1,0:T(8,128)(2,1)S(1)}, u32[]{:S(2)}, u32[]{:S(2)}) collective-permute-start(bf16[128,128]{1,0:T(8,128)(2,1)S(1)} %get-tuple-element.99), channel_id=1, source_target_pairs={{0,4},{4,0},{8,12},{12,8},{1,5},{5,1},{9,13},{13,9},{2,6},{6,2},{1... | collective-permute-start | bytes 98312 | tf_op jit(solution)/shard_map/ppermute | solution.py:74
  36.1 3.8 %collective-permute-start.19 = (bf16[64,128]{1,0:T(8,128)(2,1)S(1)}, bf16[64,128]{1,0:T(8,128)(2,1)S(1)}, u32[]{:S(2)}, u32[]{:S(2)}) collective-permute-start(bf16[64,128]{1,0:T(8,128)(2,1)S(1)} %get-tuple-element.102), channel_id=1, source_target_pairs={{0,8},{4,12},{8,0},{12,4},{1,9},{5,13},{9,1},{13,5},{2,10},{6,14},... | collective-permute-start | bytes 49160 | tf_op jit(solution)/shard_map/ppermute | solution.py:74
  40.0 5.1 %collective-permute-start.22 = (bf16[400,128]{1,0:T(8,128)(2,1)S(1)}, bf16[400,128]{1,0:T(8,128)(2,1)S(1)}, u32[]{:S(2)}, u32[]{:S(2)}) collective-permute-start(bf16[400,128]{1,0:T(8,128)(2,1)S(1)} %get-tuple-element.105.refs_0_), channel_id=1, source_target_pairs={{0,2},{1,0},{2,3},{3,1},{4,6},{5,4},{6,7},{7,5},{8,10},{9,8},{10,1... | collective-permute-start | bytes 307208 | tf_op jit(solution)/shard_map/ppermute | solution.py:86
  41.1 7.3 %collective-permute-start.21 = (bf16[400,128]{1,0:T(8,128)(2,1)S(1)}, bf16[400,128]{1,0:T(8,128)(2,1)S(1)}, u32[]{:S(2)}, u32[]{:S(2)}) collective-permute-start(bf16[400,128]{1,0:T(8,128)(2,1)S(1)} %get-tuple-element.105.refs_0_), channel_id=1, source_target_pairs={{0,3},{1,2},{2,1},{3,0},{4,7},{5,6},{6,5},{7,4},{8,11},{9,10},{10,... | collective-permute-start | bytes 307208 | tf_op jit(solution)/shard_map/ppermute | solution.py:86
  42.4 8.4 %collective-permute-start.20 = (bf16[400,128]{1,0:T(8,128)(2,1)S(1)}, bf16[400,128]{1,0:T(8,128)(2,1)S(1)}, u32[]{:S(2)}, u32[]{:S(2)}) collective-permute-start(bf16[400,128]{1,0:T(8,128)(2,1)S(1)} %get-tuple-element.105.refs_0_), channel_id=1, source_target_pairs={{0,1},{1,3},{2,0},{3,2},{4,5},{5,7},{6,4},{7,6},{8,9},{9,11},{10,8... | collective-permute-start | bytes 307208 | tf_op jit(solution)/shard_map/ppermute | solution.py:86
  50.9 5.6 %collective-permute-start.24 = (bf16[400,128]{1,0:T(8,128)(2,1)S(1)}, bf16[400,128]{1,0:T(8,128)(2,1)S(1)}, u32[]{:S(2)}, u32[]{:S(2)}) collective-permute-start(bf16[400,128]{1,0:T(8,128)(2,1)S(1)} %get-tuple-element.103.refs_0_), channel_id=1, source_target_pairs={{0,8},{4,12},{8,0},{12,4},{16,24},{20,28},{24,16},{28,20},{1,9},{5... | collective-permute-start | bytes 307208 | tf_op jit(solution)/shard_map/ppermute | solution.py:74
  52.4 5.4 %collective-permute-start.28 = (bf16[336,128]{1,0:T(8,128)(2,1)S(1)}, bf16[336,128]{1,0:T(8,128)(2,1)S(1)}, u32[]{:S(2)}, u32[]{:S(2)}) collective-permute-start(bf16[336,128]{1,0:T(8,128)(2,1)S(1)} %get-tuple-element.104), channel_id=1, source_target_pairs={{0,24},{4,28},{8,16},{12,20},{16,8},{20,12},{24,0},{28,4},{1,25},{... | collective-permute-start | bytes 258056 | tf_op jit(solution)/shard_map/ppermute | solution.py:74
  53.9 4.5 %collective-permute-start.26 = (bf16[336,128]{1,0:T(8,128)(2,1)S(1)}, bf16[336,128]{1,0:T(8,128)(2,1)S(1)}, u32[]{:S(2)}, u32[]{:S(2)}) collective-permute-start(bf16[336,128]{1,0:T(8,128)(2,1)S(1)} %get-tuple-element.104), channel_id=1, source_target_pairs={{0,16},{4,20},{8,24},{12,28},{16,0},{20,4},{24,8},{28,12},{1,17},{... | collective-permute-start | bytes 258056 | tf_op jit(solution)/shard_map/ppermute | solution.py:74
  54.4 4.0 %collective-permute-start.23 = (bf16[400,128]{1,0:T(8,128)(2,1)S(1)}, bf16[400,128]{1,0:T(8,128)(2,1)S(1)}, u32[]{:S(2)}, u32[]{:S(2)}) collective-permute-start(bf16[400,128]{1,0:T(8,128)(2,1)S(1)} %get-tuple-element.103.refs_0_), channel_id=1, source_target_pairs={{0,4},{4,0},{8,12},{12,8},{16,20},{20,16},{24,28},{28,24},{1,5},{5... | collective-permute-start | bytes 307208 | tf_op jit(solution)/shard_map/ppermute | solution.py:74
  56.5 3.1 %collective-permute-start.25 = (bf16[400,128]{1,0:T(8,128)(2,1)S(1)}, bf16[400,128]{1,0:T(8,128)(2,1)S(1)}, u32[]{:S(2)}, u32[]{:S(2)}) collective-permute-start(bf16[400,128]{1,0:T(8,128)(2,1)S(1)} %collective-permute-done.24.refs_2_), channel_id=1, source_target_pairs={{0,4},{4,0},{8,12},{12,8},{16,20},{20,16},{24,28},{28,24},{1,5},{5... | collective-permute-start | bytes 307208 | tf_op jit(solution)/shard_map/ppermute | solution.py:74
  57.8 1.3 %collective-permute-start.29 = (bf16[336,128]{1,0:T(8,128)(2,1)S(1)}, bf16[336,128]{1,0:T(8,128)(2,1)S(1)}, u32[]{:S(2)}, u32[]{:S(2)}) collective-permute-start(bf16[336,128]{1,0:T(8,128)(2,1)S(1)} %collective-permute-done.28.refs_6_), channel_id=1, source_target_pairs={{0,4},{4,0},{8,12},{12,8},{16,20},{20,16},{24,28},{28,24},{1,5},{5... | collective-permute-start | bytes 258056 | tf_op jit(solution)/shard_map/ppermute | solution.py:74
  58.4 1.3 %collective-permute-start.27 = (bf16[336,128]{1,0:T(8,128)(2,1)S(1)}, bf16[336,128]{1,0:T(8,128)(2,1)S(1)}, u32[]{:S(2)}, u32[]{:S(2)}) collective-permute-start(bf16[336,128]{1,0:T(8,128)(2,1)S(1)} %collective-permute-done.26.refs_4_), channel_id=1, source_target_pairs={{0,4},{4,0},{8,12},{12,8},{16,20},{20,16},{24,28},{28,24},{1,5},{5... | collective-permute-start | bytes 258056 | tf_op jit(solution)/shard_map/ppermute | solution.py:74

commit v8 on v7

--- a/solution.py
+++ b/solution.py
@@ -18,7 +18,7 @@
 
 
 GRAM_LIMIT = 1 << 20
-PAD = 16
+PAD = 8
 CAPACITY = 2
 VMEM_LIMIT = 12 << 20
 
@@ -339,9 +339,10 @@
     for i, layout in enumerate(layouts):
         at = 0
         for size, pair in layout:
-            out[to : to + size] = summed(parts[i :: len(layouts)], at, size, pair)
+            place = out.shape[0] - size if pair == 1 else to
+            out[place : place + size] = summed(parts[i :: len(layouts)], at, size, pair)
             at += size
-            to += size
+            to += 0 if pair == 1 else size
 
 
 def total_body(layout, *refs):
@@ -385,23 +386,16 @@
                 lower = jnp.where(rows > cols, block, jnp.zeros_like(block))
                 put(g, r, r, upper + upper.T)
                 put(g, s, s, lower + lower.T)
-        per = slots // n_base
-        wide = (full[0].shape[0] - g_rows - per * PAD) // (2 * per)
-
-        def gather(at, pitch):
-            values = []
-            for r in range(slots):
-                v = full[r // per][at + (r % per) * pitch :][:wide].astype(jnp.float32)
-                values.append(v[:chans] + v[chans:] if wide > chans else v)
-            return jnp.concatenate(values, axis=1)
-
-        datas.append(gather(g_rows, wide + PAD))
-        states.append(gather(g_rows + per * (wide + PAD), wide))
-        tails = []
-        for r in range(slots):
-            v = full[r // per][g_rows + (r % per) * (wide + PAD) + wide :][:PAD].astype(jnp.float32)
-            tails.append(v[0:1] + v[1:2])
-        diags.append(jnp.concatenate(tails, axis=1))
+        wide = (full[0].shape[0] - g_rows - PAD) // 2
+
+        def gather(at):
+            values = [v[at : at + wide].astype(jnp.float32) for v in full]
+            return jnp.concatenate([v[:chans] + v[chans:] if wide > chans else v for v in values], axis=1)
+
+        datas.append(gather(g_rows))
+        states.append(gather(g_rows + wide))
+        tails = [v[g_rows + 2 * wide :].astype(jnp.float32) for v in full]
+        diags.append(jnp.concatenate([t[0:1] + t[1:2] for t in tails], axis=1))
     tile = lambda v, r: v[:, r * TILE : (r + 1) * TILE]
     for step in range(ITERS):
         parts = [[], []]
@@ -474,8 +468,9 @@
     preds = [firsts[0]] + send(firsts[1:])
 
     per = slots // n_base
-    gram_layout = [(pack_rows(slots, n_base), 0)] + [(2 * chans, chans), (PAD, 1)] * per
-    side_layout = [(2 * chans, chans)] * per
+    gram_layout = [(pack_rows(slots, n_base), 0), (2 * chans, chans), (PAD, 1)]
+    side_layout = [(2 * chans, chans)]
+    total_layout = [gram_layout[0], gram_layout[1], *side_layout, gram_layout[2]]
     layouts = [gram_layout, side_layout]
     heights = [sum(size for size, _ in layout) for layout in layouts]
     chunk = shape((sum(heights), TILE), bf16)
@@ -516,7 +511,7 @@
     pieces = base_sum(parts)
     part = lax.cond(crowded != 0, lambda: join(base_sum(parts + rest())), lambda: join(pieces))
     total, brief = call(
-        functools.partial(total_body, gram_layout + side_layout), [chunk, short], [part] + send([part] * (n_pix - 1))
+        functools.partial(total_body, total_layout), [chunk, short], [part] + send([part] * (n_pix - 1))
     )
 
     axes = ("freq", "base")
@@ -547,7 +542,8 @@
         and (slots * TILE) ** 2 <= GRAM_LIMIT
         and n_base & (n_base - 1) == 0
         and n_pix & (n_pix - 1) == 0
-        and slots % n_base == 0
+        and slots == n_base
+        and n_base <= PAD - 2
         and slots % 2 == 0
         and len(pairs(slots)) * TILE % (n_base * 16) == 0
         and m_dev % (n_pix * TILE) == 0

time: 62.1 us -> 61.7 us (level)
  no operation moved by 1% of the time
where the time goes in v8:
time: 61.7 us; the launch traced here: 61.5 us
  waiting for transfers between devices  28.2 us (46%)
  starting transfers between devices  25.9 us (42%)
  Pallas kernels  6.61 us (11%)
  between operations  0.74 us (1%)
    ppermute x9, waiting for transfers between devices, send(): got.append(lax.ppermute(piece, 'pix', list(enumerate(route))))  17.7 us
    ppermute x9, starting transfers between devices, send(): got.append(lax.ppermute(piece, 'pix', list(enumerate(route))))  17.2 us
    ppermute x14, waiting for transfers between devices, swap(): return lax.ppermute(value, axis, [(i, i ^ offset) for i in range(size)])  10.5 us
    ppermute x14, starting transfers between devices, swap(): return lax.ppermute(value, axis, [(i, i ^ offset) for i in range(size)])  8.76 us
    pallas_call x10, Pallas kernels, call(): pl.pallas_call(body, out_shape=out_shape, in_specs=specs, out_specs=out_s...  6.61 us
  transfers between devices with their start and end apart: 23, of which 19 were waited for; matrix products, arithmetic and copies ran while one was open for 0% of the time, Pallas kernels for 2%

profile of v8, /device:TPU:0, one launch (start us, length us, event | category | flops | bytes accessed | tf_op | source)
XLA Modules:
  0.0 61.5 jit_solution(12043281464409229962)
XLA Ops:
  0.0 1.4 %shard_map.46 = (bf16[520,128]{1,0:T(8,128)(2,1)S(1)}, bf16[520,128]{1,0:T(8,128)(2,1)S(1)}, bf16[520,128]{1,0:T(8,128)(2,1)S(1)}, bf16[8,128]{1,0:T(8,128)(2,1)S(1)}, bf16[32,128]{1,0:T(8,128)(2,1)S(1)}) custom-call(s32[4,6]{1,0:T(4,128)} %bitcast.14, bf16[1024,512]{1,0:T(8,128)(2,1)} %bitcast.7, f32[32,128]{1,0:T(8,128)} %bitcast.11), custom_call_target="tpu_custom_call" | custom-call | tf_op jit(solution)/shard_map/pallas_call | solution.py:106
  1.4 3.1 %collective-permute-start.7 = (bf16[520,128]{1,0:T(8,128)(2,1)S(1)}, bf16[520,128]{1,0:T(8,128)(2,1)S(1)}, u32[]{:S(2)}, u32[]{:S(2)}) collective-permute-start(bf16[520,128]{1,0:T(8,128)(2,1)S(1)} %get-tuple-element.86), channel_id=1, source_target_pairs={{0,1},{1,3},{2,0},{3,2},{4,5},{5,7},{6,4},{7,6},{8,9},{9,11},{10,8... | collective-permute-start | bytes 399368 | tf_op jit(solution)/shard_map/ppermute | solution.py:86
  4.5 2.5 %collective-permute-start.8 = (bf16[520,128]{1,0:T(8,128)(2,1)S(1)}, bf16[520,128]{1,0:T(8,128)(2,1)S(1)}, u32[]{:S(2)}, u32[]{:S(2)}) collective-permute-start(bf16[520,128]{1,0:T(8,128)(2,1)S(1)} %get-tuple-element.87), channel_id=1, source_target_pairs={{0,3},{1,2},{2,1},{3,0},{4,7},{5,6},{6,5},{7,4},{8,11},{9,10},{10,... | collective-permute-start | bytes 399368 | tf_op jit(solution)/shard_map/ppermute | solution.py:86
  7.0 1.6 %collective-permute-start.9 = (bf16[520,128]{1,0:T(8,128)(2,1)S(1)}, bf16[520,128]{1,0:T(8,128)(2,1)S(1)}, u32[]{:S(2)}, u32[]{:S(2)}) collective-permute-start(bf16[520,128]{1,0:T(8,128)(2,1)S(1)} %get-tuple-element.88), channel_id=1, source_target_pairs={{0,2},{1,0},{2,3},{3,1},{4,6},{5,4},{6,7},{7,5},{8,10},{9,8},{10,1... | collective-permute-start | bytes 399368 | tf_op jit(solution)/shard_map/ppermute | solution.py:86
  8.6 1.2 %collective-permute-done.7.refs_1_.refs_0_ = bf16[520,128]{1,0:T(8,128)(2,1)S(1)} collective-permute-done((bf16[520,128]{1,0:T(8,128)(2,1)S(1)}, bf16[520,128]{1,0:T(8,128)(2,1)S(1)}, u32[]{:S(2)}, u32[]{:S(2)}) %collective-permute-start.7) | collective-permute-done | bytes 133152 | tf_op jit(solution)/shard_map/ppermute | solution.py:86
  9.8 4.6 %collective-permute-done.8.refs_2_.refs_1_ = bf16[520,128]{1,0:T(8,128)(2,1)S(1)} collective-permute-done((bf16[520,128]{1,0:T(8,128)(2,1)S(1)}, bf16[520,128]{1,0:T(8,128)(2,1)S(1)}, u32[]{:S(2)}, u32[]{:S(2)}) %collective-permute-start.8) | collective-permute-done | bytes 133152 | tf_op jit(solution)/shard_map/ppermute | solution.py:86
  14.4 0.5 collective-permute-done.9.refs_3_.refs_2_
  14.9 1.5 %shard_map.48 = (bf16[256,512]{1,0:T(8,128)(2,1)S(1)}, bf16[656,128]{1,0:T(8,128)(2,1)S(1)}, bf16[656,128]{1,0:T(8,128)(2,1)S(1)}) custom-call(f32[32,1024]{1,0:T(8,128)} %y_ref.3, bf16[1024,512]{1,0:T(8,128)(2,1)S(1)} %bitcast.8, bf16[8,128]{1,0:T(8,128)(2,1)S(1)} %get-tuple-element.85.refs_0_.notes_ref, ...), custom_call_target="tpu_custom_call" | custom-call | tf_op jit(solution)/shard_map/pallas_call | solution.py:106
  16.4 0.1 collective-permute-start.10
  16.5 1.4 %collective-permute-done.10.got_ref = bf16[656,128]{1,0:T(8,128)(2,1)S(1)} collective-permute-done((bf16[656,128]{1,0:T(8,128)(2,1)S(1)}, bf16[656,128]{1,0:T(8,128)(2,1)S(1)}, u32[]{:S(2)}, u32[]{:S(2)}) %collective-permute-start.10) | collective-permute-done | bytes 167968 | tf_op jit(solution)/shard_map/ppermute | solution.py:74
  17.9 0.1 shard_map.49
  17.9 1.6 %collective-permute-start.18 = (bf16[328,128]{1,0:T(8,128)(2,1)S(1)}, bf16[328,128]{1,0:T(8,128)(2,1)S(1)}, u32[]{:S(2)}, u32[]{:S(2)}) collective-permute-start(bf16[328,128]{1,0:T(8,128)(2,1)S(1)} %get-tuple-element.101), channel_id=1, source_target_pairs={{0,8},{4,12},{8,0},{12,4},{1,9},{5,13},{9,1},{13,5},{2,10},{6,14},... | collective-permute-start | bytes 251912 | tf_op jit(solution)/shard_map/ppermute | solution.py:74
  19.6 0.0 collective-permute-start.13
  19.6 1.5 %collective-permute-start.12 = (bf16[32,128]{1,0:T(8,128)(2,1)S(1)}, bf16[32,128]{1,0:T(8,128)(2,1)S(1)}, u32[]{:S(2)}, u32[]{:S(2)}) collective-permute-start(bf16[32,128]{1,0:T(8,128)(2,1)S(1)} %get-tuple-element.93.refs_0_), channel_id=1, source_target_pairs={{0,8},{4,12},{8,0},{12,4},{1,9},{5,13},{9,1},{13,5},{2,10},{6,14},... | collective-permute-start | bytes 24584 | tf_op jit(solution)/shard_map/ppermute | solution.py:74
  21.1 0.4 collective-permute-start.11
  21.4 1.3 %collective-permute-done.13.refs_3_ = bf16[32,128]{1,0:T(8,128)(2,1)S(1)} collective-permute-done((bf16[32,128]{1,0:T(8,128)(2,1)S(1)}, bf16[32,128]{1,0:T(8,128)(2,1)S(1)}, u32[]{:S(2)}, u32[]{:S(2)}) %collective-permute-start.13) | collective-permute-done | bytes 8224 | tf_op jit(solution)/shard_map/ppermute | solution.py:74
  22.7 0.5 collective-permute-done.12.refs_2_
  23.2 0.4 shard_map.50
  23.7 3.7 %collective-permute-start.14 = (bf16[32,256]{1,0:T(8,128)(2,1)S(1)}, bf16[32,256]{1,0:T(8,128)(2,1)S(1)}, u32[]{:S(2)}, u32[]{:S(2)}) collective-permute-start(bf16[32,256]{1,0:T(8,128)(2,1)S(1)} %get-tuple-element.95), channel_id=1, source_target_pairs={{0,1},{1,3},{2,0},{3,2},{4,5},{5,7},{6,4},{7,6},{8,9},{9,11},{10,8... | collective-permute-start | bytes 49160 | tf_op jit(solution)/shard_map/ppermute | solution.py:86
  27.3 3.4 %collective-permute-start.15 = (bf16[32,256]{1,0:T(8,128)(2,1)S(1)}, bf16[32,256]{1,0:T(8,128)(2,1)S(1)}, u32[]{:S(2)}, u32[]{:S(2)}) collective-permute-start(bf16[32,256]{1,0:T(8,128)(2,1)S(1)} %get-tuple-element.96), channel_id=1, source_target_pairs={{0,3},{1,2},{2,1},{3,0},{4,7},{5,6},{6,5},{7,4},{8,11},{9,10},{10,... | collective-permute-start | bytes 49160 | tf_op jit(solution)/shard_map/ppermute | solution.py:86
  30.7 0.3 collective-permute-done.14.refs_1_
  30.9 1.9 %collective-permute-done.15.refs_2_ = bf16[32,256]{1,0:T(8,128)(2,1)S(1)} collective-permute-done((bf16[32,256]{1,0:T(8,128)(2,1)S(1)}, bf16[32,256]{1,0:T(8,128)(2,1)S(1)}, u32[]{:S(2)}, u32[]{:S(2)}) %collective-permute-start.15) | collective-permute-done | bytes 16416 | tf_op jit(solution)/shard_map/ppermute | solution.py:86
  32.9 1.6 %collective-permute-done.16.refs_3_ = bf16[32,256]{1,0:T(8,128)(2,1)S(1)} collective-permute-done((bf16[32,256]{1,0:T(8,128)(2,1)S(1)}, bf16[32,256]{1,0:T(8,128)(2,1)S(1)}, u32[]{:S(2)}, u32[]{:S(2)}) %collective-permute-start.16) | collective-permute-done | bytes 16416 | tf_op jit(solution)/shard_map/ppermute | solution.py:86
  34.4 0.2 shard_map.51
  34.6 0.1 collective-permute-start.17
  34.7 1.2 %collective-permute-done.17.got_ref = bf16[128,128]{1,0:T(8,128)(2,1)S(1)} collective-permute-done((bf16[128,128]{1,0:T(8,128)(2,1)S(1)}, bf16[128,128]{1,0:T(8,128)(2,1)S(1)}, u32[]{:S(2)}, u32[]{:S(2)}) %collective-permute-start.17) | collective-permute-done | bytes 32800 | tf_op jit(solution)/shard_map/ppermute | solution.py:74
  35.9 1.6 %collective-permute-start.19 = (bf16[64,128]{1,0:T(8,128)(2,1)S(1)}, bf16[64,128]{1,0:T(8,128)(2,1)S(1)}, u32[]{:S(2)}, u32[]{:S(2)}) collective-permute-start(bf16[64,128]{1,0:T(8,128)(2,1)S(1)} %get-tuple-element.102), channel_id=1, source_target_pairs={{0,8},{4,12},{8,0},{12,4},{1,9},{5,13},{9,1},{13,5},{2,10},{6,14},... | collective-permute-start | bytes 49160 | tf_op jit(solution)/shard_map/ppermute | solution.py:74
  37.5 0.6 %shard_map.47 = s32[1]{0:T(128)} custom-call(bf16[8,128]{1,0:T(8,128)(2,1)S(1)} %get-tuple-element.85.refs_0_.notes_ref, bf16[520,128]{1,0:T(8,128)(2,1)S(1)} %collective-permute-done.7.refs_1_.refs_0_, bf16[520,128]{1,0:T(8,128)(2,1)S(1)} %collective-permute-done.8.refs_2_.refs_1_, bf16[520,128]{1,0:T(8,128)(2,1)S(1)} %collective-permute-done.9.refs_3_.refs_2_), custom_call_target="tpu_custom_call" | custom-call | tf_op jit(solution)/shard_map/pallas_call | solution.py:106
  38.8 0.9 %collective-permute-done.19 = bf16[64,128]{1,0:T(8,128)(2,1)S(1)} collective-permute-done((bf16[64,128]{1,0:T(8,128)(2,1)S(1)}, bf16[64,128]{1,0:T(8,128)(2,1)S(1)}, u32[]{:S(2)}, u32[]{:S(2)}) %collective-permute-start.19) | collective-permute-done | bytes 16416 | tf_op jit(solution)/shard_map/ppermute | solution.py:74
  39.7 0.0 collective-permute-done.18
  39.8 1.1 %collective-permute-start.22 = (bf16[392,128]{1,0:T(8,128)(2,1)S(1)}, bf16[392,128]{1,0:T(8,128)(2,1)S(1)}, u32[]{:S(2)}, u32[]{:S(2)}) collective-permute-start(bf16[392,128]{1,0:T(8,128)(2,1)S(1)} %get-tuple-element.105.refs_0_), channel_id=1, source_target_pairs={{0,2},{1,0},{2,3},{3,1},{4,6},{5,4},{6,7},{7,5},{8,10},{9,8},{10,1... | collective-permute-start | bytes 301064 | tf_op jit(solution)/shard_map/ppermute | solution.py:86
  40.9 1.4 %collective-permute-start.21 = (bf16[392,128]{1,0:T(8,128)(2,1)S(1)}, bf16[392,128]{1,0:T(8,128)(2,1)S(1)}, u32[]{:S(2)}, u32[]{:S(2)}) collective-permute-start(bf16[392,128]{1,0:T(8,128)(2,1)S(1)} %get-tuple-element.105.refs_0_), channel_id=1, source_target_pairs={{0,3},{1,2},{2,1},{3,0},{4,7},{5,6},{6,5},{7,4},{8,11},{9,10},{10,... | collective-permute-start | bytes 301064 | tf_op jit(solution)/shard_map/ppermute | solution.py:86
  42.2 0.5 collective-permute-start.20
  42.7 2.0 %collective-permute-done.22.refs_3_ = bf16[392,128]{1,0:T(8,128)(2,1)S(1)} collective-permute-done((bf16[392,128]{1,0:T(8,128)(2,1)S(1)}, bf16[392,128]{1,0:T(8,128)(2,1)S(1)}, u32[]{:S(2)}, u32[]{:S(2)}) %collective-permute-start.22) | collective-permute-done | bytes 100384 | tf_op jit(solution)/shard_map/ppermute | solution.py:86
  44.8 3.4 %collective-permute-done.21.refs_2_ = bf16[392,128]{1,0:T(8,128)(2,1)S(1)} collective-permute-done((bf16[392,128]{1,0:T(8,128)(2,1)S(1)}, bf16[392,128]{1,0:T(8,128)(2,1)S(1)}, u32[]{:S(2)}, u32[]{:S(2)}) %collective-permute-start.21) | collective-permute-done | bytes 100384 | tf_op jit(solution)/shard_map/ppermute | solution.py:86
  48.1 2.3 %collective-permute-done.20.refs_1_ = bf16[392,128]{1,0:T(8,128)(2,1)S(1)} collective-permute-done((bf16[392,128]{1,0:T(8,128)(2,1)S(1)}, bf16[392,128]{1,0:T(8,128)(2,1)S(1)}, u32[]{:S(2)}, u32[]{:S(2)}) %collective-permute-start.20) | collective-permute-done | bytes 100384 | tf_op jit(solution)/shard_map/ppermute | solution.py:86
  50.4 0.1 shard_map.53
  50.5 1.6 %collective-permute-start.24 = (bf16[392,128]{1,0:T(8,128)(2,1)S(1)}, bf16[392,128]{1,0:T(8,128)(2,1)S(1)}, u32[]{:S(2)}, u32[]{:S(2)}) collective-permute-start(bf16[392,128]{1,0:T(8,128)(2,1)S(1)} %get-tuple-element.103.refs_0_), channel_id=1, source_target_pairs={{0,8},{4,12},{8,0},{12,4},{16,24},{20,28},{24,16},{28,20},{1,9},{5... | collective-permute-start | bytes 301064 | tf_op jit(solution)/shard_map/ppermute | solution.py:74
  52.1 1.5 %collective-permute-start.28 = (bf16[328,128]{1,0:T(8,128)(2,1)S(1)}, bf16[328,128]{1,0:T(8,128)(2,1)S(1)}, u32[]{:S(2)}, u32[]{:S(2)}) collective-permute-start(bf16[328,128]{1,0:T(8,128)(2,1)S(1)} %get-tuple-element.104), channel_id=1, source_target_pairs={{0,24},{4,28},{8,16},{12,20},{16,8},{20,12},{24,0},{28,4},{1,25},{... | collective-permute-start | bytes 251912 | tf_op jit(solution)/shard_map/ppermute | solution.py:74
  53.5 0.5 collective-permute-start.26
  54.1 2.0 %collective-permute-done.24.refs_2_ = bf16[392,128]{1,0:T(8,128)(2,1)S(1)} collective-permute-done((bf16[392,128]{1,0:T(8,128)(2,1)S(1)}, bf16[392,128]{1,0:T(8,128)(2,1)S(1)}, u32[]{:S(2)}, u32[]{:S(2)}) %collective-permute-start.24) | collective-permute-done | bytes 100384 | tf_op jit(solution)/shard_map/ppermute | solution.py:74
  56.1 0.0 collective-permute-start.25
  56.1 1.3 %collective-permute-done.28.refs_6_ = bf16[328,128]{1,0:T(8,128)(2,1)S(1)} collective-permute-done((bf16[328,128]{1,0:T(8,128)(2,1)S(1)}, bf16[328,128]{1,0:T(8,128)(2,1)S(1)}, u32[]{:S(2)}, u32[]{:S(2)}) %collective-permute-start.28) | collective-permute-done | bytes 84000 | tf_op jit(solution)/shard_map/ppermute | solution.py:74
  57.4 0.6 collective-permute-done.26.refs_4_
  58.0 0.0 collective-permute-start.27
  58.0 0.7 %collective-permute-done.29.refs_7_ = bf16[328,128]{1,0:T(8,128)(2,1)S(1)} collective-permute-done((bf16[328,128]{1,0:T(8,128)(2,1)S(1)}, bf16[328,128]{1,0:T(8,128)(2,1)S(1)}, u32[]{:S(2)}, u32[]{:S(2)}) %collective-permute-start.29) | collective-permute-done | bytes 84000 | tf_op jit(solution)/shard_map/ppermute | solution.py:74
  58.7 0.6 collective-permute-done.27.refs_5_
  59.3 2.3 %shard_map.54 = f32[32,128]{1,0:T(8,128)} custom-call(bf16[8,128]{1,0:T(8,128)(2,1)S(1)} %get-tuple-element.85.refs_0_.notes_ref, bf16[392,128]{1,0:T(8,128)(2,1)S(1)} %get-tuple-element.103.refs_0_, bf16[392,128]{1,0:T(8,128)(2,1)S(1)} %collective-permute-done.23.refs_1_, bf16[392,128]{1,0:T(8,128)(2,1)S(1)} %collective-permute-done.24.refs_2_, ...), custom_call_target="tpu_custom_call" | custom-call | tf_op jit(solution)/shard_map/pallas_call | solution.py:106
  (15 shorter events, 0.1 us)
Async XLA Ops:
  0.0 14.9 %copy-start = (bf16[1,1024,512]{2,1,0:T(8,128)(2,1)S(1)}, bf16[1,1024,512]{2,1,0:T(8,128)(2,1)}, u32[]{:S(2)}) copy-start(bf16[1,1024,512]{2,1,0:T(8,128)(2,1)} %param.6) | copy-start | bytes 3145732
  1.4 8.4 %collective-permute-start.7 = (bf16[520,128]{1,0:T(8,128)(2,1)S(1)}, bf16[520,128]{1,0:T(8,128)(2,1)S(1)}, u32[]{:S(2)}, u32[]{:S(2)}) collective-permute-start(bf16[520,128]{1,0:T(8,128)(2,1)S(1)} %get-tuple-element.86), channel_id=1, source_target_pairs={{0,1},{1,3},{2,0},{3,2},{4,5},{5,7},{6,4},{7,6},{8,9},{9,11},{10,8... | collective-permute-start | bytes 399368 | tf_op jit(solution)/shard_map/ppermute | solution.py:86
  4.5 9.8 %collective-permute-start.8 = (bf16[520,128]{1,0:T(8,128)(2,1)S(1)}, bf16[520,128]{1,0:T(8,128)(2,1)S(1)}, u32[]{:S(2)}, u32[]{:S(2)}) collective-permute-start(bf16[520,128]{1,0:T(8,128)(2,1)S(1)} %get-tuple-element.87), channel_id=1, source_target_pairs={{0,3},{1,2},{2,1},{3,0},{4,7},{5,6},{6,5},{7,4},{8,11},{9,10},{10,... | collective-permute-start | bytes 399368 | tf_op jit(solution)/shard_map/ppermute | solution.py:86
  7.0 7.9 %collective-permute-start.9 = (bf16[520,128]{1,0:T(8,128)(2,1)S(1)}, bf16[520,128]{1,0:T(8,128)(2,1)S(1)}, u32[]{:S(2)}, u32[]{:S(2)}) collective-permute-start(bf16[520,128]{1,0:T(8,128)(2,1)S(1)} %get-tuple-element.88), channel_id=1, source_target_pairs={{0,2},{1,0},{2,3},{3,1},{4,6},{5,4},{6,7},{7,5},{8,10},{9,8},{10,1... | collective-permute-start | bytes 399368 | tf_op jit(solution)/shard_map/ppermute | solution.py:86
  16.4 1.5 %collective-permute-start.10 = (bf16[656,128]{1,0:T(8,128)(2,1)S(1)}, bf16[656,128]{1,0:T(8,128)(2,1)S(1)}, u32[]{:S(2)}, u32[]{:S(2)}) collective-permute-start(bf16[656,128]{1,0:T(8,128)(2,1)S(1)} %get-tuple-element.90), channel_id=1, source_target_pairs={{0,4},{4,0},{8,12},{12,8},{1,5},{5,1},{9,13},{13,9},{2,6},{6,2},{1... | collective-permute-start | bytes 503816 | tf_op jit(solution)/shard_map/ppermute | solution.py:74
  17.9 21.8 %collective-permute-start.18 = (bf16[328,128]{1,0:T(8,128)(2,1)S(1)}, bf16[328,128]{1,0:T(8,128)(2,1)S(1)}, u32[]{:S(2)}, u32[]{:S(2)}) collective-permute-start(bf16[328,128]{1,0:T(8,128)(2,1)S(1)} %get-tuple-element.101), channel_id=1, source_target_pairs={{0,8},{4,12},{8,0},{12,4},{1,9},{5,13},{9,1},{13,5},{2,10},{6,14},... | collective-permute-start | bytes 251912 | tf_op jit(solution)/shard_map/ppermute | solution.py:74
  19.6 14.8 %copy-start.1 = (f32[32,1024]{1,0:T(8,128)S(1)}, f32[32,1024]{1,0:T(8,128)}, u32[]{:S(2)}) copy-start(f32[32,1024]{1,0:T(8,128)} %y_ref.3) | copy-start | bytes 393220
  19.6 3.1 %collective-permute-start.13 = (bf16[32,128]{1,0:T(8,128)(2,1)S(1)}, bf16[32,128]{1,0:T(8,128)(2,1)S(1)}, u32[]{:S(2)}, u32[]{:S(2)}) collective-permute-start(bf16[32,128]{1,0:T(8,128)(2,1)S(1)} %get-tuple-element.93.refs_0_), channel_id=1, source_target_pairs={{0,12},{4,8},{8,4},{12,0},{1,13},{5,9},{9,5},{13,1},{2,14},{6,10},... | collective-permute-start | bytes 24584 | tf_op jit(solution)/shard_map/ppermute | solution.py:74
  19.6 3.7 %collective-permute-start.12 = (bf16[32,128]{1,0:T(8,128)(2,1)S(1)}, bf16[32,128]{1,0:T(8,128)(2,1)S(1)}, u32[]{:S(2)}, u32[]{:S(2)}) collective-permute-start(bf16[32,128]{1,0:T(8,128)(2,1)S(1)} %get-tuple-element.93.refs_0_), channel_id=1, source_target_pairs={{0,8},{4,12},{8,0},{12,4},{1,9},{5,13},{9,1},{13,5},{2,10},{6,14},... | collective-permute-start | bytes 24584 | tf_op jit(solution)/shard_map/ppermute | solution.py:74
  21.1 2.2 %collective-permute-start.11 = (bf16[32,128]{1,0:T(8,128)(2,1)S(1)}, bf16[32,128]{1,0:T(8,128)(2,1)S(1)}, u32[]{:S(2)}, u32[]{:S(2)}) collective-permute-start(bf16[32,128]{1,0:T(8,128)(2,1)S(1)} %get-tuple-element.93.refs_0_), channel_id=1, source_target_pairs={{0,4},{4,0},{8,12},{12,8},{1,5},{5,1},{9,13},{13,9},{2,6},{6,2},{1... | collective-permute-start | bytes 24584 | tf_op jit(solution)/shard_map/ppermute | solution.py:74
  23.2 11.2 %copy-start.2 = (f32[32,1,1,128]{3,2,1,0:T(1,128)S(1)}, f32[32,1,1,128]{3,2,1,0:T(1,128)}, u32[]{:S(2)}) copy-start(f32[32,1,1,128]{3,2,1,0:T(1,128)} %param.8) | copy-start | bytes 49156
  23.7 7.3 %collective-permute-start.14 = (bf16[32,256]{1,0:T(8,128)(2,1)S(1)}, bf16[32,256]{1,0:T(8,128)(2,1)S(1)}, u32[]{:S(2)}, u32[]{:S(2)}) collective-permute-start(bf16[32,256]{1,0:T(8,128)(2,1)S(1)} %get-tuple-element.95), channel_id=1, source_target_pairs={{0,1},{1,3},{2,0},{3,2},{4,5},{5,7},{6,4},{7,6},{8,9},{9,11},{10,8... | collective-permute-start | bytes 49160 | tf_op jit(solution)/shard_map/ppermute | solution.py:86
  27.3 5.5 %collective-permute-start.15 = (bf16[32,256]{1,0:T(8,128)(2,1)S(1)}, bf16[32,256]{1,0:T(8,128)(2,1)S(1)}, u32[]{:S(2)}, u32[]{:S(2)}) collective-permute-start(bf16[32,256]{1,0:T(8,128)(2,1)S(1)} %get-tuple-element.96), channel_id=1, source_target_pairs={{0,3},{1,2},{2,1},{3,0},{4,7},{5,6},{6,5},{7,4},{8,11},{9,10},{10,... | collective-permute-start | bytes 49160 | tf_op jit(solution)/shard_map/ppermute | solution.py:86
  30.7 3.7 %collective-permute-start.16 = (bf16[32,256]{1,0:T(8,128)(2,1)S(1)}, bf16[32,256]{1,0:T(8,128)(2,1)S(1)}, u32[]{:S(2)}, u32[]{:S(2)}) collective-permute-start(bf16[32,256]{1,0:T(8,128)(2,1)S(1)} %get-tuple-element.97), channel_id=1, source_target_pairs={{0,2},{1,0},{2,3},{3,1},{4,6},{5,4},{6,7},{7,5},{8,10},{9,8},{10,1... | collective-permute-start | bytes 49160 | tf_op jit(solution)/shard_map/ppermute | solution.py:86
  34.6 1.3 %collective-permute-start.17 = (bf16[128,128]{1,0:T(8,128)(2,1)S(1)}, bf16[128,128]{1,0:T(8,128)(2,1)S(1)}, u32[]{:S(2)}, u32[]{:S(2)}) collective-permute-start(bf16[128,128]{1,0:T(8,128)(2,1)S(1)} %get-tuple-element.99), channel_id=1, source_target_pairs={{0,4},{4,0},{8,12},{12,8},{1,5},{5,1},{9,13},{13,9},{2,6},{6,2},{1... | collective-permute-start | bytes 98312 | tf_op jit(solution)/shard_map/ppermute | solution.py:74
  35.9 3.8 %collective-permute-start.19 = (bf16[64,128]{1,0:T(8,128)(2,1)S(1)}, bf16[64,128]{1,0:T(8,128)(2,1)S(1)}, u32[]{:S(2)}, u32[]{:S(2)}) collective-permute-start(bf16[64,128]{1,0:T(8,128)(2,1)S(1)} %get-tuple-element.102), channel_id=1, source_target_pairs={{0,8},{4,12},{8,0},{12,4},{1,9},{5,13},{9,1},{13,5},{2,10},{6,14},... | collective-permute-start | bytes 49160 | tf_op jit(solution)/shard_map/ppermute | solution.py:74
  39.8 5.0 %collective-permute-start.22 = (bf16[392,128]{1,0:T(8,128)(2,1)S(1)}, bf16[392,128]{1,0:T(8,128)(2,1)S(1)}, u32[]{:S(2)}, u32[]{:S(2)}) collective-permute-start(bf16[392,128]{1,0:T(8,128)(2,1)S(1)} %get-tuple-element.105.refs_0_), channel_id=1, source_target_pairs={{0,2},{1,0},{2,3},{3,1},{4,6},{5,4},{6,7},{7,5},{8,10},{9,8},{10,1... | collective-permute-start | bytes 301064 | tf_op jit(solution)/shard_map/ppermute | solution.py:86
  40.9 7.2 %collective-permute-start.21 = (bf16[392,128]{1,0:T(8,128)(2,1)S(1)}, bf16[392,128]{1,0:T(8,128)(2,1)S(1)}, u32[]{:S(2)}, u32[]{:S(2)}) collective-permute-start(bf16[392,128]{1,0:T(8,128)(2,1)S(1)} %get-tuple-element.105.refs_0_), channel_id=1, source_target_pairs={{0,3},{1,2},{2,1},{3,0},{4,7},{5,6},{6,5},{7,4},{8,11},{9,10},{10,... | collective-permute-start | bytes 301064 | tf_op jit(solution)/shard_map/ppermute | solution.py:86
  42.2 8.2 %collective-permute-start.20 = (bf16[392,128]{1,0:T(8,128)(2,1)S(1)}, bf16[392,128]{1,0:T(8,128)(2,1)S(1)}, u32[]{:S(2)}, u32[]{:S(2)}) collective-permute-start(bf16[392,128]{1,0:T(8,128)(2,1)S(1)} %get-tuple-element.105.refs_0_), channel_id=1, source_target_pairs={{0,1},{1,3},{2,0},{3,2},{4,5},{5,7},{6,4},{7,6},{8,9},{9,11},{10,8... | collective-permute-start | bytes 301064 | tf_op jit(solution)/shard_map/ppermute | solution.py:86
  50.5 5.6 %collective-permute-start.24 = (bf16[392,128]{1,0:T(8,128)(2,1)S(1)}, bf16[392,128]{1,0:T(8,128)(2,1)S(1)}, u32[]{:S(2)}, u32[]{:S(2)}) collective-permute-start(bf16[392,128]{1,0:T(8,128)(2,1)S(1)} %get-tuple-element.103.refs_0_), channel_id=1, source_target_pairs={{0,8},{4,12},{8,0},{12,4},{16,24},{20,28},{24,16},{28,20},{1,9},{5... | collective-permute-start | bytes 301064 | tf_op jit(solution)/shard_map/ppermute | solution.py:74
  52.1 5.4 %collective-permute-start.28 = (bf16[328,128]{1,0:T(8,128)(2,1)S(1)}, bf16[328,128]{1,0:T(8,128)(2,1)S(1)}, u32[]{:S(2)}, u32[]{:S(2)}) collective-permute-start(bf16[328,128]{1,0:T(8,128)(2,1)S(1)} %get-tuple-element.104), channel_id=1, source_target_pairs={{0,24},{4,28},{8,16},{12,20},{16,8},{20,12},{24,0},{28,4},{1,25},{... | collective-permute-start | bytes 251912 | tf_op jit(solution)/shard_map/ppermute | solution.py:74
  53.5 4.5 %collective-permute-start.26 = (bf16[328,128]{1,0:T(8,128)(2,1)S(1)}, bf16[328,128]{1,0:T(8,128)(2,1)S(1)}, u32[]{:S(2)}, u32[]{:S(2)}) collective-permute-start(bf16[328,128]{1,0:T(8,128)(2,1)S(1)} %get-tuple-element.104), channel_id=1, source_target_pairs={{0,16},{4,20},{8,24},{12,28},{16,0},{20,4},{24,8},{28,12},{1,17},{... | collective-permute-start | bytes 251912 | tf_op jit(solution)/shard_map/ppermute | solution.py:74
  54.1 3.9 %collective-permute-start.23 = (bf16[392,128]{1,0:T(8,128)(2,1)S(1)}, bf16[392,128]{1,0:T(8,128)(2,1)S(1)}, u32[]{:S(2)}, u32[]{:S(2)}) collective-permute-start(bf16[392,128]{1,0:T(8,128)(2,1)S(1)} %get-tuple-element.103.refs_0_), channel_id=1, source_target_pairs={{0,4},{4,0},{8,12},{12,8},{16,20},{20,16},{24,28},{28,24},{1,5},{5... | collective-permute-start | bytes 301064 | tf_op jit(solution)/shard_map/ppermute | solution.py:74
  56.1 3.2 %collective-permute-start.25 = (bf16[392,128]{1,0:T(8,128)(2,1)S(1)}, bf16[392,128]{1,0:T(8,128)(2,1)S(1)}, u32[]{:S(2)}, u32[]{:S(2)}) collective-permute-start(bf16[392,128]{1,0:T(8,128)(2,1)S(1)} %collective-permute-done.24.refs_2_), channel_id=1, source_target_pairs={{0,4},{4,0},{8,12},{12,8},{16,20},{20,16},{24,28},{28,24},{1,5},{5... | collective-permute-start | bytes 301064 | tf_op jit(solution)/shard_map/ppermute | solution.py:74
  57.4 1.3 %collective-permute-start.29 = (bf16[328,128]{1,0:T(8,128)(2,1)S(1)}, bf16[328,128]{1,0:T(8,128)(2,1)S(1)}, u32[]{:S(2)}, u32[]{:S(2)}) collective-permute-start(bf16[328,128]{1,0:T(8,128)(2,1)S(1)} %collective-permute-done.28.refs_6_), channel_id=1, source_target_pairs={{0,4},{4,0},{8,12},{12,8},{16,20},{20,16},{24,28},{28,24},{1,5},{5... | collective-permute-start | bytes 251912 | tf_op jit(solution)/shard_map/ppermute | solution.py:74
  58.0 1.3 %collective-permute-start.27 = (bf16[328,128]{1,0:T(8,128)(2,1)S(1)}, bf16[328,128]{1,0:T(8,128)(2,1)S(1)}, u32[]{:S(2)}, u32[]{:S(2)}) collective-permute-start(bf16[328,128]{1,0:T(8,128)(2,1)S(1)} %collective-permute-done.26.refs_4_), channel_id=1, source_target_pairs={{0,4},{4,0},{8,12},{12,8},{16,20},{20,16},{24,28},{28,24},{1,5},{5... | collective-permute-start | bytes 251912 | tf_op jit(solution)/shard_map/ppermute | solution.py:74

commit v9 on v8

--- a/solution.py
+++ b/solution.py
@@ -96,8 +96,8 @@
     return place
 
 
-def call(body, out_shape, args, scratch=(), smem=(), scalars=()):
-    specs = [pl.BlockSpec(memory_space=pltpu.SMEM if i in smem else pltpu.VMEM) for i in range(len(args))]
+def call(body, out_shape, args, scratch=(), hbm=(), scalars=()):
+    specs = [pl.BlockSpec(memory_space=pltpu.HBM if i in hbm else pltpu.VMEM) for i in range(len(args))]
     place = lambda i: pltpu.SMEM if i in scalars else pltpu.VMEM
     if isinstance(out_shape, list):
         out_specs = [pl.BlockSpec(memory_space=place(i)) for i in range(len(out_shape))]
@@ -118,13 +118,20 @@
     return high, (value - high.astype(jnp.float32)).astype(jnp.bfloat16)
 
 
-def pack_body(slots, ranks_ref, a_ref, x0_ref, *outs):
-    *outs, notes_ref, round_ref = outs
-    round_ref[...] = x0_ref[...].astype(jnp.bfloat16)
+def pack_body(slots, n_pix, ranks_hbm, a_hbm, x0_hbm, out, notes_ref, round_ref, ranks_ref, a_ref, x0_ref, sems):
     pix, base = lax.axis_index("pix"), lax.axis_index("base")
     tiles = ranks_ref.shape[0]
-    quarter = a_ref.shape[0] // (len(outs) + 1)
-    places = (outs[0].shape[0] - PAD) // quarter
+    quarter = a_ref.shape[0]
+    places = (out.shape[0] - PAD) // quarter
+    at = pl.ds(pl.multiple_of(target(pix, 1, n_pix) * quarter, quarter), quarter)
+    copies = [
+        pltpu.make_async_copy(ranks_hbm, ranks_ref, sems.at[0]),
+        pltpu.make_async_copy(a_hbm.at[at, :], a_ref, sems.at[1]),
+        pltpu.make_async_copy(x0_hbm, x0_ref, sems.at[2]),
+    ]
+    for copy in copies:
+        copy.start()
+    copies[0].wait()
     rows = lax.broadcasted_iota(jnp.int32, (PAD, TILE), 0)
     count = jnp.int32(0)
     table = []
@@ -139,29 +146,31 @@
     notes = jnp.where(rows == PAD - 1, count, notes)
     notes_ref[...] = notes.astype(jnp.float32).astype(jnp.bfloat16)
     sent = jnp.where(rows == PAD - 1, count, -1)
+    lanes = []
     for i in range(places):
         tile = jnp.int32(0)
         for j, (slot, before) in enumerate(table):
             hit = jnp.logical_and(slot >= 0, before == i)
             tile = jnp.where(hit, j, tile)
             sent = jnp.where(jnp.logical_and(rows == i, hit), slot, sent)
-        lanes = pl.ds(pl.multiple_of(tile * TILE, TILE), TILE)
-        for d, out in enumerate(outs):
-            at = pl.ds(pl.multiple_of(target(pix, d + 1, len(outs) + 1) * quarter, quarter), quarter)
-            out[i * quarter : (i + 1) * quarter, :] = a_ref[at, lanes]
-    for out in outs:
-        out[places * quarter :, :] = sent.astype(jnp.float32).astype(jnp.bfloat16)
-
-
-def rest_body(first, notes_ref, a_ref, *outs):
+        lanes.append(pl.ds(pl.multiple_of(tile * TILE, TILE), TILE))
+    out[places * quarter :, :] = sent.astype(jnp.float32).astype(jnp.bfloat16)
+    copies[1].wait()
+    for i in range(places):
+        out[i * quarter : (i + 1) * quarter, :] = a_ref[:, lanes[i]]
+    copies[2].wait()
+    round_ref[...] = x0_ref[...].astype(jnp.bfloat16)
+
+
+def rest_body(first, route, n_pix, notes_ref, a_ref, *outs):
     pix = lax.axis_index("pix")
-    quarter = a_ref.shape[0] // (len(outs) + 1)
+    quarter = a_ref.shape[0] // n_pix
     places = (outs[0].shape[0] - PAD) // quarter
     notes = notes_ref[...].astype(jnp.float32)
     tiles = a_ref.shape[1] // TILE
     rows = lax.broadcasted_iota(jnp.int32, (PAD, TILE), 0)
     before = jnp.zeros((1, TILE), jnp.float32)
-    sent = jnp.full((PAD, TILE), -1.0, jnp.float32)
+    sent = jnp.where(rows == PAD - 1, notes, -1.0)
     hits = []
     for j in range(tiles):
         slot = notes[j : j + 1]
@@ -170,7 +179,7 @@
             sent = jnp.where(jnp.logical_and(rows == i, hits[j][i]), slot, sent)
         before = before + jnp.where(slot >= 0, 1.0, 0.0)
     for d, out in enumerate(outs):
-        at = pl.ds(pl.multiple_of(target(pix, d + 1, len(outs) + 1) * quarter, quarter), quarter)
+        at = pl.ds(pl.multiple_of(target(pix, d + route, n_pix) * quarter, quarter), quarter)
         for i in range(places):
             block = a_ref[at, :TILE]
             for j in range(1, tiles):
@@ -446,17 +455,26 @@
 
     tiles = ranks.shape[0]
     places = min(CAPACITY, tiles)
-    *packed, notes, x0_round = call(
-        functools.partial(pack_body, slots),
-        pieces_of(places) + [shape((PAD, TILE), bf16), shape(x0.shape, bf16)],
+    piece, notes, x0_round = call(
+        functools.partial(pack_body, slots, n_pix),
+        [pieces_of(places)[0], shape((PAD, TILE), bf16), shape(x0.shape, bf16)],
         (ranks, a, x0),
-        smem=(0,),
-    )
-    parts = send(packed)
+        scratch=[
+            pltpu.SMEM(ranks.shape, jnp.int32),
+            pltpu.VMEM((quarter, a.shape[1]), bf16),
+            pltpu.VMEM(x0.shape, f32),
+            pltpu.SemaphoreType.DMA((3,)),
+        ],
+        hbm=(0, 1, 2),
+    )
+
+    def pack(first, places, route):
+        return call(functools.partial(rest_body, first, route, n_pix), pieces_of(places)[route - 1 :], (notes, a))
+
+    parts = send([piece, *pack(0, places, 2)])
 
     def rest():
-        packed = call(functools.partial(rest_body, places), pieces_of(tiles - places), (notes, a))
-        return send(packed)
+        return send(pack(places, tiles - places, 1))
 
     shares = [x0_round] + [swap(x0_round, "base", d) for d in range(1, n_base)]
     firsts = call(

time: 61.7 us -> 60.4 us (0.979)
  Pallas kernels: 6.61 us -> 5.46 us
    pallas_call x10 -> x11, Pallas kernels: 6.61 us -> 5.46 us  [call(): pl.pallas_call(body, out_shape=out_shape, in_specs=specs, out_specs=out_s...]
where the time goes in v9:
time: 60.4 us; the launch traced here: 60.3 us
  waiting for transfers between devices  28.1 us (47%)
  starting transfers between devices  26 us (43%)
  Pallas kernels  5.46 us (9%)
  between operations  0.74 us (1%)
    ppermute x9, waiting for transfers between devices, send(): got.append(lax.ppermute(piece, 'pix', list(enumerate(route))))  17.6 us
    ppermute x9, starting transfers between devices, send(): got.append(lax.ppermute(piece, 'pix', list(enumerate(route))))  17.2 us
    ppermute x14, waiting for transfers between devices, swap(): return lax.ppermute(value, axis, [(i, i ^ offset) for i in range(size)])  10.5 us
    ppermute x14, starting transfers between devices, swap(): return lax.ppermute(value, axis, [(i, i ^ offset) for i in range(size)])  8.76 us
    pallas_call x11, Pallas kernels, call(): pl.pallas_call(body, out_shape=out_shape, in_specs=specs, out_specs=out_s...  5.46 us
  transfers between devices with their start and end apart: 23, of which 19 were waited for; matrix products, arithmetic and copies ran while one was open for 0% of the time, Pallas kernels for 2%

profile of v9, /device:TPU:0, one launch (start us, length us, event | category | flops | bytes accessed | tf_op | source)
XLA Modules:
  0.0 60.3 jit_solution(3459356902650175800)
XLA Ops:
  0.0 1.1 %shard_map.46 = (bf16[520,128]{1,0:T(8,128)(2,1)S(1)}, bf16[8,128]{1,0:T(8,128)(2,1)S(1)}, bf16[32,128]{1,0:T(8,128)(2,1)S(1)}) custom-call(s32[4,6]{1,0:T(4,128)} %bitcast.15, bf16[1024,512]{1,0:T(8,128)(2,1)} %bitcast.7, f32[32,128]{1,0:T(8,128)} %bitcast.12), custom_call_target="tpu_custom_call" | custom-call | tf_op jit(solution)/shard_map/pallas_call | solution.py:106
  1.1 3.1 %collective-permute-start.7 = (bf16[520,128]{1,0:T(8,128)(2,1)S(1)}, bf16[520,128]{1,0:T(8,128)(2,1)S(1)}, u32[]{:S(2)}, u32[]{:S(2)}) collective-permute-start(bf16[520,128]{1,0:T(8,128)(2,1)S(1)} %get-tuple-element.86), channel_id=1, source_target_pairs={{0,1},{1,3},{2,0},{3,2},{4,5},{5,7},{6,4},{7,6},{8,9},{9,11},{10,8... | collective-permute-start | bytes 399368 | tf_op jit(solution)/shard_map/ppermute | solution.py:86
  4.2 0.1 shard_map.47
  4.3 2.5 %collective-permute-start.8 = (bf16[520,128]{1,0:T(8,128)(2,1)S(1)}, bf16[520,128]{1,0:T(8,128)(2,1)S(1)}, u32[]{:S(2)}, u32[]{:S(2)}) collective-permute-start(bf16[520,128]{1,0:T(8,128)(2,1)S(1)} %get-tuple-element.87), channel_id=1, source_target_pairs={{0,3},{1,2},{2,1},{3,0},{4,7},{5,6},{6,5},{7,4},{8,11},{9,10},{10,... | collective-permute-start | bytes 399368 | tf_op jit(solution)/shard_map/ppermute | solution.py:86
  6.8 1.6 %collective-permute-start.9 = (bf16[520,128]{1,0:T(8,128)(2,1)S(1)}, bf16[520,128]{1,0:T(8,128)(2,1)S(1)}, u32[]{:S(2)}, u32[]{:S(2)}) collective-permute-start(bf16[520,128]{1,0:T(8,128)(2,1)S(1)} %get-tuple-element.88), channel_id=1, source_target_pairs={{0,2},{1,0},{2,3},{3,1},{4,6},{5,4},{6,7},{7,5},{8,10},{9,8},{10,1... | collective-permute-start | bytes 399368 | tf_op jit(solution)/shard_map/ppermute | solution.py:86
  8.4 0.8 %collective-permute-done.7.refs_1_.refs_0_ = bf16[520,128]{1,0:T(8,128)(2,1)S(1)} collective-permute-done((bf16[520,128]{1,0:T(8,128)(2,1)S(1)}, bf16[520,128]{1,0:T(8,128)(2,1)S(1)}, u32[]{:S(2)}, u32[]{:S(2)}) %collective-permute-start.7) | collective-permute-done | bytes 133152 | tf_op jit(solution)/shard_map/ppermute | solution.py:86
  9.2 4.9 %collective-permute-done.8.refs_2_.refs_1_ = bf16[520,128]{1,0:T(8,128)(2,1)S(1)} collective-permute-done((bf16[520,128]{1,0:T(8,128)(2,1)S(1)}, bf16[520,128]{1,0:T(8,128)(2,1)S(1)}, u32[]{:S(2)}, u32[]{:S(2)}) %collective-permute-start.8) | collective-permute-done | bytes 133152 | tf_op jit(solution)/shard_map/ppermute | solution.py:86
  14.0 0.5 collective-permute-done.9.refs_3_.refs_2_
  14.6 0.6 %shard_map.49 = (bf16[256,512]{1,0:T(8,128)(2,1)S(1)}, bf16[656,128]{1,0:T(8,128)(2,1)S(1)}, bf16[656,128]{1,0:T(8,128)(2,1)S(1)}) custom-call(f32[32,1024]{1,0:T(8,128)S(1)} %copy-done.1, bf16[1024,512]{1,0:T(8,128)(2,1)S(1)} %bitcast.9, bf16[8,128]{1,0:T(8,128)(2,1)S(1)} %get-tuple-element.85.notes_ref.refs_0_, ...), custom_call_target="tpu_custom_call" | custom-call | tf_op jit(solution)/shard_map/pallas_call | solution.py:106
  15.2 0.1 collective-permute-start.10
  15.3 1.4 %collective-permute-done.10.got_ref = bf16[656,128]{1,0:T(8,128)(2,1)S(1)} collective-permute-done((bf16[656,128]{1,0:T(8,128)(2,1)S(1)}, bf16[656,128]{1,0:T(8,128)(2,1)S(1)}, u32[]{:S(2)}, u32[]{:S(2)}) %collective-permute-start.10) | collective-permute-done | bytes 167968 | tf_op jit(solution)/shard_map/ppermute | solution.py:74
  16.6 0.1 shard_map.50
  16.7 1.6 %collective-permute-start.18 = (bf16[328,128]{1,0:T(8,128)(2,1)S(1)}, bf16[328,128]{1,0:T(8,128)(2,1)S(1)}, u32[]{:S(2)}, u32[]{:S(2)}) collective-permute-start(bf16[328,128]{1,0:T(8,128)(2,1)S(1)} %get-tuple-element.101), channel_id=1, source_target_pairs={{0,8},{4,12},{8,0},{12,4},{1,9},{5,13},{9,1},{13,5},{2,10},{6,14},... | collective-permute-start | bytes 251912 | tf_op jit(solution)/shard_map/ppermute | solution.py:74
  18.3 0.0 collective-permute-start.13
  18.3 1.5 %collective-permute-start.12 = (bf16[32,128]{1,0:T(8,128)(2,1)S(1)}, bf16[32,128]{1,0:T(8,128)(2,1)S(1)}, u32[]{:S(2)}, u32[]{:S(2)}) collective-permute-start(bf16[32,128]{1,0:T(8,128)(2,1)S(1)} %get-tuple-element.93.refs_0_), channel_id=1, source_target_pairs={{0,8},{4,12},{8,0},{12,4},{1,9},{5,13},{9,1},{13,5},{2,10},{6,14},... | collective-permute-start | bytes 24584 | tf_op jit(solution)/shard_map/ppermute | solution.py:74
  19.8 0.4 collective-permute-start.11
  20.2 1.3 %collective-permute-done.13.refs_3_ = bf16[32,128]{1,0:T(8,128)(2,1)S(1)} collective-permute-done((bf16[32,128]{1,0:T(8,128)(2,1)S(1)}, bf16[32,128]{1,0:T(8,128)(2,1)S(1)}, u32[]{:S(2)}, u32[]{:S(2)}) %collective-permute-start.13) | collective-permute-done | bytes 8224 | tf_op jit(solution)/shard_map/ppermute | solution.py:74
  21.5 0.5 collective-permute-done.12.refs_2_
  22.0 0.0 collective-permute-done.11.refs_1_
  22.0 0.4 shard_map.51
  22.4 3.7 %collective-permute-start.14 = (bf16[32,256]{1,0:T(8,128)(2,1)S(1)}, bf16[32,256]{1,0:T(8,128)(2,1)S(1)}, u32[]{:S(2)}, u32[]{:S(2)}) collective-permute-start(bf16[32,256]{1,0:T(8,128)(2,1)S(1)} %get-tuple-element.95), channel_id=1, source_target_pairs={{0,1},{1,3},{2,0},{3,2},{4,5},{5,7},{6,4},{7,6},{8,9},{9,11},{10,8... | collective-permute-start | bytes 49160 | tf_op jit(solution)/shard_map/ppermute | solution.py:86
  26.1 3.4 %collective-permute-start.15 = (bf16[32,256]{1,0:T(8,128)(2,1)S(1)}, bf16[32,256]{1,0:T(8,128)(2,1)S(1)}, u32[]{:S(2)}, u32[]{:S(2)}) collective-permute-start(bf16[32,256]{1,0:T(8,128)(2,1)S(1)} %get-tuple-element.96), channel_id=1, source_target_pairs={{0,3},{1,2},{2,1},{3,0},{4,7},{5,6},{6,5},{7,4},{8,11},{9,10},{10,... | collective-permute-start | bytes 49160 | tf_op jit(solution)/shard_map/ppermute | solution.py:86
  29.4 0.0 collective-permute-start.16
  29.4 0.3 collective-permute-done.14.refs_1_
  29.7 1.9 %collective-permute-done.15.refs_2_ = bf16[32,256]{1,0:T(8,128)(2,1)S(1)} collective-permute-done((bf16[32,256]{1,0:T(8,128)(2,1)S(1)}, bf16[32,256]{1,0:T(8,128)(2,1)S(1)}, u32[]{:S(2)}, u32[]{:S(2)}) %collective-permute-start.15) | collective-permute-done | bytes 16416 | tf_op jit(solution)/shard_map/ppermute | solution.py:86
  31.6 1.6 %collective-permute-done.16.refs_3_ = bf16[32,256]{1,0:T(8,128)(2,1)S(1)} collective-permute-done((bf16[32,256]{1,0:T(8,128)(2,1)S(1)}, bf16[32,256]{1,0:T(8,128)(2,1)S(1)}, u32[]{:S(2)}, u32[]{:S(2)}) %collective-permute-start.16) | collective-permute-done | bytes 16416 | tf_op jit(solution)/shard_map/ppermute | solution.py:86
  33.2 0.2 shard_map.52
  33.4 0.1 collective-permute-start.17
  33.4 1.2 %collective-permute-done.17.got_ref = bf16[128,128]{1,0:T(8,128)(2,1)S(1)} collective-permute-done((bf16[128,128]{1,0:T(8,128)(2,1)S(1)}, bf16[128,128]{1,0:T(8,128)(2,1)S(1)}, u32[]{:S(2)}, u32[]{:S(2)}) %collective-permute-start.17) | collective-permute-done | bytes 32800 | tf_op jit(solution)/shard_map/ppermute | solution.py:74
  34.7 1.6 %collective-permute-start.19 = (bf16[64,128]{1,0:T(8,128)(2,1)S(1)}, bf16[64,128]{1,0:T(8,128)(2,1)S(1)}, u32[]{:S(2)}, u32[]{:S(2)}) collective-permute-start(bf16[64,128]{1,0:T(8,128)(2,1)S(1)} %get-tuple-element.102), channel_id=1, source_target_pairs={{0,8},{4,12},{8,0},{12,4},{1,9},{5,13},{9,1},{13,5},{2,10},{6,14},... | collective-permute-start | bytes 49160 | tf_op jit(solution)/shard_map/ppermute | solution.py:74
  36.2 0.6 %shard_map.48 = s32[1]{0:T(128)} custom-call(bf16[8,128]{1,0:T(8,128)(2,1)S(1)} %get-tuple-element.85.notes_ref.refs_0_, bf16[520,128]{1,0:T(8,128)(2,1)S(1)} %collective-permute-done.7.refs_1_.refs_0_, bf16[520,128]{1,0:T(8,128)(2,1)S(1)} %collective-permute-done.8.refs_2_.refs_1_, bf16[520,128]{1,0:T(8,128)(2,1)S(1)} %collective-permute-done.9.refs_3_.refs_2_), custom_call_target="tpu_custom_call" | custom-call | tf_op jit(solution)/shard_map/pallas_call | solution.py:106
  37.5 1.0 %collective-permute-done.19 = bf16[64,128]{1,0:T(8,128)(2,1)S(1)} collective-permute-done((bf16[64,128]{1,0:T(8,128)(2,1)S(1)}, bf16[64,128]{1,0:T(8,128)(2,1)S(1)}, u32[]{:S(2)}, u32[]{:S(2)}) %collective-permute-start.19) | collective-permute-done | bytes 16416 | tf_op jit(solution)/shard_map/ppermute | solution.py:74
  38.5 1.1 %collective-permute-start.22 = (bf16[392,128]{1,0:T(8,128)(2,1)S(1)}, bf16[392,128]{1,0:T(8,128)(2,1)S(1)}, u32[]{:S(2)}, u32[]{:S(2)}) collective-permute-start(bf16[392,128]{1,0:T(8,128)(2,1)S(1)} %get-tuple-element.105.refs_0_), channel_id=1, source_target_pairs={{0,2},{1,0},{2,3},{3,1},{4,6},{5,4},{6,7},{7,5},{8,10},{9,8},{10,1... | collective-permute-start | bytes 301064 | tf_op jit(solution)/shard_map/ppermute | solution.py:86
  39.6 1.4 %collective-permute-start.21 = (bf16[392,128]{1,0:T(8,128)(2,1)S(1)}, bf16[392,128]{1,0:T(8,128)(2,1)S(1)}, u32[]{:S(2)}, u32[]{:S(2)}) collective-permute-start(bf16[392,128]{1,0:T(8,128)(2,1)S(1)} %get-tuple-element.105.refs_0_), channel_id=1, source_target_pairs={{0,3},{1,2},{2,1},{3,0},{4,7},{5,6},{6,5},{7,4},{8,11},{9,10},{10,... | collective-permute-start | bytes 301064 | tf_op jit(solution)/shard_map/ppermute | solution.py:86
  41.0 0.5 collective-permute-start.20
  41.5 2.0 %collective-permute-done.22.refs_3_ = bf16[392,128]{1,0:T(8,128)(2,1)S(1)} collective-permute-done((bf16[392,128]{1,0:T(8,128)(2,1)S(1)}, bf16[392,128]{1,0:T(8,128)(2,1)S(1)}, u32[]{:S(2)}, u32[]{:S(2)}) %collective-permute-start.22) | collective-permute-done | bytes 100384 | tf_op jit(solution)/shard_map/ppermute | solution.py:86
  43.5 3.4 %collective-permute-done.21.refs_2_ = bf16[392,128]{1,0:T(8,128)(2,1)S(1)} collective-permute-done((bf16[392,128]{1,0:T(8,128)(2,1)S(1)}, bf16[392,128]{1,0:T(8,128)(2,1)S(1)}, u32[]{:S(2)}, u32[]{:S(2)}) %collective-permute-start.21) | collective-permute-done | bytes 100384 | tf_op jit(solution)/shard_map/ppermute | solution.py:86
  46.9 2.3 %collective-permute-done.20.refs_1_ = bf16[392,128]{1,0:T(8,128)(2,1)S(1)} collective-permute-done((bf16[392,128]{1,0:T(8,128)(2,1)S(1)}, bf16[392,128]{1,0:T(8,128)(2,1)S(1)}, u32[]{:S(2)}, u32[]{:S(2)}) %collective-permute-start.20) | collective-permute-done | bytes 100384 | tf_op jit(solution)/shard_map/ppermute | solution.py:86
  49.2 0.1 shard_map.54
  49.2 1.6 %collective-permute-start.24 = (bf16[392,128]{1,0:T(8,128)(2,1)S(1)}, bf16[392,128]{1,0:T(8,128)(2,1)S(1)}, u32[]{:S(2)}, u32[]{:S(2)}) collective-permute-start(bf16[392,128]{1,0:T(8,128)(2,1)S(1)} %get-tuple-element.103.refs_0_), channel_id=1, source_target_pairs={{0,8},{4,12},{8,0},{12,4},{16,24},{20,28},{24,16},{28,20},{1,9},{5... | collective-permute-start | bytes 301064 | tf_op jit(solution)/shard_map/ppermute | solution.py:74
  50.8 1.5 %collective-permute-start.28 = (bf16[328,128]{1,0:T(8,128)(2,1)S(1)}, bf16[328,128]{1,0:T(8,128)(2,1)S(1)}, u32[]{:S(2)}, u32[]{:S(2)}) collective-permute-start(bf16[328,128]{1,0:T(8,128)(2,1)S(1)} %get-tuple-element.104), channel_id=1, source_target_pairs={{0,24},{4,28},{8,16},{12,20},{16,8},{20,12},{24,0},{28,4},{1,25},{... | collective-permute-start | bytes 251912 | tf_op jit(solution)/shard_map/ppermute | solution.py:74
  52.3 0.5 collective-permute-start.26
  52.8 2.0 %collective-permute-done.24.refs_2_ = bf16[392,128]{1,0:T(8,128)(2,1)S(1)} collective-permute-done((bf16[392,128]{1,0:T(8,128)(2,1)S(1)}, bf16[392,128]{1,0:T(8,128)(2,1)S(1)}, u32[]{:S(2)}, u32[]{:S(2)}) %collective-permute-start.24) | collective-permute-done | bytes 100384 | tf_op jit(solution)/shard_map/ppermute | solution.py:74
  54.9 1.3 %collective-permute-done.28.refs_6_ = bf16[328,128]{1,0:T(8,128)(2,1)S(1)} collective-permute-done((bf16[328,128]{1,0:T(8,128)(2,1)S(1)}, bf16[328,128]{1,0:T(8,128)(2,1)S(1)}, u32[]{:S(2)}, u32[]{:S(2)}) %collective-permute-start.28) | collective-permute-done | bytes 84000 | tf_op jit(solution)/shard_map/ppermute | solution.py:74
  56.2 0.6 collective-permute-done.26.refs_4_
  56.7 0.7 %collective-permute-done.29.refs_7_ = bf16[328,128]{1,0:T(8,128)(2,1)S(1)} collective-permute-done((bf16[328,128]{1,0:T(8,128)(2,1)S(1)}, bf16[328,128]{1,0:T(8,128)(2,1)S(1)}, u32[]{:S(2)}, u32[]{:S(2)}) %collective-permute-start.29) | collective-permute-done | bytes 84000 | tf_op jit(solution)/shard_map/ppermute | solution.py:74
  57.5 0.6 collective-permute-done.27.refs_5_
  58.0 2.3 %shard_map.55 = f32[32,128]{1,0:T(8,128)} custom-call(bf16[8,128]{1,0:T(8,128)(2,1)S(1)} %get-tuple-element.85.notes_ref.refs_0_, bf16[392,128]{1,0:T(8,128)(2,1)S(1)} %get-tuple-element.103.refs_0_, bf16[392,128]{1,0:T(8,128)(2,1)S(1)} %collective-permute-done.23.refs_1_, bf16[392,128]{1,0:T(8,128)(2,1)S(1)} %collective-permute-done.24.refs_2_, ...), custom_call_target="tpu_custom_call" | custom-call | tf_op jit(solution)/shard_map/pallas_call | solution.py:106
  (16 shorter events, 0.1 us)
Async XLA Ops:
  0.0 4.2 %copy-start = (bf16[1,1024,512]{2,1,0:T(8,128)(2,1)S(1)}, bf16[1,1024,512]{2,1,0:T(8,128)(2,1)}, u32[]{:S(2)}) copy-start(bf16[1,1024,512]{2,1,0:T(8,128)(2,1)} %param.6) | copy-start | bytes 3145732
  1.1 8.1 %collective-permute-start.7 = (bf16[520,128]{1,0:T(8,128)(2,1)S(1)}, bf16[520,128]{1,0:T(8,128)(2,1)S(1)}, u32[]{:S(2)}, u32[]{:S(2)}) collective-permute-start(bf16[520,128]{1,0:T(8,128)(2,1)S(1)} %get-tuple-element.86), channel_id=1, source_target_pairs={{0,1},{1,3},{2,0},{3,2},{4,5},{5,7},{6,4},{7,6},{8,9},{9,11},{10,8... | collective-permute-start | bytes 399368 | tf_op jit(solution)/shard_map/ppermute | solution.py:86
  4.2 10.3 %copy-start.1 = (f32[32,1024]{1,0:T(8,128)S(1)}, f32[32,1024]{1,0:T(8,128)}, u32[]{:S(2)}) copy-start(f32[32,1024]{1,0:T(8,128)} %y_ref.3) | copy-start | bytes 393220
  4.3 9.7 %collective-permute-start.8 = (bf16[520,128]{1,0:T(8,128)(2,1)S(1)}, bf16[520,128]{1,0:T(8,128)(2,1)S(1)}, u32[]{:S(2)}, u32[]{:S(2)}) collective-permute-start(bf16[520,128]{1,0:T(8,128)(2,1)S(1)} %get-tuple-element.87), channel_id=1, source_target_pairs={{0,3},{1,2},{2,1},{3,0},{4,7},{5,6},{6,5},{7,4},{8,11},{9,10},{10,... | collective-permute-start | bytes 399368 | tf_op jit(solution)/shard_map/ppermute | solution.py:86
  6.8 7.7 %collective-permute-start.9 = (bf16[520,128]{1,0:T(8,128)(2,1)S(1)}, bf16[520,128]{1,0:T(8,128)(2,1)S(1)}, u32[]{:S(2)}, u32[]{:S(2)}) collective-permute-start(bf16[520,128]{1,0:T(8,128)(2,1)S(1)} %get-tuple-element.88), channel_id=1, source_target_pairs={{0,2},{1,0},{2,3},{3,1},{4,6},{5,4},{6,7},{7,5},{8,10},{9,8},{10,1... | collective-permute-start | bytes 399368 | tf_op jit(solution)/shard_map/ppermute | solution.py:86
  15.2 1.5 %collective-permute-start.10 = (bf16[656,128]{1,0:T(8,128)(2,1)S(1)}, bf16[656,128]{1,0:T(8,128)(2,1)S(1)}, u32[]{:S(2)}, u32[]{:S(2)}) collective-permute-start(bf16[656,128]{1,0:T(8,128)(2,1)S(1)} %get-tuple-element.90), channel_id=1, source_target_pairs={{0,4},{4,0},{8,12},{12,8},{1,5},{5,1},{9,13},{13,9},{2,6},{6,2},{1... | collective-permute-start | bytes 503816 | tf_op jit(solution)/shard_map/ppermute | solution.py:74
  16.7 21.8 %collective-permute-start.18 = (bf16[328,128]{1,0:T(8,128)(2,1)S(1)}, bf16[328,128]{1,0:T(8,128)(2,1)S(1)}, u32[]{:S(2)}, u32[]{:S(2)}) collective-permute-start(bf16[328,128]{1,0:T(8,128)(2,1)S(1)} %get-tuple-element.101), channel_id=1, source_target_pairs={{0,8},{4,12},{8,0},{12,4},{1,9},{5,13},{9,1},{13,5},{2,10},{6,14},... | collective-permute-start | bytes 251912 | tf_op jit(solution)/shard_map/ppermute | solution.py:74
  18.3 3.1 %collective-permute-start.13 = (bf16[32,128]{1,0:T(8,128)(2,1)S(1)}, bf16[32,128]{1,0:T(8,128)(2,1)S(1)}, u32[]{:S(2)}, u32[]{:S(2)}) collective-permute-start(bf16[32,128]{1,0:T(8,128)(2,1)S(1)} %get-tuple-element.93.refs_0_), channel_id=1, source_target_pairs={{0,12},{4,8},{8,4},{12,0},{1,13},{5,9},{9,5},{13,1},{2,14},{6,10},... | collective-permute-start | bytes 24584 | tf_op jit(solution)/shard_map/ppermute | solution.py:74
  18.3 3.7 %collective-permute-start.12 = (bf16[32,128]{1,0:T(8,128)(2,1)S(1)}, bf16[32,128]{1,0:T(8,128)(2,1)S(1)}, u32[]{:S(2)}, u32[]{:S(2)}) collective-permute-start(bf16[32,128]{1,0:T(8,128)(2,1)S(1)} %get-tuple-element.93.refs_0_), channel_id=1, source_target_pairs={{0,8},{4,12},{8,0},{12,4},{1,9},{5,13},{9,1},{13,5},{2,10},{6,14},... | collective-permute-start | bytes 24584 | tf_op jit(solution)/shard_map/ppermute | solution.py:74
  19.8 2.2 %collective-permute-start.11 = (bf16[32,128]{1,0:T(8,128)(2,1)S(1)}, bf16[32,128]{1,0:T(8,128)(2,1)S(1)}, u32[]{:S(2)}, u32[]{:S(2)}) collective-permute-start(bf16[32,128]{1,0:T(8,128)(2,1)S(1)} %get-tuple-element.93.refs_0_), channel_id=1, source_target_pairs={{0,4},{4,0},{8,12},{12,8},{1,5},{5,1},{9,13},{13,9},{2,6},{6,2},{1... | collective-permute-start | bytes 24584 | tf_op jit(solution)/shard_map/ppermute | solution.py:74
  22.0 11.2 %copy-start.2 = (f32[32,1,1,128]{3,2,1,0:T(1,128)S(1)}, f32[32,1,1,128]{3,2,1,0:T(1,128)}, u32[]{:S(2)}) copy-start(f32[32,1,1,128]{3,2,1,0:T(1,128)} %param.8) | copy-start | bytes 49156
  22.4 7.3 %collective-permute-start.14 = (bf16[32,256]{1,0:T(8,128)(2,1)S(1)}, bf16[32,256]{1,0:T(8,128)(2,1)S(1)}, u32[]{:S(2)}, u32[]{:S(2)}) collective-permute-start(bf16[32,256]{1,0:T(8,128)(2,1)S(1)} %get-tuple-element.95), channel_id=1, source_target_pairs={{0,1},{1,3},{2,0},{3,2},{4,5},{5,7},{6,4},{7,6},{8,9},{9,11},{10,8... | collective-permute-start | bytes 49160 | tf_op jit(solution)/shard_map/ppermute | solution.py:86
  26.1 5.5 %collective-permute-start.15 = (bf16[32,256]{1,0:T(8,128)(2,1)S(1)}, bf16[32,256]{1,0:T(8,128)(2,1)S(1)}, u32[]{:S(2)}, u32[]{:S(2)}) collective-permute-start(bf16[32,256]{1,0:T(8,128)(2,1)S(1)} %get-tuple-element.96), channel_id=1, source_target_pairs={{0,3},{1,2},{2,1},{3,0},{4,7},{5,6},{6,5},{7,4},{8,11},{9,10},{10,... | collective-permute-start | bytes 49160 | tf_op jit(solution)/shard_map/ppermute | solution.py:86
  29.4 3.7 %collective-permute-start.16 = (bf16[32,256]{1,0:T(8,128)(2,1)S(1)}, bf16[32,256]{1,0:T(8,128)(2,1)S(1)}, u32[]{:S(2)}, u32[]{:S(2)}) collective-permute-start(bf16[32,256]{1,0:T(8,128)(2,1)S(1)} %get-tuple-element.97), channel_id=1, source_target_pairs={{0,2},{1,0},{2,3},{3,1},{4,6},{5,4},{6,7},{7,5},{8,10},{9,8},{10,1... | collective-permute-start | bytes 49160 | tf_op jit(solution)/shard_map/ppermute | solution.py:86
  33.4 1.3 %collective-permute-start.17 = (bf16[128,128]{1,0:T(8,128)(2,1)S(1)}, bf16[128,128]{1,0:T(8,128)(2,1)S(1)}, u32[]{:S(2)}, u32[]{:S(2)}) collective-permute-start(bf16[128,128]{1,0:T(8,128)(2,1)S(1)} %get-tuple-element.99), channel_id=1, source_target_pairs={{0,4},{4,0},{8,12},{12,8},{1,5},{5,1},{9,13},{13,9},{2,6},{6,2},{1... | collective-permute-start | bytes 98312 | tf_op jit(solution)/shard_map/ppermute | solution.py:74
  34.7 3.8 %collective-permute-start.19 = (bf16[64,128]{1,0:T(8,128)(2,1)S(1)}, bf16[64,128]{1,0:T(8,128)(2,1)S(1)}, u32[]{:S(2)}, u32[]{:S(2)}) collective-permute-start(bf16[64,128]{1,0:T(8,128)(2,1)S(1)} %get-tuple-element.102), channel_id=1, source_target_pairs={{0,8},{4,12},{8,0},{12,4},{1,9},{5,13},{9,1},{13,5},{2,10},{6,14},... | collective-permute-start | bytes 49160 | tf_op jit(solution)/shard_map/ppermute | solution.py:74
  38.5 5.0 %collective-permute-start.22 = (bf16[392,128]{1,0:T(8,128)(2,1)S(1)}, bf16[392,128]{1,0:T(8,128)(2,1)S(1)}, u32[]{:S(2)}, u32[]{:S(2)}) collective-permute-start(bf16[392,128]{1,0:T(8,128)(2,1)S(1)} %get-tuple-element.105.refs_0_), channel_id=1, source_target_pairs={{0,2},{1,0},{2,3},{3,1},{4,6},{5,4},{6,7},{7,5},{8,10},{9,8},{10,1... | collective-permute-start | bytes 301064 | tf_op jit(solution)/shard_map/ppermute | solution.py:86
  39.6 7.2 %collective-permute-start.21 = (bf16[392,128]{1,0:T(8,128)(2,1)S(1)}, bf16[392,128]{1,0:T(8,128)(2,1)S(1)}, u32[]{:S(2)}, u32[]{:S(2)}) collective-permute-start(bf16[392,128]{1,0:T(8,128)(2,1)S(1)} %get-tuple-element.105.refs_0_), channel_id=1, source_target_pairs={{0,3},{1,2},{2,1},{3,0},{4,7},{5,6},{6,5},{7,4},{8,11},{9,10},{10,... | collective-permute-start | bytes 301064 | tf_op jit(solution)/shard_map/ppermute | solution.py:86
  41.0 8.2 %collective-permute-start.20 = (bf16[392,128]{1,0:T(8,128)(2,1)S(1)}, bf16[392,128]{1,0:T(8,128)(2,1)S(1)}, u32[]{:S(2)}, u32[]{:S(2)}) collective-permute-start(bf16[392,128]{1,0:T(8,128)(2,1)S(1)} %get-tuple-element.105.refs_0_), channel_id=1, source_target_pairs={{0,1},{1,3},{2,0},{3,2},{4,5},{5,7},{6,4},{7,6},{8,9},{9,11},{10,8... | collective-permute-start | bytes 301064 | tf_op jit(solution)/shard_map/ppermute | solution.py:86
  49.2 5.6 %collective-permute-start.24 = (bf16[392,128]{1,0:T(8,128)(2,1)S(1)}, bf16[392,128]{1,0:T(8,128)(2,1)S(1)}, u32[]{:S(2)}, u32[]{:S(2)}) collective-permute-start(bf16[392,128]{1,0:T(8,128)(2,1)S(1)} %get-tuple-element.103.refs_0_), channel_id=1, source_target_pairs={{0,8},{4,12},{8,0},{12,4},{16,24},{20,28},{24,16},{28,20},{1,9},{5... | collective-permute-start | bytes 301064 | tf_op jit(solution)/shard_map/ppermute | solution.py:74
  50.8 5.4 %collective-permute-start.28 = (bf16[328,128]{1,0:T(8,128)(2,1)S(1)}, bf16[328,128]{1,0:T(8,128)(2,1)S(1)}, u32[]{:S(2)}, u32[]{:S(2)}) collective-permute-start(bf16[328,128]{1,0:T(8,128)(2,1)S(1)} %get-tuple-element.104), channel_id=1, source_target_pairs={{0,24},{4,28},{8,16},{12,20},{16,8},{20,12},{24,0},{28,4},{1,25},{... | collective-permute-start | bytes 251912 | tf_op jit(solution)/shard_map/ppermute | solution.py:74
  52.3 4.5 %collective-permute-start.26 = (bf16[328,128]{1,0:T(8,128)(2,1)S(1)}, bf16[328,128]{1,0:T(8,128)(2,1)S(1)}, u32[]{:S(2)}, u32[]{:S(2)}) collective-permute-start(bf16[328,128]{1,0:T(8,128)(2,1)S(1)} %get-tuple-element.104), channel_id=1, source_target_pairs={{0,16},{4,20},{8,24},{12,28},{16,0},{20,4},{24,8},{28,12},{1,17},{... | collective-permute-start | bytes 251912 | tf_op jit(solution)/shard_map/ppermute | solution.py:74
  52.8 3.9 %collective-permute-start.23 = (bf16[392,128]{1,0:T(8,128)(2,1)S(1)}, bf16[392,128]{1,0:T(8,128)(2,1)S(1)}, u32[]{:S(2)}, u32[]{:S(2)}) collective-permute-start(bf16[392,128]{1,0:T(8,128)(2,1)S(1)} %get-tuple-element.103.refs_0_), channel_id=1, source_target_pairs={{0,4},{4,0},{8,12},{12,8},{16,20},{20,16},{24,28},{28,24},{1,5},{5... | collective-permute-start | bytes 301064 | tf_op jit(solution)/shard_map/ppermute | solution.py:74
  54.9 3.2 %collective-permute-start.25 = (bf16[392,128]{1,0:T(8,128)(2,1)S(1)}, bf16[392,128]{1,0:T(8,128)(2,1)S(1)}, u32[]{:S(2)}, u32[]{:S(2)}) collective-permute-start(bf16[392,128]{1,0:T(8,128)(2,1)S(1)} %collective-permute-done.24.refs_2_), channel_id=1, source_target_pairs={{0,4},{4,0},{8,12},{12,8},{16,20},{20,16},{24,28},{28,24},{1,5},{5... | collective-permute-start | bytes 301064 | tf_op jit(solution)/shard_map/ppermute | solution.py:74
  56.2 1.3 %collective-permute-start.29 = (bf16[328,128]{1,0:T(8,128)(2,1)S(1)}, bf16[328,128]{1,0:T(8,128)(2,1)S(1)}, u32[]{:S(2)}, u32[]{:S(2)}) collective-permute-start(bf16[328,128]{1,0:T(8,128)(2,1)S(1)} %collective-permute-done.28.refs_6_), channel_id=1, source_target_pairs={{0,4},{4,0},{8,12},{12,8},{16,20},{20,16},{24,28},{28,24},{1,5},{5... | collective-permute-start | bytes 251912 | tf_op jit(solution)/shard_map/ppermute | solution.py:74
  56.7 1.3 %collective-permute-start.27 = (bf16[328,128]{1,0:T(8,128)(2,1)S(1)}, bf16[328,128]{1,0:T(8,128)(2,1)S(1)}, u32[]{:S(2)}, u32[]{:S(2)}) collective-permute-start(bf16[328,128]{1,0:T(8,128)(2,1)S(1)} %collective-permute-done.26.refs_4_), channel_id=1, source_target_pairs={{0,4},{4,0},{8,12},{12,8},{16,20},{20,16},{24,28},{28,24},{1,5},{5... | collective-permute-start | bytes 251912 | tf_op jit(solution)/shard_map/ppermute | solution.py:74

commit v10 on v9

--- a/solution.py
+++ b/solution.py
@@ -265,14 +265,19 @@
     y = y_ref[:, pl.ds(pl.multiple_of(pix * quarter, quarter), quarter)]
     both = jnp.dot(jnp.concatenate(split(y), axis=0), a, preferred_element_type=jnp.float32)
     data = both[:chans] + both[chans:]
-    gram = lax.dot_general(a, a, (((0,), (0,)), ((), ())), preferred_element_type=jnp.float32)
+    bands = [
+        lax.dot_general(
+            columns[r], a[:, r * TILE :], (((0,), (0,)), ((), ())), preferred_element_type=jnp.float32
+        )
+        for r in range(slots)
+    ]
     rows, cols = corner()
     g_rows = pack_rows(slots, n_base)
     per = slots // n_base
     half = min(TILE, g_rows & -g_rows)
 
     def block_of(r, s):
-        return gram[r * TILE : (r + 1) * TILE, s * TILE : (s + 1) * TILE]
+        return bands[r][:, (s - r) * TILE : (s - r + 1) * TILE]
 
     n_off = slots * (slots - 1) // 2
     for i, (r, s) in enumerate(pairs(slots)):

time: 60.4 us -> 60.4 us (level)
  no operation moved by 1% of the time
where the time goes in v10:
time: 60.4 us; the launch traced here: 60.3 us
  waiting for transfers between devices  28.1 us (47%)
  starting transfers between devices  26 us (43%)
  Pallas kernels  5.43 us (9%)
  between operations  0.74 us (1%)
    ppermute x9, waiting for transfers between devices, send(): got.append(lax.ppermute(piece, 'pix', list(enumerate(route))))  17.6 us
    ppermute x9, starting transfers between devices, send(): got.append(lax.ppermute(piece, 'pix', list(enumerate(route))))  17.2 us
    ppermute x14, waiting for transfers between devices, swap(): return lax.ppermute(value, axis, [(i, i ^ offset) for i in range(size)])  10.5 us
    ppermute x14, starting transfers between devices, swap(): return lax.ppermute(value, axis, [(i, i ^ offset) for i in range(size)])  8.77 us
    pallas_call x11, Pallas kernels, call(): pl.pallas_call(body, out_shape=out_shape, in_specs=specs, out_specs=out_s...  5.43 us
  transfers between devices with their start and end apart: 23, of which 19 were waited for; matrix products, arithmetic and copies ran while one was open for 0% of the time, Pallas kernels for 2%

profile of v10, /device:TPU:0, one launch (start us, length us, event | category | flops | bytes accessed | tf_op | source)
XLA Modules:
  0.0 60.3 jit_solution(1723979666197327365)
XLA Ops:
  0.0 1.1 %shard_map.46 = (bf16[520,128]{1,0:T(8,128)(2,1)S(1)}, bf16[8,128]{1,0:T(8,128)(2,1)S(1)}, bf16[32,128]{1,0:T(8,128)(2,1)S(1)}) custom-call(s32[4,6]{1,0:T(4,128)} %bitcast.15, bf16[1024,512]{1,0:T(8,128)(2,1)} %bitcast.7, f32[32,128]{1,0:T(8,128)} %bitcast.12), custom_call_target="tpu_custom_call" | custom-call | tf_op jit(solution)/shard_map/pallas_call | solution.py:106
  1.1 3.1 %collective-permute-start.7 = (bf16[520,128]{1,0:T(8,128)(2,1)S(1)}, bf16[520,128]{1,0:T(8,128)(2,1)S(1)}, u32[]{:S(2)}, u32[]{:S(2)}) collective-permute-start(bf16[520,128]{1,0:T(8,128)(2,1)S(1)} %get-tuple-element.86), channel_id=1, source_target_pairs={{0,1},{1,3},{2,0},{3,2},{4,5},{5,7},{6,4},{7,6},{8,9},{9,11},{10,8... | collective-permute-start | bytes 399368 | tf_op jit(solution)/shard_map/ppermute | solution.py:86
  4.2 0.1 shard_map.47
  4.3 2.5 %collective-permute-start.8 = (bf16[520,128]{1,0:T(8,128)(2,1)S(1)}, bf16[520,128]{1,0:T(8,128)(2,1)S(1)}, u32[]{:S(2)}, u32[]{:S(2)}) collective-permute-start(bf16[520,128]{1,0:T(8,128)(2,1)S(1)} %get-tuple-element.87), channel_id=1, source_target_pairs={{0,3},{1,2},{2,1},{3,0},{4,7},{5,6},{6,5},{7,4},{8,11},{9,10},{10,... | collective-permute-start | bytes 399368 | tf_op jit(solution)/shard_map/ppermute | solution.py:86
  6.8 1.6 %collective-permute-start.9 = (bf16[520,128]{1,0:T(8,128)(2,1)S(1)}, bf16[520,128]{1,0:T(8,128)(2,1)S(1)}, u32[]{:S(2)}, u32[]{:S(2)}) collective-permute-start(bf16[520,128]{1,0:T(8,128)(2,1)S(1)} %get-tuple-element.88), channel_id=1, source_target_pairs={{0,2},{1,0},{2,3},{3,1},{4,6},{5,4},{6,7},{7,5},{8,10},{9,8},{10,1... | collective-permute-start | bytes 399368 | tf_op jit(solution)/shard_map/ppermute | solution.py:86
  8.4 0.8 %collective-permute-done.7.refs_1_.refs_0_ = bf16[520,128]{1,0:T(8,128)(2,1)S(1)} collective-permute-done((bf16[520,128]{1,0:T(8,128)(2,1)S(1)}, bf16[520,128]{1,0:T(8,128)(2,1)S(1)}, u32[]{:S(2)}, u32[]{:S(2)}) %collective-permute-start.7) | collective-permute-done | bytes 133152 | tf_op jit(solution)/shard_map/ppermute | solution.py:86
  9.2 4.9 %collective-permute-done.8.refs_2_.refs_1_ = bf16[520,128]{1,0:T(8,128)(2,1)S(1)} collective-permute-done((bf16[520,128]{1,0:T(8,128)(2,1)S(1)}, bf16[520,128]{1,0:T(8,128)(2,1)S(1)}, u32[]{:S(2)}, u32[]{:S(2)}) %collective-permute-start.8) | collective-permute-done | bytes 133152 | tf_op jit(solution)/shard_map/ppermute | solution.py:86
  14.0 0.5 collective-permute-done.9.refs_3_.refs_2_
  14.6 0.6 shard_map.49
  15.2 0.1 collective-permute-start.10
  15.2 1.4 %collective-permute-done.10.got_ref = bf16[656,128]{1,0:T(8,128)(2,1)S(1)} collective-permute-done((bf16[656,128]{1,0:T(8,128)(2,1)S(1)}, bf16[656,128]{1,0:T(8,128)(2,1)S(1)}, u32[]{:S(2)}, u32[]{:S(2)}) %collective-permute-start.10) | collective-permute-done | bytes 167968 | tf_op jit(solution)/shard_map/ppermute | solution.py:74
  16.6 0.1 shard_map.50
  16.7 1.6 %collective-permute-start.18 = (bf16[328,128]{1,0:T(8,128)(2,1)S(1)}, bf16[328,128]{1,0:T(8,128)(2,1)S(1)}, u32[]{:S(2)}, u32[]{:S(2)}) collective-permute-start(bf16[328,128]{1,0:T(8,128)(2,1)S(1)} %get-tuple-element.101), channel_id=1, source_target_pairs={{0,8},{4,12},{8,0},{12,4},{1,9},{5,13},{9,1},{13,5},{2,10},{6,14},... | collective-permute-start | bytes 251912 | tf_op jit(solution)/shard_map/ppermute | solution.py:74
  18.3 0.0 collective-permute-start.13
  18.3 1.5 %collective-permute-start.12 = (bf16[32,128]{1,0:T(8,128)(2,1)S(1)}, bf16[32,128]{1,0:T(8,128)(2,1)S(1)}, u32[]{:S(2)}, u32[]{:S(2)}) collective-permute-start(bf16[32,128]{1,0:T(8,128)(2,1)S(1)} %get-tuple-element.93.refs_0_), channel_id=1, source_target_pairs={{0,8},{4,12},{8,0},{12,4},{1,9},{5,13},{9,1},{13,5},{2,10},{6,14},... | collective-permute-start | bytes 24584 | tf_op jit(solution)/shard_map/ppermute | solution.py:74
  19.8 0.4 collective-permute-start.11
  20.2 1.3 %collective-permute-done.13.refs_3_ = bf16[32,128]{1,0:T(8,128)(2,1)S(1)} collective-permute-done((bf16[32,128]{1,0:T(8,128)(2,1)S(1)}, bf16[32,128]{1,0:T(8,128)(2,1)S(1)}, u32[]{:S(2)}, u32[]{:S(2)}) %collective-permute-start.13) | collective-permute-done | bytes 8224 | tf_op jit(solution)/shard_map/ppermute | solution.py:74
  21.4 0.5 collective-permute-done.12.refs_2_
  22.0 0.0 collective-permute-done.11.refs_1_
  22.0 0.4 shard_map.51
  22.4 3.7 %collective-permute-start.14 = (bf16[32,256]{1,0:T(8,128)(2,1)S(1)}, bf16[32,256]{1,0:T(8,128)(2,1)S(1)}, u32[]{:S(2)}, u32[]{:S(2)}) collective-permute-start(bf16[32,256]{1,0:T(8,128)(2,1)S(1)} %get-tuple-element.95), channel_id=1, source_target_pairs={{0,1},{1,3},{2,0},{3,2},{4,5},{5,7},{6,4},{7,6},{8,9},{9,11},{10,8... | collective-permute-start | bytes 49160 | tf_op jit(solution)/shard_map/ppermute | solution.py:86
  26.1 3.4 %collective-permute-start.15 = (bf16[32,256]{1,0:T(8,128)(2,1)S(1)}, bf16[32,256]{1,0:T(8,128)(2,1)S(1)}, u32[]{:S(2)}, u32[]{:S(2)}) collective-permute-start(bf16[32,256]{1,0:T(8,128)(2,1)S(1)} %get-tuple-element.96), channel_id=1, source_target_pairs={{0,3},{1,2},{2,1},{3,0},{4,7},{5,6},{6,5},{7,4},{8,11},{9,10},{10,... | collective-permute-start | bytes 49160 | tf_op jit(solution)/shard_map/ppermute | solution.py:86
  29.4 0.0 collective-permute-start.16
  29.4 0.3 collective-permute-done.14.refs_1_
  29.7 1.9 %collective-permute-done.15.refs_2_ = bf16[32,256]{1,0:T(8,128)(2,1)S(1)} collective-permute-done((bf16[32,256]{1,0:T(8,128)(2,1)S(1)}, bf16[32,256]{1,0:T(8,128)(2,1)S(1)}, u32[]{:S(2)}, u32[]{:S(2)}) %collective-permute-start.15) | collective-permute-done | bytes 16416 | tf_op jit(solution)/shard_map/ppermute | solution.py:86
  31.6 1.6 %collective-permute-done.16.refs_3_ = bf16[32,256]{1,0:T(8,128)(2,1)S(1)} collective-permute-done((bf16[32,256]{1,0:T(8,128)(2,1)S(1)}, bf16[32,256]{1,0:T(8,128)(2,1)S(1)}, u32[]{:S(2)}, u32[]{:S(2)}) %collective-permute-start.16) | collective-permute-done | bytes 16416 | tf_op jit(solution)/shard_map/ppermute | solution.py:86
  33.2 0.2 shard_map.52
  33.4 0.1 collective-permute-start.17
  33.4 1.2 %collective-permute-done.17.got_ref = bf16[128,128]{1,0:T(8,128)(2,1)S(1)} collective-permute-done((bf16[128,128]{1,0:T(8,128)(2,1)S(1)}, bf16[128,128]{1,0:T(8,128)(2,1)S(1)}, u32[]{:S(2)}, u32[]{:S(2)}) %collective-permute-start.17) | collective-permute-done | bytes 32800 | tf_op jit(solution)/shard_map/ppermute | solution.py:74
  34.6 1.6 %collective-permute-start.19 = (bf16[64,128]{1,0:T(8,128)(2,1)S(1)}, bf16[64,128]{1,0:T(8,128)(2,1)S(1)}, u32[]{:S(2)}, u32[]{:S(2)}) collective-permute-start(bf16[64,128]{1,0:T(8,128)(2,1)S(1)} %get-tuple-element.102), channel_id=1, source_target_pairs={{0,8},{4,12},{8,0},{12,4},{1,9},{5,13},{9,1},{13,5},{2,10},{6,14},... | collective-permute-start | bytes 49160 | tf_op jit(solution)/shard_map/ppermute | solution.py:74
  36.2 0.6 %shard_map.48 = s32[1]{0:T(128)} custom-call(bf16[8,128]{1,0:T(8,128)(2,1)S(1)} %get-tuple-element.85.notes_ref.refs_0_, bf16[520,128]{1,0:T(8,128)(2,1)S(1)} %collective-permute-done.7.refs_1_.refs_0_, bf16[520,128]{1,0:T(8,128)(2,1)S(1)} %collective-permute-done.8.refs_2_.refs_1_, bf16[520,128]{1,0:T(8,128)(2,1)S(1)} %collective-permute-done.9.refs_3_.refs_2_), custom_call_target="tpu_custom_call" | custom-call | tf_op jit(solution)/shard_map/pallas_call | solution.py:106
  37.5 0.9 %collective-permute-done.19 = bf16[64,128]{1,0:T(8,128)(2,1)S(1)} collective-permute-done((bf16[64,128]{1,0:T(8,128)(2,1)S(1)}, bf16[64,128]{1,0:T(8,128)(2,1)S(1)}, u32[]{:S(2)}, u32[]{:S(2)}) %collective-permute-start.19) | collective-permute-done | bytes 16416 | tf_op jit(solution)/shard_map/ppermute | solution.py:74
  38.5 1.1 %collective-permute-start.22 = (bf16[392,128]{1,0:T(8,128)(2,1)S(1)}, bf16[392,128]{1,0:T(8,128)(2,1)S(1)}, u32[]{:S(2)}, u32[]{:S(2)}) collective-permute-start(bf16[392,128]{1,0:T(8,128)(2,1)S(1)} %get-tuple-element.105.refs_0_), channel_id=1, source_target_pairs={{0,2},{1,0},{2,3},{3,1},{4,6},{5,4},{6,7},{7,5},{8,10},{9,8},{10,1... | collective-permute-start | bytes 301064 | tf_op jit(solution)/shard_map/ppermute | solution.py:86
  39.6 1.4 %collective-permute-start.21 = (bf16[392,128]{1,0:T(8,128)(2,1)S(1)}, bf16[392,128]{1,0:T(8,128)(2,1)S(1)}, u32[]{:S(2)}, u32[]{:S(2)}) collective-permute-start(bf16[392,128]{1,0:T(8,128)(2,1)S(1)} %get-tuple-element.105.refs_0_), channel_id=1, source_target_pairs={{0,3},{1,2},{2,1},{3,0},{4,7},{5,6},{6,5},{7,4},{8,11},{9,10},{10,... | collective-permute-start | bytes 301064 | tf_op jit(solution)/shard_map/ppermute | solution.py:86
  41.0 0.5 collective-permute-start.20
  41.5 2.0 %collective-permute-done.22.refs_3_ = bf16[392,128]{1,0:T(8,128)(2,1)S(1)} collective-permute-done((bf16[392,128]{1,0:T(8,128)(2,1)S(1)}, bf16[392,128]{1,0:T(8,128)(2,1)S(1)}, u32[]{:S(2)}, u32[]{:S(2)}) %collective-permute-start.22) | collective-permute-done | bytes 100384 | tf_op jit(solution)/shard_map/ppermute | solution.py:86
  43.5 3.4 %collective-permute-done.21.refs_2_ = bf16[392,128]{1,0:T(8,128)(2,1)S(1)} collective-permute-done((bf16[392,128]{1,0:T(8,128)(2,1)S(1)}, bf16[392,128]{1,0:T(8,128)(2,1)S(1)}, u32[]{:S(2)}, u32[]{:S(2)}) %collective-permute-start.21) | collective-permute-done | bytes 100384 | tf_op jit(solution)/shard_map/ppermute | solution.py:86
  46.9 2.3 %collective-permute-done.20.refs_1_ = bf16[392,128]{1,0:T(8,128)(2,1)S(1)} collective-permute-done((bf16[392,128]{1,0:T(8,128)(2,1)S(1)}, bf16[392,128]{1,0:T(8,128)(2,1)S(1)}, u32[]{:S(2)}, u32[]{:S(2)}) %collective-permute-start.20) | collective-permute-done | bytes 100384 | tf_op jit(solution)/shard_map/ppermute | solution.py:86
  49.2 0.1 shard_map.54
  49.2 1.6 %collective-permute-start.24 = (bf16[392,128]{1,0:T(8,128)(2,1)S(1)}, bf16[392,128]{1,0:T(8,128)(2,1)S(1)}, u32[]{:S(2)}, u32[]{:S(2)}) collective-permute-start(bf16[392,128]{1,0:T(8,128)(2,1)S(1)} %get-tuple-element.103.refs_0_), channel_id=1, source_target_pairs={{0,8},{4,12},{8,0},{12,4},{16,24},{20,28},{24,16},{28,20},{1,9},{5... | collective-permute-start | bytes 301064 | tf_op jit(solution)/shard_map/ppermute | solution.py:74
  50.8 1.5 %collective-permute-start.28 = (bf16[328,128]{1,0:T(8,128)(2,1)S(1)}, bf16[328,128]{1,0:T(8,128)(2,1)S(1)}, u32[]{:S(2)}, u32[]{:S(2)}) collective-permute-start(bf16[328,128]{1,0:T(8,128)(2,1)S(1)} %get-tuple-element.104), channel_id=1, source_target_pairs={{0,24},{4,28},{8,16},{12,20},{16,8},{20,12},{24,0},{28,4},{1,25},{... | collective-permute-start | bytes 251912 | tf_op jit(solution)/shard_map/ppermute | solution.py:74
  52.3 0.5 collective-permute-start.26
  52.8 2.0 %collective-permute-done.24.refs_2_ = bf16[392,128]{1,0:T(8,128)(2,1)S(1)} collective-permute-done((bf16[392,128]{1,0:T(8,128)(2,1)S(1)}, bf16[392,128]{1,0:T(8,128)(2,1)S(1)}, u32[]{:S(2)}, u32[]{:S(2)}) %collective-permute-start.24) | collective-permute-done | bytes 100384 | tf_op jit(solution)/shard_map/ppermute | solution.py:74
  54.8 1.3 %collective-permute-done.28.refs_6_ = bf16[328,128]{1,0:T(8,128)(2,1)S(1)} collective-permute-done((bf16[328,128]{1,0:T(8,128)(2,1)S(1)}, bf16[328,128]{1,0:T(8,128)(2,1)S(1)}, u32[]{:S(2)}, u32[]{:S(2)}) %collective-permute-start.28) | collective-permute-done | bytes 84000 | tf_op jit(solution)/shard_map/ppermute | solution.py:74
  56.2 0.6 collective-permute-done.26.refs_4_
  56.7 0.7 %collective-permute-done.29.refs_7_ = bf16[328,128]{1,0:T(8,128)(2,1)S(1)} collective-permute-done((bf16[328,128]{1,0:T(8,128)(2,1)S(1)}, bf16[328,128]{1,0:T(8,128)(2,1)S(1)}, u32[]{:S(2)}, u32[]{:S(2)}) %collective-permute-start.29) | collective-permute-done | bytes 84000 | tf_op jit(solution)/shard_map/ppermute | solution.py:74
  57.4 0.6 collective-permute-done.27.refs_5_
  58.0 2.3 %shard_map.55 = f32[32,128]{1,0:T(8,128)} custom-call(bf16[8,128]{1,0:T(8,128)(2,1)S(1)} %get-tuple-element.85.notes_ref.refs_0_, bf16[392,128]{1,0:T(8,128)(2,1)S(1)} %get-tuple-element.103.refs_0_, bf16[392,128]{1,0:T(8,128)(2,1)S(1)} %collective-permute-done.23.refs_1_, bf16[392,128]{1,0:T(8,128)(2,1)S(1)} %collective-permute-done.24.refs_2_, ...), custom_call_target="tpu_custom_call" | custom-call | tf_op jit(solution)/shard_map/pallas_call | solution.py:106
  (16 shorter events, 0.1 us)
Async XLA Ops:
  0.0 4.2 %copy-start = (bf16[1,1024,512]{2,1,0:T(8,128)(2,1)S(1)}, bf16[1,1024,512]{2,1,0:T(8,128)(2,1)}, u32[]{:S(2)}) copy-start(bf16[1,1024,512]{2,1,0:T(8,128)(2,1)} %param.6) | copy-start | bytes 3145732
  1.1 8.1 %collective-permute-start.7 = (bf16[520,128]{1,0:T(8,128)(2,1)S(1)}, bf16[520,128]{1,0:T(8,128)(2,1)S(1)}, u32[]{:S(2)}, u32[]{:S(2)}) collective-permute-start(bf16[520,128]{1,0:T(8,128)(2,1)S(1)} %get-tuple-element.86), channel_id=1, source_target_pairs={{0,1},{1,3},{2,0},{3,2},{4,5},{5,7},{6,4},{7,6},{8,9},{9,11},{10,8... | collective-permute-start | bytes 399368 | tf_op jit(solution)/shard_map/ppermute | solution.py:86
  4.2 10.3 %copy-start.1 = (f32[32,1024]{1,0:T(8,128)S(1)}, f32[32,1024]{1,0:T(8,128)}, u32[]{:S(2)}) copy-start(f32[32,1024]{1,0:T(8,128)} %y_ref.3) | copy-start | bytes 393220
  4.3 9.7 %collective-permute-start.8 = (bf16[520,128]{1,0:T(8,128)(2,1)S(1)}, bf16[520,128]{1,0:T(8,128)(2,1)S(1)}, u32[]{:S(2)}, u32[]{:S(2)}) collective-permute-start(bf16[520,128]{1,0:T(8,128)(2,1)S(1)} %get-tuple-element.87), channel_id=1, source_target_pairs={{0,3},{1,2},{2,1},{3,0},{4,7},{5,6},{6,5},{7,4},{8,11},{9,10},{10,... | collective-permute-start | bytes 399368 | tf_op jit(solution)/shard_map/ppermute | solution.py:86
  6.8 7.7 %collective-permute-start.9 = (bf16[520,128]{1,0:T(8,128)(2,1)S(1)}, bf16[520,128]{1,0:T(8,128)(2,1)S(1)}, u32[]{:S(2)}, u32[]{:S(2)}) collective-permute-start(bf16[520,128]{1,0:T(8,128)(2,1)S(1)} %get-tuple-element.88), channel_id=1, source_target_pairs={{0,2},{1,0},{2,3},{3,1},{4,6},{5,4},{6,7},{7,5},{8,10},{9,8},{10,1... | collective-permute-start | bytes 399368 | tf_op jit(solution)/shard_map/ppermute | solution.py:86
  15.2 1.5 %collective-permute-start.10 = (bf16[656,128]{1,0:T(8,128)(2,1)S(1)}, bf16[656,128]{1,0:T(8,128)(2,1)S(1)}, u32[]{:S(2)}, u32[]{:S(2)}) collective-permute-start(bf16[656,128]{1,0:T(8,128)(2,1)S(1)} %get-tuple-element.90), channel_id=1, source_target_pairs={{0,4},{4,0},{8,12},{12,8},{1,5},{5,1},{9,13},{13,9},{2,6},{6,2},{1... | collective-permute-start | bytes 503816 | tf_op jit(solution)/shard_map/ppermute | solution.py:74
  16.7 21.8 %collective-permute-start.18 = (bf16[328,128]{1,0:T(8,128)(2,1)S(1)}, bf16[328,128]{1,0:T(8,128)(2,1)S(1)}, u32[]{:S(2)}, u32[]{:S(2)}) collective-permute-start(bf16[328,128]{1,0:T(8,128)(2,1)S(1)} %get-tuple-element.101), channel_id=1, source_target_pairs={{0,8},{4,12},{8,0},{12,4},{1,9},{5,13},{9,1},{13,5},{2,10},{6,14},... | collective-permute-start | bytes 251912 | tf_op jit(solution)/shard_map/ppermute | solution.py:74
  18.3 3.1 %collective-permute-start.13 = (bf16[32,128]{1,0:T(8,128)(2,1)S(1)}, bf16[32,128]{1,0:T(8,128)(2,1)S(1)}, u32[]{:S(2)}, u32[]{:S(2)}) collective-permute-start(bf16[32,128]{1,0:T(8,128)(2,1)S(1)} %get-tuple-element.93.refs_0_), channel_id=1, source_target_pairs={{0,12},{4,8},{8,4},{12,0},{1,13},{5,9},{9,5},{13,1},{2,14},{6,10},... | collective-permute-start | bytes 24584 | tf_op jit(solution)/shard_map/ppermute | solution.py:74
  18.3 3.7 %collective-permute-start.12 = (bf16[32,128]{1,0:T(8,128)(2,1)S(1)}, bf16[32,128]{1,0:T(8,128)(2,1)S(1)}, u32[]{:S(2)}, u32[]{:S(2)}) collective-permute-start(bf16[32,128]{1,0:T(8,128)(2,1)S(1)} %get-tuple-element.93.refs_0_), channel_id=1, source_target_pairs={{0,8},{4,12},{8,0},{12,4},{1,9},{5,13},{9,1},{13,5},{2,10},{6,14},... | collective-permute-start | bytes 24584 | tf_op jit(solution)/shard_map/ppermute | solution.py:74
  19.8 2.2 %collective-permute-start.11 = (bf16[32,128]{1,0:T(8,128)(2,1)S(1)}, bf16[32,128]{1,0:T(8,128)(2,1)S(1)}, u32[]{:S(2)}, u32[]{:S(2)}) collective-permute-start(bf16[32,128]{1,0:T(8,128)(2,1)S(1)} %get-tuple-element.93.refs_0_), channel_id=1, source_target_pairs={{0,4},{4,0},{8,12},{12,8},{1,5},{5,1},{9,13},{13,9},{2,6},{6,2},{1... | collective-permute-start | bytes 24584 | tf_op jit(solution)/shard_map/ppermute | solution.py:74
  22.0 11.2 %copy-start.2 = (f32[32,1,1,128]{3,2,1,0:T(1,128)S(1)}, f32[32,1,1,128]{3,2,1,0:T(1,128)}, u32[]{:S(2)}) copy-start(f32[32,1,1,128]{3,2,1,0:T(1,128)} %param.8) | copy-start | bytes 49156
  22.4 7.3 %collective-permute-start.14 = (bf16[32,256]{1,0:T(8,128)(2,1)S(1)}, bf16[32,256]{1,0:T(8,128)(2,1)S(1)}, u32[]{:S(2)}, u32[]{:S(2)}) collective-permute-start(bf16[32,256]{1,0:T(8,128)(2,1)S(1)} %get-tuple-element.95), channel_id=1, source_target_pairs={{0,1},{1,3},{2,0},{3,2},{4,5},{5,7},{6,4},{7,6},{8,9},{9,11},{10,8... | collective-permute-start | bytes 49160 | tf_op jit(solution)/shard_map/ppermute | solution.py:86
  26.1 5.5 %collective-permute-start.15 = (bf16[32,256]{1,0:T(8,128)(2,1)S(1)}, bf16[32,256]{1,0:T(8,128)(2,1)S(1)}, u32[]{:S(2)}, u32[]{:S(2)}) collective-permute-start(bf16[32,256]{1,0:T(8,128)(2,1)S(1)} %get-tuple-element.96), channel_id=1, source_target_pairs={{0,3},{1,2},{2,1},{3,0},{4,7},{5,6},{6,5},{7,4},{8,11},{9,10},{10,... | collective-permute-start | bytes 49160 | tf_op jit(solution)/shard_map/ppermute | solution.py:86
  29.4 3.7 %collective-permute-start.16 = (bf16[32,256]{1,0:T(8,128)(2,1)S(1)}, bf16[32,256]{1,0:T(8,128)(2,1)S(1)}, u32[]{:S(2)}, u32[]{:S(2)}) collective-permute-start(bf16[32,256]{1,0:T(8,128)(2,1)S(1)} %get-tuple-element.97), channel_id=1, source_target_pairs={{0,2},{1,0},{2,3},{3,1},{4,6},{5,4},{6,7},{7,5},{8,10},{9,8},{10,1... | collective-permute-start | bytes 49160 | tf_op jit(solution)/shard_map/ppermute | solution.py:86
  33.4 1.3 %collective-permute-start.17 = (bf16[128,128]{1,0:T(8,128)(2,1)S(1)}, bf16[128,128]{1,0:T(8,128)(2,1)S(1)}, u32[]{:S(2)}, u32[]{:S(2)}) collective-permute-start(bf16[128,128]{1,0:T(8,128)(2,1)S(1)} %get-tuple-element.99), channel_id=1, source_target_pairs={{0,4},{4,0},{8,12},{12,8},{1,5},{5,1},{9,13},{13,9},{2,6},{6,2},{1... | collective-permute-start | bytes 98312 | tf_op jit(solution)/shard_map/ppermute | solution.py:74
  34.6 3.8 %collective-permute-start.19 = (bf16[64,128]{1,0:T(8,128)(2,1)S(1)}, bf16[64,128]{1,0:T(8,128)(2,1)S(1)}, u32[]{:S(2)}, u32[]{:S(2)}) collective-permute-start(bf16[64,128]{1,0:T(8,128)(2,1)S(1)} %get-tuple-element.102), channel_id=1, source_target_pairs={{0,8},{4,12},{8,0},{12,4},{1,9},{5,13},{9,1},{13,5},{2,10},{6,14},... | collective-permute-start | bytes 49160 | tf_op jit(solution)/shard_map/ppermute | solution.py:74
  38.5 5.0 %collective-permute-start.22 = (bf16[392,128]{1,0:T(8,128)(2,1)S(1)}, bf16[392,128]{1,0:T(8,128)(2,1)S(1)}, u32[]{:S(2)}, u32[]{:S(2)}) collective-permute-start(bf16[392,128]{1,0:T(8,128)(2,1)S(1)} %get-tuple-element.105.refs_0_), channel_id=1, source_target_pairs={{0,2},{1,0},{2,3},{3,1},{4,6},{5,4},{6,7},{7,5},{8,10},{9,8},{10,1... | collective-permute-start | bytes 301064 | tf_op jit(solution)/shard_map/ppermute | solution.py:86
  39.6 7.2 %collective-permute-start.21 = (bf16[392,128]{1,0:T(8,128)(2,1)S(1)}, bf16[392,128]{1,0:T(8,128)(2,1)S(1)}, u32[]{:S(2)}, u32[]{:S(2)}) collective-permute-start(bf16[392,128]{1,0:T(8,128)(2,1)S(1)} %get-tuple-element.105.refs_0_), channel_id=1, source_target_pairs={{0,3},{1,2},{2,1},{3,0},{4,7},{5,6},{6,5},{7,4},{8,11},{9,10},{10,... | collective-permute-start | bytes 301064 | tf_op jit(solution)/shard_map/ppermute | solution.py:86
  41.0 8.2 %collective-permute-start.20 = (bf16[392,128]{1,0:T(8,128)(2,1)S(1)}, bf16[392,128]{1,0:T(8,128)(2,1)S(1)}, u32[]{:S(2)}, u32[]{:S(2)}) collective-permute-start(bf16[392,128]{1,0:T(8,128)(2,1)S(1)} %get-tuple-element.105.refs_0_), channel_id=1, source_target_pairs={{0,1},{1,3},{2,0},{3,2},{4,5},{5,7},{6,4},{7,6},{8,9},{9,11},{10,8... | collective-permute-start | bytes 301064 | tf_op jit(solution)/shard_map/ppermute | solution.py:86
  49.2 5.6 %collective-permute-start.24 = (bf16[392,128]{1,0:T(8,128)(2,1)S(1)}, bf16[392,128]{1,0:T(8,128)(2,1)S(1)}, u32[]{:S(2)}, u32[]{:S(2)}) collective-permute-start(bf16[392,128]{1,0:T(8,128)(2,1)S(1)} %get-tuple-element.103.refs_0_), channel_id=1, source_target_pairs={{0,8},{4,12},{8,0},{12,4},{16,24},{20,28},{24,16},{28,20},{1,9},{5... | collective-permute-start | bytes 301064 | tf_op jit(solution)/shard_map/ppermute | solution.py:74
  50.8 5.4 %collective-permute-start.28 = (bf16[328,128]{1,0:T(8,128)(2,1)S(1)}, bf16[328,128]{1,0:T(8,128)(2,1)S(1)}, u32[]{:S(2)}, u32[]{:S(2)}) collective-permute-start(bf16[328,128]{1,0:T(8,128)(2,1)S(1)} %get-tuple-element.104), channel_id=1, source_target_pairs={{0,24},{4,28},{8,16},{12,20},{16,8},{20,12},{24,0},{28,4},{1,25},{... | collective-permute-start | bytes 251912 | tf_op jit(solution)/shard_map/ppermute | solution.py:74
  52.3 4.5 %collective-permute-start.26 = (bf16[328,128]{1,0:T(8,128)(2,1)S(1)}, bf16[328,128]{1,0:T(8,128)(2,1)S(1)}, u32[]{:S(2)}, u32[]{:S(2)}) collective-permute-start(bf16[328,128]{1,0:T(8,128)(2,1)S(1)} %get-tuple-element.104), channel_id=1, source_target_pairs={{0,16},{4,20},{8,24},{12,28},{16,0},{20,4},{24,8},{28,12},{1,17},{... | collective-permute-start | bytes 251912 | tf_op jit(solution)/shard_map/ppermute | solution.py:74
  52.8 3.9 %collective-permute-start.23 = (bf16[392,128]{1,0:T(8,128)(2,1)S(1)}, bf16[392,128]{1,0:T(8,128)(2,1)S(1)}, u32[]{:S(2)}, u32[]{:S(2)}) collective-permute-start(bf16[392,128]{1,0:T(8,128)(2,1)S(1)} %get-tuple-element.103.refs_0_), channel_id=1, source_target_pairs={{0,4},{4,0},{8,12},{12,8},{16,20},{20,16},{24,28},{28,24},{1,5},{5... | collective-permute-start | bytes 301064 | tf_op jit(solution)/shard_map/ppermute | solution.py:74
  54.8 3.2 %collective-permute-start.25 = (bf16[392,128]{1,0:T(8,128)(2,1)S(1)}, bf16[392,128]{1,0:T(8,128)(2,1)S(1)}, u32[]{:S(2)}, u32[]{:S(2)}) collective-permute-start(bf16[392,128]{1,0:T(8,128)(2,1)S(1)} %collective-permute-done.24.refs_2_), channel_id=1, source_target_pairs={{0,4},{4,0},{8,12},{12,8},{16,20},{20,16},{24,28},{28,24},{1,5},{5... | collective-permute-start | bytes 301064 | tf_op jit(solution)/shard_map/ppermute | solution.py:74
  56.2 1.3 %collective-permute-start.29 = (bf16[328,128]{1,0:T(8,128)(2,1)S(1)}, bf16[328,128]{1,0:T(8,128)(2,1)S(1)}, u32[]{:S(2)}, u32[]{:S(2)}) collective-permute-start(bf16[328,128]{1,0:T(8,128)(2,1)S(1)} %collective-permute-done.28.refs_6_), channel_id=1, source_target_pairs={{0,4},{4,0},{8,12},{12,8},{16,20},{20,16},{24,28},{28,24},{1,5},{5... | collective-permute-start | bytes 251912 | tf_op jit(solution)/shard_map/ppermute | solution.py:74
  56.7 1.3 %collective-permute-start.27 = (bf16[328,128]{1,0:T(8,128)(2,1)S(1)}, bf16[328,128]{1,0:T(8,128)(2,1)S(1)}, u32[]{:S(2)}, u32[]{:S(2)}) collective-permute-start(bf16[328,128]{1,0:T(8,128)(2,1)S(1)} %collective-permute-done.26.refs_4_), channel_id=1, source_target_pairs={{0,4},{4,0},{8,12},{12,8},{16,20},{20,16},{24,28},{28,24},{1,5},{5... | collective-permute-start | bytes 251912 | tf_op jit(solution)/shard_map/ppermute | solution.py:74
